TPU v7x, 32 devices: a whole 2x2x4 slice. The times are simulated.
32 devices in a mesh: dp: 2 (over y), row: 4 (over z), col: 4 (over x, core).
Axes of the slice: x: 2, y: 2, z: 4, core: 2. Of those that a mesh axis runs over, the one named last changes fastest.
Arguments:
- tokens: bfloat16 [8192, 768], P(('dp', 'row'), 'col'), may hold values from -6 to 6
- prev_logits: float32 [8192, 12], P(('dp', 'row')), may hold values from -3 to 3
- routes: int32 [8192, 2], P('dp'), may hold values from 0 to 11, all different within a row; in each aligned block of 4096 rows (0 to 4095, 4096 to 8191, ...) at most 1280 rows name the same one
- prefix_len: int32 [8], P('dp'), may hold values from 0 to 1024
- norm1_gain: float32 [768], P('col'), may hold values from 0.5 to 1.5
- qkv_weight: bfloat16 [3, 768, 768], P(None, 'col', 'row'), may hold values from -0.21875 to 0.21875
- out_weight: bfloat16 [768, 768], P('row', 'col'), may hold values from -0.875 to 0.875
- norm2_gain: float32 [768], P('col'), may hold values from 0.5 to 1.5
- router_weight: bfloat16 [768, 12], P('col'), may hold values from -0.15625 to 0.15625
- const_weight: bfloat16 [768, 4], P('col'), may hold values from -0.21875 to 0.21875
- const_values: float32 [2, 768], P(None, 'col'), may hold values from -6 to 6
- gate_weight: bfloat16 [8, 768, 2048], P(None, 'col', 'row'), may hold values from -0.21875 to 0.21875
- up_weight: bfloat16 [8, 768, 2048], P(None, 'col', 'row'), may hold values from -0.21875 to 0.21875
- down_weight: bfloat16 [8, 2048, 768], P(None, 'row', 'col'), may hold values from -0.25 to 0.25
- cotangent: bfloat16 [8192, 768], P(('dp', 'row'), 'col'), may hold values from -6 to 6
Outputs:
- layer_out: float32 [8192, 768], P(('dp', 'row'), 'col')
- tokens_grad: float32 [8192, 768], P(('dp', 'row'), 'col')
- prev_grad: float32 [8192, 12], P(('dp', 'row'))
- norm1_gain_grad: float32 [768], P('col')
- qkv_grad: float32 [3, 768, 768], P(None, 'col', 'row')
- out_weight_grad: float32 [768, 768], P('row', 'col')
- norm2_gain_grad: float32 [768], P('col')
- router_grad: float32 [768, 12], P('col')
- const_weight_grad: float32 [768, 4], P('col')
- const_values_grad: float32 [2, 768], P(None, 'col')
- gate_grad: float32 [8, 768, 2048], P(None, 'col', 'row')
- up_grad: float32 [8, 768, 2048], P(None, 'col', 'row')
- down_grad: float32 [8, 2048, 768], P(None, 'row', 'col')
Inputs may be any that keep to these rules, and one draw needn't show every extreme that they name: `routes`: each token names two different experts: 0 to 7 are feed-forward experts, 8 the zero expert, 9 the copy expert, 10 and 11 the constant experts. Within each dp group's 4096 tokens no expert is named more than 1280 times, a bound that some block reaches. The first prefix_len tokens of a sequence see one another in both directions; later tokens see the prefix and the tokens before them.
All inputs are finite; a program needn't handle non-finite values.
Results may differ from a plain program's by a relative error of at most 0.015.
Values may be sent and summed in bfloat16 or wider, within the bound.
No kernel may reach another device: no remote copies, remote signals or barrier semaphores. Data moves between devices by JAX's collectives and lax.ppermute only.
A program may use at most 256 MiB of HBM per device.

v0:
```python
import jax
import jax.numpy as jnp
from jax import lax
from jax.sharding import PartitionSpec as P

HD = 64
LEN = 1024
CAP = 1280


EPS = 1e-06
HIGH = lax.Precision.HIGHEST
NEGATIVE = -1e30


def rotate(vec, positions, sign):
    half = vec.shape[-1] // 2
    freq = 10000.0 ** (-jnp.arange(half, dtype=jnp.float32) / half)
    angle = positions[:, None].astype(jnp.float32) * freq[None, :]
    cosine = jnp.cos(angle)[:, None, :]
    sine = sign * jnp.sin(angle)[:, None, :]
    first = vec[..., :half]
    second = vec[..., half:]
    return jnp.concatenate(
        [first * cosine - second * sine, second * cosine + first * sine], axis=-1
    )


def visible(prefix, length):
    places = jnp.arange(length, dtype=jnp.int32)
    return (places[None, :] <= places[:, None]) | (places[None, :] < prefix)


def slot_tables(routes, experts, kinds, capacity):
    flat = routes.reshape(-1)
    pairs = flat.shape[0]
    onehot = (flat[:, None] == jnp.arange(kinds, dtype=jnp.int32)[None, :]).astype(jnp.int32)
    before = jnp.cumsum(onehot, axis=0) - onehot
    place = jnp.sum(before * onehot, axis=1)
    usable = flat < experts
    target = jnp.where(usable, flat * capacity + place, experts * capacity)
    table = jnp.full((experts * capacity,), -1, dtype=jnp.int32)
    table = table.at[target].set(jnp.arange(pairs, dtype=jnp.int32), mode="drop")
    slot_of = jnp.where(usable, target, 0)
    return (table.reshape(experts, capacity), slot_of.reshape(-1, 2), usable.reshape(-1, 2))


def scaled_scores(query, keys, prefix):
    scores = jnp.einsum("qhd,khd->hqk", query, keys, preferred_element_type=jnp.float32) * HD ** (
        -0.5
    )
    return jnp.where(visible(prefix, query.shape[0])[None], scores, NEGATIVE)


def attend_forward(pieces):
    query, keys, values, prefix = pieces
    scores = scaled_scores(query, keys, prefix)
    row_max = jnp.max(scores, axis=-1, keepdims=True)
    weights = jnp.exp(scores - row_max)
    total = jnp.sum(weights, axis=-1, keepdims=True)
    probs = (weights / total).astype(jnp.bfloat16)
    mixed = jnp.einsum("hqk,khd->qhd", probs, values, preferred_element_type=jnp.float32)
    return (mixed.reshape(query.shape[0], -1), (row_max + jnp.log(total))[..., 0])


def attend_backward(pieces):
    query, keys, values, prefix, logsum, grad = pieces
    scores = scaled_scores(query, keys, prefix)
    probs = jnp.exp(scores - logsum[..., None])
    grad_probs = jnp.einsum("qhd,khd->hqk", grad, values, preferred_element_type=jnp.float32)
    inner = jnp.sum(probs * grad_probs, axis=-1, keepdims=True)
    grad_scores = (probs * (grad_probs - inner)).astype(jnp.bfloat16)
    scale = HD ** (-0.5)
    grad_query = (
        jnp.einsum("hqk,khd->qhd", grad_scores, keys, preferred_element_type=jnp.float32) * scale
    )
    grad_keys = (
        jnp.einsum("hqk,qhd->khd", grad_scores, query, preferred_element_type=jnp.float32) * scale
    )
    grad_values = jnp.einsum(
        "hqk,qhd->khd", probs.astype(jnp.bfloat16), grad, preferred_element_type=jnp.float32
    )
    return (grad_query, grad_keys, grad_values)


def total_features(values):
    return lax.psum(values, "col")


def gather_tokens(values):
    return lax.all_gather(values, "row", axis=0, tiled=True)


def gather_slots(values):
    return lax.all_gather(values, "col", axis=0, tiled=True)


def cols_total(term, rows):
    return lax.psum_scatter(
        term(jnp.int32(0), lax.axis_size("col") * rows), "col", scatter_dimension=0, tiled=True
    )


def rows_total(term, rows):
    return lax.psum_scatter(
        term(jnp.int32(0), lax.axis_size("row") * rows), "row", scatter_dimension=0, tiled=True
    )


def shards(
    tokens,
    prev_logits,
    routes,
    prefix_len,
    norm1_gain,
    qkv_weight,
    out_weight,
    norm2_gain,
    router_weight,
    const_weight,
    const_values,
    gate_weight,
    up_weight,
    down_weight,
    cotangent,
):
    row_index = lax.axis_index("row")
    col_index = lax.axis_index("col")
    col_count = lax.axis_size("col")
    local_rows, local_width = tokens.shape
    group_rows = routes.shape[0]
    width = local_width * col_count
    col_rows = group_rows // col_count
    quarter = CAP // col_count
    experts = gate_weight.shape[0]
    hidden_width = gate_weight.shape[2]
    kinds = router_weight.shape[1]
    heads_here = qkv_weight.shape[2] // HD
    seqs_here = col_rows // LEN
    hidden = tokens.astype(jnp.float32)
    square1 = total_features(jnp.sum(hidden * hidden, axis=1))
    inverse1 = lax.rsqrt(square1 / width + EPS)[:, None]
    normed1 = hidden * inverse1 * norm1_gain[None, :]
    act_all = gather_tokens(normed1.astype(jnp.bfloat16))

    def qkv_term(start, count):
        return jnp.einsum("td,jde->tje", act_all, qkv_weight, preferred_element_type=jnp.float32)

    qkv = cols_total(qkv_term, col_rows)
    positions = jnp.arange(col_rows, dtype=jnp.int32) % LEN
    spread = (col_rows, heads_here, HD)
    query = rotate(qkv[:, 0].reshape(spread), positions, 1.0).astype(jnp.bfloat16)
    keys = rotate(qkv[:, 1].reshape(spread), positions, 1.0).astype(jnp.bfloat16)
    values = qkv[:, 2].reshape(spread).astype(jnp.bfloat16)
    split = (seqs_here, LEN, heads_here, HD)
    prefix_here = lax.dynamic_slice_in_dim(prefix_len, col_index * seqs_here, seqs_here, 0)
    mixed, logsum = lax.map(
        attend_forward,
        (query.reshape(split), keys.reshape(split), values.reshape(split), prefix_here),
    )
    attn_all = gather_slots(mixed.reshape(col_rows, -1).astype(jnp.bfloat16))

    def proj_term(start, count):
        return jnp.dot(attn_all, out_weight, preferred_element_type=jnp.float32)

    mid = hidden + rows_total(proj_term, local_rows)
    scaled2 = mid * norm2_gain[None, :]
    router_all = jnp.concatenate([router_weight, const_weight], axis=1).astype(jnp.float32)
    router_part = jnp.dot(scaled2, router_all, precision=HIGH, preferred_element_type=jnp.float32)
    square2, summed = total_features((jnp.sum(mid * mid, axis=1), router_part))
    inverse2 = lax.rsqrt(square2 / width + EPS)[:, None]
    normed2 = scaled2 * inverse2
    logits = summed[:, :kinds] * inverse2 + prev_logits
    alpha = jax.nn.softmax((summed[:, kinds:] * inverse2).reshape(local_rows, 2, 2), axis=-1)
    local_routes = lax.dynamic_slice_in_dim(routes, row_index * local_rows, local_rows, 0)
    route_hot = (
        local_routes[..., None] == jnp.arange(kinds, dtype=jnp.int32)[None, None, :]
    ).astype(jnp.float32)
    chosen = jnp.sum(route_hot * logits[:, None, :], axis=-1)
    gates = jax.nn.softmax(chosen, axis=-1)
    moe_in = gather_tokens(normed2.astype(jnp.bfloat16))
    table, slot_of, usable = slot_tables(routes, experts, kinds, CAP)
    source = jnp.maximum(table, 0) // 2
    filled = (table >= 0).astype(jnp.bfloat16)
    gate_up_all = jnp.concatenate([gate_weight, up_weight], axis=2)
    full_in = lax.all_gather(moe_in, "col", axis=1, tiled=True)
    full_weights = lax.all_gather(gate_up_all, "col", axis=1, tiled=True)
    picked_rows = []
    gate_parts = []
    up_parts = []
    hidden_parts = []
    slot_outputs = []
    for expert in range(experts):
        picked = jnp.take(moe_in, source[expert], axis=0)
        my_slots = lax.dynamic_slice_in_dim(source[expert], col_index * quarter, quarter, 0)
        picked_full = jnp.take(full_in, my_slots, axis=0)
        gate_up = jnp.dot(picked_full, full_weights[expert], preferred_element_type=jnp.float32)
        gate_part = gate_up[:, :hidden_width]
        up_part = gate_up[:, hidden_width:]
        hidden_all = gather_slots((jax.nn.silu(gate_part) * up_part).astype(jnp.bfloat16))
        slot_outputs.append(
            jnp.dot(hidden_all, down_weight[expert], preferred_element_type=jnp.float32)
        )
        picked_rows.append(picked)
        gate_parts.append(gate_part)
        up_parts.append(up_part)
        hidden_parts.append(hidden_all)
    slot_out = jnp.concatenate(slot_outputs, axis=0)

    def combine_term(start, count):
        located = slot_of.reshape(-1)
        alive_mask = usable.astype(jnp.float32)
        fetched = jnp.take(slot_out, located, axis=0).reshape(count, 2, local_width)
        return fetched * alive_mask[..., None]

    ffn_out = rows_total(combine_term, local_rows)
    is_ffn = (local_routes < experts).astype(jnp.float32)[..., None]
    is_copy = (local_routes == experts + 1).astype(jnp.float32)[..., None]
    first_const = (local_routes == experts + 2).astype(jnp.float32)[..., None]
    second_const = (local_routes == experts + 3).astype(jnp.float32)[..., None]
    constant = alpha[:, :, 0:1] * normed2[:, None, :] + alpha[:, :, 1:2] * const_values[None, :, :]
    branch = (
        ffn_out
        + is_copy * normed2[:, None, :]
        + first_const * constant[:, 0:1, :]
        + second_const * constant[:, 1:2, :]
    )
    result = mid + jnp.sum(gates[..., None] * branch, axis=1)
    grad_out = cotangent.astype(jnp.float32)
    grad_branch = gates[..., None] * grad_out[:, None, :]
    grad_const = jnp.stack(
        [jnp.sum(first_const * grad_branch, axis=1), jnp.sum(second_const * grad_branch, axis=1)],
        axis=1,
    )
    alpha_local = jnp.stack(
        [
            jnp.sum(grad_const * normed2[:, None, :], axis=-1),
            jnp.sum(grad_const * const_values[None, :, :], axis=-1),
        ],
        axis=-1,
    )
    grad_gate, grad_alpha = total_features(
        (jnp.sum(grad_out[:, None, :] * branch, axis=-1), alpha_local)
    )
    grad_chosen = gates * (grad_gate - jnp.sum(gates * grad_gate, axis=-1, keepdims=True))
    grad_logits = jnp.sum(grad_chosen[..., None] * route_hot, axis=1)
    grad_const_logits = (
        alpha * (grad_alpha - jnp.sum(alpha * grad_alpha, axis=-1, keepdims=True))
    ).reshape(local_rows, 4)
    grad_router_in = jnp.concatenate([grad_logits, grad_const_logits], axis=1)
    grad_normed2 = jnp.sum(is_copy * grad_branch, axis=1) + jnp.sum(
        alpha[:, :, 0:1] * grad_const, axis=1
    )
    grad_normed2 = grad_normed2 + jnp.einsum(
        "tk,dk->td", grad_router_in, router_all, precision=HIGH
    )
    router_part_grad = jnp.einsum("td,tk->dk", normed2, grad_router_in, precision=HIGH)
    const_values_part = jnp.sum(alpha[:, :, 1:2] * grad_const, axis=0)
    slot_grads_in = gather_tokens((grad_branch * is_ffn).astype(jnp.bfloat16))
    pair_rows = slot_grads_in.reshape(group_rows * 2, local_width)
    slot_grads = []
    for expert in range(experts):
        slot_grads.append(
            jnp.take(pair_rows, jnp.maximum(table[expert], 0), axis=0) * filled[expert][:, None]
        )
    down_full = lax.all_gather(down_weight, "col", axis=2, tiled=True)
    mine_full = lax.all_to_all(
        jnp.stack(slot_grads, axis=0), "col", split_axis=1, concat_axis=2, tiled=True
    )
    grad_inputs = []
    gate_up_grads = []
    down_grads = []
    for expert in range(experts):
        slot_grad = slot_grads[expert]
        grad_hidden = jnp.einsum(
            "cd,fd->cf", mine_full[expert], down_full[expert], preferred_element_type=jnp.float32
        )
        gate_part = gate_parts[expert]
        sigma = jax.nn.sigmoid(gate_part)
        grad_gate_part = grad_hidden * up_parts[expert] * sigma * (1.0 + gate_part * (1.0 - sigma))
        grad_up_part = grad_hidden * gate_part * sigma
        grad_both = gather_slots(
            jnp.concatenate([grad_gate_part, grad_up_part], axis=1).astype(jnp.bfloat16)
        )
        grad_inputs.append(
            jnp.einsum(
                "cf,df->cd", grad_both, gate_up_all[expert], preferred_element_type=jnp.float32
            )
        )
        gate_up_grads.append(
            jnp.einsum(
                "cd,cf->df", picked_rows[expert], grad_both, preferred_element_type=jnp.float32
            )
        )
        down_grads.append(
            jnp.einsum(
                "cf,cd->fd", hidden_parts[expert], slot_grad, preferred_element_type=jnp.float32
            )
        )
    gate_up_part = jnp.stack(gate_up_grads, axis=0)
    down_part = jnp.stack(down_grads, axis=0)
    grad_slot_all = jnp.concatenate(grad_inputs, axis=0)

    def return_term(start, count):
        located = slot_of.reshape(-1)
        alive_mask = usable.astype(jnp.float32)
        fetched = jnp.take(grad_slot_all, located, axis=0).reshape(count, 2, local_width)
        return jnp.sum(fetched * alive_mask[..., None], axis=1)

    grad_normed2 = grad_normed2 + rows_total(return_term, local_rows)
    inner2 = total_features(jnp.sum(mid * norm2_gain[None, :] * grad_normed2, axis=1))
    gain2_part = jnp.sum(mid * inverse2 * grad_normed2, axis=0)
    grad_mid = (
        grad_out
        + inverse2 * norm2_gain[None, :] * grad_normed2
        - mid * inverse2**3 * (inner2[:, None] / width)
    )
    grad_mid_all = gather_tokens(grad_mid.astype(jnp.bfloat16))
    out_weight_part = jnp.einsum(
        "ta,td->ad", attn_all, grad_mid_all, preferred_element_type=jnp.float32
    )

    def attn_term(start, count):
        return jnp.einsum("td,ad->ta", grad_mid_all, out_weight, preferred_element_type=jnp.float32)

    grad_attn = cols_total(attn_term, col_rows).astype(jnp.bfloat16)
    grad_query, grad_keys, grad_values = lax.map(
        attend_backward,
        (
            query.reshape(split),
            keys.reshape(split),
            values.reshape(split),
            prefix_here,
            logsum,
            grad_attn.reshape(split),
        ),
    )
    grad_query = rotate(grad_query.reshape(spread), positions, -1.0)
    grad_keys = rotate(grad_keys.reshape(spread), positions, -1.0)
    grad_qkv = (
        jnp.stack([grad_query, grad_keys, grad_values.reshape(spread)], axis=1)
        .reshape(col_rows, 3, -1)
        .astype(jnp.bfloat16)
    )
    grad_qkv_all = gather_slots(grad_qkv)
    qkv_part = jnp.einsum("td,tje->jde", act_all, grad_qkv_all, preferred_element_type=jnp.float32)

    def input_term(start, count):
        return jnp.einsum(
            "tje,jde->td", grad_qkv_all, qkv_weight, preferred_element_type=jnp.float32
        )

    grad_normed1 = rows_total(input_term, local_rows)
    inner1 = total_features(jnp.sum(hidden * norm1_gain[None, :] * grad_normed1, axis=1))
    gain1_part = jnp.sum(hidden * inverse1 * grad_normed1, axis=0)
    grad_tokens = (
        grad_mid
        + inverse1 * norm1_gain[None, :] * grad_normed1
        - hidden * inverse1**3 * (inner1[:, None] / width)
    )
    gain1_grad, gain2_grad, router_sums, const_values_grad = lax.psum(
        (gain1_part, gain2_part, router_part_grad, const_values_part), ("dp", "row")
    )
    gate_up_sum, down_sum, out_weight_sum, qkv_sum = (
        lax.psum(gate_up_part.astype(jnp.bfloat16), "dp").astype(jnp.float32),
        lax.psum(down_part.astype(jnp.bfloat16), "dp").astype(jnp.float32),
        lax.psum(out_weight_part.astype(jnp.bfloat16), "dp").astype(jnp.float32),
        lax.psum(qkv_part.astype(jnp.bfloat16), "dp").astype(jnp.float32),
    )
    return (
        result,
        grad_tokens,
        grad_logits,
        gain1_grad,
        qkv_sum,
        out_weight_sum,
        gain2_grad,
        router_sums[:, :kinds],
        router_sums[:, kinds:],
        const_values_grad,
        gate_up_sum[:, :, :hidden_width],
        gate_up_sum[:, :, hidden_width:],
        down_sum,
    )


def solution(mesh):
    return jax.shard_map(
        shards,
        mesh=mesh,
        in_specs=(
            P(("dp", "row"), "col"),
            P(("dp", "row"), None),
            P("dp", None),
            P("dp"),
            P("col"),
            P(None, "col", "row"),
            P("row", "col"),
            P("col"),
            P("col", None),
            P("col", None),
            P(None, "col"),
            P(None, "col", "row"),
            P(None, "col", "row"),
            P(None, "row", "col"),
            P(("dp", "row"), "col"),
        ),
        out_specs=(
            P(("dp", "row"), "col"),
            P(("dp", "row"), "col"),
            P(("dp", "row"), None),
            P("col"),
            P(None, "col", "row"),
            P("row", "col"),
            P("col"),
            P("col", None),
            P("col", None),
            P(None, "col"),
            P(None, "col", "row"),
            P(None, "col", "row"),
            P(None, "row", "col"),
        ),
        check_vma=False,
    )
```

profile of v0, /device:TPU:0, one launch (start us, length us, event | category | flops | bytes accessed | tf_op | source)
XLA Modules:
  0.0 1883.9 jit_solution(7624814079427374899)
XLA Ops:
  8.3 8.4 psum.105
  21.0 36.3 %all-gather.26.cloned.1.call-done = bf16[4096,192]{0,1:T(8,128)(2,1)} async-done(((bf16[1024,192]{0,1:T(8,128)(2,1)}), bf16[4096,192]{0,1:T(8,128)(2,1)}) %all-gather.26.cloned.1.call-update) | async-done | bytes 1572880 | tf_op jit(solution)/shard_map/all_gather | solution.py:91
  57.3 6.5 fusion.213
  67.3 73.3 %reduce-scatter.6.cloned.1.call-done = f32[1024,3,192]{0,2,1:T(8,128)} async-done(((f32[4096,3,192]{0,2,1:T(8,128)}), f32[1024,3,192]{0,2,1:T(8,128)}) %reduce-scatter.6.cloned.1.call-update) | async-done | bytes 2359312 | tf_op jit(solution)/shard_map/reduce_scatter | solution.py:99
  152.8 19.7 %all-gather.28.cloned.1.call-done = bf16[4096,192]{0,1:T(8,128)(2,1)} async-done(((bf16[1024,192]{0,1:T(8,128)(2,1)}), bf16[4096,192]{0,1:T(8,128)(2,1)}) %all-gather.28.cloned.1.call-update) | async-done | bytes 1572880 | tf_op jit(solution)/shard_map/all_gather | solution.py:95
  176.4 60.5 %reduce-scatter.8.cloned.1.call-done = f32[1024,192]{0,1:T(8,128)} async-done(((f32[4096,192]{0,1:T(8,128)}), f32[1024,192]{0,1:T(8,128)}) %reduce-scatter.8.cloned.1.call-update) | async-done | bytes 786448 | tf_op jit(solution)/shard_map/reduce_scatter | solution.py:105
  238.2 6.3 psum.107
  247.6 29.9 %all-reduce.8.cloned.1.call-done = f32[1024,16]{0,1:T(8,128)} async-done(((f32[1024,16]{0,1:T(8,128)}), f32[1024,16]{0,1:T(8,128)}) %all-reduce.8.cloned.1.call-update) | async-done | bytes 65552 | tf_op jit(solution)/shard_map/psum | solution.py:87
  279.7 36.9 %all-gather.30.cloned.1.call-done = bf16[4096,192]{0,1:T(8,128)(2,1)} async-done(((bf16[1024,192]{0,1:T(8,128)(2,1)}), bf16[4096,192]{0,1:T(8,128)(2,1)}) %all-gather.30.cloned.1.call-update) | async-done | bytes 1572880 | tf_op jit(solution)/shard_map/all_gather | solution.py:91
  335.0 30.9 %scatter_custom_fusion = s32[10240]{0:T(1024)S(1)} fusion(s32[8192]{0:T(1024)S(1)} %bitcast.354, s32[8192]{0:T(1024)S(1)} %iota.111, s32[]{:T(128)} %constant.186.clone.1), kind=kCustom, calls=%fused_computation.381 | custom fusion | bytes 40964 | tf_op jit(solution)/shard_map/scatter | solution.py:43
  367.3 13.8 all-gather.52.cloned.1.call-done
  381.1 11.2 copy.296
  392.3 8.3 reshape.442
  400.6 5.9 gather_fusion.13
  406.6 6.1 gather_fusion.12
  412.7 7.0 gather_fusion.11
  419.7 6.7 gather_fusion.10
  426.4 6.8 gather_fusion.9
  433.1 5.9 gather_fusion.14
  439.0 6.8 gather_fusion.15
  445.8 6.3 gather_fusion.16
  458.1 14.2 copy.297
  478.5 97.7 %all-to-all-done = bf16[8,1280,192]{2,0,1:T(8,128)(2,1)} async-done(((bf16[8,1280,192]{2,0,1:T(8,128)(2,1)}), bf16[8,1280,192]{2,0,1:T(8,128)(2,1)}, u32[]{:S(2)}, u32[]{:S(2)}) %all-to-all-start) | async-done | bytes 3932192 | tf_op jit(solution)/shard_map/all_to_all | solution.py:267
  576.2 8.5 copy.298
  588.8 8.7 copy.271
  597.5 6.6 gather_fusion
  610.7 6.6 gather_fusion.1
  622.9 6.6 gather_fusion.2
  634.7 7.2 gather_fusion.3
  647.2 6.1 gather_fusion.4
  658.2 6.1 gather_fusion.5
  669.5 6.1 gather_fusion.6
  680.9 6.1 gather_fusion.7
  715.6 11.5 all-gather.46.cloned.1.call-done
  730.1 16.7 all-gather.48.cloned.1.call-done
  749.6 16.7 all-gather.50.cloned.1.call-done
  769.3 10.6 copy.279
  779.9 35.5 %gather_fusion.8 = f32[8192,192]{1,0:T(8,128)} fusion(f32[10240,192]{1,0:T(8,128)} %copy.279, s32[8192]{0:T(1024)S(1)} %broadcast_clamp_fusion), kind=kCustom, calls=%fused_computation.1.clone | custom fusion | bytes 12615680 | tf_op jit(solution)/shard_map/jit(_take)/gather | solution.py:213
  824.8 23.4 %all-gather.60.cloned.1.call-done = bf16[1280,1024]{1,0:T(8,128)(2,1)} async-done(((bf16[320,1024]{1,0:T(8,128)(2,1)}), bf16[1280,1024]{1,0:T(8,128)(2,1)}) %all-gather.60.cloned.1.call-update) | async-done | bytes 2621456 | tf_op jit(solution)/shard_map/all_gather | solution.py:95
  852.0 23.3 %all-gather.62.cloned.1.call-done = bf16[1280,1024]{1,0:T(8,128)(2,1)} async-done(((bf16[320,1024]{1,0:T(8,128)(2,1)}), bf16[1280,1024]{1,0:T(8,128)(2,1)}) %all-gather.62.cloned.1.call-update) | async-done | bytes 2621456 | tf_op jit(solution)/shard_map/all_gather | solution.py:95
  879.1 23.4 %all-gather.64.cloned.1.call-done = bf16[1280,1024]{1,0:T(8,128)(2,1)} async-done(((bf16[320,1024]{1,0:T(8,128)(2,1)}), bf16[1280,1024]{1,0:T(8,128)(2,1)}) %all-gather.64.cloned.1.call-update) | async-done | bytes 2621456 | tf_op jit(solution)/shard_map/all_gather | solution.py:95
  906.2 23.2 %all-gather.66.cloned.1.call-done = bf16[1280,1024]{1,0:T(8,128)(2,1)} async-done(((bf16[320,1024]{1,0:T(8,128)(2,1)}), bf16[1280,1024]{1,0:T(8,128)(2,1)}) %all-gather.66.cloned.1.call-update) | async-done | bytes 2621456 | tf_op jit(solution)/shard_map/all_gather | solution.py:95
  933.2 23.3 %all-gather.68.cloned.1.call-done = bf16[1280,1024]{1,0:T(8,128)(2,1)} async-done(((bf16[320,1024]{1,0:T(8,128)(2,1)}), bf16[1280,1024]{1,0:T(8,128)(2,1)}) %all-gather.68.cloned.1.call-update) | async-done | bytes 2621456 | tf_op jit(solution)/shard_map/all_gather | solution.py:95
  960.3 23.2 %all-gather.70.cloned.1.call-done = bf16[1280,1024]{1,0:T(8,128)(2,1)} async-done(((bf16[320,1024]{1,0:T(8,128)(2,1)}), bf16[1280,1024]{1,0:T(8,128)(2,1)}) %all-gather.70.cloned.1.call-update) | async-done | bytes 2621456 | tf_op jit(solution)/shard_map/all_gather | solution.py:95
  987.3 10.3 copy.299
  997.6 35.5 %gather_fusion.17 = f32[8192,192]{1,0:T(8,128)} fusion(f32[10240,192]{1,0:T(8,128)} %copy.299, s32[8192]{0:T(1024)S(1)} %broadcast_clamp_fusion), kind=kCustom, calls=%fused_computation.11.clone | custom fusion | bytes 12615680 | tf_op jit(solution)/shard_map/jit(_take)/gather | solution.py:307
  1033.1 14.3 broadcast_select_fusion
  1047.4 10.5 reshape.439
  1057.9 10.5 reshape.443
  1068.4 27.2 %multiply_reduce_fusion.1 = (f32[4096,192]{1,0:T(8,128)}, f32[4096,2,192]{2,1,0:T(2,128)}) fusion(f32[4096,2,192]{2,1,0:T(2,128)} %reshape.443, f32[4096,2]{1,0:T(8,128)S(1)} %copy.280, f32[4096,2,192]{2,1,0:T(2,128)} %reshape.439), kind=kLoop, calls=%fused_computation.37 | loop fusion | flops 3932160 | bytes 22052864 | tf_op jit(solution)/shard_map/reduce_sum | solution.py:308
  1095.7 5.3 copy.300
  1105.4 281.2 %all-reduce.10.cloned.1.call-done = f32[4096,2,192]{2,1,0:T(2,128)} async-done(((f32[4096,2,192]{2,1,0:T(2,128)}), f32[4096,2,192]{2,1,0:T(2,128)}) %all-reduce.10.cloned.1.call-update) | async-done | bytes 6291472
  1398.0 11.7 all-reduce.2
  1410.0 39.0 %reduce-scatter.10.cloned.1.call-done = f32[1024,192]{0,1:T(8,128)} async-done(((f32[4096,192]{0,1:T(8,128)}), f32[1024,192]{0,1:T(8,128)}) %reduce-scatter.10.cloned.1.call-update) | async-done | bytes 786448 | tf_op jit(solution)/shard_map/reduce_scatter | solution.py:105
  1451.7 6.1 psum.110
  1458.9 36.8 %all-gather.72.cloned.1.call-done = bf16[4096,192]{0,1:T(8,128)(2,1)} async-done(((bf16[1024,192]{0,1:T(8,128)(2,1)}), bf16[4096,192]{0,1:T(8,128)(2,1)}) %all-gather.72.cloned.1.call-update) | async-done | bytes 1572880 | tf_op jit(solution)/shard_map/all_gather | solution.py:91
  1502.6 33.6 %reduce-scatter.12.cloned.1.call-done = f32[1024,192]{0,1:T(8,128)} async-done(((f32[4096,192]{0,1:T(8,128)}), f32[1024,192]{0,1:T(8,128)}) %reduce-scatter.12.cloned.1.call-update) | async-done | bytes 786448 | tf_op jit(solution)/shard_map/reduce_scatter | solution.py:99
  1537.4 6.3 multiply_reduce_fusion
  1639.8 5.6 convolution_bitcast_fusion
  1647.3 119.6 %all-reduce.12.cloned.1.call-done = (bf16[3,192,192]{1,2,0:T(8,128)(2,1)}, bf16[8,192,1024]{2,1,0:T(8,128)(2,1)}, bf16[192,192]{1,0:T(8,128)(2,1)}, bf16[8,512,192]{1,2,0:T(8,128)(2,1)}) async-done(((bf16[3,192,192]{1,2,0:T(8,128)(2,1)}, bf16[8,192,1024]{2,1,0:T(8,128)(2,1)}, bf16[192,192]{1,0:T(8,128)(2,1)}, bf16[8,512,192]{1,2,0:T(8,128)(2,1)}), (bf16[3,192,192]{1,2,0:T(8,128)(2,1)}, ...) | async-done | bytes 5013520 | tf_op jit(solution)/shard_map/psum | solution.py:368
  1772.2 5.6 fusion.206
  1777.8 51.7 %reduce-scatter.14.cloned.1.call-done = f32[1024,192]{0,1:T(8,128)} async-done(((f32[4096,192]{0,1:T(8,128)}), f32[1024,192]{0,1:T(8,128)}) %reduce-scatter.14.cloned.1.call-update) | async-done | bytes 786448 | tf_op jit(solution)/shard_map/reduce_scatter | solution.py:105
  1830.9 36.7 %all-reduce.1 = (f32[192]{0:T(256)}, f32[192]{0:T(256)}, f32[192,16]{0,1:T(8,128)S(1)}, f32[2,192]{1,0:T(2,128)}) all-reduce(f32[192]{0:T(256)S(1)} %get-tuple-element.154, f32[192]{0:T(256)S(1)} %copy-done.161, f32[192,16]{0,1:T(8,128)S(1)} %fusion.160, ...), channel_id=1, replica_groups=mesh['dp'=2,'row'=4,'col'=4] {'dp','row'}, use_global_device_ids=true, to_apply=%region_42.46 | all-reduce | flops 3840 | bytes 30720 | tf_op jit(solution)/shard_map/psum | solution.py:361
  1868.2 5.6 psum.111
  (651 shorter events, 308.1 us)
Async XLA Ops:
  7.2 165.4 %copy-start = (bf16[192,192]{1,0:T(8,128)(2,1)S(1)}, bf16[192,192]{1,0:T(8,128)(2,1)}, u32[]{:S(2)}) copy-start(bf16[192,192]{1,0:T(8,128)(2,1)} %param.29) | copy-start | bytes 221188
  7.2 50.1 %all-gather.26.cloned.1.call-start = ((), (), s32[]{:S(2)}) async-start(), calls=%async_computation.6 | async-start | bytes 1966080 | tf_op jit(solution)/shard_map/all_gather | solution.py:91
  19.8 120.8 %reduce-scatter.6.cloned.1.call-start = ((), (), s32[]{:S(2)}) async-start(), calls=%async_computation.7 | async-start | bytes 11796480 | tf_op jit(solution)/shard_map/reduce_scatter | solution.py:99
  63.8 108.8 %all-gather.28.cloned.1.call-start = ((), (), s32[]{:S(2)}) async-start(), calls=%async_computation.8 | async-start | bytes 1966080 | tf_op jit(solution)/shard_map/all_gather | solution.py:95
  66.9 75.4 %copy-start.56 = (f32[1024,32]{0,1:T(8,128)}, f32[1024,32]{0,1:T(8,128)S(1)}, u32[]{:S(2)}) copy-start(f32[1024,32]{0,1:T(8,128)S(1)} %get-tuple-element.282) | copy-start | bytes 393220
  152.8 84.1 %reduce-scatter.8.cloned.1.call-start = ((), (), s32[]{:S(2)}) async-start(), calls=%async_computation.9 | async-start | bytes 3932160 | tf_op jit(solution)/shard_map/reduce_scatter | solution.py:105
  176.3 60.6 %copy-start.7 = (bf16[1024,192]{0,1:T(8,128)(2,1)S(1)}, bf16[1024,192]{0,1:T(8,128)(2,1)}, u32[]{:S(2)}) copy-start(bf16[1024,192]{0,1:T(8,128)(2,1)} %param.23) | copy-start | bytes 1179652
  176.3 68.8 %copy-start.116 = (bf16[192,12]{0,1:T(8,128)(2,1)S(1)}, bf16[192,12]{0,1:T(8,128)(2,1)}, u32[]{:S(2)}) copy-start(bf16[192,12]{0,1:T(8,128)(2,1)} %param.31) | copy-start | bytes 13828
  176.3 68.8 %copy-start.125 = (f32[192]{0:T(256)S(1)}, f32[192]{0:T(256)}, u32[]{:S(2)}) copy-start(f32[192]{0:T(256)} %param.30) | copy-start | bytes 2308
  176.3 68.8 %copy-start.143 = (bf16[192,4]{0,1:T(4,128)(2,1)S(1)}, bf16[192,4]{0,1:T(4,128)(2,1)}, u32[]{:S(2)}) copy-start(bf16[192,4]{0,1:T(4,128)(2,1)} %param.32) | copy-start | bytes 4612
  176.3 71.2 %copy-start.14 = (bf16[1024,192]{0,1:T(8,128)(2,1)S(1)}, bf16[1024,192]{0,1:T(8,128)(2,1)}, u32[]{:S(2)}) copy-start(bf16[1024,192]{0,1:T(8,128)(2,1)} %param.37) | copy-start | bytes 1179652
  176.3 101.3 %all-reduce.8.cloned.1.call-start = ((), (), s32[]{:S(2)}) async-start(), calls=%async_computation.10 | async-start | bytes 131072 | tf_op jit(solution)/shard_map/psum | solution.py:87
  246.2 70.4 %all-gather.30.cloned.1.call-start = ((), (), s32[]{:S(2)}) async-start(), calls=%async_computation.11 | async-start | bytes 1966080 | tf_op jit(solution)/shard_map/all_gather | solution.py:91
  247.4 133.7 %all-gather.52.cloned.1.call-start = ((), (), s32[]{:S(2)}) async-start(), calls=%async_computation.22 | async-start | bytes 3932160 | tf_op jit(solution)/shard_map/all_gather | solution.py:91
  247.6 69.1 %copy-start.10 = (f32[1024,192]{0,1:T(8,128)}, f32[1024,192]{0,1:T(8,128)S(1)}, u32[]{:S(2)}) copy-start(f32[1024,192]{0,1:T(8,128)S(1)} %convert_element_type.197) | copy-start | bytes 2359300
  247.6 69.0 %copy-start.91 = (s32[1024,2]{0,1:T(2,128)}, s32[1024,2]{0,1:T(2,128)S(1)}, u32[]{:S(2)}) copy-start(s32[1024,2]{0,1:T(2,128)S(1)} %get-tuple-element.178) | copy-start | bytes 24580
  279.7 309.1 %all-gather.32.cloned.1.call-start = ((), (), s32[]{:S(2)}) async-start(), calls=%async_computation.12 | async-start | bytes 7864320 | tf_op jit(solution)/shard_map/all_gather | solution.py:186
  316.7 287.3 %all-gather.34.cloned.1.call-start = ((), (), s32[]{:S(2)}) async-start(), calls=%async_computation.13 | async-start | bytes 15728640 | tf_op jit(solution)/shard_map/all_gather | solution.py:187
  321.7 285.7 %all-gather.54.cloned.1.call-start = ((), (), s32[]{:S(2)}) async-start(), calls=%async_computation.23 | async-start | bytes 7864320 | tf_op jit(solution)/shard_map/all_gather | solution.py:266
  367.3 88.6 %copy-start.136 = (bf16[1280]{0:T(1024)(128)(2,1)}, bf16[1280]{0:T(1024)(128)(2,1)S(1)}, u32[]{:S(2)}) copy-start(bf16[1280]{0:T(1024)(128)(2,1)S(1)} %get-tuple-element.269) | copy-start | bytes 7684
  367.3 89.1 %copy-start.134 = (bf16[1280]{0:T(1024)(128)(2,1)}, bf16[1280]{0:T(1024)(128)(2,1)S(1)}, u32[]{:S(2)}) copy-start(bf16[1280]{0:T(1024)(128)(2,1)S(1)} %get-tuple-element.268) | copy-start | bytes 7684
  367.3 89.5 %copy-start.132 = (bf16[1280]{0:T(1024)(128)(2,1)}, bf16[1280]{0:T(1024)(128)(2,1)S(1)}, u32[]{:S(2)}) copy-start(bf16[1280]{0:T(1024)(128)(2,1)S(1)} %get-tuple-element.267) | copy-start | bytes 7684
  367.3 89.9 %copy-start.130 = (bf16[1280]{0:T(1024)(128)(2,1)}, bf16[1280]{0:T(1024)(128)(2,1)S(1)}, u32[]{:S(2)}) copy-start(bf16[1280]{0:T(1024)(128)(2,1)S(1)} %get-tuple-element.266) | copy-start | bytes 7684
  367.3 90.4 %copy-start.128 = (bf16[1280]{0:T(1024)(128)(2,1)}, bf16[1280]{0:T(1024)(128)(2,1)S(1)}, u32[]{:S(2)}) copy-start(bf16[1280]{0:T(1024)(128)(2,1)S(1)} %get-tuple-element.265) | copy-start | bytes 7684
  406.6 49.8 %copy-start.24 = (bf16[1280,192]{1,0:T(8,128)(2,1)}, bf16[1280,192]{1,0:T(8,128)(2,1)S(1)}, u32[]{:S(2)}) copy-start(bf16[1280,192]{1,0:T(8,128)(2,1)S(1)} %gather_fusion.13) | copy-start | bytes 1474564
  472.3 103.9 %all-to-all-start = ((bf16[8,1280,192]{2,0,1:T(8,128)(2,1)}), bf16[8,1280,192]{2,0,1:T(8,128)(2,1)}, u32[]{:S(2)}, u32[]{:S(2)}) async-start(bf16[8,1280,192]{2,0,1:T(8,128)(2,1)} %copy.297), calls=%async_computation.2 | async-start | bytes 10485760 | tf_op jit(solution)/shard_map/all_to_all | solution.py:267
  477.4 223.7 %all-gather.36.cloned.1.call-start = ((), (), s32[]{:S(2)}) async-start(), calls=%async_computation.14 | async-start | bytes 1638400 | tf_op jit(solution)/shard_map/all_gather | solution.py:95
  610.6 93.4 %all-gather.38.cloned.1.call-start = ((), (), s32[]{:S(2)}) async-start(), calls=%async_computation.15 | async-start | bytes 1638400 | tf_op jit(solution)/shard_map/all_gather | solution.py:95
  622.6 84.3 %all-gather.40.cloned.1.call-start = ((), (), s32[]{:S(2)}) async-start(), calls=%async_computation.16 | async-start | bytes 1638400 | tf_op jit(solution)/shard_map/all_gather | solution.py:95
  634.7 75.2 %all-gather.42.cloned.1.call-start = ((), (), s32[]{:S(2)}) async-start(), calls=%async_computation.17 | async-start | bytes 1638400 | tf_op jit(solution)/shard_map/all_gather | solution.py:95
  647.0 65.7 %all-gather.44.cloned.1.call-start = ((), (), s32[]{:S(2)}) async-start(), calls=%async_computation.18 | async-start | bytes 1638400 | tf_op jit(solution)/shard_map/all_gather | solution.py:95
  658.2 69.0 %all-gather.46.cloned.1.call-start = ((), (), s32[]{:S(2)}) async-start(), calls=%async_computation.19 | async-start | bytes 1638400 | tf_op jit(solution)/shard_map/all_gather | solution.py:95
  669.2 77.5 %all-gather.48.cloned.1.call-start = ((), (), s32[]{:S(2)}) async-start(), calls=%async_computation.20 | async-start | bytes 1638400 | tf_op jit(solution)/shard_map/all_gather | solution.py:95
  680.6 85.7 %all-gather.50.cloned.1.call-start = ((), (), s32[]{:S(2)}) async-start(), calls=%async_computation.21 | async-start | bytes 1638400 | tf_op jit(solution)/shard_map/all_gather | solution.py:95
  692.0 123.4 %all-gather.56.cloned.1.call-start = ((), (), s32[]{:S(2)}) async-start(), calls=%async_computation.24 | async-start | bytes 3276800 | tf_op jit(solution)/shard_map/all_gather | solution.py:95
  693.0 128.0 %all-gather.58.cloned.1.call-start = ((), (), s32[]{:S(2)}) async-start(), calls=%async_computation.25 | async-start | bytes 3276800 | tf_op jit(solution)/shard_map/all_gather | solution.py:95
  694.1 154.1 %all-gather.60.cloned.1.call-start = ((), (), s32[]{:S(2)}) async-start(), calls=%async_computation.26 | async-start | bytes 3276800 | tf_op jit(solution)/shard_map/all_gather | solution.py:95
  695.1 180.2 %all-gather.62.cloned.1.call-start = ((), (), s32[]{:S(2)}) async-start(), calls=%async_computation.27 | async-start | bytes 3276800 | tf_op jit(solution)/shard_map/all_gather | solution.py:95
  696.2 206.2 %all-gather.64.cloned.1.call-start = ((), (), s32[]{:S(2)}) async-start(), calls=%async_computation.28 | async-start | bytes 3276800 | tf_op jit(solution)/shard_map/all_gather | solution.py:95
  697.2 232.2 %all-gather.66.cloned.1.call-start = ((), (), s32[]{:S(2)}) async-start(), calls=%async_computation.29 | async-start | bytes 3276800 | tf_op jit(solution)/shard_map/all_gather | solution.py:95
  698.3 258.3 %all-gather.68.cloned.1.call-start = ((), (), s32[]{:S(2)}) async-start(), calls=%async_computation.30 | async-start | bytes 3276800 | tf_op jit(solution)/shard_map/all_gather | solution.py:95
  699.3 284.2 %all-gather.70.cloned.1.call-start = ((), (), s32[]{:S(2)}) async-start(), calls=%async_computation.31 | async-start | bytes 3276800 | tf_op jit(solution)/shard_map/all_gather | solution.py:95
  701.0 685.6 %all-reduce.10.cloned.1.call-start = ((), (), s32[]{:S(2)}) async-start(), calls=%async_computation.37 | async-start | bytes 16777216
  1095.6 353.3 %reduce-scatter.10.cloned.1.call-start = ((), (), s32[]{:S(2)}) async-start(), calls=%async_computation.32 | async-start | bytes 3932160 | tf_op jit(solution)/shard_map/reduce_scatter | solution.py:105
  1101.0 394.7 %all-gather.72.cloned.1.call-start = ((), (), s32[]{:S(2)}) async-start(), calls=%async_computation.33 | async-start | bytes 1966080 | tf_op jit(solution)/shard_map/all_gather | solution.py:91
  1395.5 53.4 %copy-start.4 = (f32[1024,192]{0,1:T(8,128)S(1)}, f32[1024,192]{0,1:T(8,128)}, u32[]{:S(2)}) copy-start(f32[1024,192]{0,1:T(8,128)} %copy-done.3) | copy-start | bytes 2359300
  1395.5 53.4 %copy-start.117 = (bf16[192,12]{0,1:T(8,128)(2,1)S(1)}, bf16[192,12]{0,1:T(8,128)(2,1)}, u32[]{:S(2)}) copy-start(bf16[192,12]{0,1:T(8,128)(2,1)} %param.31) | copy-start | bytes 13828
  1395.5 53.4 %copy-start.126 = (f32[192]{0:T(256)S(1)}, f32[192]{0:T(256)}, u32[]{:S(2)}) copy-start(f32[192]{0:T(256)} %param.30) | copy-start | bytes 2308
  1395.5 53.4 %copy-start.144 = (bf16[192,4]{0,1:T(4,128)(2,1)S(1)}, bf16[192,4]{0,1:T(4,128)(2,1)}, u32[]{:S(2)}) copy-start(bf16[192,4]{0,1:T(4,128)(2,1)} %param.32) | copy-start | bytes 4612
  1397.7 60.1 %copy-start.15 = (bf16[1024,192]{0,1:T(8,128)(2,1)S(1)}, bf16[1024,192]{0,1:T(8,128)(2,1)}, u32[]{:S(2)}) copy-start(bf16[1024,192]{0,1:T(8,128)(2,1)} %param.37) | copy-start | bytes 1179652
  1397.8 60.1 %copy-start.115 = (f32[1024]{0:T(1024)S(1)}, f32[1024]{0:T(1024)}, u32[]{:S(2)}) copy-start(f32[1024]{0:T(1024)} %get-tuple-element.285) | copy-start | bytes 12292
  1409.9 235.5 %copy-start.67 = (f32[1024,12]{0,1:T(8,128)}, f32[1024,12]{0,1:T(8,128)S(1)}, u32[]{:S(2)}) copy-start(f32[1024,12]{0,1:T(8,128)S(1)} %select_reduce_fusion) | copy-start | bytes 147460
  1458.9 77.3 %reduce-scatter.12.cloned.1.call-start = ((), (), s32[]{:S(2)}) async-start(), calls=%async_computation.34 | async-start | bytes 3932160 | tf_op jit(solution)/shard_map/reduce_scatter | solution.py:99
  1499.4 134.7 %all-gather.74.cloned.1.call-start = ((), (), s32[]{:S(2)}) async-start(), calls=%async_computation.35 | async-start | bytes 5898240 | tf_op jit(solution)/shard_map/all_gather | solution.py:95
  1560.7 206.2 %all-reduce.12.cloned.1.call-start = ((), (), s32[]{:S(2)}) async-start(), calls=%async_computation.38 | async-start | bytes 10223616 | tf_op jit(solution)/shard_map/psum | solution.py:368
  1638.9 190.6 %reduce-scatter.14.cloned.1.call-start = ((), (), s32[]{:S(2)}) async-start(), calls=%async_computation.36 | async-start | bytes 3932160 | tf_op jit(solution)/shard_map/reduce_scatter | solution.py:105
  1772.1 57.3 %copy-start.8 = (bf16[1024,192]{0,1:T(8,128)(2,1)S(1)}, bf16[1024,192]{0,1:T(8,128)(2,1)}, u32[]{:S(2)}) copy-start(bf16[1024,192]{0,1:T(8,128)(2,1)} %param.23) | copy-start | bytes 1179652
  1772.1 57.3 %copy-start.107 = (f32[1024]{0:T(1024)S(1)}, f32[1024]{0:T(1024)}, u32[]{:S(2)}) copy-start(f32[1024]{0:T(1024)} %copy-done.106) | copy-start | bytes 12292
  1772.1 57.3 %copy-start.142 = (f32[192]{0:T(256)S(1)}, f32[192]{0:T(256)}, u32[]{:S(2)}) copy-start(f32[192]{0:T(256)} %param.27) | copy-start | bytes 2308
  1772.1 58.8 %copy-start.159 = (f32[2,192]{1,0:T(2,128)S(1)}, f32[2,192]{1,0:T(2,128)}, u32[]{:S(2)}) copy-start(f32[2,192]{1,0:T(2,128)} %get-tuple-element.148) | copy-start | bytes 4612
  1772.1 58.8 %copy-start.161 = (f32[192]{0:T(256)S(1)}, f32[192]{0:T(256)}, u32[]{:S(2)}) copy-start(f32[192]{0:T(256)} %get-tuple-element.152) | copy-start | bytes 2308
  1772.2 101.7 %copy-start.12 = (f32[1024,192]{0,1:T(8,128)S(1)}, f32[1024,192]{0,1:T(8,128)}, u32[]{:S(2)}) copy-start(f32[1024,192]{0,1:T(8,128)} %copy-done.11) | copy-start | bytes 2359300
  1772.2 101.7 %copy-start.16 = (f32[1024,192]{0,1:T(8,128)S(1)}, f32[1024,192]{0,1:T(8,128)}, u32[]{:S(2)}) copy-start(f32[1024,192]{0,1:T(8,128)} %get-tuple-element.147) | copy-start | bytes 2359300
  1772.2 101.7 %copy-start.127 = (f32[1024]{0:T(1024)S(1)}, f32[1024]{0:T(1024)}, u32[]{:S(2)}) copy-start(f32[1024]{0:T(1024)} %get-tuple-element.283) | copy-start | bytes 12292
  (140 other events, 867.1 us)
Sparse Core Ops, SparseCore 0:
  19.9 37.3 all-gather.25
  63.9 76.6 reduce-scatter.5
  152.9 19.6 all-gather.27
  176.4 60.3 reduce-scatter.7
  246.3 31.1 all-reduce.7
  279.6 37.0 all-gather.29
  318.8 62.2 all-gather.51
  382.7 44.9 all-gather.31
  429.8 111.5 all-gather.33
  542.9 58.6 all-gather.53
  610.7 18.1 all-gather.35
  630.4 18.1 all-gather.37
  650.1 18.1 all-gather.39
  669.7 18.1 all-gather.41
  689.3 18.1 all-gather.43
  708.9 18.1 all-gather.45
  728.6 18.1 all-gather.47
  748.2 18.1 all-gather.49
  768.5 25.5 all-gather.55
  795.5 25.5 all-gather.57
  822.6 25.5 all-gather.59
  849.7 25.5 all-gather.61
  876.9 25.5 all-gather.63
  903.8 25.5 all-gather.65
  931.0 25.5 all-gather.67
  957.9 25.5 all-gather.69
  1095.7 290.8 all-reduce.9
  1389.5 59.3 reduce-scatter.9
  1459.0 36.6 all-gather.71
  1499.6 36.5 reduce-scatter.11
  1560.9 37.4 all-gather.73
  1639.0 127.8 all-reduce.11
  1769.0 60.3 reduce-scatter.13
where the time goes:
time: 1900 us; the launch traced here: 1880 us
  waiting for transfers between devices  1120 us (59%)
  local copies, waits for them, and re-layouts  392 us (21%)
  matrix products  173 us (9%)
  other arithmetic  102 us (5%)
  blocking collectives  74.8 us (4%)
    unnamed x34, waiting for transfers between devices  282 us
    all_gather x18, waiting for transfers between devices, gather_slots(): return lax.all_gather(values, 'col', axis=0, tiled=True)  206 us
    reduce_scatter x3, waiting for transfers between devices, rows_total(): lax.psum_scatter(term(jnp.int32(0), lax.axis_size('row') * rows), 'row',...  151 us
    all_gather x4, waiting for transfers between devices, gather_tokens(): return lax.all_gather(values, 'row', axis=0, tiled=True)  124 us
    psum x1, waiting for transfers between devices, shards(): lax.psum(qkv_part.astype(jnp.bfloat16), 'dp').astype(jnp.float32)  120 us
    reduce_scatter x2, waiting for transfers between devices, cols_total(): lax.psum_scatter(term(jnp.int32(0), lax.axis_size('col') * rows), 'col',...  107 us
    all_to_all x1, waiting for transfers between devices, shards(): lax.all_to_all(jnp.stack(slot_grads, axis=0), 'col', split_axis=1, concat...  97.7 us
    gather x8, local copies, waits for them, and re-layouts, shards(): jnp.take(pair_rows, jnp.maximum(table[expert], 0), axis=0)  51.4 us
  transfers between devices with their start and end apart: 34, of which 24 were waited for; matrix products, arithmetic and copies ran while one was open for 25% of the time, Pallas kernels for 0%

commit v1 on v0

v1 whole, which is shorter than its diff:
```python
import jax
import jax.numpy as jnp
from jax import lax
from jax.experimental import pallas as pl
from jax.experimental.pallas import tpu as pltpu
from jax.sharding import PartitionSpec as P

HD = 64
LEN = 1024
EPS = 1e-06
HIGH = lax.Precision.HIGHEST
NEGATIVE = -1e30
TILE = 256
VMEM_LIMIT = 60 * 1024 * 1024
F32 = jnp.float32
BF16 = jnp.bfloat16
GAIN1, GAIN2, VALUE0, VALUE1 = 16, 17, 18, 19


def mm(left, right, over_left, over_right, precision=None):
    return lax.dot_general(
        left,
        right,
        (((over_left,), (over_right,)), ((), ())),
        preferred_element_type=F32,
        precision=precision,
    )


def after(value, *others):
    return lax.optimization_barrier((value,) + others)[0]


def col_swap(value, bits):
    count = lax.axis_size("col")
    return lax.ppermute(value, "col", [(i, i ^ bits) for i in range(count)])


def row_swap(value, bits):
    count = lax.axis_size("row")
    return lax.ppermute(value, "row", [(i, i ^ bits) for i in range(count)])


def row_shift(value, steps):
    count = lax.axis_size("row")
    return lax.ppermute(value, "row", [(i, (i + steps) % count) for i in range(count)])


def col_gather(value):
    count = lax.axis_size("col")
    found = {0: value}
    bit = count // 2
    while bit:
        found.update({k | bit: col_swap(v, bit) for k, v in found.items()})
        bit //= 2
    return [found[k] for k in range(count)]


def row_gather(value):
    count = lax.axis_size("row")
    return [value] + [row_shift(value, s) for s in range(1, count)]


def dp_total(value):
    count = lax.axis_size("dp")
    if count == 2:
        other = lax.ppermute(value, "dp", [(0, 1), (1, 0)])
        return value.astype(F32) + other.astype(F32)
    return lax.psum(value.astype(F32), "dp")


def row_total(value):
    bit = 1
    while bit < lax.axis_size("row"):
        value = value + row_swap(value, bit)
        bit *= 2
    return value


def rotate_halves(block, cosine, sine):
    half = HD // 2
    out = []
    for head in range(block.shape[0] // HD):
        first = block[head * HD : head * HD + half]
        second = block[head * HD + half : (head + 1) * HD]
        out.append(first * cosine - second * sine)
        out.append(second * cosine + first * sine)
    return jnp.concatenate(out, axis=0)


def attend_kernel(
    place, t0, t1, t2, t3, p0, p1, p2, p3, weight, cosine, sine,
    query_out, key_out, value_out, attn_out, logsum_out, act, w_all,
):
    block = pl.program_id(0)
    row = place[0]
    prefix = place[2]
    size = t0.shape[0]
    heads = query_out.shape[1] // HD
    width = heads * HD
    count = query_out.shape[0]
    span = query_out.shape[2]

    @pl.when(block == 0)
    def _():
        square = jnp.zeros((1, t0.shape[1]), F32)
        for ref in (t0, t1, t2, t3):
            hidden = ref[...].astype(F32)
            square = square + jnp.sum(hidden * hidden, axis=0, keepdims=True)
        inverse = lax.rsqrt(square / (size * 4) + EPS)
        for k, (ref, params) in enumerate(((t0, p0), (t1, p1), (t2, p2), (t3, p3))):
            gain = params[:, GAIN1 : GAIN1 + 1]
            act[k * size : (k + 1) * size] = (ref[...].astype(F32) * inverse * gain).astype(BF16)
            w_all[k * size : (k + 1) * size] = weight[row ^ k]
        qkv = mm(w_all[...], act[...], 0, 0)
        query = rotate_halves(qkv[:width], cosine[...], sine[...]).astype(BF16)
        keys = rotate_halves(qkv[width : 2 * width], cosine[...], sine[...]).astype(BF16)
        for i in range(count):
            query_out[i] = query[:, i * span : (i + 1) * span]
        key_out[...] = keys
        value_out[...] = qkv[2 * width :].astype(BF16)

    length = key_out.shape[1]
    places = lax.broadcasted_iota(jnp.int32, (length, span), 0)
    mine = lax.broadcasted_iota(jnp.int32, (1, span), 1) + block * span
    seen = places <= jnp.maximum(mine, prefix - 1)
    rows = []
    for head in range(heads):
        cut = slice(head * HD, (head + 1) * HD)
        query = (query_out[block, cut].astype(F32) * HD ** (-0.5)).astype(BF16)
        scores = jnp.where(seen, mm(key_out[cut], query, 0, 0), NEGATIVE)
        top = jnp.max(scores, axis=0, keepdims=True)
        weights = jnp.exp(scores - top)
        total = jnp.sum(weights, axis=0, keepdims=True)
        mixed = mm(value_out[cut], weights.astype(BF16), 1, 0)
        attn_out[0, cut] = (mixed / total).astype(BF16)
        rows.append(top + jnp.log(total))
    rows.append(jnp.zeros((8 - heads, span), F32))
    logsum_out[...] = jnp.concatenate(rows, axis=0)


def attend(place, toks, params, weight, cosine, sine):
    size, length = toks[0].shape
    count = lax.axis_size("col")
    span = length // count
    width = weight.shape[2] // 3

    def whole(array):
        zeros = (0,) * array.ndim
        return pl.BlockSpec(array.shape, lambda q, s: zeros)

    args = (*toks, *params, weight, cosine, sine)
    return pl.pallas_call(
        attend_kernel,
        name="attend",
        grid_spec=pltpu.PrefetchScalarGridSpec(
            num_scalar_prefetch=1,
            grid=(count,),
            in_specs=[whole(a) for a in args],
            out_specs=[
                pl.BlockSpec((count, width, span), lambda q, s: (0, 0, 0)),
                pl.BlockSpec((width, length), lambda q, s: (0, 0)),
                pl.BlockSpec((width, length), lambda q, s: (0, 0)),
                pl.BlockSpec((1, width, span), lambda q, s: (q ^ s[1], 0, 0)),
                pl.BlockSpec((8, span), lambda q, s: (0, q)),
            ],
            scratch_shapes=[
                pltpu.VMEM((size * count, length), BF16),
                pltpu.VMEM((size * count, 3 * width), BF16),
            ],
        ),
        out_shape=[
            jax.ShapeDtypeStruct((count, width, span), BF16),
            jax.ShapeDtypeStruct((width, length), BF16),
            jax.ShapeDtypeStruct((width, length), BF16),
            jax.ShapeDtypeStruct((count, width, span), BF16),
            jax.ShapeDtypeStruct((8, length), F32),
        ],
        compiler_params=pltpu.CompilerParams(vmem_limit_bytes=VMEM_LIMIT),
    )(place, *args)


def attend_back_kernel(
    place, t0, t1, t2, t3, p0, p1, p2, p3, weight, proj, cosine, sine,
    query, keys, values, attn, logsum, d0, d1, d2, d3, grad_mid,
    tokens_out, qkv_out, proj_out, gain_out,
    dmid, proj_all, proj_acc, key_acc, value_acc, grad_all,
):
    block = pl.program_id(0)
    row = place[0]
    col = place[1]
    prefix = place[2]
    size, length = t0.shape
    count, width, span = query.shape
    heads = width // HD
    last = count - 1

    @pl.when(block == 0)
    def _():
        for k in range(count):
            proj_all[k * size : (k + 1) * size] = proj[row ^ k]
        proj_acc[...] = jnp.zeros_like(proj_acc)
        key_acc[...] = jnp.zeros_like(key_acc)
        value_acc[...] = jnp.zeros_like(value_acc)

    for k, ref in enumerate((d0, d1, d2, d3)):

        @pl.when((block ^ col) == k)
        def _():
            for j in range(count):
                dmid[j * size : (j + 1) * size] = ref[(k ^ j) * size : ((k ^ j) + 1) * size]

    low = dmid[...]
    grad_attn = mm(proj_all[...], low, 0, 0).astype(BF16)
    proj_acc[...] += mm(low, attn[0], 1, 1)
    places = lax.broadcasted_iota(jnp.int32, (length, span), 0)
    mine = lax.broadcasted_iota(jnp.int32, (1, span), 1) + block * span
    seen = places <= jnp.maximum(mine, prefix - 1)
    scale = HD ** (-0.5)
    parts = []
    for head in range(heads):
        cut = slice(head * HD, (head + 1) * HD)
        plain = query[block, cut]
        scaled = (plain.astype(F32) * scale).astype(BF16)
        scores = mm(keys[cut], scaled, 0, 0)
        probs = jnp.where(seen, jnp.exp(scores - logsum[head : head + 1]), 0.0)
        above = grad_attn[cut]
        grad_probs = mm(values[cut], above, 0, 0)
        inner = jnp.sum(probs * grad_probs, axis=0, keepdims=True)
        grad_scores = (probs * (grad_probs - inner)).astype(BF16)
        parts.append(mm(keys[cut], grad_scores, 1, 0) * scale)
        key_acc[cut] += mm(plain, grad_scores, 1, 1)
        value_acc[cut] += mm(above, probs.astype(BF16), 1, 1)
    for i in range(count):

        @pl.when(block == i)
        def _():
            here = slice(i * span, (i + 1) * span)
            turned = rotate_halves(
                jnp.concatenate(parts, axis=0), cosine[:, here], -sine[:, here]
            )
            grad_all[:width, here] = turned.astype(BF16)

    @pl.when(block == last)
    def _():
        turned = rotate_halves(key_acc[...] * scale, cosine[...], -sine[...])
        grad_all[width : 2 * width] = turned.astype(BF16)
        grad_all[2 * width :] = value_acc[...].astype(BF16)
        refs = (t0, t1, t2, t3)
        gains = [params[:, GAIN1 : GAIN1 + 1] for params in (p0, p1, p2, p3)]
        square = jnp.zeros((1, length), F32)
        for ref in refs:
            hidden = ref[...].astype(F32)
            square = square + jnp.sum(hidden * hidden, axis=0, keepdims=True)
        inverse = lax.rsqrt(square / (size * count) + EPS)
        backs = []
        inner = jnp.zeros((1, length), F32)
        for k in range(count):
            hidden = refs[k][...].astype(F32)
            act = (hidden * inverse * gains[k]).astype(BF16)
            qkv_out[row ^ col ^ k] = mm(act, grad_all[...], 1, 1).astype(BF16)
            proj_out[row ^ col ^ k] = proj_acc[k * size : (k + 1) * size].astype(BF16)
            back = mm(weight[row ^ k], grad_all[...], 1, 0)
            inner = inner + jnp.sum(hidden * gains[k] * back, axis=0, keepdims=True)
            summed = jnp.sum(hidden * inverse * back, axis=1, keepdims=True)
            gain_out[k] = jnp.transpose(jnp.broadcast_to(summed, (size, 128)))[:8]
            backs.append(back)
        inner = inner * (inverse * inverse * inverse) / (size * count)
        for k in range(count):
            hidden = refs[k][...].astype(F32)
            grad = inverse * gains[k] * backs[k] - hidden * inner
            for i in range(count):
                here = slice(i * span, (i + 1) * span)
                extra = jnp.where(col == i, grad_mid[k * size : (k + 1) * size], 0.0)
                tokens_out[k, :, here] = (grad[:, here] + extra).astype(BF16)


def attend_back(
    place, toks, params, weight, proj, cosine, sine, query, keys, values, attn, logsum, lows, grad_mid
):
    size, length = toks[0].shape
    count, width, span = query.shape

    def whole(array):
        zeros = (0,) * array.ndim
        return pl.BlockSpec(array.shape, lambda q, s: zeros)

    args = (
        *toks, *params, weight, proj, cosine, sine, query, keys, values, attn, logsum, *lows, grad_mid,
    )
    specs = [whole(a) for a in args]
    at = len(toks) + len(params) + 4 + 3
    specs[at] = pl.BlockSpec((1, width, span), lambda q, s: (q ^ s[1], 0, 0))
    specs[at + 1] = pl.BlockSpec((8, span), lambda q, s: (0, q))
    return pl.pallas_call(
        attend_back_kernel,
        name="attend_back",
        grid_spec=pltpu.PrefetchScalarGridSpec(
            num_scalar_prefetch=1,
            grid=(count,),
            in_specs=specs,
            out_specs=[
                pl.BlockSpec((count, size, length), lambda q, s: (0, 0, 0)),
                pl.BlockSpec((count, size, 3 * width), lambda q, s: (0, 0, 0)),
                pl.BlockSpec((count, size, width), lambda q, s: (0, 0, 0)),
                pl.BlockSpec((count, 8, size), lambda q, s: (0, 0, 0)),
            ],
            scratch_shapes=[
                pltpu.VMEM((size * count, span), BF16),
                pltpu.VMEM((size * count, width), BF16),
                pltpu.VMEM((size * count, width), F32),
                pltpu.VMEM((width, length), F32),
                pltpu.VMEM((width, length), F32),
                pltpu.VMEM((3 * width, length), BF16),
            ],
        ),
        out_shape=[
            jax.ShapeDtypeStruct((count, size, length), BF16),
            jax.ShapeDtypeStruct((count, size, 3 * width), BF16),
            jax.ShapeDtypeStruct((count, size, width), BF16),
            jax.ShapeDtypeStruct((count, 8, size), F32),
        ],
        compiler_params=pltpu.CompilerParams(vmem_limit_bytes=VMEM_LIMIT),
    )(place, *args)


def route_rows(routes, logits):
    places = lax.broadcasted_iota(jnp.int32, logits.shape, 0)
    hots = [places == routes[k : k + 1] for k in range(2)]
    return hots, [jnp.sum(jnp.where(hot, logits, 0.0), axis=0, keepdims=True) for hot in hots]


def pair_softmax(first, second):
    top = jnp.maximum(first, second)
    first = jnp.exp(first - top)
    second = jnp.exp(second - top)
    total = first + second
    return first / total, second / total


def middle_kernel(
    place, t0, t1, t2, t3, p0, p1, p2, p3, a0, a1, a2, a3, o0, o1, o2, o3, previous, routes,
    mid_out, rows_out, stats_out,
):
    row = place[0]
    size, span = t0.shape
    params = (p0, p1, p2, p3)
    kinds = previous.shape[0]
    square = jnp.zeros((1, span), F32)
    for j, ref in enumerate((t0, t1, t2, t3)):
        mid = ref[...].astype(F32)
        for k, (part, proj) in enumerate(((a0, o0), (a1, o1), (a2, o2), (a3, o3))):
            mid = mid + mm(proj[row ^ k ^ j], part[...], 1, 0)
        square = square + jnp.sum(mid * mid, axis=0, keepdims=True)
        mid_out[j * size : (j + 1) * size] = mid
    inverse = lax.rsqrt(square / (size * 4) + EPS)
    summed = jnp.zeros((128, span), F32)
    normed = []
    for j in range(4):
        norm = mid_out[j * size : (j + 1) * size] * inverse * params[j][:, GAIN2 : GAIN2 + 1]
        summed = summed + mm(params[j][...], norm, 0, 0, HIGH)
        normed.append(norm)
    rows_out[...] = jnp.transpose(jnp.concatenate(normed, axis=0)).astype(BF16)
    logits = summed[:kinds] + previous[...]
    _, chosen = route_rows(routes[...], logits)
    gates = pair_softmax(*chosen)
    alpha = [
        *pair_softmax(summed[12:13], summed[13:14]),
        *pair_softmax(summed[14:15], summed[15:16]),
    ]
    stats_out[...] = jnp.concatenate([*gates, inverse, *alpha, jnp.zeros((1, span), F32)], axis=0)


def middle(place, toks, params, parts, projs, previous, routes):
    size, length = toks[0].shape
    span = parts[0].shape[1]
    count = lax.axis_size("col")

    def whole(array):
        zeros = (0,) * array.ndim
        return pl.BlockSpec(array.shape, lambda i, s: zeros)

    args = (*toks, *params, *parts, *projs, previous, routes)
    specs = [pl.BlockSpec((size, span), lambda i, s: (0, s[1])) for _ in toks]
    specs += [whole(a) for a in (*params, *parts, *projs)]
    specs += [
        pl.BlockSpec((previous.shape[0], span), lambda i, s: (0, s[1])),
        pl.BlockSpec((2, span), lambda i, s: (0, s[0] * count + s[1])),
    ]
    full = size * count
    return pl.pallas_call(
        middle_kernel,
        name="middle",
        grid_spec=pltpu.PrefetchScalarGridSpec(
            num_scalar_prefetch=1,
            grid=(1,),
            in_specs=specs,
            out_specs=[
                pl.BlockSpec((full, span), lambda i, s: (0, 0)),
                pl.BlockSpec((span, full), lambda i, s: (0, 0)),
                pl.BlockSpec((8, span), lambda i, s: (0, 0)),
            ],
        ),
        out_shape=[
            jax.ShapeDtypeStruct((full, span), F32),
            jax.ShapeDtypeStruct((span, full), BF16),
            jax.ShapeDtypeStruct((8, span), F32),
        ],
        compiler_params=pltpu.CompilerParams(vmem_limit_bytes=VMEM_LIMIT),
    )(place, *args)


def middle_back_kernel(
    place, p0, p1, p2, p3, mid, grad, stats, routes, x0, x1, x2, x3, g0, g1, g2, g3,
    low_out, mid_out, logits_out, small_out,
):
    params = (p0, p1, p2, p3)
    full, span = mid.shape
    size = p0.shape[0]
    kinds = logits_out.shape[0]
    gates = [stats[0:1], stats[1:2]]
    inverse = stats[2:3]
    alpha = [stats[3:4], stats[4:5], stats[5:6], stats[6:7]]
    names = [routes[0:1], routes[1:2]]
    moe = x0[...].astype(F32) + x1[...].astype(F32) + x2[...].astype(F32) + x3[...].astype(F32)
    moe = jnp.transpose(moe)
    ffn = g0[...] + g1[...] + g2[...] + g3[...]
    flow = grad[...].astype(F32)
    normed = []
    dot_norm = jnp.zeros((1, span), F32)
    dot_value = [jnp.zeros((1, span), F32), jnp.zeros((1, span), F32)]
    for j in range(4):
        here = slice(j * size, (j + 1) * size)
        norm = mid[here] * inverse * params[j][:, GAIN2 : GAIN2 + 1]
        dot_norm = dot_norm + jnp.sum(flow[here] * norm, axis=0, keepdims=True)
        for c, column in enumerate((VALUE0, VALUE1)):
            value = params[j][:, column : column + 1]
            dot_value[c] = dot_value[c] + jnp.sum(flow[here] * value, axis=0, keepdims=True)
        normed.append(norm)
    experts = kinds - 4
    is_copy = [(name == experts + 1).astype(F32) for name in names]
    is_const = [[(name == experts + 2 + c).astype(F32) for name in names] for c in range(2)]
    grad_gate = []
    for k in range(2):
        value = ffn[k : k + 1] + is_copy[k] * dot_norm
        for c in range(2):
            value = value + is_const[c][k] * (
                alpha[2 * c] * dot_norm + alpha[2 * c + 1] * dot_value[c]
            )
        grad_gate.append(value)
    shared = gates[0] * grad_gate[0] + gates[1] * grad_gate[1]
    chosen = [gates[k] * (grad_gate[k] - shared) for k in range(2)]
    places = lax.broadcasted_iota(jnp.int32, (kinds, span), 0)
    logits = jnp.where(places == names[0], chosen[0], 0.0) + jnp.where(
        places == names[1], chosen[1], 0.0
    )
    logits_out[...] = logits
    direct = gates[0] * is_copy[0] + gates[1] * is_copy[1]
    rows = [logits]
    portions = []
    for c in range(2):
        portion = gates[0] * is_const[c][0] + gates[1] * is_const[c][1]
        first, second = alpha[2 * c], alpha[2 * c + 1]
        along = [portion * dot_norm, portion * dot_value[c]]
        mean = first * along[0] + second * along[1]
        rows += [first * (along[0] - mean), second * (along[1] - mean)]
        direct = direct + first * portion
        portions.append(second * portion)
    rows.append(jnp.zeros((128 - kinds - 4, span), F32))
    routed = jnp.concatenate(rows, axis=0)
    lanes = lax.broadcasted_iota(jnp.int32, (size, 128), 1)
    backs = []
    inner = jnp.zeros((1, span), F32)
    for j in range(4):
        here = slice(j * size, (j + 1) * size)
        back = moe[here] + direct * flow[here] + mm(params[j][...], routed, 1, 0, HIGH)
        small = mm(normed[j], routed, 1, 1, HIGH)
        columns = (
            (GAIN2, mid[here] * inverse * back),
            (VALUE0, portions[0] * flow[here]),
            (VALUE1, portions[1] * flow[here]),
        )
        for column, terms in columns:
            total = jnp.sum(terms, axis=1, keepdims=True)
            small = jnp.where(lanes == column, total, small)
        small_out[j] = jnp.transpose(small)[:32]
        gain = params[j][:, GAIN2 : GAIN2 + 1]
        inner = inner + jnp.sum(mid[here] * gain * back, axis=0, keepdims=True)
        backs.append(back)
    inner = inner * (inverse * inverse * inverse) / full
    for j in range(4):
        here = slice(j * size, (j + 1) * size)
        gain = params[j][:, GAIN2 : GAIN2 + 1]
        value = flow[here] + inverse * gain * backs[j] - mid[here] * inner
        mid_out[here] = value
        low_out[here] = value.astype(BF16)


def middle_back(place, params, mid, grad, stats, routes, pieces, gate_pieces, kinds):
    full, span = mid.shape
    count = lax.axis_size("col")
    size = full // count

    def whole(array):
        zeros = (0,) * array.ndim
        return pl.BlockSpec(array.shape, lambda i, s: zeros)

    args = (*params, mid, grad, stats, routes, *pieces, *gate_pieces)
    specs = [whole(a) for a in args]
    specs[len(params) + 3] = pl.BlockSpec((2, span), lambda i, s: (0, s[0] * count + s[1]))
    return pl.pallas_call(
        middle_back_kernel,
        name="middle_back",
        grid_spec=pltpu.PrefetchScalarGridSpec(
            num_scalar_prefetch=1,
            grid=(1,),
            in_specs=specs,
            out_specs=[
                pl.BlockSpec((full, span), lambda i, s: (0, 0)),
                pl.BlockSpec((full, span), lambda i, s: (0, 0)),
                pl.BlockSpec((kinds, span), lambda i, s: (0, 0)),
                pl.BlockSpec((count, 32, size), lambda i, s: (0, 0, 0)),
            ],
        ),
        out_shape=[
            jax.ShapeDtypeStruct((full, span), BF16),
            jax.ShapeDtypeStruct((full, span), F32),
            jax.ShapeDtypeStruct((kinds, span), F32),
            jax.ShapeDtypeStruct((count, 32, size), F32),
        ],
        compiler_params=pltpu.CompilerParams(vmem_limit_bytes=VMEM_LIMIT),
    )(place, *args)


def result_kernel(place, p0, p1, p2, p3, mid, stats, routes, y0, y1, y2, y3, out):
    params = (p0, p1, p2, p3)
    size = p0.shape[0]
    experts = place[3]
    inverse = stats[2:3]
    names = [routes[0:1], routes[1:2]]
    gates = [stats[0:1], stats[1:2]]

    def portion(kind):
        return jnp.where(names[0] == kind, gates[0], 0.0) + jnp.where(
            names[1] == kind, gates[1], 0.0
        )

    first, second = portion(experts + 2), portion(experts + 3)
    direct = portion(experts + 1) + first * stats[3:4] + second * stats[5:6]
    moe = y0[...].astype(F32) + y1[...].astype(F32) + y2[...].astype(F32) + y3[...].astype(F32)
    moe = jnp.transpose(moe)
    for j in range(4):
        here = slice(j * size, (j + 1) * size)
        norm = mid[here] * inverse * params[j][:, GAIN2 : GAIN2 + 1]
        out[j] = (
            mid[here]
            + moe[here]
            + direct * norm
            + first * stats[4:5] * params[j][:, VALUE0 : VALUE0 + 1]
            + second * stats[6:7] * params[j][:, VALUE1 : VALUE1 + 1]
        )


def result(place, params, mid, stats, routes, pieces):
    full, span = mid.shape
    count = lax.axis_size("col")

    def whole(array):
        zeros = (0,) * array.ndim
        return pl.BlockSpec(array.shape, lambda i, s: zeros)

    args = (*params, mid, stats, routes, *pieces)
    specs = [whole(a) for a in args]
    specs[len(params) + 2] = pl.BlockSpec((2, span), lambda i, s: (0, s[0] * count + s[1]))
    return pl.pallas_call(
        result_kernel,
        name="result",
        grid_spec=pltpu.PrefetchScalarGridSpec(
            num_scalar_prefetch=1,
            grid=(1,),
            in_specs=specs,
            out_specs=pl.BlockSpec((count, full // count, span), lambda i, s: (0, 0, 0)),
        ),
        out_shape=jax.ShapeDtypeStruct((count, full // count, span), F32),
        compiler_params=pltpu.CompilerParams(vmem_limit_bytes=VMEM_LIMIT),
    )(place, *args)


def experts_kernel(
    order, x0, x1, x2, x3, g0, g1, g2, g3, s0, s1, s2, s3, ranks, routes,
    w0, w1, near2, far2, near3, far3,
    y_out, dx_out, gate_out, grad0, grad1, grad2, grad3,
    weight, y_acc, dx_acc, gate_rows, acc,
):
    step = pl.program_id(0)
    steps = pl.num_programs(0)
    expert = order[step]
    tiles = order[steps + step]
    size = w0.shape[1]
    span = x0.shape[0]
    hidden_width = w0.shape[2] // 3
    both = 2 * hidden_width
    tokens = ranks.shape[1]
    xs = (x0, x1, x2, x3)
    gs = (g0, g1, g2, g3)

    @pl.when(step == 0)
    def _():
        y_acc[...] = jnp.zeros_like(y_acc)
        dx_acc[...] = jnp.zeros_like(dx_acc)
        gate_out[...] = jnp.zeros_like(gate_out)
        for i, ref in enumerate((s0, s1, s2, s3)):
            gate_rows[:, i * span : (i + 1) * span] = ref[...]

    weight[:size] = w0[0]
    weight[size : 2 * size] = w1[0]

    @pl.when(step < steps // 2)
    def _():
        weight[2 * size : 3 * size] = near2[0]
        weight[3 * size :] = near3[0]

    @pl.when(step >= steps // 2)
    def _():
        weight[2 * size : 3 * size] = far2[0]
        weight[3 * size :] = far3[0]

    rank = ranks[pl.ds(expert, 1), :]
    hit0 = routes[0:1] == expert
    hit1 = routes[1:2] == expert
    gate_row = jnp.where(hit0, gate_rows[0:1], 0.0) + jnp.where(hit1, gate_rows[1:2], 0.0)

    def tile(index, carry):
        slots = lax.broadcasted_iota(jnp.int32, (TILE, tokens), 0) + index * TILE
        hot = slots == rank
        pick = hot.astype(F32).astype(BF16)
        gate = jnp.sum(jnp.where(hot, gate_row, 0.0), axis=1, keepdims=True)
        rows = jnp.zeros((TILE, x0.shape[1]), F32)
        flow = jnp.zeros((TILE, x0.shape[1]), F32)
        for i in range(4):
            cut = pick[:, i * span : (i + 1) * span]
            rows = rows + mm(cut, xs[i][...], 1, 0)
            flow = flow + mm(cut, gs[i][...], 1, 0)
        rows = rows.astype(BF16)
        flow = flow.astype(BF16)
        gate_up = mm(rows, weight[:, :both], 1, 0)
        pre = gate_up[:, :hidden_width]
        up = gate_up[:, hidden_width:]
        sigma = 1.0 / (1.0 + jnp.exp(-pre))
        lifted = pre * sigma
        hidden = lifted * up
        scaled = (hidden * gate).astype(BF16)
        back = mm(flow, weight[:, both:], 1, 0)
        grad_gate = jnp.sum(hidden * back, axis=1, keepdims=True)
        back = back * gate
        grad_pre = back * up * sigma * (1.0 + pre * (1.0 - sigma))
        grad_up = back * lifted
        grad_both = jnp.concatenate([grad_pre.astype(BF16), grad_up.astype(BF16)], axis=1)
        y = mm(scaled, weight[:, both:], 1, 1).astype(BF16)
        dx = mm(grad_both, weight[:, :both], 1, 1).astype(BF16)
        for i in range(4):
            cut = pick[:, i * span : (i + 1) * span]
            y_acc[i * span : (i + 1) * span] += mm(cut, y, 0, 0)
            dx_acc[i * span : (i + 1) * span] += mm(cut, dx, 0, 0)
        row = jnp.sum(jnp.where(hot, grad_gate, 0.0), axis=0, keepdims=True)
        gate_out[0:1] += jnp.where(hit0, row, 0.0)
        gate_out[1:2] += jnp.where(hit1, row, 0.0)
        grad_weight = mm(rows, grad_both, 0, 0)
        grad_down = mm(flow, scaled, 0, 0)

        @pl.when(index == 0)
        def _():
            acc[:, :both] = grad_weight
            acc[:, both:] = grad_down

        @pl.when(index > 0)
        def _():
            acc[:, :both] += grad_weight
            acc[:, both:] += grad_down

        return carry

    lax.fori_loop(0, tiles, tile, 0)
    for k, ref in enumerate((grad0, grad1, grad2, grad3)):
        ref[0] = acc[k * size : (k + 1) * size].astype(BF16)

    @pl.when(step == steps - 1)
    def _():
        y_out[...] = y_acc[...].astype(BF16)
        dx_out[...] = dx_acc[...].astype(BF16)


def run_experts(order, xs, gs, gate_parts, ranks, routes, w0, w1, near2, far2, near3, far3):
    experts, size, wide = w0.shape
    half = experts // 2
    tokens = ranks.shape[1]
    full = xs[0].shape[1]

    def whole(array):
        zeros = (0,) * array.ndim
        return pl.BlockSpec(array.shape, lambda e, s: zeros)

    args = (*xs, *gs, *gate_parts, ranks, routes, w0, w1, near2, far2, near3, far3)
    near = pl.BlockSpec((1, size, wide), lambda e, s: (jnp.minimum(e, half - 1), 0, 0))
    far = pl.BlockSpec((1, size, wide), lambda e, s: (jnp.maximum(e - half, 0), 0, 0))
    mine = pl.BlockSpec((1, size, wide), lambda e, s: (s[e], 0, 0))
    specs = [whole(a) for a in args[:-6]] + [mine, mine, near, far, near, far]
    grad = pl.BlockSpec((1, size, wide), lambda e, s: (e, 0, 0))
    rows = pl.BlockSpec((tokens, full), lambda e, s: (0, 0))
    return pl.pallas_call(
        experts_kernel,
        name="experts",
        grid_spec=pltpu.PrefetchScalarGridSpec(
            num_scalar_prefetch=1,
            grid=(experts,),
            in_specs=specs,
            out_specs=[rows, rows, pl.BlockSpec((8, tokens), lambda e, s: (0, 0))] + [grad] * 4,
            scratch_shapes=[
                pltpu.VMEM((full, wide), BF16),
                pltpu.VMEM((tokens, full), F32),
                pltpu.VMEM((tokens, full), F32),
                pltpu.VMEM((8, tokens), F32),
                pltpu.VMEM((full, wide), F32),
            ],
        ),
        out_shape=[
            jax.ShapeDtypeStruct((tokens, full), BF16),
            jax.ShapeDtypeStruct((tokens, full), BF16),
            jax.ShapeDtypeStruct((8, tokens), F32),
        ]
        + [jax.ShapeDtypeStruct((experts, size, wide), BF16)] * 4,
        compiler_params=pltpu.CompilerParams(vmem_limit_bytes=VMEM_LIMIT),
    )(order, *args)


def shards(
    tokens,
    prev_logits,
    routes,
    prefix_len,
    norm1_gain,
    qkv_weight,
    out_weight,
    norm2_gain,
    router_weight,
    const_weight,
    const_values,
    gate_weight,
    up_weight,
    down_weight,
    cotangent,
):
    row = lax.axis_index("row")
    col = lax.axis_index("col")
    rows = lax.axis_size("row")
    cols = lax.axis_size("col")
    groups = lax.axis_size("dp")
    length, size = tokens.shape
    span = length // cols
    kinds = router_weight.shape[1]
    experts = gate_weight.shape[0]
    half = experts // 2
    hidden_width = gate_weight.shape[2]
    first_half = lax.axis_index("dp") if groups == 2 else jnp.int32(0)
    prefix = lax.dynamic_index_in_dim(prefix_len, row, 0, False)
    place = jnp.stack([row, col, prefix, jnp.int32(experts)]).astype(jnp.int32)
    flat = [(i // cols, i % cols) for i in range(rows * cols)]

    def spread(value, turn):
        pairs = [(c * cols + (c ^ r ^ turn), r * cols + c) for r, c in flat]
        return lax.ppermute(value, ("row", "col"), pairs)

    def collect(value, turn):
        pairs = [(r * cols + c, c * cols + (r ^ turn)) for r, c in flat]
        return lax.ppermute(value, ("row", "col"), pairs)

    toks = col_gather(tokens.T)
    packed = jnp.concatenate(
        [
            router_weight.astype(F32),
            const_weight.astype(F32),
            norm1_gain[:, None],
            norm2_gain[:, None],
            const_values.T,
            jnp.zeros((size, 128 - kinds - 8), F32),
        ],
        axis=1,
    )
    params = col_gather(packed)
    piece = jnp.concatenate([qkv_weight[0], qkv_weight[1], qkv_weight[2]], axis=1)
    weight = jnp.stack([spread(piece, m) for m in range(rows)])
    proj_piece = after(out_weight.T, piece)
    proj = jnp.stack([spread(proj_piece, m) for m in range(rows)])
    halves = HD // 2
    freq = 10000.0 ** (-jnp.arange(halves, dtype=F32) / halves)
    angle = freq[:, None] * jnp.arange(length, dtype=F32)[None, :]
    cosine = jnp.cos(angle)
    sine = jnp.sin(angle)

    own = jnp.concatenate([gate_weight, up_weight, down_weight.transpose(0, 2, 1)], axis=2)
    side = col_swap(own, 1)
    near_mine = lax.dynamic_slice_in_dim(own, first_half * half, half, 0)
    near_two = col_swap(near_mine, 2)
    if groups == 2:
        far_two = lax.ppermute(near_two, "dp", [(0, 1), (1, 0)])
    else:
        far_two = col_swap(lax.dynamic_slice_in_dim(own, half, half, 0), 2)
    near_three = col_swap(near_two, 1)
    far_three = col_swap(far_two, 1)

    flow = cotangent.T.reshape(size, cols, span)
    flow_parts = [lax.dynamic_index_in_dim(flow, col ^ k, 1, False) for k in range(cols)]
    flow_quarter = jnp.concatenate(
        [flow_parts[0]] + [col_swap(flow_parts[k], k) for k in range(1, cols)], axis=0
    )
    flow_rows = row_gather(flow_quarter.T)

    routes_t = routes.T
    share = lax.dynamic_index_in_dim(routes_t.reshape(2, rows, cols, span), col, 2, False)
    turned = (row - jnp.arange(rows)) % rows
    share = jnp.take(share, turned, axis=1).reshape(2, rows * span)
    ids = jnp.arange(experts, dtype=jnp.int32)[:, None]
    hits = (share[0][None] == ids) | (share[1][None] == ids)
    counts = jnp.cumsum(hits.astype(jnp.int32), axis=1)
    ranks = jnp.where(hits, counts - 1, -1)
    order = (first_half * half + jnp.arange(experts, dtype=jnp.int32)) % experts
    tiles = jnp.maximum((counts[:, -1] + TILE - 1) // TILE, 1)
    order = jnp.concatenate([order, jnp.take(tiles, order)]).astype(jnp.int32)

    query, keys, values, attn, logsum = attend(place, toks, params, weight, cosine, sine)
    parts = [attn[0]] + [col_swap(attn[k], k) for k in range(1, cols)]
    projs = col_gather(proj)
    mid, in_rows, stats = middle(place, toks, params, parts, projs, prev_logits.T, routes_t)
    x_rows = row_gather(in_rows)
    gate_parts = row_gather(stats)
    y, dx, gate_grad, *weight_grads = run_experts(
        order, x_rows, flow_rows, gate_parts, ranks, share,
        own, side, near_two, far_two, near_three, far_three,
    )

    def row_scatter(value, axis):
        pieces = [lax.slice_in_dim(value, s * span, (s + 1) * span, axis=axis) for s in range(rows)]
        return [pieces[0]] + [row_shift(pieces[s], -s) for s in range(1, rows)]

    low, grad_mid, grad_logits, small = middle_back(
        place, params, mid, flow_quarter, stats, routes_t,
        row_scatter(dx, 0), row_scatter(gate_grad, 1), kinds,
    )
    lows = col_gather(low)
    tokens_parts, qkv_parts, proj_parts, gain_parts = attend_back(
        place, toks, params, weight, proj, cosine, sine,
        query, keys, values, attn, logsum, lows, grad_mid,
    )

    def col_scatter(value):
        total = value[0].astype(F32)
        for k in range(1, cols):
            total = total + col_swap(value[k], k).astype(F32)
        return total

    grad_tokens = col_scatter(tokens_parts).T

    def weight_total(value):
        total = collect(value[0], 0).astype(F32)
        for m in range(1, rows):
            total = total + collect(value[m], m).astype(F32)
        return dp_total(total.astype(BF16))

    qkv_sum = weight_total(qkv_parts)
    qkv_sum = jnp.stack([qkv_sum[:, j * size : (j + 1) * size] for j in range(3)])
    proj_sum = weight_total(proj_parts).T

    small = dp_total(row_total(col_scatter(small)))
    gain1 = dp_total(row_total(col_scatter(gain_parts)))[0]

    from_side = col_swap(weight_grads[1], 1)
    across = col_swap(weight_grads[3], 1)
    kept = weight_grads[0].astype(F32) + from_side.astype(F32)
    sent = (weight_grads[2].astype(F32) + across.astype(F32)).astype(BF16)
    kept = (kept + col_swap(sent, 2).astype(F32)).astype(BF16)
    first = first_half == 0
    if groups == 2:
        ahead = lax.ppermute(kept[:half], "dp", [(0, 1), (1, 0)]).astype(F32)
        behind = lax.ppermute(kept[half:], "dp", [(0, 1), (1, 0)]).astype(F32)
        near = kept[:half].astype(F32) + behind
        far = kept[half:].astype(F32) + ahead
    else:
        both = lax.psum(kept.astype(F32), "dp")
        near, far = both[:half], both[half:]
    summed = jnp.concatenate([jnp.where(first, near, far), jnp.where(first, far, near)])

    def col_join(value, axis):
        got = [value(0)] + [col_swap(value(k), k) for k in range(1, cols)]
        stacked = jnp.stack(got)
        stacked = jnp.take(stacked, col ^ jnp.arange(cols), axis=0)
        return jnp.concatenate([stacked[i] for i in range(cols)], axis=axis)

    out = result(place, params, mid, stats, routes_t, row_scatter(y, 0))
    layer_out = col_join(lambda k: out[k], 1).T
    prev_grad = col_join(lambda k: grad_logits, 1).T

    return (
        layer_out,
        grad_tokens,
        prev_grad,
        gain1,
        qkv_sum,
        proj_sum,
        small[GAIN2],
        small[:kinds].T,
        small[kinds : kinds + 4].T,
        small[VALUE0 : VALUE1 + 1],
        summed[:, :, :hidden_width],
        summed[:, :, hidden_width : 2 * hidden_width],
        summed[:, :, 2 * hidden_width :].transpose(0, 2, 1),
    )


def solution(mesh):
    return jax.shard_map(
        shards,
        mesh=mesh,
        in_specs=(
            P(("dp", "row"), "col"),
            P(("dp", "row"), None),
            P("dp", None),
            P("dp"),
            P("col"),
            P(None, "col", "row"),
            P("row", "col"),
            P("col"),
            P("col", None),
            P("col", None),
            P(None, "col"),
            P(None, "col", "row"),
            P(None, "col", "row"),
            P(None, "row", "col"),
            P(("dp", "row"), "col"),
        ),
        out_specs=(
            P(("dp", "row"), "col"),
            P(("dp", "row"), "col"),
            P(("dp", "row"), None),
            P("col"),
            P(None, "col", "row"),
            P("row", "col"),
            P("col"),
            P("col", None),
            P("col", None),
            P(None, "col"),
            P(None, "col", "row"),
            P(None, "col", "row"),
            P(None, "row", "col"),
            P(None, "row", "col"),
        )[:13],
        check_vma=False,
    )
```

time: 1900 us -> 660 us (0.35)
  waiting for transfers between devices: 1120 us -> 315 us
  local copies, waits for them, and re-layouts: 392 us -> 32.3 us
  matrix products: 173 us -> 0 us
  starting transfers between devices: 6.79 us -> 147 us
  Pallas kernels: 0 us -> 110 us
  blocking collectives: 74.8 us -> 0 us
  other arithmetic: 102 us -> 46.3 us
    all_gather x25 -> x0, waiting for transfers between devices: 330 us -> none  [the longest x18 206 us: gather_slots(): return lax.all_gather(values, 'col', axis=0, tiled=True)]
    ppermute x0 -> x85, waiting for transfers between devices: none -> 315 us  [the longest x4 101 us: dp_total(): other = lax.ppermute(value, 'dp', [(0, 1), (1, 0)])]
    unnamed x34 -> x0, waiting for transfers between devices: 282 us -> none
    reduce_scatter x5 -> x0, waiting for transfers between devices: 258 us -> none  [the longest x3 151 us: rows_total(): lax.psum_scatter(term(jnp.int32(0), lax.axis_size('row') * rows), 'row',...]
    gather x26 -> x4, local copies, waits for them, and re-layouts: 211 us -> 2.61 us  [the longest x2 1.4 us: col_join(): stacked = jnp.take(stacked, col ^ jnp.arange(cols), axis=0)]
    dot_general x62 -> x0, matrix products: 167 us -> none  [the longest x8 30.2 us: shards(): jnp.einsum('cf,df->cd', grad_both, gate_up_all[expert], preferred_element...]
    psum x2 -> x0, waiting for transfers between devices: 149 us -> none  [the longest x1 120 us: shards(): lax.psum(qkv_part.astype(jnp.bfloat16), 'dp').astype(jnp.float32)]
    ppermute x0 -> x85, starting transfers between devices: none -> 147 us  [the longest x40 55.2 us: col_swap(): return lax.ppermute(value, 'col', [(i, i ^ bits) for i in range(count)])]
  transfers between devices with their start and end apart: 34 -> 85, of which waited for: 24 -> 30; matrix products, arithmetic and copies ran while one was open for 25% -> 9% of each run, Pallas kernels for 0% -> 8%
where the time goes in v1:
time: 660 us; the launch traced here: 653 us
  waiting for transfers between devices  315 us (48%)
  starting transfers between devices  147 us (22%)
  Pallas kernels  110 us (17%)
  other arithmetic  46.3 us (7%)
  local copies, waits for them, and re-layouts  32.3 us (5%)
    ppermute x4, waiting for transfers between devices, dp_total(): other = lax.ppermute(value, 'dp', [(0, 1), (1, 0)])  101 us
    ppermute x40, waiting for transfers between devices, col_swap(): return lax.ppermute(value, 'col', [(i, i ^ bits) for i in range(count)])  96 us
    ppermute x18, waiting for transfers between devices, row_shift(): lax.ppermute(value, 'row', [(i, (i + steps) % count) for i in range(count)])  90.4 us
    pallas_call x1, Pallas kernels, run_experts(): pl.pallas_call(experts_kernel, name='experts', grid_spec=pltpu.PrefetchSc...  57.8 us
    ppermute x40, starting transfers between devices, col_swap(): return lax.ppermute(value, 'col', [(i, i ^ bits) for i in range(count)])  55.2 us
    ppermute x18, starting transfers between devices, row_shift(): lax.ppermute(value, 'row', [(i, (i + steps) % count) for i in range(count)])  36.6 us
    ppermute x8, starting transfers between devices, spread(): return lax.ppermute(value, ('row', 'col'), pairs)  25 us
    pallas_call x1, Pallas kernels, attend_back(): pl.pallas_call(attend_back_kernel, name='attend_back', grid_spec=pltpu.Pr...  23.7 us
  transfers between devices with their start and end apart: 85, of which 30 were waited for; matrix products, arithmetic and copies ran while one was open for 9% of the time, Pallas kernels for 8%

profile of v1, /device:TPU:0, one launch (start us, length us, event | category | flops | bytes accessed | tf_op | source)
XLA Modules:
  0.0 653.3 jit_solution(6681423381287325149)
XLA Ops:
  0.7 3.9 pad_maximum_fusion.w0
  4.6 2.0 constant_dynamic-slice_fusion
  6.6 3.0 collective-permute-start.33
  9.7 51.4 %collective-permute-done.33.near2 = bf16[4,192,1536]{2,1,0:T(8,128)(2,1)} collective-permute-done((bf16[4,192,1536]{2,1,0:T(8,128)(2,1)S(1)}, bf16[4,192,1536]{2,1,0:T(8,128)(2,1)}, u32[]{:S(2)}, u32[]{:S(2)}) %collective-permute-start.33) | collective-permute-done | bytes 2359328 | tf_op jit(solution)/shard_map/ppermute | solution.py:36
  61.0 1.8 collective-permute-start.34
  63.0 5.5 collective-permute-start.16
  68.6 2.3 collective-permute-start.15
  70.8 3.2 collective-permute-start.14
  77.0 2.8 collective-permute-start.1
  81.0 6.5 %collective-permute-start.25 = (bf16[192,256]{1,0:T(8,128)(2,1)S(1)}, bf16[192,256]{1,0:T(8,128)(2,1)}, u32[]{:S(2)}, u32[]{:S(2)}) collective-permute-start(bf16[192,256]{1,0:T(8,128)(2,1)S(1)} %bitcast.201), channel_id=1, source_target_pairs={{0,3},{1,2},{2,1},{3,0},{4,7},{5,6},{6,5},{7,4},{8,11},{9,10},{10,... | collective-permute-start | bytes 294920 | tf_op jit(solution)/shard_map/ppermute | solution.py:36
  87.6 2.7 collective-permute-start.24
  90.4 6.8 %collective-permute-start.9 = (bf16[192,576]{1,0:T(8,128)(2,1)S(1)}, bf16[192,576]{1,0:T(8,128)(2,1)S(1)}, u32[]{:S(2)}, u32[]{:S(2)}) collective-permute-start(bf16[192,576]{1,0:T(8,128)(2,1)S(1)} %pad_maximum_fusion.7), channel_id=1, source_target_pairs={{3,0},{6,1},{9,2},{12,3},{2,4},{7,5},{8,6},{13,7},{1,8},{4,9},{11,... | collective-permute-start | bytes 663560 | tf_op jit(solution)/shard_map/ppermute | solution.py:771
  97.3 2.6 collective-permute-start.8
  101.4 3.3 collective-permute-start.7
  107.7 14.3 %collective-permute-start.4 = (bf16[192,1024]{1,0:T(8,128)(2,1)S(1)}, bf16[192,1024]{1,0:T(8,128)(2,1)S(1)}, u32[]{:S(2)}, u32[]{:S(2)}) collective-permute-start(bf16[192,1024]{1,0:T(8,128)(2,1)S(1)} %bitcast.175), channel_id=1, source_target_pairs={{0,2},{1,3},{2,0},{3,1},{4,6},{5,7},{6,4},{7,5},{8,10},{9,11},{10,... | collective-permute-start | bytes 1179656 | tf_op jit(solution)/shard_map/ppermute | solution.py:36
  122.9 2.3 reduce-window.6
  125.2 2.5 collective-permute-done.4.t2
  131.7 4.8 collective-permute-start.18
  136.5 1.8 pad_maximum_fusion.6
  140.5 2.5 pad_maximum_fusion.2.weight
  143.0 13.5 %attend.1 = (bf16[4,192,256]{2,1,0:T(8,128)(2,1)}, bf16[192,1024]{1,0:T(8,128)(2,1)}, bf16[192,1024]{1,0:T(8,128)(2,1)}, bf16[4,192,256]{2,1,0:T(8,128)(2,1)}, f32[8,1024]{1,0:T(8,128)}) custom-call(s32[4]{0:T(128)} %pad_add_fusion.place, bf16[192,1024]{1,0:T(8,128)(2,1)} %bitcast.172, bf16[192,1024]{1,0:T(8,128)(2,1)} %copy-done.6, ...), custom_call_target="tpu_custom_call" | custom-call | tf_op jit(solution)/shard_map/attend/pallas_call | solution.py:153
  160.8 4.0 collective-permute-done.11.a2
  164.7 2.6 collective-permute-start.27
  167.3 2.6 collective-permute-start.28
  170.6 5.3 middle.1
  175.8 10.3 %collective-permute-done.27 = bf16[256,768]{0,1:T(8,128)(2,1)S(1)} collective-permute-done((bf16[256,768]{0,1:T(8,128)(2,1)S(1)}, bf16[256,768]{0,1:T(8,128)(2,1)S(1)}, u32[]{:S(2)}, u32[]{:S(2)}) %collective-permute-start.27) | collective-permute-done | bytes 393248 | tf_op jit(solution)/shard_map/ppermute | solution.py:46
  186.1 6.7 %collective-permute-start.20 = (bf16[256,768]{1,0:T(8,128)(2,1)}, bf16[256,768]{1,0:T(8,128)(2,1)S(1)}, u32[]{:S(2)}, u32[]{:S(2)}) collective-permute-start(bf16[256,768]{1,0:T(8,128)(2,1)} %get-tuple-element.41.x0), channel_id=1, source_target_pairs={{0,4},{4,8},{8,12},{12,0},{1,5},{5,9},{9,13},{13,1},{2,6},{6,10},{... | collective-permute-start | bytes 1179656 | tf_op jit(solution)/shard_map/ppermute | solution.py:46
  193.4 11.2 %collective-permute-done.29.s1 = f32[8,256]{1,0:T(8,128)S(1)} collective-permute-done((f32[8,256]{1,0:T(8,128)}, f32[8,256]{1,0:T(8,128)S(1)}, u32[]{:S(2)}, u32[]{:S(2)}) %collective-permute-start.29) | collective-permute-done | bytes 8224 | tf_op jit(solution)/shard_map/ppermute | solution.py:46
  205.3 4.1 collective-permute-done.30.s2
  209.4 2.1 collective-permute-start.31
  211.5 2.1 collective-permute-done.31.s3
  213.9 3.4 collective-permute-start.22
  219.5 1.9 copy.53.g1
  223.3 8.0 %collective-permute-done.21.x2 = bf16[256,768]{1,0:T(8,128)(2,1)S(1)} collective-permute-done((bf16[256,768]{1,0:T(8,128)(2,1)}, bf16[256,768]{1,0:T(8,128)(2,1)S(1)}, u32[]{:S(2)}, u32[]{:S(2)}) %collective-permute-start.21) | collective-permute-done | bytes 393248 | tf_op jit(solution)/shard_map/ppermute | solution.py:46
  232.2 57.8 %experts.1 = (bf16[1024,768]{1,0:T(8,128)(2,1)}, bf16[1024,768]{1,0:T(8,128)(2,1)}, f32[8,1024]{1,0:T(8,128)}, bf16[8,192,1536]{2,1,0:T(8,128)(2,1)}, bf16[8,192...) custom-call(s32[16]{0:T(128)} %pad_add_fusion.1.order, ...), custom_call_target="tpu_custom_call" | custom-call | tf_op jit(solution)/shard_map/experts/pallas_call | solution.py:710
  290.6 7.6 %collective-permute-done.81 = bf16[8,192,1536]{2,1,0:T(8,128)(2,1)S(1)} collective-permute-done((bf16[8,192,1536]{2,1,0:T(8,128)(2,1)}, bf16[8,192,1536]{2,1,0:T(8,128)(2,1)S(1)}, u32[]{:S(2)}, u32[]{:S(2)}) %collective-permute-start.81) | collective-permute-done | bytes 4718624 | tf_op jit(solution)/shard_map/ppermute | solution.py:36
  298.2 6.0 add_convert_fusion.1
  305.8 8.9 %collective-permute-start.46 = (f32[8,256]{1,0:T(8,128)S(1)}, f32[8,256]{1,0:T(8,128)S(1)}, u32[]{:S(2)}, u32[]{:S(2)}) collective-permute-start(f32[8,256]{1,0:T(8,128)S(1)} %get-tuple-element.149), channel_id=1, source_target_pairs={{0,12},{4,0},{8,4},{12,8},{1,13},{5,1},{9,5},{13,9},{2,14},{6,2},{... | collective-permute-start | bytes 24584 | tf_op jit(solution)/shard_map/ppermute | solution.py:46
  316.2 4.0 collective-permute-start.43
  321.7 8.0 %collective-permute-done.43.x1 = bf16[256,768]{1,0:T(8,128)(2,1)S(1)} collective-permute-done((bf16[256,768]{1,0:T(8,128)(2,1)S(1)}, bf16[256,768]{1,0:T(8,128)(2,1)S(1)}, u32[]{:S(2)}, u32[]{:S(2)}) %collective-permute-start.43) | collective-permute-done | bytes 393248 | tf_op jit(solution)/shard_map/ppermute | solution.py:46
  329.7 4.3 collective-permute-start.37
  334.0 34.4 %collective-permute-done.44.x2 = bf16[256,768]{1,0:T(8,128)(2,1)S(1)} collective-permute-done((bf16[256,768]{1,0:T(8,128)(2,1)S(1)}, bf16[256,768]{1,0:T(8,128)(2,1)S(1)}, u32[]{:S(2)}, u32[]{:S(2)}) %collective-permute-start.44) | collective-permute-done | bytes 393248 | tf_op jit(solution)/shard_map/ppermute | solution.py:46
  369.3 6.2 middle_back.1
  375.6 12.0 %collective-permute-done.38.y2 = bf16[256,768]{1,0:T(8,128)(2,1)S(1)} collective-permute-done((bf16[256,768]{1,0:T(8,128)(2,1)S(1)}, bf16[256,768]{1,0:T(8,128)(2,1)S(1)}, u32[]{:S(2)}, u32[]{:S(2)}) %collective-permute-start.38) | collective-permute-done | bytes 393248 | tf_op jit(solution)/shard_map/ppermute | solution.py:46
  389.5 4.0 result.1
  394.7 13.0 %collective-permute-done.57 = f32[12,256]{1,0:T(8,128)S(1)} collective-permute-done((f32[12,256]{1,0:T(8,128)}, f32[12,256]{1,0:T(8,128)S(1)}, u32[]{:S(2)}, u32[]{:S(2)}) %collective-permute-start.57) | collective-permute-done | bytes 12320 | tf_op jit(solution)/shard_map/ppermute | solution.py:36
  414.4 8.2 %collective-permute-start.77 = (f32[32,192]{1,0:T(8,128)S(1)}, f32[32,192]{1,0:T(8,128)S(1)}, u32[]{:S(2)}, u32[]{:S(2)}) collective-permute-start(f32[32,192]{1,0:T(8,128)S(1)} %fusion.11), channel_id=1, source_target_pairs={{0,4},{4,0},{8,12},{12,8},{1,5},{5,1},{9,13},{13,9},{2,6},{6,2},{1... | collective-permute-start | bytes 73736 | tf_op jit(solution)/shard_map/ppermute | solution.py:41
  422.6 1.8 collective-permute-done.77
  425.9 3.4 collective-permute-done.78
  430.5 2.7 collective-permute-done.79
  438.2 2.8 collective-permute-done.50.d2
  443.4 23.7 %attend_back.1 = (bf16[4,192,1024]{2,1,0:T(8,128)(2,1)}, bf16[4,192,576]{2,1,0:T(8,128)(2,1)}, bf16[4,192,192]{2,1,0:T(8,128)(2,1)}, f32[4,8,192]{2,1,0:T(8,128)}) custom-call(s32[4]{0:T(128)} %pad_add_fusion.place, bf16[192,1024]{1,0:T(8,128)(2,1)} %bitcast.174, bf16[192,1024]{1,0:T(8,128)(2,1)} %copy-done.6, bf16[192,1024]{1,0:T(8,128)(2,1)} %copy-done.5, ...), custom_call_target="tpu_custom_call" | custom-call | tf_op jit(solution)/shard_map/attend_back/pallas_call | solution.py:295
  472.9 2.0 collective-permute-start.61
  479.4 6.2 collective-permute-start.62
  485.6 7.1 %add_convert_fusion = bf16[8,192,1536]{2,1,0:T(8,128)(2,1)S(1)} fusion(bf16[8,192,1536]{2,1,0:T(8,128)(2,1)} %collective-permute-done.82, bf16[8,192,1536]{2,1,0:T(8,128)(2,1)} %collective-permute-done.80, bf16[8,192,1536]{2,1,0:T(8,128)(2,1)} %get-tuple-element.57), kind=kLoop, calls=%fused_computation.8 | loop fusion | flops 14155776 | bytes 18874368 | tf_op jit(solution)/shard_map/convert_element_type | solution.py:880
  492.7 2.6 fusion.27
  501.9 98.1 %collective-permute-done.63 = f32[8,192]{1,0:T(8,128)S(1)} collective-permute-done((f32[8,192]{1,0:T(8,128)S(1)}, f32[8,192]{1,0:T(8,128)S(1)}, u32[]{:S(2)}, u32[]{:S(2)}) %collective-permute-start.63) | collective-permute-done | bytes 6176 | tf_op jit(solution)/shard_map/ppermute | solution.py:67
  603.1 20.9 %collective-permute-done.66 = bf16[192,576]{1,0:T(8,128)(2,1)S(1)} collective-permute-done((bf16[192,576]{1,0:T(8,128)(2,1)S(1)}, bf16[192,576]{1,0:T(8,128)(2,1)S(1)}, u32[]{:S(2)}, u32[]{:S(2)}) %collective-permute-start.66) | collective-permute-done | bytes 221216 | tf_op jit(solution)/shard_map/ppermute | solution.py:775
  624.2 6.2 collective-permute-start.52
  632.8 2.6 collective-permute-done.54
  635.4 6.7 %collective-permute-done.53 = bf16[192,1024]{1,0:T(8,128)(2,1)} collective-permute-done((bf16[192,1024]{1,0:T(8,128)(2,1)S(1)}, bf16[192,1024]{1,0:T(8,128)(2,1)}, u32[]{:S(2)}, u32[]{:S(2)}) %collective-permute-start.53) | collective-permute-done | bytes 393248 | tf_op jit(solution)/shard_map/ppermute | solution.py:36
  642.1 2.5 fusion.7
  645.6 3.2 fusion
  648.9 4.2 fusion.4
  (347 shorter events, 76.7 us)
Async XLA Ops:
  6.6 54.4 %collective-permute-start.33 = (bf16[4,192,1536]{2,1,0:T(8,128)(2,1)S(1)}, bf16[4,192,1536]{2,1,0:T(8,128)(2,1)}, u32[]{:S(2)}, u32[]{:S(2)}) collective-permute-start(bf16[4,192,1536]{2,1,0:T(8,128)(2,1)S(1)} %constant_dynamic-slice_fusion), channel_id=1, source_target_pairs={{0,2},{1,3},{2,0},{3,1},{4,6},{5,7},{6,4},{7,5},{8,10},{9,11},{10,... | collective-permute-start | bytes 7077896 | tf_op jit(solution)/shard_map/ppermute | solution.py:36
  61.0 68.5 %collective-permute-start.34 = (bf16[4,192,1536]{2,1,0:T(8,128)(2,1)}, bf16[4,192,1536]{2,1,0:T(8,128)(2,1)}, u32[]{:S(2)}, u32[]{:S(2)}) collective-permute-start(bf16[4,192,1536]{2,1,0:T(8,128)(2,1)} %collective-permute-done.33.near2), channel_id=1, source_target_pairs={{0,16},{16,0},{1,17},{17,1},{2,18},{18,2},{3,19},{19,3},{4,20},{20... | collective-permute-start | bytes 7077896 | tf_op jit(solution)/shard_map/ppermute | solution.py:805
  62.8 168.5 %collective-permute-start.32 = (bf16[8,192,1536]{2,1,0:T(8,128)(2,1)}, bf16[8,192,1536]{2,1,0:T(8,128)(2,1)}, u32[]{:S(2)}, u32[]{:S(2)}) collective-permute-start(bf16[8,192,1536]{2,1,0:T(8,128)(2,1)} %pad_maximum_fusion.w0), channel_id=1, source_target_pairs={{0,1},{1,0},{2,3},{3,2},{4,5},{5,4},{6,7},{7,6},{8,9},{9,8},{10,11... | collective-permute-start | bytes 14155784 | tf_op jit(solution)/shard_map/ppermute | solution.py:36
  63.0 13.8 %collective-permute-start.16 = (bf16[192,192]{1,0:T(8,128)(2,1)S(1)}, bf16[192,192]{1,0:T(8,128)(2,1)S(1)}, u32[]{:S(2)}, u32[]{:S(2)}) collective-permute-start(bf16[192,192]{1,0:T(8,128)(2,1)S(1)} %bitcast.195), channel_id=1, source_target_pairs={{3,0},{6,1},{9,2},{12,3},{2,4},{7,5},{8,6},{13,7},{1,8},{4,9},{11,... | collective-permute-start | bytes 221192 | tf_op jit(solution)/shard_map/ppermute | solution.py:771
  68.6 8.4 %collective-permute-start.15 = (bf16[192,192]{1,0:T(8,128)(2,1)S(1)}, bf16[192,192]{1,0:T(8,128)(2,1)S(1)}, u32[]{:S(2)}, u32[]{:S(2)}) collective-permute-start(bf16[192,192]{1,0:T(8,128)(2,1)S(1)} %bitcast.196), channel_id=1, source_target_pairs={{2,0},{7,1},{8,2},{13,3},{3,4},{6,5},{9,6},{12,7},{0,8},{5,9},{10,... | collective-permute-start | bytes 221192 | tf_op jit(solution)/shard_map/ppermute | solution.py:771
  70.8 8.9 %collective-permute-start.14 = (bf16[192,192]{1,0:T(8,128)(2,1)S(1)}, bf16[192,192]{1,0:T(8,128)(2,1)S(1)}, u32[]{:S(2)}, u32[]{:S(2)}) collective-permute-start(bf16[192,192]{1,0:T(8,128)(2,1)S(1)} %bitcast.197), channel_id=1, source_target_pairs={{1,0},{4,1},{11,2},{14,3},{0,4},{5,5},{10,6},{15,7},{3,8},{6,9},{9... | collective-permute-start | bytes 221192 | tf_op jit(solution)/shard_map/ppermute | solution.py:771
  76.9 10.7 %collective-permute-start = (f32[192,128]{1,0:T(8,128)S(1)}, f32[192,128]{1,0:T(8,128)S(1)}, u32[]{:S(2)}, u32[]{:S(2)}) collective-permute-start(f32[192,128]{1,0:T(8,128)S(1)} %concatenate.24.p0), channel_id=1, source_target_pairs={{0,1},{1,0},{2,3},{3,2},{4,5},{5,4},{6,7},{7,6},{8,9},{9,8},{10,11... | collective-permute-start | bytes 294920 | tf_op jit(solution)/shard_map/ppermute | solution.py:36
  77.0 13.3 %collective-permute-start.1 = (f32[192,128]{1,0:T(8,128)S(1)}, f32[192,128]{1,0:T(8,128)S(1)}, u32[]{:S(2)}, u32[]{:S(2)}) collective-permute-start(f32[192,128]{1,0:T(8,128)S(1)} %concatenate.24.p0), channel_id=1, source_target_pairs={{0,2},{1,3},{2,0},{3,1},{4,6},{5,7},{6,4},{7,5},{8,10},{9,11},{10,... | collective-permute-start | bytes 294920 | tf_op jit(solution)/shard_map/ppermute | solution.py:36
  81.0 9.4 %collective-permute-start.25 = (bf16[192,256]{1,0:T(8,128)(2,1)S(1)}, bf16[192,256]{1,0:T(8,128)(2,1)}, u32[]{:S(2)}, u32[]{:S(2)}) collective-permute-start(bf16[192,256]{1,0:T(8,128)(2,1)S(1)} %bitcast.201), channel_id=1, source_target_pairs={{0,3},{1,2},{2,1},{3,0},{4,7},{5,6},{6,5},{7,4},{8,11},{9,10},{10,... | collective-permute-start | bytes 294920 | tf_op jit(solution)/shard_map/ppermute | solution.py:36
  87.6 9.7 %collective-permute-start.24 = (bf16[192,256]{1,0:T(8,128)(2,1)S(1)}, bf16[192,256]{1,0:T(8,128)(2,1)S(1)}, u32[]{:S(2)}, u32[]{:S(2)}) collective-permute-start(bf16[192,256]{1,0:T(8,128)(2,1)S(1)} %bitcast.200), channel_id=1, source_target_pairs={{0,2},{1,3},{2,0},{3,1},{4,6},{5,7},{6,4},{7,5},{8,10},{9,11},{10,... | collective-permute-start | bytes 294920 | tf_op jit(solution)/shard_map/ppermute | solution.py:36
  90.2 9.6 %collective-permute-start.23 = (bf16[192,256]{1,0:T(8,128)(2,1)S(1)}, bf16[192,256]{1,0:T(8,128)(2,1)}, u32[]{:S(2)}, u32[]{:S(2)}) collective-permute-start(bf16[192,256]{1,0:T(8,128)(2,1)S(1)} %bitcast.199), channel_id=1, source_target_pairs={{0,1},{1,0},{2,3},{3,2},{4,5},{5,4},{6,7},{7,6},{8,9},{9,8},{10,11... | collective-permute-start | bytes 294920 | tf_op jit(solution)/shard_map/ppermute | solution.py:36
  90.4 14.3 %collective-permute-start.9 = (bf16[192,576]{1,0:T(8,128)(2,1)S(1)}, bf16[192,576]{1,0:T(8,128)(2,1)S(1)}, u32[]{:S(2)}, u32[]{:S(2)}) collective-permute-start(bf16[192,576]{1,0:T(8,128)(2,1)S(1)} %pad_maximum_fusion.7), channel_id=1, source_target_pairs={{3,0},{6,1},{9,2},{12,3},{2,4},{7,5},{8,6},{13,7},{1,8},{4,9},{11,... | collective-permute-start | bytes 663560 | tf_op jit(solution)/shard_map/ppermute | solution.py:771
  97.3 9.7 %collective-permute-start.8 = (bf16[192,576]{1,0:T(8,128)(2,1)S(1)}, bf16[192,576]{1,0:T(8,128)(2,1)S(1)}, u32[]{:S(2)}, u32[]{:S(2)}) collective-permute-start(bf16[192,576]{1,0:T(8,128)(2,1)S(1)} %pad_maximum_fusion.7), channel_id=1, source_target_pairs={{2,0},{7,1},{8,2},{13,3},{3,4},{6,5},{9,6},{12,7},{0,8},{5,9},{10,... | collective-permute-start | bytes 663560 | tf_op jit(solution)/shard_map/ppermute | solution.py:771
  101.4 20.8 %collective-permute-start.7 = (bf16[192,576]{1,0:T(8,128)(2,1)S(1)}, bf16[192,576]{1,0:T(8,128)(2,1)}, u32[]{:S(2)}, u32[]{:S(2)}) collective-permute-start(bf16[192,576]{1,0:T(8,128)(2,1)S(1)} %pad_maximum_fusion.7), channel_id=1, source_target_pairs={{1,0},{4,1},{11,2},{14,3},{0,4},{5,5},{10,6},{15,7},{3,8},{6,9},{9... | collective-permute-start | bytes 663560 | tf_op jit(solution)/shard_map/ppermute | solution.py:771
  104.7 17.5 %collective-permute-start.6 = (bf16[192,576]{1,0:T(8,128)(2,1)S(1)}, bf16[192,576]{1,0:T(8,128)(2,1)S(1)}, u32[]{:S(2)}, u32[]{:S(2)}) collective-permute-start(bf16[192,576]{1,0:T(8,128)(2,1)S(1)} %pad_maximum_fusion.7), channel_id=1, source_target_pairs={{0,0},{5,1},{10,2},{15,3},{1,4},{4,5},{11,6},{14,7},{2,8},{7,9},{8... | collective-permute-start | bytes 663560 | tf_op jit(solution)/shard_map/ppermute | solution.py:771
  107.7 20.0 %collective-permute-start.4 = (bf16[192,1024]{1,0:T(8,128)(2,1)S(1)}, bf16[192,1024]{1,0:T(8,128)(2,1)S(1)}, u32[]{:S(2)}, u32[]{:S(2)}) collective-permute-start(bf16[192,1024]{1,0:T(8,128)(2,1)S(1)} %bitcast.175), channel_id=1, source_target_pairs={{0,2},{1,3},{2,0},{3,1},{4,6},{5,7},{6,4},{7,5},{8,10},{9,11},{10,... | collective-permute-start | bytes 1179656 | tf_op jit(solution)/shard_map/ppermute | solution.py:36
  122.1 9.6 %collective-permute-start.3 = (bf16[192,1024]{1,0:T(8,128)(2,1)S(1)}, bf16[192,1024]{1,0:T(8,128)(2,1)S(1)}, u32[]{:S(2)}, u32[]{:S(2)}) collective-permute-start(bf16[192,1024]{1,0:T(8,128)(2,1)S(1)} %bitcast.176), channel_id=1, source_target_pairs={{0,1},{1,0},{2,3},{3,2},{4,5},{5,4},{6,7},{7,6},{8,9},{9,8},{10,11... | collective-permute-start | bytes 1179656 | tf_op jit(solution)/shard_map/ppermute | solution.py:36
  122.2 6.8 %collective-permute-start.17 = (bf16[4,192,192]{2,1,0:T(8,128)(2,1)S(1)}, bf16[4,192,192]{2,1,0:T(8,128)(2,1)S(1)}, u32[]{:S(2)}, u32[]{:S(2)}) collective-permute-start(bf16[4,192,192]{2,1,0:T(8,128)(2,1)S(1)} %pad_maximum_fusion.5.o0.proj), channel_id=1, source_target_pairs={{0,1},{1,0},{2,3},{3,2},{4,5},{5,4},{6,7},{7,6},{8,9},{9,8},{10,11... | collective-permute-start | bytes 884744 | tf_op jit(solution)/shard_map/ppermute | solution.py:36
  127.7 10.6 %collective-permute-start.5 = (bf16[192,1024]{1,0:T(8,128)(2,1)S(1)}, bf16[192,1024]{1,0:T(8,128)(2,1)S(1)}, u32[]{:S(2)}, u32[]{:S(2)}) collective-permute-start(bf16[192,1024]{1,0:T(8,128)(2,1)S(1)} %collective-permute-done.4.t2), channel_id=1, source_target_pairs={{0,1},{1,0},{2,3},{3,2},{4,5},{5,4},{6,7},{7,6},{8,9},{9,8},{10,11... | collective-permute-start | bytes 1179656 | tf_op jit(solution)/shard_map/ppermute | solution.py:36
  129.0 102.3 %collective-permute-start.35 = (bf16[4,192,1536]{2,1,0:T(8,128)(2,1)}, bf16[4,192,1536]{2,1,0:T(8,128)(2,1)}, u32[]{:S(2)}, u32[]{:S(2)}) collective-permute-start(bf16[4,192,1536]{2,1,0:T(8,128)(2,1)} %collective-permute-done.33.near2), channel_id=1, source_target_pairs={{0,1},{1,0},{2,3},{3,2},{4,5},{5,4},{6,7},{7,6},{8,9},{9,8},{10,11... | collective-permute-start | bytes 7077896 | tf_op jit(solution)/shard_map/ppermute | solution.py:36
  129.5 101.8 %collective-permute-start.36 = (bf16[4,192,1536]{2,1,0:T(8,128)(2,1)}, bf16[4,192,1536]{2,1,0:T(8,128)(2,1)}, u32[]{:S(2)}, u32[]{:S(2)}) collective-permute-start(bf16[4,192,1536]{2,1,0:T(8,128)(2,1)} %collective-permute-done.34.far2), channel_id=1, source_target_pairs={{0,1},{1,0},{2,3},{3,2},{4,5},{5,4},{6,7},{7,6},{8,9},{9,8},{10,11... | collective-permute-start | bytes 7077896 | tf_op jit(solution)/shard_map/ppermute | solution.py:36
  131.7 24.8 %collective-permute-start.18 = (bf16[4,192,192]{2,1,0:T(8,128)(2,1)S(1)}, bf16[4,192,192]{2,1,0:T(8,128)(2,1)S(1)}, u32[]{:S(2)}, u32[]{:S(2)}) collective-permute-start(bf16[4,192,192]{2,1,0:T(8,128)(2,1)S(1)} %pad_maximum_fusion.5.o0.proj), channel_id=1, source_target_pairs={{0,2},{1,3},{2,0},{3,1},{4,6},{5,7},{6,4},{7,5},{8,10},{9,11},{10,... | collective-permute-start | bytes 884744 | tf_op jit(solution)/shard_map/ppermute | solution.py:36
  138.3 20.1 %collective-permute-start.26 = (bf16[256,768]{0,1:T(8,128)(2,1)S(1)}, bf16[256,768]{0,1:T(8,128)(2,1)}, u32[]{:S(2)}, u32[]{:S(2)}) collective-permute-start(bf16[256,768]{0,1:T(8,128)(2,1)S(1)} %get-tuple-element.125), channel_id=1, source_target_pairs={{0,4},{4,8},{8,12},{12,0},{1,5},{5,9},{9,13},{13,1},{2,6},{6,10},{... | collective-permute-start | bytes 1179656 | tf_op jit(solution)/shard_map/ppermute | solution.py:46
  159.8 7.6 %collective-permute-start.12 = (bf16[192,256]{1,0:T(8,128)(2,1)S(1)}, bf16[192,256]{1,0:T(8,128)(2,1)S(1)}, u32[]{:S(2)}, u32[]{:S(2)}) collective-permute-start(bf16[192,256]{1,0:T(8,128)(2,1)S(1)} %get-tuple-element.130), channel_id=1, source_target_pairs={{0,3},{1,2},{2,1},{3,0},{4,7},{5,6},{6,5},{7,4},{8,11},{9,10},{10,... | collective-permute-start | bytes 294920 | tf_op jit(solution)/shard_map/ppermute | solution.py:36
  164.7 21.4 %collective-permute-start.27 = (bf16[256,768]{0,1:T(8,128)(2,1)S(1)}, bf16[256,768]{0,1:T(8,128)(2,1)S(1)}, u32[]{:S(2)}, u32[]{:S(2)}) collective-permute-start(bf16[256,768]{0,1:T(8,128)(2,1)S(1)} %get-tuple-element.125), channel_id=1, source_target_pairs={{0,8},{4,12},{8,0},{12,4},{1,9},{5,13},{9,1},{13,5},{2,10},{6,14},... | collective-permute-start | bytes 1179656 | tf_op jit(solution)/shard_map/ppermute | solution.py:46
  167.3 25.5 %collective-permute-start.28 = (bf16[256,768]{0,1:T(8,128)(2,1)S(1)}, bf16[256,768]{0,1:T(8,128)(2,1)S(1)}, u32[]{:S(2)}, u32[]{:S(2)}) collective-permute-start(bf16[256,768]{0,1:T(8,128)(2,1)S(1)} %get-tuple-element.125), channel_id=1, source_target_pairs={{0,12},{4,0},{8,4},{12,8},{1,13},{5,1},{9,5},{13,9},{2,14},{6,2},{... | collective-permute-start | bytes 1179656 | tf_op jit(solution)/shard_map/ppermute | solution.py:46
  186.1 27.8 %collective-permute-start.20 = (bf16[256,768]{1,0:T(8,128)(2,1)}, bf16[256,768]{1,0:T(8,128)(2,1)S(1)}, u32[]{:S(2)}, u32[]{:S(2)}) collective-permute-start(bf16[256,768]{1,0:T(8,128)(2,1)} %get-tuple-element.41.x0), channel_id=1, source_target_pairs={{0,4},{4,8},{8,12},{12,0},{1,5},{5,9},{9,13},{13,1},{2,6},{6,10},{... | collective-permute-start | bytes 1179656 | tf_op jit(solution)/shard_map/ppermute | solution.py:46
  192.8 11.8 %collective-permute-start.29 = (f32[8,256]{1,0:T(8,128)}, f32[8,256]{1,0:T(8,128)S(1)}, u32[]{:S(2)}, u32[]{:S(2)}) collective-permute-start(f32[8,256]{1,0:T(8,128)} %get-tuple-element.40.s0.stats), channel_id=1, source_target_pairs={{0,4},{4,8},{8,12},{12,0},{1,5},{5,9},{9,13},{13,1},{2,6},{6,10},{... | collective-permute-start | bytes 24584 | tf_op jit(solution)/shard_map/ppermute | solution.py:46
  213.6 17.7 %collective-permute-start.21 = (bf16[256,768]{1,0:T(8,128)(2,1)}, bf16[256,768]{1,0:T(8,128)(2,1)S(1)}, u32[]{:S(2)}, u32[]{:S(2)}) collective-permute-start(bf16[256,768]{1,0:T(8,128)(2,1)} %get-tuple-element.41.x0), channel_id=1, source_target_pairs={{0,8},{4,12},{8,0},{12,4},{1,9},{5,13},{9,1},{13,5},{2,10},{6,14},... | collective-permute-start | bytes 1179656 | tf_op jit(solution)/shard_map/ppermute | solution.py:46
  213.9 17.4 %collective-permute-start.22 = (bf16[256,768]{1,0:T(8,128)(2,1)}, bf16[256,768]{1,0:T(8,128)(2,1)S(1)}, u32[]{:S(2)}, u32[]{:S(2)}) collective-permute-start(bf16[256,768]{1,0:T(8,128)(2,1)} %get-tuple-element.41.x0), channel_id=1, source_target_pairs={{0,12},{4,0},{8,4},{12,8},{1,13},{5,1},{9,5},{13,9},{2,14},{6,2},{... | collective-permute-start | bytes 1179656 | tf_op jit(solution)/shard_map/ppermute | solution.py:46
  290.0 8.2 %collective-permute-start.81 = (bf16[8,192,1536]{2,1,0:T(8,128)(2,1)}, bf16[8,192,1536]{2,1,0:T(8,128)(2,1)S(1)}, u32[]{:S(2)}, u32[]{:S(2)}) collective-permute-start(bf16[8,192,1536]{2,1,0:T(8,128)(2,1)} %get-tuple-element.60), channel_id=1, source_target_pairs={{0,1},{1,0},{2,3},{3,2},{4,5},{5,4},{6,7},{7,6},{8,9},{9,8},{10,11... | collective-permute-start | bytes 14155784 | tf_op jit(solution)/shard_map/ppermute | solution.py:36
  290.1 188.6 %collective-permute-start.80 = (bf16[8,192,1536]{2,1,0:T(8,128)(2,1)}, bf16[8,192,1536]{2,1,0:T(8,128)(2,1)}, u32[]{:S(2)}, u32[]{:S(2)}) collective-permute-start(bf16[8,192,1536]{2,1,0:T(8,128)(2,1)} %get-tuple-element.58), channel_id=1, source_target_pairs={{0,1},{1,0},{2,3},{3,2},{4,5},{5,4},{6,7},{7,6},{8,9},{9,8},{10,11... | collective-permute-start | bytes 14155784 | tf_op jit(solution)/shard_map/ppermute | solution.py:36
  304.2 175.2 %collective-permute-start.82 = (bf16[8,192,1536]{2,1,0:T(8,128)(2,1)}, bf16[8,192,1536]{2,1,0:T(8,128)(2,1)}, u32[]{:S(2)}, u32[]{:S(2)}) collective-permute-start(bf16[8,192,1536]{2,1,0:T(8,128)(2,1)} %add_convert_fusion.1), channel_id=1, source_target_pairs={{0,2},{1,3},{2,0},{3,1},{4,6},{5,7},{6,4},{7,5},{8,10},{9,11},{10,... | collective-permute-start | bytes 14155784 | tf_op jit(solution)/shard_map/ppermute | solution.py:36
  305.8 10.4 %collective-permute-start.46 = (f32[8,256]{1,0:T(8,128)S(1)}, f32[8,256]{1,0:T(8,128)S(1)}, u32[]{:S(2)}, u32[]{:S(2)}) collective-permute-start(f32[8,256]{1,0:T(8,128)S(1)} %get-tuple-element.149), channel_id=1, source_target_pairs={{0,12},{4,0},{8,4},{12,8},{1,13},{5,1},{9,5},{13,9},{2,14},{6,2},{... | collective-permute-start | bytes 24584 | tf_op jit(solution)/shard_map/ppermute | solution.py:46
  316.2 13.5 %collective-permute-start.43 = (bf16[256,768]{1,0:T(8,128)(2,1)S(1)}, bf16[256,768]{1,0:T(8,128)(2,1)S(1)}, u32[]{:S(2)}, u32[]{:S(2)}) collective-permute-start(bf16[256,768]{1,0:T(8,128)(2,1)S(1)} %get-tuple-element.99), channel_id=1, source_target_pairs={{0,12},{4,0},{8,4},{12,8},{1,13},{5,1},{9,5},{13,9},{2,14},{6,2},{... | collective-permute-start | bytes 1179656 | tf_op jit(solution)/shard_map/ppermute | solution.py:46
  320.2 48.2 %collective-permute-start.44 = (bf16[256,768]{1,0:T(8,128)(2,1)S(1)}, bf16[256,768]{1,0:T(8,128)(2,1)S(1)}, u32[]{:S(2)}, u32[]{:S(2)}) collective-permute-start(bf16[256,768]{1,0:T(8,128)(2,1)S(1)} %get-tuple-element.98), channel_id=1, source_target_pairs={{0,8},{4,12},{8,0},{12,4},{1,9},{5,13},{9,1},{13,5},{2,10},{6,14},... | collective-permute-start | bytes 1179656 | tf_op jit(solution)/shard_map/ppermute | solution.py:46
  320.9 47.5 %collective-permute-start.45 = (bf16[256,768]{1,0:T(8,128)(2,1)S(1)}, bf16[256,768]{1,0:T(8,128)(2,1)S(1)}, u32[]{:S(2)}, u32[]{:S(2)}) collective-permute-start(bf16[256,768]{1,0:T(8,128)(2,1)S(1)} %get-tuple-element.97), channel_id=1, source_target_pairs={{0,4},{4,8},{8,12},{12,0},{1,5},{5,9},{9,13},{13,1},{2,6},{6,10},{... | collective-permute-start | bytes 1179656 | tf_op jit(solution)/shard_map/ppermute | solution.py:46
  329.7 45.8 %collective-permute-start.37 = (bf16[256,768]{1,0:T(8,128)(2,1)S(1)}, bf16[256,768]{1,0:T(8,128)(2,1)S(1)}, u32[]{:S(2)}, u32[]{:S(2)}) collective-permute-start(bf16[256,768]{1,0:T(8,128)(2,1)S(1)} %get-tuple-element.103), channel_id=1, source_target_pairs={{0,12},{4,0},{8,4},{12,8},{1,13},{5,1},{9,5},{13,9},{2,14},{6,2},{... | collective-permute-start | bytes 1179656 | tf_op jit(solution)/shard_map/ppermute | solution.py:46
  368.4 19.2 %collective-permute-start.38 = (bf16[256,768]{1,0:T(8,128)(2,1)S(1)}, bf16[256,768]{1,0:T(8,128)(2,1)S(1)}, u32[]{:S(2)}, u32[]{:S(2)}) collective-permute-start(bf16[256,768]{1,0:T(8,128)(2,1)S(1)} %get-tuple-element.102), channel_id=1, source_target_pairs={{0,8},{4,12},{8,0},{12,4},{1,9},{5,13},{9,1},{13,5},{2,10},{6,14},... | collective-permute-start | bytes 1179656 | tf_op jit(solution)/shard_map/ppermute | solution.py:46
  368.4 20.3 %collective-permute-start.39 = (bf16[256,768]{1,0:T(8,128)(2,1)S(1)}, bf16[256,768]{1,0:T(8,128)(2,1)S(1)}, u32[]{:S(2)}, u32[]{:S(2)}) collective-permute-start(bf16[256,768]{1,0:T(8,128)(2,1)S(1)} %get-tuple-element.101), channel_id=1, source_target_pairs={{0,4},{4,8},{8,12},{12,0},{1,5},{5,9},{9,13},{13,1},{2,6},{6,10},{... | collective-permute-start | bytes 1179656 | tf_op jit(solution)/shard_map/ppermute | solution.py:46
  375.5 32.2 %collective-permute-start.57 = (f32[12,256]{1,0:T(8,128)}, f32[12,256]{1,0:T(8,128)S(1)}, u32[]{:S(2)}, u32[]{:S(2)}) collective-permute-start(f32[12,256]{1,0:T(8,128)} %get-tuple-element.52), channel_id=1, source_target_pairs={{0,3},{1,2},{2,1},{3,0},{4,7},{5,6},{6,5},{7,4},{8,11},{9,10},{10,... | collective-permute-start | bytes 36872 | tf_op jit(solution)/shard_map/ppermute | solution.py:36
  387.6 21.8 %collective-permute-start.56 = (f32[12,256]{1,0:T(8,128)}, f32[12,256]{1,0:T(8,128)S(1)}, u32[]{:S(2)}, u32[]{:S(2)}) collective-permute-start(f32[12,256]{1,0:T(8,128)} %get-tuple-element.52), channel_id=1, source_target_pairs={{0,2},{1,3},{2,0},{3,1},{4,6},{5,7},{6,4},{7,5},{8,10},{9,11},{10,... | collective-permute-start | bytes 36872 | tf_op jit(solution)/shard_map/ppermute | solution.py:36
  388.7 21.8 %collective-permute-start.55 = (f32[12,256]{1,0:T(8,128)}, f32[12,256]{1,0:T(8,128)S(1)}, u32[]{:S(2)}, u32[]{:S(2)}) collective-permute-start(f32[12,256]{1,0:T(8,128)} %get-tuple-element.52), channel_id=1, source_target_pairs={{0,1},{1,0},{2,3},{3,2},{4,5},{5,4},{6,7},{7,6},{8,9},{9,8},{10,11... | collective-permute-start | bytes 36872 | tf_op jit(solution)/shard_map/ppermute | solution.py:36
  411.2 24.8 %collective-permute-start.42 = (f32[192,256]{1,0:T(8,128)S(1)}, f32[192,256]{1,0:T(8,128)S(1)}, u32[]{:S(2)}, u32[]{:S(2)}) collective-permute-start(f32[192,256]{1,0:T(8,128)S(1)} %get-tuple-element.114), channel_id=1, source_target_pairs={{0,3},{1,2},{2,1},{3,0},{4,7},{5,6},{6,5},{7,4},{8,11},{9,10},{10,... | collective-permute-start | bytes 589832 | tf_op jit(solution)/shard_map/ppermute | solution.py:36
  413.3 23.2 %collective-permute-start.41 = (f32[192,256]{1,0:T(8,128)S(1)}, f32[192,256]{1,0:T(8,128)S(1)}, u32[]{:S(2)}, u32[]{:S(2)}) collective-permute-start(f32[192,256]{1,0:T(8,128)S(1)} %get-tuple-element.115), channel_id=1, source_target_pairs={{0,2},{1,3},{2,0},{3,1},{4,6},{5,7},{6,4},{7,5},{8,10},{9,11},{10,... | collective-permute-start | bytes 589832 | tf_op jit(solution)/shard_map/ppermute | solution.py:36
  414.4 10.1 %collective-permute-start.77 = (f32[32,192]{1,0:T(8,128)S(1)}, f32[32,192]{1,0:T(8,128)S(1)}, u32[]{:S(2)}, u32[]{:S(2)}) collective-permute-start(f32[32,192]{1,0:T(8,128)S(1)} %fusion.11), channel_id=1, source_target_pairs={{0,4},{4,0},{8,12},{12,8},{1,5},{5,1},{9,13},{13,9},{2,6},{6,2},{1... | collective-permute-start | bytes 73736 | tf_op jit(solution)/shard_map/ppermute | solution.py:41
  433.2 7.8 %collective-permute-start.50 = (bf16[768,256]{1,0:T(8,128)(2,1)S(1)}, bf16[768,256]{1,0:T(8,128)(2,1)S(1)}, u32[]{:S(2)}, u32[]{:S(2)}) collective-permute-start(bf16[768,256]{1,0:T(8,128)(2,1)S(1)} %copy-done.26), channel_id=1, source_target_pairs={{0,2},{1,3},{2,0},{3,1},{4,6},{5,7},{6,4},{7,5},{8,10},{9,11},{10,... | collective-permute-start | bytes 1179656 | tf_op jit(solution)/shard_map/ppermute | solution.py:36
  476.0 21.1 %collective-permute-start.72 = (bf16[192,192]{1,0:T(8,128)(2,1)S(1)}, bf16[192,192]{1,0:T(8,128)(2,1)S(1)}, u32[]{:S(2)}, u32[]{:S(2)}) collective-permute-start(bf16[192,192]{1,0:T(8,128)(2,1)S(1)} %get-tuple-element.121), channel_id=1, source_target_pairs={{0,3},{1,7},{2,11},{3,15},{4,2},{5,6},{6,10},{7,14},{8,1},{9,5},{1... | collective-permute-start | bytes 221192 | tf_op jit(solution)/shard_map/ppermute | solution.py:775
  476.1 22.6 %collective-permute-start.71 = (bf16[192,192]{1,0:T(8,128)(2,1)S(1)}, bf16[192,192]{1,0:T(8,128)(2,1)S(1)}, u32[]{:S(2)}, u32[]{:S(2)}) collective-permute-start(bf16[192,192]{1,0:T(8,128)(2,1)S(1)} %get-tuple-element.122), channel_id=1, source_target_pairs={{0,2},{1,6},{2,10},{3,14},{4,3},{5,7},{6,11},{7,15},{8,0},{9,4},{1... | collective-permute-start | bytes 221192 | tf_op jit(solution)/shard_map/ppermute | solution.py:775
  477.2 21.6 %collective-permute-start.70 = (bf16[192,192]{1,0:T(8,128)(2,1)S(1)}, bf16[192,192]{1,0:T(8,128)(2,1)S(1)}, u32[]{:S(2)}, u32[]{:S(2)}) collective-permute-start(bf16[192,192]{1,0:T(8,128)(2,1)S(1)} %get-tuple-element.123), channel_id=1, source_target_pairs={{0,1},{1,5},{2,9},{3,13},{4,0},{5,4},{6,8},{7,12},{8,3},{9,7},{10,... | collective-permute-start | bytes 221192 | tf_op jit(solution)/shard_map/ppermute | solution.py:775
  478.7 20.7 %collective-permute-start.69 = (bf16[192,192]{1,0:T(8,128)(2,1)S(1)}, bf16[192,192]{1,0:T(8,128)(2,1)S(1)}, u32[]{:S(2)}, u32[]{:S(2)}) collective-permute-start(bf16[192,192]{1,0:T(8,128)(2,1)S(1)} %get-tuple-element.120), channel_id=1, source_target_pairs={{0,0},{1,4},{2,8},{3,12},{4,1},{5,5},{6,9},{7,13},{8,2},{9,6},{10,... | collective-permute-start | bytes 221192 | tf_op jit(solution)/shard_map/ppermute | solution.py:775
  479.4 17.2 %collective-permute-start.62 = (f32[8,192]{1,0:T(8,128)S(1)}, f32[8,192]{1,0:T(8,128)S(1)}, u32[]{:S(2)}, u32[]{:S(2)}) collective-permute-start(f32[8,192]{1,0:T(8,128)S(1)} %add.239), channel_id=1, source_target_pairs={{0,8},{4,12},{8,0},{12,4},{1,9},{5,13},{9,1},{13,5},{2,10},{6,14},... | collective-permute-start | bytes 18440 | tf_op jit(solution)/shard_map/ppermute | solution.py:41
  496.6 149.0 %collective-permute-start.83 = (bf16[4,192,1536]{2,1,0:T(8,128)(2,1)}, bf16[4,192,1536]{2,1,0:T(8,128)(2,1)S(1)}, u32[]{:S(2)}, u32[]{:S(2)}) collective-permute-start(bf16[4,192,1536]{2,1,0:T(8,128)(2,1)} %get-tuple-element.93), channel_id=1, source_target_pairs={{0,16},{16,0},{1,17},{17,1},{2,18},{18,2},{3,19},{19,3},{4,20},{20... | collective-permute-start | bytes 7077896 | tf_op jit(solution)/shard_map/ppermute | solution.py:884
  497.1 148.5 %collective-permute-start.84 = (bf16[4,192,1536]{2,1,0:T(8,128)(2,1)}, bf16[4,192,1536]{2,1,0:T(8,128)(2,1)}, u32[]{:S(2)}, u32[]{:S(2)}) collective-permute-start(bf16[4,192,1536]{2,1,0:T(8,128)(2,1)} %get-tuple-element.92), channel_id=1, source_target_pairs={{0,16},{16,0},{1,17},{17,1},{2,18},{18,2},{3,19},{19,3},{4,20},{20... | collective-permute-start | bytes 7077896 | tf_op jit(solution)/shard_map/ppermute | solution.py:883
  498.7 102.9 %collective-permute-start.67 = (bf16[192,576]{1,0:T(8,128)(2,1)S(1)}, bf16[192,576]{1,0:T(8,128)(2,1)S(1)}, u32[]{:S(2)}, u32[]{:S(2)}) collective-permute-start(bf16[192,576]{1,0:T(8,128)(2,1)S(1)} %get-tuple-element.106), channel_id=1, source_target_pairs={{0,3},{1,7},{2,11},{3,15},{4,2},{5,6},{6,10},{7,14},{8,1},{9,5},{1... | collective-permute-start | bytes 663560 | tf_op jit(solution)/shard_map/ppermute | solution.py:775
  498.8 101.2 %collective-permute-start.63 = (f32[8,192]{1,0:T(8,128)S(1)}, f32[8,192]{1,0:T(8,128)S(1)}, u32[]{:S(2)}, u32[]{:S(2)}) collective-permute-start(f32[8,192]{1,0:T(8,128)S(1)} %add.240), channel_id=1, source_target_pairs={{0,16},{16,0},{1,17},{17,1},{2,18},{18,2},{3,19},{19,3},{4,20},{20... | collective-permute-start | bytes 18440 | tf_op jit(solution)/shard_map/ppermute | solution.py:67
  499.5 102.2 %collective-permute-start.73 = (bf16[192,192]{1,0:T(8,128)(2,1)S(1)}, bf16[192,192]{1,0:T(8,128)(2,1)S(1)}, u32[]{:S(2)}, u32[]{:S(2)}) collective-permute-start(bf16[192,192]{1,0:T(8,128)(2,1)S(1)} %add_convert_fusion.3), channel_id=1, source_target_pairs={{0,16},{16,0},{1,17},{17,1},{2,18},{18,2},{3,19},{19,3},{4,20},{20... | collective-permute-start | bytes 221192 | tf_op jit(solution)/shard_map/ppermute | solution.py:67
  600.0 24.1 %collective-permute-start.66 = (bf16[192,576]{1,0:T(8,128)(2,1)S(1)}, bf16[192,576]{1,0:T(8,128)(2,1)S(1)}, u32[]{:S(2)}, u32[]{:S(2)}) collective-permute-start(bf16[192,576]{1,0:T(8,128)(2,1)S(1)} %get-tuple-element.107), channel_id=1, source_target_pairs={{0,2},{1,6},{2,10},{3,14},{4,3},{5,7},{6,11},{7,15},{8,0},{9,4},{1... | collective-permute-start | bytes 663560 | tf_op jit(solution)/shard_map/ppermute | solution.py:775
  601.7 22.4 %collective-permute-start.65 = (bf16[192,576]{1,0:T(8,128)(2,1)S(1)}, bf16[192,576]{1,0:T(8,128)(2,1)S(1)}, u32[]{:S(2)}, u32[]{:S(2)}) collective-permute-start(bf16[192,576]{1,0:T(8,128)(2,1)S(1)} %get-tuple-element.108), channel_id=1, source_target_pairs={{0,1},{1,5},{2,9},{3,13},{4,0},{5,4},{6,8},{7,12},{8,3},{9,7},{10,... | collective-permute-start | bytes 663560 | tf_op jit(solution)/shard_map/ppermute | solution.py:775
  601.7 22.5 %collective-permute-start.64 = (bf16[192,576]{1,0:T(8,128)(2,1)S(1)}, bf16[192,576]{1,0:T(8,128)(2,1)S(1)}, u32[]{:S(2)}, u32[]{:S(2)}) collective-permute-start(bf16[192,576]{1,0:T(8,128)(2,1)S(1)} %get-tuple-element.105), channel_id=1, source_target_pairs={{0,0},{1,4},{2,8},{3,12},{4,1},{5,5},{6,9},{7,13},{8,2},{9,6},{10,... | collective-permute-start | bytes 663560 | tf_op jit(solution)/shard_map/ppermute | solution.py:775
  624.1 11.3 %collective-permute-start.54 = (bf16[192,1024]{1,0:T(8,128)(2,1)}, bf16[192,1024]{1,0:T(8,128)(2,1)}, u32[]{:S(2)}, u32[]{:S(2)}) collective-permute-start(bf16[192,1024]{1,0:T(8,128)(2,1)} %get-tuple-element.95), channel_id=1, source_target_pairs={{0,3},{1,2},{2,1},{3,0},{4,7},{5,6},{6,5},{7,4},{8,11},{9,10},{10,... | collective-permute-start | bytes 1179656 | tf_op jit(solution)/shard_map/ppermute | solution.py:36
  624.1 18.0 %collective-permute-start.53 = (bf16[192,1024]{1,0:T(8,128)(2,1)S(1)}, bf16[192,1024]{1,0:T(8,128)(2,1)}, u32[]{:S(2)}, u32[]{:S(2)}) collective-permute-start(bf16[192,1024]{1,0:T(8,128)(2,1)S(1)} %get-tuple-element.96), channel_id=1, source_target_pairs={{0,2},{1,3},{2,0},{3,1},{4,6},{5,7},{6,4},{7,5},{8,10},{9,11},{10,... | collective-permute-start | bytes 1179656 | tf_op jit(solution)/shard_map/ppermute | solution.py:36
  624.2 17.9 %collective-permute-start.52 = (bf16[192,1024]{1,0:T(8,128)(2,1)S(1)}, bf16[192,1024]{1,0:T(8,128)(2,1)}, u32[]{:S(2)}, u32[]{:S(2)}) collective-permute-start(bf16[192,1024]{1,0:T(8,128)(2,1)S(1)} %get-tuple-element.94), channel_id=1, source_target_pairs={{0,1},{1,0},{2,3},{3,2},{4,5},{5,4},{6,7},{7,6},{8,9},{9,8},{10,11... | collective-permute-start | bytes 1179656 | tf_op jit(solution)/shard_map/ppermute | solution.py:36
  635.4 9.3 %collective-permute-start.68 = (bf16[192,576]{1,0:T(8,128)(2,1)S(1)}, bf16[192,576]{1,0:T(8,128)(2,1)S(1)}, u32[]{:S(2)}, u32[]{:S(2)}) collective-permute-start(bf16[192,576]{1,0:T(8,128)(2,1)S(1)} %add_convert_fusion.2), channel_id=1, source_target_pairs={{0,16},{16,0},{1,17},{17,1},{2,18},{18,2},{3,19},{19,3},{4,20},{20... | collective-permute-start | bytes 663560 | tf_op jit(solution)/shard_map/ppermute | solution.py:67
  (87 other events, 2006.2 us)

commit v2 on v1

--- a/solution.py
+++ b/solution.py
@@ -14,7 +14,10 @@
 VMEM_LIMIT = 60 * 1024 * 1024
 F32 = jnp.float32
 BF16 = jnp.bfloat16
-GAIN1, GAIN2, VALUE0, VALUE1 = 16, 17, 18, 19
+PARAMS = 128
+GAIN1, GAIN2, VALUE0, VALUE1 = 16, 19, 22, 25
+SUM_GAIN2, SUM_VALUE0, SUM_VALUE1, SUM_GAIN1 = 16, 17, 18, 19
+EXTRA = 16
 
 
 def mm(left, right, over_left, over_right, precision=None):
@@ -27,8 +30,36 @@
     )
 
 
-def after(value, *others):
-    return lax.optimization_barrier((value,) + others)[0]
+def parts_of(value):
+    high = lax.reduce_precision(value, 8, 7)
+    middle = lax.reduce_precision(value - high, 8, 7)
+    return [high.astype(BF16), middle.astype(BF16), (value - high - middle).astype(BF16)]
+
+
+def column(params, first):
+    low = params[:, first : first + 3].astype(F32)
+    return low[:, 0:1] + low[:, 1:2] + low[:, 2:3]
+
+
+def pack_rows(rows, width):
+    out = []
+    for row in rows:
+        high = row.astype(BF16).astype(F32)
+        middle = (row - high).astype(BF16).astype(F32)
+        out += [high, middle, row - high - middle]
+    out.append(jnp.zeros((EXTRA - len(out), rows[0].shape[1]), F32))
+    packed = jnp.concatenate(out, axis=0)
+    rest = jnp.zeros((EXTRA, width - packed.shape[1]), F32)
+    return jnp.concatenate([packed, rest], axis=1).astype(BF16)
+
+
+def unpack_row(ref, base, span, k):
+    parts = ref[base : base + EXTRA, :span].astype(F32)
+    return parts[3 * k : 3 * k + 1] + parts[3 * k + 1 : 3 * k + 2] + parts[3 * k + 2 : 3 * k + 3]
+
+
+def join(*values):
+    return lax.optimization_barrier(values)
 
 
 def col_swap(value, bits):
@@ -89,7 +120,7 @@
 
 
 def attend_kernel(
-    place, t0, t1, t2, t3, p0, p1, p2, p3, weight, cosine, sine,
+    place, t0, t1, t2, t3, weight, cosine, sine,
     query_out, key_out, value_out, attn_out, logsum_out, act, w_all,
 ):
     block = pl.program_id(0)
@@ -100,18 +131,20 @@
     width = heads * HD
     count = query_out.shape[0]
     span = query_out.shape[2]
+    length = key_out.shape[1]
 
     @pl.when(block == 0)
     def _():
-        square = jnp.zeros((1, t0.shape[1]), F32)
+        square = jnp.zeros((1, length), F32)
         for ref in (t0, t1, t2, t3):
-            hidden = ref[...].astype(F32)
+            hidden = ref[:, :length].astype(F32)
             square = square + jnp.sum(hidden * hidden, axis=0, keepdims=True)
         inverse = lax.rsqrt(square / (size * 4) + EPS)
-        for k, (ref, params) in enumerate(((t0, p0), (t1, p1), (t2, p2), (t3, p3))):
-            gain = params[:, GAIN1 : GAIN1 + 1]
-            act[k * size : (k + 1) * size] = (ref[...].astype(F32) * inverse * gain).astype(BF16)
-            w_all[k * size : (k + 1) * size] = weight[row ^ k]
+        for k, ref in enumerate((t0, t1, t2, t3)):
+            gain = column(ref[:, length:], GAIN1)
+            hidden = ref[:, :length].astype(F32)
+            act[k * size : (k + 1) * size] = (hidden * inverse * gain).astype(BF16)
+            w_all[k * size : (k + 1) * size] = weight[row ^ k, :, : 3 * width]
         qkv = mm(w_all[...], act[...], 0, 0)
         query = rotate_halves(qkv[:width], cosine[...], sine[...]).astype(BF16)
         keys = rotate_halves(qkv[width : 2 * width], cosine[...], sine[...]).astype(BF16)
@@ -120,7 +153,6 @@
         key_out[...] = keys
         value_out[...] = qkv[2 * width :].astype(BF16)
 
-    length = key_out.shape[1]
     places = lax.broadcasted_iota(jnp.int32, (length, span), 0)
     mine = lax.broadcasted_iota(jnp.int32, (1, span), 1) + block * span
     seen = places <= jnp.maximum(mine, prefix - 1)
@@ -139,17 +171,18 @@
     logsum_out[...] = jnp.concatenate(rows, axis=0)
 
 
-def attend(place, toks, params, weight, cosine, sine):
-    size, length = toks[0].shape
+def attend(place, toks, weight, cosine, sine):
+    size = toks[0].shape[0]
+    length = cosine.shape[1]
     count = lax.axis_size("col")
     span = length // count
-    width = weight.shape[2] // 3
+    width = weight.shape[2] // 4
 
     def whole(array):
         zeros = (0,) * array.ndim
         return pl.BlockSpec(array.shape, lambda q, s: zeros)
 
-    args = (*toks, *params, weight, cosine, sine)
+    args = (*toks, weight, cosine, sine)
     return pl.pallas_call(
         attend_kernel,
         name="attend",
@@ -181,16 +214,17 @@
 
 
 def attend_back_kernel(
-    place, t0, t1, t2, t3, p0, p1, p2, p3, weight, proj, cosine, sine,
-    query, keys, values, attn, logsum, d0, d1, d2, d3, grad_mid,
-    tokens_out, qkv_out, proj_out, gain_out,
+    place, t0, t1, t2, t3, weight, cosine, sine,
+    query, keys, values, attn, logsum, d0, d1, d2, d3, grad_mid, small,
+    tokens_out, weight_out, small_out,
     dmid, proj_all, proj_acc, key_acc, value_acc, grad_all,
 ):
     block = pl.program_id(0)
     row = place[0]
     col = place[1]
     prefix = place[2]
-    size, length = t0.shape
+    size = t0.shape[0]
+    length = cosine.shape[1]
     count, width, span = query.shape
     heads = width // HD
     last = count - 1
@@ -198,7 +232,7 @@
     @pl.when(block == 0)
     def _():
         for k in range(count):
-            proj_all[k * size : (k + 1) * size] = proj[row ^ k]
+            proj_all[k * size : (k + 1) * size] = weight[row ^ k, :, 3 * width :]
         proj_acc[...] = jnp.zeros_like(proj_acc)
         key_acc[...] = jnp.zeros_like(key_acc)
         value_acc[...] = jnp.zeros_like(value_acc)
@@ -247,27 +281,31 @@
         grad_all[width : 2 * width] = turned.astype(BF16)
         grad_all[2 * width :] = value_acc[...].astype(BF16)
         refs = (t0, t1, t2, t3)
-        gains = [params[:, GAIN1 : GAIN1 + 1] for params in (p0, p1, p2, p3)]
+        gains = [column(ref[:, length:], GAIN1) for ref in refs]
         square = jnp.zeros((1, length), F32)
         for ref in refs:
-            hidden = ref[...].astype(F32)
+            hidden = ref[:, :length].astype(F32)
             square = square + jnp.sum(hidden * hidden, axis=0, keepdims=True)
         inverse = lax.rsqrt(square / (size * count) + EPS)
         backs = []
         inner = jnp.zeros((1, length), F32)
         for k in range(count):
-            hidden = refs[k][...].astype(F32)
+            hidden = refs[k][:, :length].astype(F32)
             act = (hidden * inverse * gains[k]).astype(BF16)
-            qkv_out[row ^ col ^ k] = mm(act, grad_all[...], 1, 1).astype(BF16)
-            proj_out[row ^ col ^ k] = proj_acc[k * size : (k + 1) * size].astype(BF16)
-            back = mm(weight[row ^ k], grad_all[...], 1, 0)
+            weight_out[row ^ col ^ k, :, : 3 * width] = mm(act, grad_all[...], 1, 1).astype(BF16)
+            weight_out[row ^ col ^ k, :, 3 * width :] = proj_acc[
+                k * size : (k + 1) * size
+            ].astype(BF16)
+            back = mm(weight[row ^ k, :, : 3 * width], grad_all[...], 1, 0)
             inner = inner + jnp.sum(hidden * gains[k] * back, axis=0, keepdims=True)
             summed = jnp.sum(hidden * inverse * back, axis=1, keepdims=True)
-            gain_out[k] = jnp.transpose(jnp.broadcast_to(summed, (size, 128)))[:8]
+            turned = jnp.transpose(jnp.broadcast_to(summed, (size, 128)))[: small.shape[1]]
+            places = lax.broadcasted_iota(jnp.int32, turned.shape, 0)
+            small_out[k] = jnp.where(places == SUM_GAIN1, turned, small[k])
             backs.append(back)
         inner = inner * (inverse * inverse * inverse) / (size * count)
         for k in range(count):
-            hidden = refs[k][...].astype(F32)
+            hidden = refs[k][:, :length].astype(F32)
             grad = inverse * gains[k] * backs[k] - hidden * inner
             for i in range(count):
                 here = slice(i * span, (i + 1) * span)
@@ -276,9 +314,10 @@
 
 
 def attend_back(
-    place, toks, params, weight, proj, cosine, sine, query, keys, values, attn, logsum, lows, grad_mid
+    place, toks, weight, cosine, sine, query, keys, values, attn, logsum, lows, grad_mid, small
 ):
-    size, length = toks[0].shape
+    size = toks[0].shape[0]
+    length = cosine.shape[1]
     count, width, span = query.shape
 
     def whole(array):
@@ -286,10 +325,10 @@
         return pl.BlockSpec(array.shape, lambda q, s: zeros)
 
     args = (
-        *toks, *params, weight, proj, cosine, sine, query, keys, values, attn, logsum, *lows, grad_mid,
+        *toks, weight, cosine, sine, query, keys, values, attn, logsum, *lows, grad_mid, small,
     )
     specs = [whole(a) for a in args]
-    at = len(toks) + len(params) + 4 + 3
+    at = len(toks) + 3 + 3
     specs[at] = pl.BlockSpec((1, width, span), lambda q, s: (q ^ s[1], 0, 0))
     specs[at + 1] = pl.BlockSpec((8, span), lambda q, s: (0, q))
     return pl.pallas_call(
@@ -301,9 +340,8 @@
             in_specs=specs,
             out_specs=[
                 pl.BlockSpec((count, size, length), lambda q, s: (0, 0, 0)),
-                pl.BlockSpec((count, size, 3 * width), lambda q, s: (0, 0, 0)),
-                pl.BlockSpec((count, size, width), lambda q, s: (0, 0, 0)),
-                pl.BlockSpec((count, 8, size), lambda q, s: (0, 0, 0)),
+                pl.BlockSpec((count, size, 4 * width), lambda q, s: (0, 0, 0)),
+                pl.BlockSpec(small.shape, lambda q, s: (0, 0, 0)),
             ],
             scratch_shapes=[
                 pltpu.VMEM((size * count, span), BF16),
@@ -316,9 +354,8 @@
         ),
         out_shape=[
             jax.ShapeDtypeStruct((count, size, length), BF16),
-            jax.ShapeDtypeStruct((count, size, 3 * width), BF16),
-            jax.ShapeDtypeStruct((count, size, width), BF16),
-            jax.ShapeDtypeStruct((count, 8, size), F32),
+            jax.ShapeDtypeStruct((count, size, 4 * width), BF16),
+            jax.ShapeDtypeStruct(small.shape, F32),
         ],
         compiler_params=pltpu.CompilerParams(vmem_limit_bytes=VMEM_LIMIT),
     )(place, *args)
@@ -357,13 +394,14 @@
     summed = jnp.zeros((128, span), F32)
     normed = []
     for j in range(4):
-        norm = mid_out[j * size : (j + 1) * size] * inverse * params[j][:, GAIN2 : GAIN2 + 1]
-        summed = summed + mm(params[j][...], norm, 0, 0, HIGH)
+        norm = mid_out[j * size : (j + 1) * size] * inverse * column(params[j], GAIN2)
+        summed = summed + mm(params[j][...].astype(F32), norm, 0, 0, HIGH)
         normed.append(norm)
-    rows_out[...] = jnp.transpose(jnp.concatenate(normed, axis=0)).astype(BF16)
+    rows_out[:span] = jnp.transpose(jnp.concatenate(normed, axis=0)).astype(BF16)
     logits = summed[:kinds] + previous[...]
     _, chosen = route_rows(routes[...], logits)
     gates = pair_softmax(*chosen)
+    rows_out[span:] = pack_rows(gates, rows_out.shape[1])
     alpha = [
         *pair_softmax(summed[12:13], summed[13:14]),
         *pair_softmax(summed[14:15], summed[15:16]),
@@ -371,8 +409,13 @@
     stats_out[...] = jnp.concatenate([*gates, inverse, *alpha, jnp.zeros((1, span), F32)], axis=0)
 
 
-def middle(place, toks, params, parts, projs, previous, routes):
-    size, length = toks[0].shape
+def param_spec(array):
+    size, width = array.shape
+    return pl.BlockSpec((size, PARAMS), lambda i, s: (0, width // PARAMS - 1))
+
+
+def middle(place, toks, parts, projs, previous, routes):
+    size = toks[0].shape[0]
     span = parts[0].shape[1]
     count = lax.axis_size("col")
 
@@ -380,9 +423,10 @@
         zeros = (0,) * array.ndim
         return pl.BlockSpec(array.shape, lambda i, s: zeros)
 
-    args = (*toks, *params, *parts, *projs, previous, routes)
+    args = (*toks, *toks, *parts, *projs, previous, routes)
     specs = [pl.BlockSpec((size, span), lambda i, s: (0, s[1])) for _ in toks]
-    specs += [whole(a) for a in (*params, *parts, *projs)]
+    specs += [param_spec(a) for a in toks]
+    specs += [whole(a) for a in (*parts, *projs)]
     specs += [
         pl.BlockSpec((previous.shape[0], span), lambda i, s: (0, s[1])),
         pl.BlockSpec((2, span), lambda i, s: (0, s[0] * count + s[1])),
@@ -397,13 +441,13 @@
             in_specs=specs,
             out_specs=[
                 pl.BlockSpec((full, span), lambda i, s: (0, 0)),
-                pl.BlockSpec((span, full), lambda i, s: (0, 0)),
+                pl.BlockSpec((span + EXTRA, full), lambda i, s: (0, 0)),
                 pl.BlockSpec((8, span), lambda i, s: (0, 0)),
             ],
         ),
         out_shape=[
             jax.ShapeDtypeStruct((full, span), F32),
-            jax.ShapeDtypeStruct((span, full), BF16),
+            jax.ShapeDtypeStruct((span + EXTRA, full), BF16),
             jax.ShapeDtypeStruct((8, span), F32),
         ],
         compiler_params=pltpu.CompilerParams(vmem_limit_bytes=VMEM_LIMIT),
@@ -411,7 +455,7 @@
 
 
 def middle_back_kernel(
-    place, p0, p1, p2, p3, mid, grad, stats, routes, x0, x1, x2, x3, g0, g1, g2, g3,
+    place, p0, p1, p2, p3, mid, grad, stats, routes, x0, x1, x2, x3,
     low_out, mid_out, logits_out, small_out,
 ):
     params = (p0, p1, p2, p3)
@@ -422,19 +466,19 @@
     inverse = stats[2:3]
     alpha = [stats[3:4], stats[4:5], stats[5:6], stats[6:7]]
     names = [routes[0:1], routes[1:2]]
-    moe = x0[...].astype(F32) + x1[...].astype(F32) + x2[...].astype(F32) + x3[...].astype(F32)
-    moe = jnp.transpose(moe)
-    ffn = g0[...] + g1[...] + g2[...] + g3[...]
+    xs = (x0, x1, x2, x3)
+    moe = jnp.transpose(sum(x[:span].astype(F32) for x in xs))
+    ffn = [sum(unpack_row(x, span, span, k) for x in xs) for k in range(2)]
     flow = grad[...].astype(F32)
     normed = []
     dot_norm = jnp.zeros((1, span), F32)
     dot_value = [jnp.zeros((1, span), F32), jnp.zeros((1, span), F32)]
     for j in range(4):
         here = slice(j * size, (j + 1) * size)
-        norm = mid[here] * inverse * params[j][:, GAIN2 : GAIN2 + 1]
+        norm = mid[here] * inverse * column(params[j], GAIN2)
         dot_norm = dot_norm + jnp.sum(flow[here] * norm, axis=0, keepdims=True)
-        for c, column in enumerate((VALUE0, VALUE1)):
-            value = params[j][:, column : column + 1]
+        for c, first in enumerate((VALUE0, VALUE1)):
+            value = column(params[j], first)
             dot_value[c] = dot_value[c] + jnp.sum(flow[here] * value, axis=0, keepdims=True)
         normed.append(norm)
     experts = kinds - 4
@@ -442,7 +486,7 @@
     is_const = [[(name == experts + 2 + c).astype(F32) for name in names] for c in range(2)]
     grad_gate = []
     for k in range(2):
-        value = ffn[k : k + 1] + is_copy[k] * dot_norm
+        value = ffn[k] + is_copy[k] * dot_norm
         for c in range(2):
             value = value + is_const[c][k] * (
                 alpha[2 * c] * dot_norm + alpha[2 * c + 1] * dot_value[c]
@@ -473,30 +517,30 @@
     inner = jnp.zeros((1, span), F32)
     for j in range(4):
         here = slice(j * size, (j + 1) * size)
-        back = moe[here] + direct * flow[here] + mm(params[j][...], routed, 1, 0, HIGH)
+        back = moe[here] + direct * flow[here] + mm(params[j][...].astype(F32), routed, 1, 0, HIGH)
         small = mm(normed[j], routed, 1, 1, HIGH)
         columns = (
-            (GAIN2, mid[here] * inverse * back),
-            (VALUE0, portions[0] * flow[here]),
-            (VALUE1, portions[1] * flow[here]),
+            (SUM_GAIN2, mid[here] * inverse * back),
+            (SUM_VALUE0, portions[0] * flow[here]),
+            (SUM_VALUE1, portions[1] * flow[here]),
         )
-        for column, terms in columns:
+        for lane, terms in columns:
             total = jnp.sum(terms, axis=1, keepdims=True)
-            small = jnp.where(lanes == column, total, small)
-        small_out[j] = jnp.transpose(small)[:32]
-        gain = params[j][:, GAIN2 : GAIN2 + 1]
+            small = jnp.where(lanes == lane, total, small)
+        small_out[j] = jnp.transpose(small)[:24]
+        gain = column(params[j], GAIN2)
         inner = inner + jnp.sum(mid[here] * gain * back, axis=0, keepdims=True)
         backs.append(back)
     inner = inner * (inverse * inverse * inverse) / full
     for j in range(4):
         here = slice(j * size, (j + 1) * size)
-        gain = params[j][:, GAIN2 : GAIN2 + 1]
+        gain = column(params[j], GAIN2)
         value = flow[here] + inverse * gain * backs[j] - mid[here] * inner
         mid_out[here] = value
         low_out[here] = value.astype(BF16)
 
 
-def middle_back(place, params, mid, grad, stats, routes, pieces, gate_pieces, kinds):
+def middle_back(place, toks, mid, grad, stats, routes, pieces, kinds):
     full, span = mid.shape
     count = lax.axis_size("col")
     size = full // count
@@ -505,9 +549,9 @@
         zeros = (0,) * array.ndim
         return pl.BlockSpec(array.shape, lambda i, s: zeros)
 
-    args = (*params, mid, grad, stats, routes, *pieces, *gate_pieces)
-    specs = [whole(a) for a in args]
-    specs[len(params) + 3] = pl.BlockSpec((2, span), lambda i, s: (0, s[0] * count + s[1]))
+    args = (*toks, mid, grad, stats, routes, *pieces)
+    specs = [param_spec(a) for a in toks] + [whole(a) for a in args[len(toks) :]]
+    specs[len(toks) + 3] = pl.BlockSpec((2, span), lambda i, s: (0, s[0] * count + s[1]))
     return pl.pallas_call(
         middle_back_kernel,
         name="middle_back",
@@ -519,20 +563,20 @@
                 pl.BlockSpec((full, span), lambda i, s: (0, 0)),
                 pl.BlockSpec((full, span), lambda i, s: (0, 0)),
                 pl.BlockSpec((kinds, span), lambda i, s: (0, 0)),
-                pl.BlockSpec((count, 32, size), lambda i, s: (0, 0, 0)),
+                pl.BlockSpec((count, 24, size), lambda i, s: (0, 0, 0)),
             ],
         ),
         out_shape=[
             jax.ShapeDtypeStruct((full, span), BF16),
             jax.ShapeDtypeStruct((full, span), F32),
             jax.ShapeDtypeStruct((kinds, span), F32),
-            jax.ShapeDtypeStruct((count, 32, size), F32),
+            jax.ShapeDtypeStruct((count, 24, size), F32),
         ],
         compiler_params=pltpu.CompilerParams(vmem_limit_bytes=VMEM_LIMIT),
     )(place, *args)
 
 
-def result_kernel(place, p0, p1, p2, p3, mid, stats, routes, y0, y1, y2, y3, out):
+def result_kernel(place, p0, p1, p2, p3, mid, stats, routes, logits, y0, y1, y2, y3, out):
     params = (p0, p1, p2, p3)
     size = p0.shape[0]
     experts = place[3]
@@ -551,27 +595,31 @@
     moe = jnp.transpose(moe)
     for j in range(4):
         here = slice(j * size, (j + 1) * size)
-        norm = mid[here] * inverse * params[j][:, GAIN2 : GAIN2 + 1]
-        out[j] = (
+        norm = mid[here] * inverse * column(params[j], GAIN2)
+        out[j, :size] = (
             mid[here]
             + moe[here]
             + direct * norm
-            + first * stats[4:5] * params[j][:, VALUE0 : VALUE0 + 1]
-            + second * stats[6:7] * params[j][:, VALUE1 : VALUE1 + 1]
+            + first * stats[4:5] * column(params[j], VALUE0)
+            + second * stats[6:7] * column(params[j], VALUE1)
         )
-
-
-def result(place, params, mid, stats, routes, pieces):
+        out[j, size:] = jnp.concatenate(
+            [logits[...], jnp.zeros((EXTRA - logits.shape[0], logits.shape[1]), F32)], axis=0
+        )
+
+
+def result(place, toks, mid, stats, routes, logits, pieces):
     full, span = mid.shape
     count = lax.axis_size("col")
+    tall = full // count + EXTRA
 
     def whole(array):
         zeros = (0,) * array.ndim
         return pl.BlockSpec(array.shape, lambda i, s: zeros)
 
-    args = (*params, mid, stats, routes, *pieces)
-    specs = [whole(a) for a in args]
-    specs[len(params) + 2] = pl.BlockSpec((2, span), lambda i, s: (0, s[0] * count + s[1]))
+    args = (*toks, mid, stats, routes, logits, *pieces)
+    specs = [param_spec(a) for a in toks] + [whole(a) for a in args[len(toks) :]]
+    specs[len(toks) + 2] = pl.BlockSpec((2, span), lambda i, s: (0, s[0] * count + s[1]))
     return pl.pallas_call(
         result_kernel,
         name="result",
@@ -579,51 +627,65 @@
             num_scalar_prefetch=1,
             grid=(1,),
             in_specs=specs,
-            out_specs=pl.BlockSpec((count, full // count, span), lambda i, s: (0, 0, 0)),
+            out_specs=pl.BlockSpec((count, tall, span), lambda i, s: (0, 0, 0)),
         ),
-        out_shape=jax.ShapeDtypeStruct((count, full // count, span), F32),
+        out_shape=jax.ShapeDtypeStruct((count, tall, span), F32),
         compiler_params=pltpu.CompilerParams(vmem_limit_bytes=VMEM_LIMIT),
     )(place, *args)
 
 
-def experts_kernel(
-    order, x0, x1, x2, x3, g0, g1, g2, g3, s0, s1, s2, s3, ranks, routes,
-    w0, w1, near2, far2, near3, far3,
-    y_out, dx_out, gate_out, grad0, grad1, grad2, grad3,
-    weight, y_acc, dx_acc, gate_rows, acc,
-):
+def experts_kernel(chunks, last, *refs):
+    order, x0, x1, x2, x3, g0, g1, g2, g3, ranks, routes, w0, w1 = refs[:13]
+    refs = refs[13:]
+    twos, refs = refs[: len(chunks)], refs[len(chunks) :]
+    threes, refs = refs[: len(chunks)], refs[len(chunks) :]
+    if last:
+        y_in, dx_in, gate_in = refs[:3]
+        refs = refs[3:]
+    y_out, dx_out = refs[:2]
+    refs = refs[2:]
+    if not last:
+        gate_out = refs[0]
+        refs = refs[1:]
+    grad0, grad1, grad2, grad3, weight, y_acc, dx_acc, gate_sum, gate_rows, acc = refs
     step = pl.program_id(0)
     steps = pl.num_programs(0)
     expert = order[step]
     tiles = order[steps + step]
     size = w0.shape[1]
-    span = x0.shape[0]
+    tokens = ranks.shape[1]
+    span = tokens // 4
+    full = x0.shape[1]
     hidden_width = w0.shape[2] // 3
     both = 2 * hidden_width
-    tokens = ranks.shape[1]
     xs = (x0, x1, x2, x3)
     gs = (g0, g1, g2, g3)
 
     @pl.when(step == 0)
     def _():
-        y_acc[...] = jnp.zeros_like(y_acc)
-        dx_acc[...] = jnp.zeros_like(dx_acc)
-        gate_out[...] = jnp.zeros_like(gate_out)
-        for i, ref in enumerate((s0, s1, s2, s3)):
-            gate_rows[:, i * span : (i + 1) * span] = ref[...]
+        if last:
+            y_acc[...] = y_in[...]
+            dx_acc[...] = dx_in[...]
+            gate_sum[...] = gate_in[...]
+        else:
+            y_acc[...] = jnp.zeros_like(y_acc)
+            dx_acc[...] = jnp.zeros_like(dx_acc)
+            gate_sum[...] = jnp.zeros_like(gate_sum)
+        for i, ref in enumerate(xs):
+            for k in range(2):
+                gate_rows[k : k + 1, i * span : (i + 1) * span] = unpack_row(ref, span, span, k)
 
     weight[:size] = w0[0]
     weight[size : 2 * size] = w1[0]
-
-    @pl.when(step < steps // 2)
-    def _():
-        weight[2 * size : 3 * size] = near2[0]
-        weight[3 * size :] = near3[0]
-
-    @pl.when(step >= steps // 2)
-    def _():
-        weight[2 * size : 3 * size] = far2[0]
-        weight[3 * size :] = far3[0]
+    start = 0
+    for two, three, count in zip(twos, threes, chunks):
+
+        @pl.when((step >= start) & (step < start + count))
+        def _():
+            weight[2 * size : 3 * size] = two[0]
+            weight[3 * size :] = three[0]
+
+        start += count
 
     rank = ranks[pl.ds(expert, 1), :]
     hit0 = routes[0:1] == expert
@@ -635,11 +697,11 @@
         hot = slots == rank
         pick = hot.astype(F32).astype(BF16)
         gate = jnp.sum(jnp.where(hot, gate_row, 0.0), axis=1, keepdims=True)
-        rows = jnp.zeros((TILE, x0.shape[1]), F32)
-        flow = jnp.zeros((TILE, x0.shape[1]), F32)
+        rows = jnp.zeros((TILE, full), F32)
+        flow = jnp.zeros((TILE, full), F32)
         for i in range(4):
             cut = pick[:, i * span : (i + 1) * span]
-            rows = rows + mm(cut, xs[i][...], 1, 0)
+            rows = rows + mm(cut, xs[i][:span], 1, 0)
             flow = flow + mm(cut, gs[i][...], 1, 0)
         rows = rows.astype(BF16)
         flow = flow.astype(BF16)
@@ -663,8 +725,8 @@
             y_acc[i * span : (i + 1) * span] += mm(cut, y, 0, 0)
             dx_acc[i * span : (i + 1) * span] += mm(cut, dx, 0, 0)
         row = jnp.sum(jnp.where(hot, grad_gate, 0.0), axis=0, keepdims=True)
-        gate_out[0:1] += jnp.where(hit0, row, 0.0)
-        gate_out[1:2] += jnp.where(hit1, row, 0.0)
+        gate_sum[0:1] += jnp.where(hit0, row, 0.0)
+        gate_sum[1:2] += jnp.where(hit1, row, 0.0)
         grad_weight = mm(rows, grad_both, 0, 0)
         grad_down = mm(flow, scaled, 0, 0)
 
@@ -686,49 +748,71 @@
 
     @pl.when(step == steps - 1)
     def _():
-        y_out[...] = y_acc[...].astype(BF16)
-        dx_out[...] = dx_acc[...].astype(BF16)
-
-
-def run_experts(order, xs, gs, gate_parts, ranks, routes, w0, w1, near2, far2, near3, far3):
-    experts, size, wide = w0.shape
-    half = experts // 2
+        if last:
+            for i in range(4):
+                here = slice(i * span, (i + 1) * span)
+                y_out[i] = y_acc[here].astype(BF16)
+                dx_out[i, :span] = dx_acc[here].astype(BF16)
+                rows = [gate_sum[0:1, here], gate_sum[1:2, here]]
+                dx_out[i, span:] = pack_rows(rows, full)
+        else:
+            y_out[...] = y_acc[...]
+            dx_out[...] = dx_acc[...]
+            gate_out[...] = gate_sum[...]
+
+
+def run_experts(order, xs, gs, ranks, routes, w0, w1, twos, threes, carried):
+    size, wide = w0.shape[1:]
     tokens = ranks.shape[1]
+    span = tokens // 4
     full = xs[0].shape[1]
-
-    def whole(array):
-        zeros = (0,) * array.ndim
-        return pl.BlockSpec(array.shape, lambda e, s: zeros)
-
-    args = (*xs, *gs, *gate_parts, ranks, routes, w0, w1, near2, far2, near3, far3)
-    near = pl.BlockSpec((1, size, wide), lambda e, s: (jnp.minimum(e, half - 1), 0, 0))
-    far = pl.BlockSpec((1, size, wide), lambda e, s: (jnp.maximum(e - half, 0), 0, 0))
+    chunks = tuple(a.shape[0] for a in twos)
+    steps = sum(chunks)
+    last = carried is not None
+
+    def whole(shape):
+        zeros = (0,) * len(shape)
+        return pl.BlockSpec(shape, lambda e, s: zeros)
+
+    def chunk(start, count):
+        return pl.BlockSpec(
+            (1, size, wide), lambda e, s: (jnp.clip(e - start, 0, count - 1), 0, 0)
+        )
+
     mine = pl.BlockSpec((1, size, wide), lambda e, s: (s[e], 0, 0))
-    specs = [whole(a) for a in args[:-6]] + [mine, mine, near, far, near, far]
+    pieces = [chunk(sum(chunks[:i]), count) for i, count in enumerate(chunks)]
+    args = (*xs, *gs, ranks, routes, w0, w1, *twos, *threes)
+    specs = [whole(a.shape) for a in args[:10]] + [mine, mine] + pieces + pieces
+    if last:
+        args += tuple(carried)
+        specs += [whole(a.shape) for a in carried]
+        shapes = [((4, span, full), BF16), ((4, span + EXTRA, full), BF16)]
+    else:
+        shapes = [((tokens, full), F32), ((tokens, full), F32), ((8, tokens), F32)]
     grad = pl.BlockSpec((1, size, wide), lambda e, s: (e, 0, 0))
-    rows = pl.BlockSpec((tokens, full), lambda e, s: (0, 0))
+
+    def body(*refs):
+        experts_kernel(chunks, last, *refs)
+
     return pl.pallas_call(
-        experts_kernel,
+        body,
         name="experts",
         grid_spec=pltpu.PrefetchScalarGridSpec(
             num_scalar_prefetch=1,
-            grid=(experts,),
+            grid=(steps,),
             in_specs=specs,
-            out_specs=[rows, rows, pl.BlockSpec((8, tokens), lambda e, s: (0, 0))] + [grad] * 4,
+            out_specs=[whole(shape) for shape, _ in shapes] + [grad] * 4,
             scratch_shapes=[
                 pltpu.VMEM((full, wide), BF16),
                 pltpu.VMEM((tokens, full), F32),
                 pltpu.VMEM((tokens, full), F32),
                 pltpu.VMEM((8, tokens), F32),
+                pltpu.VMEM((8, tokens), F32),
                 pltpu.VMEM((full, wide), F32),
             ],
         ),
-        out_shape=[
-            jax.ShapeDtypeStruct((tokens, full), BF16),
-            jax.ShapeDtypeStruct((tokens, full), BF16),
-            jax.ShapeDtypeStruct((8, tokens), F32),
-        ]
-        + [jax.ShapeDtypeStruct((experts, size, wide), BF16)] * 4,
+        out_shape=[jax.ShapeDtypeStruct(shape, dtype) for shape, dtype in shapes]
+        + [jax.ShapeDtypeStruct((steps, size, wide), BF16)] * 4,
         compiler_params=pltpu.CompilerParams(vmem_limit_bytes=VMEM_LIMIT),
     )(order, *args)
 
@@ -774,46 +858,31 @@
         pairs = [(r * cols + c, c * cols + (r ^ turn)) for r, c in flat]
         return lax.ppermute(value, ("row", "col"), pairs)
 
-    toks = col_gather(tokens.T)
-    packed = jnp.concatenate(
-        [
-            router_weight.astype(F32),
-            const_weight.astype(F32),
-            norm1_gain[:, None],
-            norm2_gain[:, None],
-            const_values.T,
-            jnp.zeros((size, 128 - kinds - 8), F32),
-        ],
-        axis=1,
-    )
-    params = col_gather(packed)
-    piece = jnp.concatenate([qkv_weight[0], qkv_weight[1], qkv_weight[2]], axis=1)
+    def across_groups(value):
+        return lax.ppermute(value, "dp", [(0, 1), (1, 0)])
+
+
+    values = [norm1_gain, norm2_gain, const_values[0], const_values[1]]
+    lanes = [router_weight, const_weight]
+    for value in values:
+        lanes += [part[:, None] for part in parts_of(value)]
+    lanes.append(jnp.zeros((size, PARAMS - kinds - 4 - 3 * len(values)), BF16))
+    toks = col_gather(jnp.concatenate([tokens.T] + lanes, axis=1))
+    piece = jnp.concatenate([qkv_weight[0], qkv_weight[1], qkv_weight[2], out_weight.T], axis=1)
     weight = jnp.stack([spread(piece, m) for m in range(rows)])
-    proj_piece = after(out_weight.T, piece)
-    proj = jnp.stack([spread(proj_piece, m) for m in range(rows)])
+    flow = cotangent.T.reshape(size, cols, span)
+    flow_parts = [lax.dynamic_index_in_dim(flow, col ^ k, 1, False) for k in range(cols)]
+    flow_quarter = jnp.concatenate(
+        [flow_parts[0]] + [col_swap(flow_parts[k], k) for k in range(1, cols)], axis=0
+    )
+    own = jnp.concatenate([gate_weight, up_weight, down_weight.transpose(0, 2, 1)], axis=2)
+    near_own = lax.dynamic_slice_in_dim(own, first_half * half, half, 0)
+    two_a = col_swap(near_own[:1], 2)
     halves = HD // 2
     freq = 10000.0 ** (-jnp.arange(halves, dtype=F32) / halves)
     angle = freq[:, None] * jnp.arange(length, dtype=F32)[None, :]
     cosine = jnp.cos(angle)
     sine = jnp.sin(angle)
-
-    own = jnp.concatenate([gate_weight, up_weight, down_weight.transpose(0, 2, 1)], axis=2)
-    side = col_swap(own, 1)
-    near_mine = lax.dynamic_slice_in_dim(own, first_half * half, half, 0)
-    near_two = col_swap(near_mine, 2)
-    if groups == 2:
-        far_two = lax.ppermute(near_two, "dp", [(0, 1), (1, 0)])
-    else:
-        far_two = col_swap(lax.dynamic_slice_in_dim(own, half, half, 0), 2)
-    near_three = col_swap(near_two, 1)
-    far_three = col_swap(far_two, 1)
-
-    flow = cotangent.T.reshape(size, cols, span)
-    flow_parts = [lax.dynamic_index_in_dim(flow, col ^ k, 1, False) for k in range(cols)]
-    flow_quarter = jnp.concatenate(
-        [flow_parts[0]] + [col_swap(flow_parts[k], k) for k in range(1, cols)], axis=0
-    )
-    flow_rows = row_gather(flow_quarter.T)
 
     routes_t = routes.T
     share = lax.dynamic_index_in_dim(routes_t.reshape(2, rows, cols, span), col, 2, False)
@@ -824,33 +893,106 @@
     counts = jnp.cumsum(hits.astype(jnp.int32), axis=1)
     ranks = jnp.where(hits, counts - 1, -1)
     order = (first_half * half + jnp.arange(experts, dtype=jnp.int32)) % experts
-    tiles = jnp.maximum((counts[:, -1] + TILE - 1) // TILE, 1)
-    order = jnp.concatenate([order, jnp.take(tiles, order)]).astype(jnp.int32)
-
-    query, keys, values, attn, logsum = attend(place, toks, params, weight, cosine, sine)
+    tiles = jnp.take(jnp.maximum((counts[:, -1] + TILE - 1) // TILE, 1), order)
+    order_near = jnp.concatenate([order[:half], tiles[:half]]).astype(jnp.int32)
+    order_far = jnp.concatenate([order[half:], tiles[half:]]).astype(jnp.int32)
+    toks, weight, flow_quarter, two_a, own, near_own, cosine, sine, ranks, share = join(
+        toks, weight, flow_quarter, two_a, own, near_own, cosine, sine, ranks, share
+    )
+
+    projs = col_gather(weight[:, :, 3 * size :])
+    flow_turned = flow_quarter.T
+    flow_rows = {0: flow_turned, 1: row_shift(flow_turned, 1), 3: row_shift(flow_turned, 3)}
+    side = col_swap(own, 1)
+    three_a = col_swap(two_a, 1)
+    query, keys, values, attn, logsum = attend(place, toks, weight, cosine, sine)
+    attn, projs, flow_rows, side, three_a = join(attn, projs, flow_rows, side, three_a)
+
     parts = [attn[0]] + [col_swap(attn[k], k) for k in range(1, cols)]
-    projs = col_gather(proj)
-    mid, in_rows, stats = middle(place, toks, params, parts, projs, prev_logits.T, routes_t)
+    flow_rows[2] = row_shift(flow_rows[0], 2)
+    two_b = col_swap(near_own[1:2], 2)
+    if groups == 2:
+        far_two_a = across_groups(two_a)
+    else:
+        far_two_a = col_swap(own[half : half + 1], 2)
+    parts, flow_rows, two_b, far_two_a = join(parts, flow_rows, two_b, far_two_a)
+
+    mid, in_rows, stats = middle(place, toks, parts, projs, prev_logits.T, routes_t)
     x_rows = row_gather(in_rows)
-    gate_parts = row_gather(stats)
-    y, dx, gate_grad, *weight_grads = run_experts(
-        order, x_rows, flow_rows, gate_parts, ranks, share,
-        own, side, near_two, far_two, near_three, far_three,
-    )
-
-    def row_scatter(value, axis):
-        pieces = [lax.slice_in_dim(value, s * span, (s + 1) * span, axis=axis) for s in range(rows)]
-        return [pieces[0]] + [row_shift(pieces[s], -s) for s in range(1, rows)]
+    two_c = col_swap(near_own[2:], 2)
+    three_b = col_swap(two_b, 1)
+    three_c = col_swap(two_c, 1)
+    if groups == 2:
+        far_two_b = across_groups(two_b)
+    else:
+        far_two_b = col_swap(own[half + 1 : half + 2], 2)
+    far_three_a = col_swap(far_two_a, 1)
+    far_three_b = col_swap(far_two_b, 1)
+    x_rows, two_c, three_b, three_c, far_two_b, far_three_a, far_three_b = join(
+        x_rows, two_c, three_b, three_c, far_two_b, far_three_a, far_three_b
+    )
+    flow_rows = [flow_rows[s] for s in range(rows)]
+
+    if groups == 2:
+        far_two_c = across_groups(two_c)
+    else:
+        far_two_c = col_swap(own[half + 2 :], 2)
+    far_three_c = col_swap(far_two_c, 1)
+    near_out = run_experts(
+        order_near, x_rows, flow_rows, ranks, share, own, side,
+        [two_a, two_b, two_c], [three_a, three_b, three_c], None,
+    )
+    near_out, far_two_c, far_three_c = join(near_out, far_two_c, far_three_c)
+    *carried, near0, near1, near2, near3 = near_out
+
+    near1 = col_swap(near1, 1)
+    near3 = col_swap(near3, 1)
+    far_out = run_experts(
+        order_far, x_rows, flow_rows, ranks, share, own, side,
+        [far_two_a, far_two_b, far_two_c], [far_three_a, far_three_b, far_three_c], carried,
+    )
+    far_out, near1, near3 = join(far_out, near1, near3)
+    y, dx, far0, far1, far2, far3 = far_out
+
+    def low_sum(left, right):
+        return (left.astype(F32) + right.astype(F32)).astype(BF16)
+
+    def row_scatter(value):
+        return [value[0]] + [row_shift(value[s], -s) for s in range(1, rows)]
+
+    quarter = half // 2
+    dx = row_scatter(dx)
+    near_sent = [low_sum(near2[:quarter], near3[:quarter]), low_sum(near2[quarter:], near3[quarter:])]
+    near_kept = low_sum(near0, near1)
+    near_got = [col_swap(near_sent[0], 2)]
+    far1 = col_swap(far1, 1)
+    far3 = col_swap(far3, 1)
+    dx, near_got, near_sent, near_kept, far1, far3 = join(
+        dx, near_got, near_sent, near_kept, far1, far3
+    )
 
     low, grad_mid, grad_logits, small = middle_back(
-        place, params, mid, flow_quarter, stats, routes_t,
-        row_scatter(dx, 0), row_scatter(gate_grad, 1), kinds,
+        place, toks, mid, flow_quarter, stats, routes_t, dx, kinds
     )
     lows = col_gather(low)
-    tokens_parts, qkv_parts, proj_parts, gain_parts = attend_back(
-        place, toks, params, weight, proj, cosine, sine,
-        query, keys, values, attn, logsum, lows, grad_mid,
-    )
+    near_sum = [low_sum(near_kept[:quarter], near_got[0])]
+    lows, near_sum = join(lows, near_sum)
+
+    y = row_scatter(y)
+    near_got.append(col_swap(near_sent[1], 2))
+    if groups == 2:
+        near_other = [across_groups(near_sum[0])]
+    far_sent = [low_sum(far2[:quarter], far3[:quarter]), low_sum(far2[quarter:], far3[quarter:])]
+    far_kept = low_sum(far0, far1)
+    tokens_parts, weight_parts, small = attend_back(
+        place, toks, weight, cosine, sine,
+        query, keys, values, attn, logsum, lows, grad_mid, small,
+    )
+    y, near_got, far_sent, far_kept, tokens_parts, weight_parts, small = join(
+        y, near_got, far_sent, far_kept, tokens_parts, weight_parts, small
+    )
+    if groups == 2:
+        near_other, near_got = join(near_other, near_got)
 
     def col_scatter(value):
         total = value[0].astype(F32)
@@ -858,61 +1000,62 @@
             total = total + col_swap(value[k], k).astype(F32)
         return total
 
-    grad_tokens = col_scatter(tokens_parts).T
-
-    def weight_total(value):
-        total = collect(value[0], 0).astype(F32)
-        for m in range(1, rows):
-            total = total + collect(value[m], m).astype(F32)
-        return dp_total(total.astype(BF16))
-
-    qkv_sum = weight_total(qkv_parts)
-    qkv_sum = jnp.stack([qkv_sum[:, j * size : (j + 1) * size] for j in range(3)])
-    proj_sum = weight_total(proj_parts).T
-
-    small = dp_total(row_total(col_scatter(small)))
-    gain1 = dp_total(row_total(col_scatter(gain_parts)))[0]
-
-    from_side = col_swap(weight_grads[1], 1)
-    across = col_swap(weight_grads[3], 1)
-    kept = weight_grads[0].astype(F32) + from_side.astype(F32)
-    sent = (weight_grads[2].astype(F32) + across.astype(F32)).astype(BF16)
-    kept = (kept + col_swap(sent, 2).astype(F32)).astype(BF16)
-    first = first_half == 0
+    grad_tokens = col_scatter(tokens_parts)
+    total = collect(weight_parts[0], 0).astype(F32)
+    for m in range(1, rows):
+        total = total + collect(weight_parts[m], m).astype(F32)
+    small = col_scatter(small)
+    near_sum.append(low_sum(near_kept[quarter:], near_got[1]))
     if groups == 2:
-        ahead = lax.ppermute(kept[:half], "dp", [(0, 1), (1, 0)]).astype(F32)
-        behind = lax.ppermute(kept[half:], "dp", [(0, 1), (1, 0)]).astype(F32)
-        near = kept[:half].astype(F32) + behind
-        far = kept[half:].astype(F32) + ahead
+        near_other.append(across_groups(near_sum[1]))
+    far_got = [col_swap(far_sent[0], 2)]
+    out = result(place, toks, mid, stats, routes_t, grad_logits, y)
+    grad_tokens, total, small, far_got, out = join(grad_tokens, total, small, far_got, out)
+
+    far_sum = [low_sum(far_kept[:quarter], far_got[0])]
+    far_got.append(col_swap(far_sent[1], 2))
+    far_sum.append(low_sum(far_kept[quarter:], far_got[1]))
+    total = dp_total(total.astype(BF16))
+    qkv_sum = jnp.stack([total[:, j * size : (j + 1) * size] for j in range(3)])
+    proj_sum = total[:, 3 * size :].T
+    small = dp_total(row_total(small))
+    out = jnp.stack([out[0]] + [col_swap(out[k], k) for k in range(1, cols)])
+    out = jnp.take(out, col ^ jnp.arange(cols), axis=0)
+    out = jnp.concatenate([out[i] for i in range(cols)], axis=1)
+    if groups == 2:
+        far_other = [across_groups(s) for s in far_sum]
+        near_start = first_half * half
+        far_start = half - near_start
+        grads = []
+        for j in range(3):
+            wide = slice(j * hidden_width, (j + 1) * hidden_width)
+            grad = jnp.zeros((experts, size, hidden_width), F32)
+            for i in range(2):
+                for start, mine, other in (
+                    (near_start, near_sum[i], far_other[i]),
+                    (far_start, far_sum[i], near_other[i]),
+                ):
+                    both = mine[:, :, wide].astype(F32) + other[:, :, wide].astype(F32)
+                    grad = lax.dynamic_update_slice_in_dim(grad, both, start + i * quarter, 0)
+            grads.append(grad)
     else:
-        both = lax.psum(kept.astype(F32), "dp")
-        near, far = both[:half], both[half:]
-    summed = jnp.concatenate([jnp.where(first, near, far), jnp.where(first, far, near)])
-
-    def col_join(value, axis):
-        got = [value(0)] + [col_swap(value(k), k) for k in range(1, cols)]
-        stacked = jnp.stack(got)
-        stacked = jnp.take(stacked, col ^ jnp.arange(cols), axis=0)
-        return jnp.concatenate([stacked[i] for i in range(cols)], axis=axis)
-
-    out = result(place, params, mid, stats, routes_t, row_scatter(y, 0))
-    layer_out = col_join(lambda k: out[k], 1).T
-    prev_grad = col_join(lambda k: grad_logits, 1).T
+        both = lax.psum(jnp.concatenate(near_sum + far_sum).astype(F32), "dp")
+        grads = [both[:, :, j * hidden_width : (j + 1) * hidden_width] for j in range(3)]
 
     return (
-        layer_out,
-        grad_tokens,
-        prev_grad,
-        gain1,
+        out[:size].T,
+        grad_tokens.T,
+        out[size : size + kinds].T,
+        small[SUM_GAIN1],
         qkv_sum,
         proj_sum,
-        small[GAIN2],
+        small[SUM_GAIN2],
         small[:kinds].T,
         small[kinds : kinds + 4].T,
-        small[VALUE0 : VALUE1 + 1],
-        summed[:, :, :hidden_width],
-        summed[:, :, hidden_width : 2 * hidden_width],
-        summed[:, :, 2 * hidden_width :].transpose(0, 2, 1),
+        small[SUM_VALUE0 : SUM_VALUE1 + 1],
+        grads[0],
+        grads[1],
+        grads[2].transpose(0, 2, 1),
     )
 
 
@@ -951,7 +1094,6 @@
             P(None, "col", "row"),
             P(None, "col", "row"),
             P(None, "row", "col"),
-            P(None, "row", "col"),
-        )[:13],
+        ),
         check_vma=False,
     )

time: 660 us -> 607 us (0.920)
  waiting for transfers between devices: 315 us -> 223 us
  local copies, waits for them, and re-layouts: 32.3 us -> 54.9 us
  Pallas kernels: 110 us -> 118 us
    ppermute x4 -> x2, waiting for transfers between devices: 101 us -> 51.7 us  [dp_total(): other = lax.ppermute(value, 'dp', [(0, 1), (1, 0)])]
    ppermute x18 -> x12, waiting for transfers between devices: 90.4 us -> 46.4 us  [row_shift(): lax.ppermute(value, 'row', [(i, (i + steps) % count) for i in range(count)])]
    ppermute x3 -> x7, waiting for transfers between devices: 0.01 us -> 33.5 us  [across_groups(): return lax.ppermute(value, 'dp', [(0, 1), (1, 0)])]
    ppermute x8 -> x4, starting transfers between devices: 5.91 us -> 36.6 us  [collect(): return lax.ppermute(value, ('row', 'col'), pairs)]
    ppermute x40 -> x42, waiting for transfers between devices: 96 us -> 65.3 us  [col_swap(): return lax.ppermute(value, 'col', [(i, i ^ bits) for i in range(count)])]
    ppermute x4 -> x2, starting transfers between devices: 17.9 us -> 3 us  [row_swap(): return lax.ppermute(value, 'row', [(i, i ^ bits) for i in range(count)])]
    ppermute x40 -> x42, starting transfers between devices: 55.2 us -> 40.9 us  [col_swap(): return lax.ppermute(value, 'col', [(i, i ^ bits) for i in range(count)])]
    ppermute x8 -> x4, waiting for transfers between devices: 1.62 us -> 11.6 us  [spread(): return lax.ppermute(value, ('row', 'col'), pairs)]
  transfers between devices with their start and end apart: 85 -> 73, of which waited for: 30 -> 24; matrix products, arithmetic and copies ran while one was open for 9% -> 15% of each run, Pallas kernels for 8% -> 20%
where the time goes in v2:
time: 607 us; the launch traced here: 600 us
  waiting for transfers between devices  223 us (37%)
  starting transfers between devices  151 us (25%)
  Pallas kernels  118 us (19%)
  local copies, waits for them, and re-layouts  54.9 us (9%)
  other arithmetic  51.3 us (8%)
    ppermute x42, waiting for transfers between devices, col_swap(): return lax.ppermute(value, 'col', [(i, i ^ bits) for i in range(count)])  65.3 us
    pallas_call x2, Pallas kernels, run_experts(): pl.pallas_call(body, name='experts', grid_spec=pltpu.PrefetchScalarGridSp...  64.6 us
    ppermute x2, waiting for transfers between devices, dp_total(): other = lax.ppermute(value, 'dp', [(0, 1), (1, 0)])  51.7 us
    ppermute x12, waiting for transfers between devices, row_shift(): lax.ppermute(value, 'row', [(i, (i + steps) % count) for i in range(count)])  46.4 us
    ppermute x42, starting transfers between devices, col_swap(): return lax.ppermute(value, 'col', [(i, i ^ bits) for i in range(count)])  40.9 us
    ppermute x12, starting transfers between devices, row_shift(): lax.ppermute(value, 'row', [(i, (i + steps) % count) for i in range(count)])  40.3 us
    ppermute x4, starting transfers between devices, collect(): return lax.ppermute(value, ('row', 'col'), pairs)  36.6 us
    ppermute x7, waiting for transfers between devices, across_groups(): return lax.ppermute(value, 'dp', [(0, 1), (1, 0)])  33.5 us
  transfers between devices with their start and end apart: 73, of which 24 were waited for; matrix products, arithmetic and copies ran while one was open for 15% of the time, Pallas kernels for 20%

profile of v2, /device:TPU:0, one launch (start us, length us, event | category | flops | bytes accessed | tf_op | source)
XLA Modules:
  0.0 600.0 jit_solution(8436363448941264298)
XLA Ops:
  3.6 3.7 collective-permute-start.3
  7.3 3.1 collective-permute-start.4
  14.1 4.3 collective-permute-start.8
  21.7 2.1 pad_maximum_fusion.refs_11_
  28.3 2.3 reduce-window.6
  35.2 1.9 collective-permute-done.9
  37.5 7.6 %collective-permute-start.5 = (bf16[192,768]{1,0:T(8,128)(2,1)}, bf16[192,768]{1,0:T(8,128)(2,1)S(1)}, u32[]{:S(2)}, u32[]{:S(2)}) collective-permute-start(bf16[192,768]{1,0:T(8,128)(2,1)} %pad_maximum_fusion.6), channel_id=1, source_target_pairs={{2,0},{7,1},{8,2},{13,3},{3,4},{6,5},{9,6},{12,7},{0,8},{5,9},{10,... | collective-permute-start | bytes 884744 | tf_op jit(solution)/shard_map/ppermute | solution.py:855
  45.1 4.3 collective-permute-start.6
  51.1 11.6 %collective-permute-done.5 = bf16[192,768]{1,0:T(8,128)(2,1)S(1)} collective-permute-done((bf16[192,768]{1,0:T(8,128)(2,1)}, bf16[192,768]{1,0:T(8,128)(2,1)S(1)}, u32[]{:S(2)}, u32[]{:S(2)}) %collective-permute-start.5) | collective-permute-done | bytes 294944 | tf_op jit(solution)/shard_map/ppermute | solution.py:855
  64.1 3.0 slice.312
  67.1 9.5 %collective-permute-start.27 = (bf16[2,192,1536]{2,1,0:T(8,128)(2,1)}, bf16[2,192,1536]{2,1,0:T(8,128)(2,1)}, u32[]{:S(2)}, u32[]{:S(2)}) collective-permute-start(bf16[2,192,1536]{2,1,0:T(8,128)(2,1)} %slice.312), channel_id=1, source_target_pairs={{0,2},{1,3},{2,0},{3,1},{4,6},{5,7},{6,4},{7,5},{8,10},{9,11},{10,... | collective-permute-start | bytes 3538952 | tf_op jit(solution)/shard_map/ppermute | solution.py:67
  78.1 33.1 %collective-permute-done.12.o2 = bf16[4,192,192]{2,1,0:T(8,128)(2,1)S(1)} collective-permute-done((bf16[4,192,192]{2,1,0:T(8,128)(2,1)S(1)}, bf16[4,192,192]{2,1,0:T(8,128)(2,1)S(1)}, u32[]{:S(2)}, u32[]{:S(2)}) %collective-permute-start.12) | collective-permute-done | bytes 294944 | tf_op jit(solution)/shard_map/ppermute | solution.py:67
  114.5 1.9 slice.311
  116.4 5.4 collective-permute-done.15
  127.3 13.6 %attend.1 = (bf16[4,192,256]{2,1,0:T(8,128)(2,1)}, bf16[192,1024]{1,0:T(8,128)(2,1)}, bf16[192,1024]{1,0:T(8,128)(2,1)}, bf16[4,192,256]{2,1,0:T(8,128)(2,1)}, f32[8,1024]{1,0:T(8,128)}) custom-call(s32[4]{0:T(128)} %pad_add_fusion.1.place, bf16[192,1152]{1,0:T(8,128)(2,1)} %copy-done.1, bf16[192,1152]{1,0:T(8,128)(2,1)} %copy-done.3, ...), custom_call_target="tpu_custom_call" | custom-call | tf_op jit(solution)/shard_map/attend/pallas_call | solution.py:186
  140.9 2.4 collective-permute-start.21
  146.9 4.0 collective-permute-done.19.a2
  151.6 10.2 %collective-permute-done.21 = bf16[256,768]{0,1:T(8,128)(2,1)S(1)} collective-permute-done((bf16[256,768]{0,1:T(8,128)(2,1)S(1)}, bf16[256,768]{0,1:T(8,128)(2,1)S(1)}, u32[]{:S(2)}, u32[]{:S(2)}) %collective-permute-start.21) | collective-permute-done | bytes 393248 | tf_op jit(solution)/shard_map/ppermute | solution.py:77
  162.6 5.4 middle.1
  168.8 8.1 %collective-permute-done.30.refs_14_ = bf16[1,192,1536]{2,1,0:T(8,128)(2,1)S(1)} collective-permute-done((bf16[1,192,1536]{2,1,0:T(8,128)(2,1)}, bf16[1,192,1536]{2,1,0:T(8,128)(2,1)S(1)}, u32[]{:S(2)}, u32[]{:S(2)}) %collective-permute-start.30) | collective-permute-done | bytes 589856 | tf_op jit(solution)/shard_map/ppermute | solution.py:862
  177.0 4.2 collective-permute-done.24.refs_2_
  182.7 16.9 %collective-permute-done.25.refs_3_ = bf16[272,768]{1,0:T(8,128)(2,1)S(1)} collective-permute-done((bf16[272,768]{1,0:T(8,128)(2,1)}, bf16[272,768]{1,0:T(8,128)(2,1)S(1)}, u32[]{:S(2)}, u32[]{:S(2)}) %collective-permute-start.25) | collective-permute-done | bytes 417824 | tf_op jit(solution)/shard_map/ppermute | solution.py:77
  203.4 25.3 %collective-permute-done.33.refs_15_ = bf16[2,192,1536]{2,1,0:T(8,128)(2,1)S(1)} collective-permute-done((bf16[2,192,1536]{2,1,0:T(8,128)(2,1)}, bf16[2,192,1536]{2,1,0:T(8,128)(2,1)S(1)}, u32[]{:S(2)}, u32[]{:S(2)}) %collective-permute-start.33) | collective-permute-done | bytes 1179680 | tf_op jit(solution)/shard_map/ppermute | solution.py:862
  232.1 1.9 copy.97.refs_7_
  234.0 1.9 copy.98.refs_8_
  236.0 27.5 %experts.2 = (f32[1024,768]{1,0:T(8,128)}, f32[1024,768]{1,0:T(8,128)}, f32[8,1024]{1,0:T(8,128)}, bf16[4,192,1536]{2,1,0:T(8,128)(2,1)}, bf16[4,192,1536]{2,1,0...) custom-call(s32[8]{0:T(128)} %pad_add_fusion.2.refs_0_, ...), custom_call_target="tpu_custom_call" | custom-call | tf_op jit(solution)/shard_map/experts/pallas_call | solution.py:797
  264.7 37.2 %experts.3 = (bf16[4,256,768]{2,1,0:T(8,128)(2,1)}, bf16[4,272,768]{2,1,0:T(8,128)(2,1)}, bf16[4,192,1536]{2,1,0:T(8,128)(2,1)}, bf16[4,192,1536]{2,1,0:T(8,128)...) custom-call(s32[8]{0:T(128)} %pad_add_fusion.refs_0_, bf16[272,768]{1,0:T(8,128)(2,1)} %get-tuple-element.160.refs_1_, ...), custom_call_target="tpu_custom_call" | custom-call | tf_op jit(solution)/shard_map/experts/pallas_call | solution.py:797
  302.5 3.2 slice_bitcast_fusion.1
  305.6 10.5 %collective-permute-start.40 = (bf16[272,768]{1,0:T(8,128)(2,1)S(1)}, bf16[272,768]{1,0:T(8,128)(2,1)S(1)}, u32[]{:S(2)}, u32[]{:S(2)}) collective-permute-start(bf16[272,768]{1,0:T(8,128)(2,1)S(1)} %get-tuple-element.309), channel_id=1, source_target_pairs={{0,12},{4,0},{8,4},{12,8},{1,13},{5,1},{9,5},{13,9},{2,14},{6,2},{... | collective-permute-start | bytes 1253384 | tf_op jit(solution)/shard_map/ppermute | solution.py:77
  316.1 3.3 add_convert_fusion.8
  321.1 5.0 collective-permute-done.40.x1
  326.2 19.4 %collective-permute-start.42 = (bf16[272,768]{1,0:T(8,128)(2,1)S(1)}, bf16[272,768]{1,0:T(8,128)(2,1)S(1)}, u32[]{:S(2)}, u32[]{:S(2)}) collective-permute-start(bf16[272,768]{1,0:T(8,128)(2,1)S(1)} %get-tuple-element.307), channel_id=1, source_target_pairs={{0,4},{4,8},{8,12},{12,0},{1,5},{5,9},{9,13},{13,1},{2,6},{6,10},{... | collective-permute-start | bytes 1253384 | tf_op jit(solution)/shard_map/ppermute | solution.py:77
  345.6 2.3 add_convert_fusion.1
  349.1 4.3 collective-permute-done.41.x2
  353.5 2.4 collective-permute-start.38
  355.9 6.7 %middle_back.1 = (bf16[768,256]{1,0:T(8,128)(2,1)}, f32[768,256]{1,0:T(8,128)}, f32[12,256]{1,0:T(8,128)}, f32[4,24,192]{2,1,0:T(8,128)}) custom-call(s32[4]{0:T(128)} %pad_add_fusion.1.place, bf16[192,1152]{1,0:T(8,128)(2,1)} %copy-done.1, bf16[192,1152]{1,0:T(8,128)(2,1)} %copy-done.3, bf16[192,1152]{1,0:T(8,128)(2,1)} %copy-done.2, ...), custom_call_target="tpu_custom_call" | custom-call | tf_op jit(solution)/shard_map/middle_back/pallas_call | solution.py:555
  364.6 4.4 add_convert_fusion
  369.0 3.6 add_convert_fusion.6
  372.7 2.1 collective-permute-done.48.d2
  376.9 2.5 collective-permute-start.69
  379.4 23.5 %attend_back.1 = (bf16[4,192,1024]{2,1,0:T(8,128)(2,1)}, bf16[4,192,768]{2,1,0:T(8,128)(2,1)}, f32[4,24,192]{2,1,0:T(8,128)}) custom-call(s32[4]{0:T(128)} %pad_add_fusion.1.place, bf16[192,1152]{1,0:T(8,128)(2,1)} %copy-done.1, bf16[192,1152]{1,0:T(8,128)(2,1)} %copy-done.3, bf16[192,1152]{1,0:T(8,128)(2,1)} %copy-done.2, bf16[192,1152]{1,0:T(8,128)(2,1)} %copy-done.4, ...), custom_call_target="tpu_custom_call" | custom-call | tf_op jit(solution)/shard_map/attend_back/pallas_call | solution.py:334
  405.7 2.1 slice_bitcast_fusion.15
  410.8 3.3 collective-permute-start.60
  415.7 22.1 %collective-permute-start.55 = (bf16[192,768]{1,0:T(8,128)(2,1)}, bf16[192,768]{1,0:T(8,128)(2,1)}, u32[]{:S(2)}, u32[]{:S(2)}) collective-permute-start(bf16[192,768]{1,0:T(8,128)(2,1)} %get-tuple-element.320), channel_id=1, source_target_pairs={{0,2},{1,6},{2,10},{3,14},{4,3},{5,7},{6,11},{7,15},{8,0},{9,4},{1... | collective-permute-start | bytes 884744 | tf_op jit(solution)/shard_map/ppermute | solution.py:859
  438.5 12.2 %collective-permute-start.56 = (bf16[192,768]{1,0:T(8,128)(2,1)}, bf16[192,768]{1,0:T(8,128)(2,1)}, u32[]{:S(2)}, u32[]{:S(2)}) collective-permute-start(bf16[192,768]{1,0:T(8,128)(2,1)} %get-tuple-element.319), channel_id=1, source_target_pairs={{0,3},{1,7},{2,11},{3,15},{4,2},{5,6},{6,10},{7,14},{8,1},{9,5},{1... | collective-permute-start | bytes 884744 | tf_op jit(solution)/shard_map/ppermute | solution.py:859
  450.7 4.5 result.1
  455.3 10.4 %collective-permute-done.55 = bf16[192,768]{1,0:T(8,128)(2,1)} collective-permute-done((bf16[192,768]{1,0:T(8,128)(2,1)}, bf16[192,768]{1,0:T(8,128)(2,1)}, u32[]{:S(2)}, u32[]{:S(2)}) %collective-permute-start.55) | collective-permute-done | bytes 294944 | tf_op jit(solution)/shard_map/ppermute | solution.py:859
  465.7 2.5 collective-permute-start.51
  468.2 2.6 collective-permute-done.56
  470.8 2.1 collective-permute-start.52
  473.7 2.1 convert_add_fusion.2
  475.8 3.5 collective-permute-done.51
  479.2 8.3 %collective-permute-done.52 = bf16[192,1024]{1,0:T(8,128)(2,1)S(1)} collective-permute-done((bf16[192,1024]{1,0:T(8,128)(2,1)S(1)}, bf16[192,1024]{1,0:T(8,128)(2,1)S(1)}, u32[]{:S(2)}, u32[]{:S(2)}) %collective-permute-start.52) | collective-permute-done | bytes 393248 | tf_op jit(solution)/shard_map/ppermute | solution.py:67
  487.6 2.2 fusion.1
  493.7 2.9 collective-permute-start.65
  496.6 11.2 %collective-permute-done.70 = bf16[2,192,1536]{2,1,0:T(8,128)(2,1)S(1)} collective-permute-done((bf16[2,192,1536]{2,1,0:T(8,128)(2,1)}, bf16[2,192,1536]{2,1,0:T(8,128)(2,1)S(1)}, u32[]{:S(2)}, u32[]{:S(2)}) %collective-permute-start.70) | collective-permute-done | bytes 1179680 | tf_op jit(solution)/shard_map/ppermute | solution.py:67
  507.8 1.9 add_convert_fusion.2
  512.0 2.4 collective-permute-start.62
  514.4 27.7 %collective-permute-done.66 = f32[24,192]{1,0:T(8,128)S(1)} collective-permute-done((f32[24,192]{1,0:T(8,128)S(1)}, f32[24,192]{1,0:T(8,128)S(1)}, u32[]{:S(2)}, u32[]{:S(2)}) %collective-permute-start.66) | collective-permute-done | bytes 18464 | tf_op jit(solution)/shard_map/ppermute | solution.py:98
  542.1 3.0 collective-permute-start.63
  550.9 2.7 gather_fusion.2
  556.6 24.0 %collective-permute-done.67 = bf16[192,768]{1,0:T(8,128)(2,1)} collective-permute-done((bf16[192,768]{1,0:T(8,128)(2,1)}, bf16[192,768]{1,0:T(8,128)(2,1)}, u32[]{:S(2)}, u32[]{:S(2)}) %collective-permute-start.67) | collective-permute-done | bytes 294944 | tf_op jit(solution)/shard_map/ppermute | solution.py:98
  582.7 1.7 copy.99
  584.4 2.1 pad_maximum_fusion.4
  (335 shorter events, 94.7 us)
Async XLA Ops:
  3.6 33.9 %collective-permute-start.3 = (bf16[192,768]{1,0:T(8,128)(2,1)}, bf16[192,768]{1,0:T(8,128)(2,1)}, u32[]{:S(2)}, u32[]{:S(2)}) collective-permute-start(bf16[192,768]{1,0:T(8,128)(2,1)} %pad_maximum_fusion.6), channel_id=1, source_target_pairs={{0,0},{5,1},{10,2},{15,3},{1,4},{4,5},{11,6},{14,7},{2,8},{7,9},{8... | collective-permute-start | bytes 884744 | tf_op jit(solution)/shard_map/ppermute | solution.py:855
  7.3 37.7 %collective-permute-start.4 = (bf16[192,768]{1,0:T(8,128)(2,1)}, bf16[192,768]{1,0:T(8,128)(2,1)}, u32[]{:S(2)}, u32[]{:S(2)}) collective-permute-start(bf16[192,768]{1,0:T(8,128)(2,1)} %pad_maximum_fusion.6), channel_id=1, source_target_pairs={{1,0},{4,1},{11,2},{14,3},{0,4},{5,5},{10,6},{15,7},{3,8},{6,9},{9... | collective-permute-start | bytes 884744 | tf_op jit(solution)/shard_map/ppermute | solution.py:855
  13.3 19.0 %collective-permute-start.7 = (bf16[192,256]{1,0:T(8,128)(2,1)}, bf16[192,256]{1,0:T(8,128)(2,1)}, u32[]{:S(2)}, u32[]{:S(2)}) collective-permute-start(bf16[192,256]{1,0:T(8,128)(2,1)} %bitcast.153), channel_id=1, source_target_pairs={{0,1},{1,0},{2,3},{3,2},{4,5},{5,4},{6,7},{7,6},{8,9},{9,8},{10,11... | collective-permute-start | bytes 294920 | tf_op jit(solution)/shard_map/ppermute | solution.py:67
  14.1 19.9 %collective-permute-start.8 = (bf16[192,256]{1,0:T(8,128)(2,1)}, bf16[192,256]{1,0:T(8,128)(2,1)}, u32[]{:S(2)}, u32[]{:S(2)}) collective-permute-start(bf16[192,256]{1,0:T(8,128)(2,1)} %bitcast.152), channel_id=1, source_target_pairs={{0,2},{1,3},{2,0},{3,1},{4,6},{5,7},{6,4},{7,5},{8,10},{9,11},{10,... | collective-permute-start | bytes 294920 | tf_op jit(solution)/shard_map/ppermute | solution.py:67
  21.6 27.8 %collective-permute-start.1 = (bf16[192,1152]{1,0:T(8,128)(2,1)S(1)}, bf16[192,1152]{1,0:T(8,128)(2,1)S(1)}, u32[]{:S(2)}, u32[]{:S(2)}) collective-permute-start(bf16[192,1152]{1,0:T(8,128)(2,1)S(1)} %concatenate.22.t0.p0), channel_id=1, source_target_pairs={{0,2},{1,3},{2,0},{3,1},{4,6},{5,7},{6,4},{7,5},{8,10},{9,11},{10,... | collective-permute-start | bytes 1327112 | tf_op jit(solution)/shard_map/ppermute | solution.py:67
  33.9 30.1 %collective-permute-start.10 = (bf16[1,192,1536]{2,1,0:T(8,128)(2,1)}, bf16[1,192,1536]{2,1,0:T(8,128)(2,1)}, u32[]{:S(2)}, u32[]{:S(2)}) collective-permute-start(bf16[1,192,1536]{2,1,0:T(8,128)(2,1)} %constant_dynamic-slice_fusion), channel_id=1, source_target_pairs={{0,2},{1,3},{2,0},{3,1},{4,6},{5,7},{6,4},{7,5},{8,10},{9,11},{10,... | collective-permute-start | bytes 1769480 | tf_op jit(solution)/shard_map/ppermute | solution.py:67
  37.1 26.9 %collective-permute-start = (bf16[192,1152]{1,0:T(8,128)(2,1)S(1)}, bf16[192,1152]{1,0:T(8,128)(2,1)S(1)}, u32[]{:S(2)}, u32[]{:S(2)}) collective-permute-start(bf16[192,1152]{1,0:T(8,128)(2,1)S(1)} %concatenate.22.t0.p0), channel_id=1, source_target_pairs={{0,1},{1,0},{2,3},{3,2},{4,5},{5,4},{6,7},{7,6},{8,9},{9,8},{10,11... | collective-permute-start | bytes 1327112 | tf_op jit(solution)/shard_map/ppermute | solution.py:67
  37.5 25.3 %collective-permute-start.5 = (bf16[192,768]{1,0:T(8,128)(2,1)}, bf16[192,768]{1,0:T(8,128)(2,1)S(1)}, u32[]{:S(2)}, u32[]{:S(2)}) collective-permute-start(bf16[192,768]{1,0:T(8,128)(2,1)} %pad_maximum_fusion.6), channel_id=1, source_target_pairs={{2,0},{7,1},{8,2},{13,3},{3,4},{6,5},{9,6},{12,7},{0,8},{5,9},{10,... | collective-permute-start | bytes 884744 | tf_op jit(solution)/shard_map/ppermute | solution.py:855
  45.1 17.7 %collective-permute-start.6 = (bf16[192,768]{1,0:T(8,128)(2,1)}, bf16[192,768]{1,0:T(8,128)(2,1)S(1)}, u32[]{:S(2)}, u32[]{:S(2)}) collective-permute-start(bf16[192,768]{1,0:T(8,128)(2,1)} %pad_maximum_fusion.6), channel_id=1, source_target_pairs={{3,0},{6,1},{9,2},{12,3},{2,4},{7,5},{8,6},{13,7},{1,8},{4,9},{11,... | collective-permute-start | bytes 884744 | tf_op jit(solution)/shard_map/ppermute | solution.py:855
  49.4 14.6 %collective-permute-start.2 = (bf16[192,1152]{1,0:T(8,128)(2,1)S(1)}, bf16[192,1152]{1,0:T(8,128)(2,1)S(1)}, u32[]{:S(2)}, u32[]{:S(2)}) collective-permute-start(bf16[192,1152]{1,0:T(8,128)(2,1)S(1)} %collective-permute-done.1.t2.p2), channel_id=1, source_target_pairs={{0,1},{1,0},{2,3},{3,2},{4,5},{5,4},{6,7},{7,6},{8,9},{9,8},{10,11... | collective-permute-start | bytes 1327112 | tf_op jit(solution)/shard_map/ppermute | solution.py:67
  64.0 76.9 %collective-permute-start.16 = (bf16[8,192,1536]{2,1,0:T(8,128)(2,1)}, bf16[8,192,1536]{2,1,0:T(8,128)(2,1)}, u32[]{:S(2)}, u32[]{:S(2)}) collective-permute-start(bf16[8,192,1536]{2,1,0:T(8,128)(2,1)} %copy-done), channel_id=1, source_target_pairs={{0,1},{1,0},{2,3},{3,2},{4,5},{5,4},{6,7},{7,6},{8,9},{9,8},{10,11... | collective-permute-start | bytes 14155784 | tf_op jit(solution)/shard_map/ppermute | solution.py:67
  67.1 59.0 %collective-permute-start.27 = (bf16[2,192,1536]{2,1,0:T(8,128)(2,1)}, bf16[2,192,1536]{2,1,0:T(8,128)(2,1)}, u32[]{:S(2)}, u32[]{:S(2)}) collective-permute-start(bf16[2,192,1536]{2,1,0:T(8,128)(2,1)} %slice.312), channel_id=1, source_target_pairs={{0,2},{1,3},{2,0},{3,1},{4,6},{5,7},{6,4},{7,5},{8,10},{9,11},{10,... | collective-permute-start | bytes 3538952 | tf_op jit(solution)/shard_map/ppermute | solution.py:67
  76.8 34.5 %collective-permute-start.12 = (bf16[4,192,192]{2,1,0:T(8,128)(2,1)S(1)}, bf16[4,192,192]{2,1,0:T(8,128)(2,1)S(1)}, u32[]{:S(2)}, u32[]{:S(2)}) collective-permute-start(bf16[4,192,192]{2,1,0:T(8,128)(2,1)S(1)} %slice.306.o0), channel_id=1, source_target_pairs={{0,2},{1,3},{2,0},{3,1},{4,6},{5,7},{6,4},{7,5},{8,10},{9,11},{10,... | collective-permute-start | bytes 884744 | tf_op jit(solution)/shard_map/ppermute | solution.py:67
  76.8 36.1 %collective-permute-start.14 = (bf16[256,768]{0,1:T(8,128)(2,1)S(1)}, bf16[256,768]{0,1:T(8,128)(2,1)S(1)}, u32[]{:S(2)}, u32[]{:S(2)}) collective-permute-start(bf16[256,768]{0,1:T(8,128)(2,1)S(1)} %bitcast.158), channel_id=1, source_target_pairs={{0,4},{4,8},{8,12},{12,0},{1,5},{5,9},{9,13},{13,1},{2,6},{6,10},{... | collective-permute-start | bytes 1179656 | tf_op jit(solution)/shard_map/ppermute | solution.py:77
  78.1 34.8 %collective-permute-start.11 = (bf16[4,192,192]{2,1,0:T(8,128)(2,1)S(1)}, bf16[4,192,192]{2,1,0:T(8,128)(2,1)S(1)}, u32[]{:S(2)}, u32[]{:S(2)}) collective-permute-start(bf16[4,192,192]{2,1,0:T(8,128)(2,1)S(1)} %slice.306.o0), channel_id=1, source_target_pairs={{0,1},{1,0},{2,3},{3,2},{4,5},{5,4},{6,7},{7,6},{8,9},{9,8},{10,11... | collective-permute-start | bytes 884744 | tf_op jit(solution)/shard_map/ppermute | solution.py:67
  111.2 10.5 %collective-permute-start.15 = (bf16[256,768]{0,1:T(8,128)(2,1)S(1)}, bf16[256,768]{0,1:T(8,128)(2,1)S(1)}, u32[]{:S(2)}, u32[]{:S(2)}) collective-permute-start(bf16[256,768]{0,1:T(8,128)(2,1)S(1)} %bitcast.159), channel_id=1, source_target_pairs={{0,12},{4,0},{8,4},{12,8},{1,13},{5,1},{9,5},{13,9},{2,14},{6,2},{... | collective-permute-start | bytes 1179656 | tf_op jit(solution)/shard_map/ppermute | solution.py:77
  112.9 28.0 %collective-permute-start.17 = (bf16[1,192,1536]{2,1,0:T(8,128)(2,1)}, bf16[1,192,1536]{2,1,0:T(8,128)(2,1)}, u32[]{:S(2)}, u32[]{:S(2)}) collective-permute-start(bf16[1,192,1536]{2,1,0:T(8,128)(2,1)} %collective-permute-done.10.refs_13_), channel_id=1, source_target_pairs={{0,1},{1,0},{2,3},{3,2},{4,5},{5,4},{6,7},{7,6},{8,9},{9,8},{10,11... | collective-permute-start | bytes 1769480 | tf_op jit(solution)/shard_map/ppermute | solution.py:67
  114.4 8.7 %collective-permute-start.13 = (bf16[4,192,192]{2,1,0:T(8,128)(2,1)S(1)}, bf16[4,192,192]{2,1,0:T(8,128)(2,1)S(1)}, u32[]{:S(2)}, u32[]{:S(2)}) collective-permute-start(bf16[4,192,192]{2,1,0:T(8,128)(2,1)S(1)} %collective-permute-done.12.o2), channel_id=1, source_target_pairs={{0,1},{1,0},{2,3},{3,2},{4,5},{5,4},{6,7},{7,6},{8,9},{9,8},{10,11... | collective-permute-start | bytes 884744 | tf_op jit(solution)/shard_map/ppermute | solution.py:67
  121.7 23.5 %collective-permute-start.22 = (bf16[1,192,1536]{2,1,0:T(8,128)(2,1)}, bf16[1,192,1536]{2,1,0:T(8,128)(2,1)}, u32[]{:S(2)}, u32[]{:S(2)}) collective-permute-start(bf16[1,192,1536]{2,1,0:T(8,128)(2,1)} %slice.311), channel_id=1, source_target_pairs={{0,2},{1,3},{2,0},{3,1},{4,6},{5,7},{6,4},{7,5},{8,10},{9,11},{10,... | collective-permute-start | bytes 1769480 | tf_op jit(solution)/shard_map/ppermute | solution.py:67
  123.9 22.6 %collective-permute-start.23 = (bf16[1,192,1536]{2,1,0:T(8,128)(2,1)}, bf16[1,192,1536]{2,1,0:T(8,128)(2,1)}, u32[]{:S(2)}, u32[]{:S(2)}) collective-permute-start(bf16[1,192,1536]{2,1,0:T(8,128)(2,1)} %collective-permute-done.10.refs_13_), channel_id=1, source_target_pairs={{0,16},{16,0},{1,17},{17,1},{2,18},{18,2},{3,19},{19,3},{4,20},{20... | collective-permute-start | bytes 1769480 | tf_op jit(solution)/shard_map/ppermute | solution.py:862
  126.1 50.9 %collective-permute-start.29 = (bf16[2,192,1536]{2,1,0:T(8,128)(2,1)}, bf16[2,192,1536]{2,1,0:T(8,128)(2,1)}, u32[]{:S(2)}, u32[]{:S(2)}) collective-permute-start(bf16[2,192,1536]{2,1,0:T(8,128)(2,1)} %collective-permute-done.27.refs_15_), channel_id=1, source_target_pairs={{0,1},{1,0},{2,3},{3,2},{4,5},{5,4},{6,7},{7,6},{8,9},{9,8},{10,11... | collective-permute-start | bytes 3538952 | tf_op jit(solution)/shard_map/ppermute | solution.py:67
  140.9 20.9 %collective-permute-start.21 = (bf16[256,768]{0,1:T(8,128)(2,1)S(1)}, bf16[256,768]{0,1:T(8,128)(2,1)S(1)}, u32[]{:S(2)}, u32[]{:S(2)}) collective-permute-start(bf16[256,768]{0,1:T(8,128)(2,1)S(1)} %bitcast.160), channel_id=1, source_target_pairs={{0,8},{4,12},{8,0},{12,4},{1,9},{5,13},{9,1},{13,5},{2,10},{6,14},... | collective-permute-start | bytes 1179656 | tf_op jit(solution)/shard_map/ppermute | solution.py:77
  161.8 15.1 %collective-permute-start.30 = (bf16[1,192,1536]{2,1,0:T(8,128)(2,1)}, bf16[1,192,1536]{2,1,0:T(8,128)(2,1)S(1)}, u32[]{:S(2)}, u32[]{:S(2)}) collective-permute-start(bf16[1,192,1536]{2,1,0:T(8,128)(2,1)} %collective-permute-done.22.refs_14_), channel_id=1, source_target_pairs={{0,16},{16,0},{1,17},{17,1},{2,18},{18,2},{3,19},{19,3},{4,20},{20... | collective-permute-start | bytes 1769480 | tf_op jit(solution)/shard_map/ppermute | solution.py:862
  168.0 13.2 %collective-permute-start.24 = (bf16[272,768]{1,0:T(8,128)(2,1)}, bf16[272,768]{1,0:T(8,128)(2,1)S(1)}, u32[]{:S(2)}, u32[]{:S(2)}) collective-permute-start(bf16[272,768]{1,0:T(8,128)(2,1)} %get-tuple-element.160.refs_1_), channel_id=1, source_target_pairs={{0,4},{4,8},{8,12},{12,0},{1,5},{5,9},{9,13},{13,1},{2,6},{6,10},{... | collective-permute-start | bytes 1253384 | tf_op jit(solution)/shard_map/ppermute | solution.py:77
  168.3 31.8 %collective-permute-start.28 = (bf16[1,192,1536]{2,1,0:T(8,128)(2,1)}, bf16[1,192,1536]{2,1,0:T(8,128)(2,1)S(1)}, u32[]{:S(2)}, u32[]{:S(2)}) collective-permute-start(bf16[1,192,1536]{2,1,0:T(8,128)(2,1)} %collective-permute-done.22.refs_14_), channel_id=1, source_target_pairs={{0,1},{1,0},{2,3},{3,2},{4,5},{5,4},{6,7},{7,6},{8,9},{9,8},{10,11... | collective-permute-start | bytes 1769480 | tf_op jit(solution)/shard_map/ppermute | solution.py:67
  168.3 31.8 %collective-permute-start.31 = (bf16[1,192,1536]{2,1,0:T(8,128)(2,1)}, bf16[1,192,1536]{2,1,0:T(8,128)(2,1)S(1)}, u32[]{:S(2)}, u32[]{:S(2)}) collective-permute-start(bf16[1,192,1536]{2,1,0:T(8,128)(2,1)} %collective-permute-done.23.refs_13_), channel_id=1, source_target_pairs={{0,1},{1,0},{2,3},{3,2},{4,5},{5,4},{6,7},{7,6},{8,9},{9,8},{10,11... | collective-permute-start | bytes 1769480 | tf_op jit(solution)/shard_map/ppermute | solution.py:67
  176.9 24.0 %collective-permute-start.32 = (bf16[1,192,1536]{2,1,0:T(8,128)(2,1)S(1)}, bf16[1,192,1536]{2,1,0:T(8,128)(2,1)S(1)}, u32[]{:S(2)}, u32[]{:S(2)}) collective-permute-start(bf16[1,192,1536]{2,1,0:T(8,128)(2,1)S(1)} %collective-permute-done.30.refs_14_), channel_id=1, source_target_pairs={{0,1},{1,0},{2,3},{3,2},{4,5},{5,4},{6,7},{7,6},{8,9},{9,8},{10,11... | collective-permute-start | bytes 1769480 | tf_op jit(solution)/shard_map/ppermute | solution.py:67
  176.9 22.7 %collective-permute-start.25 = (bf16[272,768]{1,0:T(8,128)(2,1)}, bf16[272,768]{1,0:T(8,128)(2,1)S(1)}, u32[]{:S(2)}, u32[]{:S(2)}) collective-permute-start(bf16[272,768]{1,0:T(8,128)(2,1)} %get-tuple-element.160.refs_1_), channel_id=1, source_target_pairs={{0,8},{4,12},{8,0},{12,4},{1,9},{5,13},{9,1},{13,5},{2,10},{6,14},... | collective-permute-start | bytes 1253384 | tf_op jit(solution)/shard_map/ppermute | solution.py:77
  181.2 18.8 %collective-permute-start.26 = (bf16[272,768]{1,0:T(8,128)(2,1)}, bf16[272,768]{1,0:T(8,128)(2,1)S(1)}, u32[]{:S(2)}, u32[]{:S(2)}) collective-permute-start(bf16[272,768]{1,0:T(8,128)(2,1)} %get-tuple-element.160.refs_1_), channel_id=1, source_target_pairs={{0,12},{4,0},{8,4},{12,8},{1,13},{5,1},{9,5},{13,9},{2,14},{6,2},{... | collective-permute-start | bytes 1253384 | tf_op jit(solution)/shard_map/ppermute | solution.py:77
  201.9 26.9 %collective-permute-start.33 = (bf16[2,192,1536]{2,1,0:T(8,128)(2,1)}, bf16[2,192,1536]{2,1,0:T(8,128)(2,1)S(1)}, u32[]{:S(2)}, u32[]{:S(2)}) collective-permute-start(bf16[2,192,1536]{2,1,0:T(8,128)(2,1)} %collective-permute-done.27.refs_15_), channel_id=1, source_target_pairs={{0,16},{16,0},{1,17},{17,1},{2,18},{18,2},{3,19},{19,3},{4,20},{20... | collective-permute-start | bytes 3538952 | tf_op jit(solution)/shard_map/ppermute | solution.py:862
  228.8 34.7 %collective-permute-start.34 = (bf16[2,192,1536]{2,1,0:T(8,128)(2,1)S(1)}, bf16[2,192,1536]{2,1,0:T(8,128)(2,1)}, u32[]{:S(2)}, u32[]{:S(2)}) collective-permute-start(bf16[2,192,1536]{2,1,0:T(8,128)(2,1)S(1)} %collective-permute-done.33.refs_15_), channel_id=1, source_target_pairs={{0,1},{1,0},{2,3},{3,2},{4,5},{5,4},{6,7},{7,6},{8,9},{9,8},{10,11... | collective-permute-start | bytes 3538952 | tf_op jit(solution)/shard_map/ppermute | solution.py:67
  263.4 38.4 %collective-permute-start.35 = (bf16[4,192,1536]{2,1,0:T(8,128)(2,1)}, bf16[4,192,1536]{2,1,0:T(8,128)(2,1)S(1)}, u32[]{:S(2)}, u32[]{:S(2)}) collective-permute-start(bf16[4,192,1536]{2,1,0:T(8,128)(2,1)} %get-tuple-element.196), channel_id=1, source_target_pairs={{0,1},{1,0},{2,3},{3,2},{4,5},{5,4},{6,7},{7,6},{8,9},{9,8},{10,11... | collective-permute-start | bytes 7077896 | tf_op jit(solution)/shard_map/ppermute | solution.py:67
  264.0 37.9 %collective-permute-start.36 = (bf16[4,192,1536]{2,1,0:T(8,128)(2,1)}, bf16[4,192,1536]{2,1,0:T(8,128)(2,1)}, u32[]{:S(2)}, u32[]{:S(2)}) collective-permute-start(bf16[4,192,1536]{2,1,0:T(8,128)(2,1)} %get-tuple-element.197), channel_id=1, source_target_pairs={{0,1},{1,0},{2,3},{3,2},{4,5},{5,4},{6,7},{7,6},{8,9},{9,8},{10,11... | collective-permute-start | bytes 7077896 | tf_op jit(solution)/shard_map/ppermute | solution.py:67
  301.9 54.0 %collective-permute-start.44 = (bf16[4,192,1536]{2,1,0:T(8,128)(2,1)}, bf16[4,192,1536]{2,1,0:T(8,128)(2,1)}, u32[]{:S(2)}, u32[]{:S(2)}) collective-permute-start(bf16[4,192,1536]{2,1,0:T(8,128)(2,1)} %get-tuple-element.204), channel_id=1, source_target_pairs={{0,1},{1,0},{2,3},{3,2},{4,5},{5,4},{6,7},{7,6},{8,9},{9,8},{10,11... | collective-permute-start | bytes 7077896 | tf_op jit(solution)/shard_map/ppermute | solution.py:67
  302.4 53.5 %collective-permute-start.45 = (bf16[4,192,1536]{2,1,0:T(8,128)(2,1)}, bf16[4,192,1536]{2,1,0:T(8,128)(2,1)}, u32[]{:S(2)}, u32[]{:S(2)}) collective-permute-start(bf16[4,192,1536]{2,1,0:T(8,128)(2,1)} %get-tuple-element.205), channel_id=1, source_target_pairs={{0,1},{1,0},{2,3},{3,2},{4,5},{5,4},{6,7},{7,6},{8,9},{9,8},{10,11... | collective-permute-start | bytes 7077896 | tf_op jit(solution)/shard_map/ppermute | solution.py:67
  305.6 20.5 %collective-permute-start.40 = (bf16[272,768]{1,0:T(8,128)(2,1)S(1)}, bf16[272,768]{1,0:T(8,128)(2,1)S(1)}, u32[]{:S(2)}, u32[]{:S(2)}) collective-permute-start(bf16[272,768]{1,0:T(8,128)(2,1)S(1)} %get-tuple-element.309), channel_id=1, source_target_pairs={{0,12},{4,0},{8,4},{12,8},{1,13},{5,1},{9,5},{13,9},{2,14},{6,2},{... | collective-permute-start | bytes 1253384 | tf_op jit(solution)/shard_map/ppermute | solution.py:77
  319.4 36.4 %collective-permute-start.43 = (bf16[2,192,1536]{2,1,0:T(8,128)(2,1)S(1)}, bf16[2,192,1536]{2,1,0:T(8,128)(2,1)}, u32[]{:S(2)}, u32[]{:S(2)}) collective-permute-start(bf16[2,192,1536]{2,1,0:T(8,128)(2,1)S(1)} %get-tuple-element.295), channel_id=1, source_target_pairs={{0,2},{1,3},{2,0},{3,1},{4,6},{5,7},{6,4},{7,5},{8,10},{9,11},{10,... | collective-permute-start | bytes 3538952 | tf_op jit(solution)/shard_map/ppermute | solution.py:67
  320.6 32.8 %collective-permute-start.41 = (bf16[272,768]{1,0:T(8,128)(2,1)S(1)}, bf16[272,768]{1,0:T(8,128)(2,1)S(1)}, u32[]{:S(2)}, u32[]{:S(2)}) collective-permute-start(bf16[272,768]{1,0:T(8,128)(2,1)S(1)} %get-tuple-element.308), channel_id=1, source_target_pairs={{0,8},{4,12},{8,0},{12,4},{1,9},{5,13},{9,1},{13,5},{2,10},{6,14},... | collective-permute-start | bytes 1253384 | tf_op jit(solution)/shard_map/ppermute | solution.py:77
  326.2 27.3 %collective-permute-start.42 = (bf16[272,768]{1,0:T(8,128)(2,1)S(1)}, bf16[272,768]{1,0:T(8,128)(2,1)S(1)}, u32[]{:S(2)}, u32[]{:S(2)}) collective-permute-start(bf16[272,768]{1,0:T(8,128)(2,1)S(1)} %get-tuple-element.307), channel_id=1, source_target_pairs={{0,4},{4,8},{8,12},{12,0},{1,5},{5,9},{9,13},{13,1},{2,6},{6,10},{... | collective-permute-start | bytes 1253384 | tf_op jit(solution)/shard_map/ppermute | solution.py:77
  353.4 49.4 %collective-permute-start.37 = (bf16[256,768]{1,0:T(8,128)(2,1)}, bf16[256,768]{1,0:T(8,128)(2,1)}, u32[]{:S(2)}, u32[]{:S(2)}) collective-permute-start(bf16[256,768]{1,0:T(8,128)(2,1)} %get-tuple-element.316), channel_id=1, source_target_pairs={{0,12},{4,0},{8,4},{12,8},{1,13},{5,1},{9,5},{13,9},{2,14},{6,2},{... | collective-permute-start | bytes 1179656 | tf_op jit(solution)/shard_map/ppermute | solution.py:77
  353.5 49.4 %collective-permute-start.38 = (bf16[256,768]{1,0:T(8,128)(2,1)}, bf16[256,768]{1,0:T(8,128)(2,1)}, u32[]{:S(2)}, u32[]{:S(2)}) collective-permute-start(bf16[256,768]{1,0:T(8,128)(2,1)} %get-tuple-element.315), channel_id=1, source_target_pairs={{0,8},{4,12},{8,0},{12,4},{1,9},{5,13},{9,1},{13,5},{2,10},{6,14},... | collective-permute-start | bytes 1179656 | tf_op jit(solution)/shard_map/ppermute | solution.py:77
  362.5 12.3 %collective-permute-start.48 = (bf16[768,256]{1,0:T(8,128)(2,1)}, bf16[768,256]{1,0:T(8,128)(2,1)S(1)}, u32[]{:S(2)}, u32[]{:S(2)}) collective-permute-start(bf16[768,256]{1,0:T(8,128)(2,1)} %get-tuple-element.224.d0), channel_id=1, source_target_pairs={{0,2},{1,3},{2,0},{3,1},{4,6},{5,7},{6,4},{7,5},{8,10},{9,11},{10,... | collective-permute-start | bytes 1179656 | tf_op jit(solution)/shard_map/ppermute | solution.py:67
  363.8 11.3 %collective-permute-start.47 = (bf16[768,256]{1,0:T(8,128)(2,1)}, bf16[768,256]{1,0:T(8,128)(2,1)S(1)}, u32[]{:S(2)}, u32[]{:S(2)}) collective-permute-start(bf16[768,256]{1,0:T(8,128)(2,1)} %get-tuple-element.224.d0), channel_id=1, source_target_pairs={{0,1},{1,0},{2,3},{3,2},{4,5},{5,4},{6,7},{7,6},{8,9},{9,8},{10,11... | collective-permute-start | bytes 1179656 | tf_op jit(solution)/shard_map/ppermute | solution.py:67
  363.8 39.1 %collective-permute-start.46 = (bf16[2,192,1536]{2,1,0:T(8,128)(2,1)}, bf16[2,192,1536]{2,1,0:T(8,128)(2,1)}, u32[]{:S(2)}, u32[]{:S(2)}) collective-permute-start(bf16[2,192,1536]{2,1,0:T(8,128)(2,1)} %get-tuple-element.207), channel_id=1, source_target_pairs={{0,2},{1,3},{2,0},{3,1},{4,6},{5,7},{6,4},{7,5},{8,10},{9,11},{10,... | collective-permute-start | bytes 3538952 | tf_op jit(solution)/shard_map/ppermute | solution.py:67
  374.8 28.1 %collective-permute-start.39 = (bf16[256,768]{1,0:T(8,128)(2,1)}, bf16[256,768]{1,0:T(8,128)(2,1)}, u32[]{:S(2)}, u32[]{:S(2)}) collective-permute-start(bf16[256,768]{1,0:T(8,128)(2,1)} %get-tuple-element.314), channel_id=1, source_target_pairs={{0,4},{4,8},{8,12},{12,0},{1,5},{5,9},{9,13},{13,1},{2,6},{6,10},{... | collective-permute-start | bytes 1179656 | tf_op jit(solution)/shard_map/ppermute | solution.py:77
  376.9 112.9 %collective-permute-start.69 = (bf16[2,192,1536]{2,1,0:T(8,128)(2,1)S(1)}, bf16[2,192,1536]{2,1,0:T(8,128)(2,1)}, u32[]{:S(2)}, u32[]{:S(2)}) collective-permute-start(bf16[2,192,1536]{2,1,0:T(8,128)(2,1)S(1)} %add_convert_fusion.5), channel_id=1, source_target_pairs={{0,16},{16,0},{1,17},{17,1},{2,18},{18,2},{3,19},{19,3},{4,20},{20... | collective-permute-start | bytes 3538952 | tf_op jit(solution)/shard_map/ppermute | solution.py:862
  405.1 10.0 %collective-permute-start.59 = (f32[24,192]{1,0:T(8,128)S(1)}, f32[24,192]{1,0:T(8,128)S(1)}, u32[]{:S(2)}, u32[]{:S(2)}) collective-permute-start(f32[24,192]{1,0:T(8,128)S(1)} %get-tuple-element.350), channel_id=1, source_target_pairs={{0,3},{1,2},{2,1},{3,0},{4,7},{5,6},{6,5},{7,4},{8,11},{9,10},{10,... | collective-permute-start | bytes 55304 | tf_op jit(solution)/shard_map/ppermute | solution.py:67
  407.8 7.8 %collective-permute-start.53 = (bf16[192,768]{1,0:T(8,128)(2,1)S(1)}, bf16[192,768]{1,0:T(8,128)(2,1)S(1)}, u32[]{:S(2)}, u32[]{:S(2)}) collective-permute-start(bf16[192,768]{1,0:T(8,128)(2,1)S(1)} %get-tuple-element.318), channel_id=1, source_target_pairs={{0,0},{1,4},{2,8},{3,12},{4,1},{5,5},{6,9},{7,13},{8,2},{9,6},{10,... | collective-permute-start | bytes 884744 | tf_op jit(solution)/shard_map/ppermute | solution.py:859
  409.1 28.7 %collective-permute-start.54 = (bf16[192,768]{1,0:T(8,128)(2,1)S(1)}, bf16[192,768]{1,0:T(8,128)(2,1)S(1)}, u32[]{:S(2)}, u32[]{:S(2)}) collective-permute-start(bf16[192,768]{1,0:T(8,128)(2,1)S(1)} %get-tuple-element.321), channel_id=1, source_target_pairs={{0,1},{1,5},{2,9},{3,13},{4,0},{5,4},{6,8},{7,12},{8,3},{9,7},{10,... | collective-permute-start | bytes 884744 | tf_op jit(solution)/shard_map/ppermute | solution.py:859
  410.8 79.1 %collective-permute-start.60 = (bf16[2,192,1536]{2,1,0:T(8,128)(2,1)}, bf16[2,192,1536]{2,1,0:T(8,128)(2,1)}, u32[]{:S(2)}, u32[]{:S(2)}) collective-permute-start(bf16[2,192,1536]{2,1,0:T(8,128)(2,1)} %get-tuple-element.236), channel_id=1, source_target_pairs={{0,2},{1,3},{2,0},{3,1},{4,6},{5,7},{6,4},{7,5},{8,10},{9,11},{10,... | collective-permute-start | bytes 3538952 | tf_op jit(solution)/shard_map/ppermute | solution.py:67
  415.1 57.8 %collective-permute-start.50 = (bf16[192,1024]{1,0:T(8,128)(2,1)}, bf16[192,1024]{1,0:T(8,128)(2,1)}, u32[]{:S(2)}, u32[]{:S(2)}) collective-permute-start(bf16[192,1024]{1,0:T(8,128)(2,1)} %get-tuple-element.311), channel_id=1, source_target_pairs={{0,1},{1,0},{2,3},{3,2},{4,5},{5,4},{6,7},{7,6},{8,9},{9,8},{10,11... | collective-permute-start | bytes 1179656 | tf_op jit(solution)/shard_map/ppermute | solution.py:67
  415.7 50.0 %collective-permute-start.55 = (bf16[192,768]{1,0:T(8,128)(2,1)}, bf16[192,768]{1,0:T(8,128)(2,1)}, u32[]{:S(2)}, u32[]{:S(2)}) collective-permute-start(bf16[192,768]{1,0:T(8,128)(2,1)} %get-tuple-element.320), channel_id=1, source_target_pairs={{0,2},{1,6},{2,10},{3,14},{4,3},{5,7},{6,11},{7,15},{8,0},{9,4},{1... | collective-permute-start | bytes 884744 | tf_op jit(solution)/shard_map/ppermute | solution.py:859
  438.5 32.3 %collective-permute-start.56 = (bf16[192,768]{1,0:T(8,128)(2,1)}, bf16[192,768]{1,0:T(8,128)(2,1)}, u32[]{:S(2)}, u32[]{:S(2)}) collective-permute-start(bf16[192,768]{1,0:T(8,128)(2,1)} %get-tuple-element.319), channel_id=1, source_target_pairs={{0,3},{1,7},{2,11},{3,15},{4,2},{5,6},{6,10},{7,14},{8,1},{9,5},{1... | collective-permute-start | bytes 884744 | tf_op jit(solution)/shard_map/ppermute | solution.py:859
  465.7 13.5 %collective-permute-start.51 = (bf16[192,1024]{1,0:T(8,128)(2,1)}, bf16[192,1024]{1,0:T(8,128)(2,1)S(1)}, u32[]{:S(2)}, u32[]{:S(2)}) collective-permute-start(bf16[192,1024]{1,0:T(8,128)(2,1)} %get-tuple-element.313), channel_id=1, source_target_pairs={{0,2},{1,3},{2,0},{3,1},{4,6},{5,7},{6,4},{7,5},{8,10},{9,11},{10,... | collective-permute-start | bytes 1179656 | tf_op jit(solution)/shard_map/ppermute | solution.py:67
  470.8 16.7 %collective-permute-start.52 = (bf16[192,1024]{1,0:T(8,128)(2,1)S(1)}, bf16[192,1024]{1,0:T(8,128)(2,1)S(1)}, u32[]{:S(2)}, u32[]{:S(2)}) collective-permute-start(bf16[192,1024]{1,0:T(8,128)(2,1)S(1)} %copy-done.39), channel_id=1, source_target_pairs={{0,3},{1,2},{2,1},{3,0},{4,7},{5,6},{6,5},{7,4},{8,11},{9,10},{10,... | collective-permute-start | bytes 1179656 | tf_op jit(solution)/shard_map/ppermute | solution.py:67
  472.9 34.9 %collective-permute-start.70 = (bf16[2,192,1536]{2,1,0:T(8,128)(2,1)}, bf16[2,192,1536]{2,1,0:T(8,128)(2,1)S(1)}, u32[]{:S(2)}, u32[]{:S(2)}) collective-permute-start(bf16[2,192,1536]{2,1,0:T(8,128)(2,1)} %get-tuple-element.252), channel_id=1, source_target_pairs={{0,2},{1,3},{2,0},{3,1},{4,6},{5,7},{6,4},{7,5},{8,10},{9,11},{10,... | collective-permute-start | bytes 3538952 | tf_op jit(solution)/shard_map/ppermute | solution.py:67
  491.6 102.8 %collective-permute-start.72 = (bf16[2,192,1536]{2,1,0:T(8,128)(2,1)S(1)}, bf16[2,192,1536]{2,1,0:T(8,128)(2,1)}, u32[]{:S(2)}, u32[]{:S(2)}) collective-permute-start(bf16[2,192,1536]{2,1,0:T(8,128)(2,1)S(1)} %add_convert_fusion.3), channel_id=1, source_target_pairs={{0,16},{16,0},{1,17},{17,1},{2,18},{18,2},{3,19},{19,3},{4,20},{20... | collective-permute-start | bytes 3538952 | tf_op jit(solution)/shard_map/ppermute | solution.py:862
  493.7 17.0 %collective-permute-start.65 = (f32[24,192]{1,0:T(8,128)S(1)}, f32[24,192]{1,0:T(8,128)S(1)}, u32[]{:S(2)}, u32[]{:S(2)}) collective-permute-start(f32[24,192]{1,0:T(8,128)S(1)} %add.301), channel_id=1, source_target_pairs={{0,8},{4,12},{8,0},{12,4},{1,9},{5,13},{9,1},{13,5},{2,10},{6,14},... | collective-permute-start | bytes 55304 | tf_op jit(solution)/shard_map/ppermute | solution.py:72
  509.7 76.7 %collective-permute-start.68 = (bf16[2,192,1536]{2,1,0:T(8,128)(2,1)S(1)}, bf16[2,192,1536]{2,1,0:T(8,128)(2,1)}, u32[]{:S(2)}, u32[]{:S(2)}) collective-permute-start(bf16[2,192,1536]{2,1,0:T(8,128)(2,1)S(1)} %get-tuple-element.306), channel_id=1, source_target_pairs={{0,16},{16,0},{1,17},{17,1},{2,18},{18,2},{3,19},{19,3},{4,20},{20... | collective-permute-start | bytes 3538952 | tf_op jit(solution)/shard_map/ppermute | solution.py:862
  510.7 31.4 %collective-permute-start.66 = (f32[24,192]{1,0:T(8,128)S(1)}, f32[24,192]{1,0:T(8,128)S(1)}, u32[]{:S(2)}, u32[]{:S(2)}) collective-permute-start(f32[24,192]{1,0:T(8,128)S(1)} %add.302), channel_id=1, source_target_pairs={{0,16},{16,0},{1,17},{17,1},{2,18},{18,2},{3,19},{19,3},{4,20},{20... | collective-permute-start | bytes 55304 | tf_op jit(solution)/shard_map/ppermute | solution.py:98
  512.0 35.5 %collective-permute-start.61 = (f32[208,256]{1,0:T(8,128)S(1)}, f32[208,256]{1,0:T(8,128)S(1)}, u32[]{:S(2)}, u32[]{:S(2)}) collective-permute-start(f32[208,256]{1,0:T(8,128)S(1)} %get-tuple-element.329), channel_id=1, source_target_pairs={{0,1},{1,0},{2,3},{3,2},{4,5},{5,4},{6,7},{7,6},{8,9},{9,8},{10,11... | collective-permute-start | bytes 638984 | tf_op jit(solution)/shard_map/ppermute | solution.py:67
  512.0 36.2 %collective-permute-start.62 = (f32[208,256]{1,0:T(8,128)S(1)}, f32[208,256]{1,0:T(8,128)S(1)}, u32[]{:S(2)}, u32[]{:S(2)}) collective-permute-start(f32[208,256]{1,0:T(8,128)S(1)} %get-tuple-element.328), channel_id=1, source_target_pairs={{0,2},{1,3},{2,0},{3,1},{4,6},{5,7},{6,4},{7,5},{8,10},{9,11},{10,... | collective-permute-start | bytes 638984 | tf_op jit(solution)/shard_map/ppermute | solution.py:67
  547.5 45.2 %collective-permute-start.71 = (bf16[2,192,1536]{2,1,0:T(8,128)(2,1)S(1)}, bf16[2,192,1536]{2,1,0:T(8,128)(2,1)}, u32[]{:S(2)}, u32[]{:S(2)}) collective-permute-start(bf16[2,192,1536]{2,1,0:T(8,128)(2,1)S(1)} %get-tuple-element.305), channel_id=1, source_target_pairs={{0,16},{16,0},{1,17},{17,1},{2,18},{18,2},{3,19},{19,3},{4,20},{20... | collective-permute-start | bytes 3538952 | tf_op jit(solution)/shard_map/ppermute | solution.py:862
  548.2 32.3 %collective-permute-start.67 = (bf16[192,768]{1,0:T(8,128)(2,1)}, bf16[192,768]{1,0:T(8,128)(2,1)}, u32[]{:S(2)}, u32[]{:S(2)}) collective-permute-start(bf16[192,768]{1,0:T(8,128)(2,1)} %convert_add_fusion.2), channel_id=1, source_target_pairs={{0,16},{16,0},{1,17},{17,1},{2,18},{18,2},{3,19},{19,3},{4,20},{20... | collective-permute-start | bytes 884744 | tf_op jit(solution)/shard_map/ppermute | solution.py:98
  (71 other events, 1393.2 us)

commit v3 on v2

--- a/solution.py
+++ b/solution.py
@@ -56,6 +56,16 @@
 def unpack_row(ref, base, span, k):
     parts = ref[base : base + EXTRA, :span].astype(F32)
     return parts[3 * k : 3 * k + 1] + parts[3 * k + 1 : 3 * k + 2] + parts[3 * k + 2 : 3 * k + 3]
+
+
+def span_of(micros):
+    return pl.CostEstimate(
+        flops=int(micros * 1.1e9), transcendentals=0, bytes_accessed=int(micros * 3.6e6)
+    )
+
+
+def after(value, *others):
+    return lax.optimization_barrier((value,) + others)[0]
 
 
 def join(*values):
@@ -186,6 +196,7 @@
     return pl.pallas_call(
         attend_kernel,
         name="attend",
+        cost_estimate=span_of(14),
         grid_spec=pltpu.PrefetchScalarGridSpec(
             num_scalar_prefetch=1,
             grid=(count,),
@@ -334,6 +345,7 @@
     return pl.pallas_call(
         attend_back_kernel,
         name="attend_back",
+        cost_estimate=span_of(24),
         grid_spec=pltpu.PrefetchScalarGridSpec(
             num_scalar_prefetch=1,
             grid=(count,),
@@ -435,6 +447,7 @@
     return pl.pallas_call(
         middle_kernel,
         name="middle",
+        cost_estimate=span_of(6),
         grid_spec=pltpu.PrefetchScalarGridSpec(
             num_scalar_prefetch=1,
             grid=(1,),
@@ -555,6 +568,7 @@
     return pl.pallas_call(
         middle_back_kernel,
         name="middle_back",
+        cost_estimate=span_of(7),
         grid_spec=pltpu.PrefetchScalarGridSpec(
             num_scalar_prefetch=1,
             grid=(1,),
@@ -623,6 +637,7 @@
     return pl.pallas_call(
         result_kernel,
         name="result",
+        cost_estimate=span_of(5),
         grid_spec=pltpu.PrefetchScalarGridSpec(
             num_scalar_prefetch=1,
             grid=(1,),
@@ -647,7 +662,7 @@
     if not last:
         gate_out = refs[0]
         refs = refs[1:]
-    grad0, grad1, grad2, grad3, weight, y_acc, dx_acc, gate_sum, gate_rows, acc = refs
+    grad_mine, grad_next, weight, y_acc, dx_acc, gate_sum, gate_rows, acc = refs
     step = pl.program_id(0)
     steps = pl.num_programs(0)
     expert = order[step]
@@ -743,8 +758,9 @@
         return carry
 
     lax.fori_loop(0, tiles, tile, 0)
-    for k, ref in enumerate((grad0, grad1, grad2, grad3)):
-        ref[0] = acc[k * size : (k + 1) * size].astype(BF16)
+    for k in range(4):
+        ref = grad_next if k % 2 else grad_mine
+        ref[k // 2, 0] = acc[k * size : (k + 1) * size].astype(BF16)
 
     @pl.when(step == steps - 1)
     def _():
@@ -789,7 +805,7 @@
         shapes = [((4, span, full), BF16), ((4, span + EXTRA, full), BF16)]
     else:
         shapes = [((tokens, full), F32), ((tokens, full), F32), ((8, tokens), F32)]
-    grad = pl.BlockSpec((1, size, wide), lambda e, s: (e, 0, 0))
+    grad = pl.BlockSpec((2, 1, size, wide), lambda e, s: (0, e, 0, 0))
 
     def body(*refs):
         experts_kernel(chunks, last, *refs)
@@ -797,11 +813,12 @@
     return pl.pallas_call(
         body,
         name="experts",
+        cost_estimate=span_of(36),
         grid_spec=pltpu.PrefetchScalarGridSpec(
             num_scalar_prefetch=1,
             grid=(steps,),
             in_specs=specs,
-            out_specs=[whole(shape) for shape, _ in shapes] + [grad] * 4,
+            out_specs=[whole(shape) for shape, _ in shapes] + [grad] * 2,
             scratch_shapes=[
                 pltpu.VMEM((full, wide), BF16),
                 pltpu.VMEM((tokens, full), F32),
@@ -812,7 +829,7 @@
             ],
         ),
         out_shape=[jax.ShapeDtypeStruct(shape, dtype) for shape, dtype in shapes]
-        + [jax.ShapeDtypeStruct((steps, size, wide), BF16)] * 4,
+        + [jax.ShapeDtypeStruct((2, steps, size, wide), BF16)] * 2,
         compiler_params=pltpu.CompilerParams(vmem_limit_bytes=VMEM_LIMIT),
     )(order, *args)
 
@@ -867,22 +884,28 @@
     for value in values:
         lanes += [part[:, None] for part in parts_of(value)]
     lanes.append(jnp.zeros((size, PARAMS - kinds - 4 - 3 * len(values)), BF16))
+    piece = jnp.concatenate([qkv_weight[0], qkv_weight[1], qkv_weight[2], out_weight.T], axis=1)
     toks = col_gather(jnp.concatenate([tokens.T] + lanes, axis=1))
-    piece = jnp.concatenate([qkv_weight[0], qkv_weight[1], qkv_weight[2], out_weight.T], axis=1)
     weight = jnp.stack([spread(piece, m) for m in range(rows)])
-    flow = cotangent.T.reshape(size, cols, span)
-    flow_parts = [lax.dynamic_index_in_dim(flow, col ^ k, 1, False) for k in range(cols)]
-    flow_quarter = jnp.concatenate(
-        [flow_parts[0]] + [col_swap(flow_parts[k], k) for k in range(1, cols)], axis=0
-    )
-    own = jnp.concatenate([gate_weight, up_weight, down_weight.transpose(0, 2, 1)], axis=2)
-    near_own = lax.dynamic_slice_in_dim(own, first_half * half, half, 0)
-    two_a = col_swap(near_own[:1], 2)
     halves = HD // 2
     freq = 10000.0 ** (-jnp.arange(halves, dtype=F32) / halves)
     angle = freq[:, None] * jnp.arange(length, dtype=F32)[None, :]
     cosine = jnp.cos(angle)
     sine = jnp.sin(angle)
+
+    flow = after(cotangent.T, toks[2]).reshape(size, cols, span)
+    flow_parts = [lax.dynamic_index_in_dim(flow, col ^ k, 1, False) for k in range(cols)]
+    flow_quarter = jnp.concatenate(
+        [flow_parts[0]] + [col_swap(flow_parts[k], k) for k in range(1, cols)], axis=0
+    )
+    flow_rows = row_gather(flow_quarter.T)
+
+    own = jnp.concatenate([gate_weight, up_weight, down_weight.transpose(0, 2, 1)], axis=2)
+    near_own = lax.dynamic_slice_in_dim(own, first_half * half, half, 0)
+    pair = half // 2
+    two_a = col_swap(after(near_own[:pair], flow_quarter), 2)
+    side = col_swap(after(own, weight), 1)
+    projs = col_gather(after(weight[:, :, 3 * size :], toks[2]))
 
     routes_t = routes.T
     share = lax.dynamic_index_in_dim(routes_t.reshape(2, rows, cols, span), col, 2, False)
@@ -896,63 +919,35 @@
     tiles = jnp.take(jnp.maximum((counts[:, -1] + TILE - 1) // TILE, 1), order)
     order_near = jnp.concatenate([order[:half], tiles[:half]]).astype(jnp.int32)
     order_far = jnp.concatenate([order[half:], tiles[half:]]).astype(jnp.int32)
-    toks, weight, flow_quarter, two_a, own, near_own, cosine, sine, ranks, share = join(
-        toks, weight, flow_quarter, two_a, own, near_own, cosine, sine, ranks, share
-    )
-
-    projs = col_gather(weight[:, :, 3 * size :])
-    flow_turned = flow_quarter.T
-    flow_rows = {0: flow_turned, 1: row_shift(flow_turned, 1), 3: row_shift(flow_turned, 3)}
-    side = col_swap(own, 1)
-    three_a = col_swap(two_a, 1)
+
     query, keys, values, attn, logsum = attend(place, toks, weight, cosine, sine)
-    attn, projs, flow_rows, side, three_a = join(attn, projs, flow_rows, side, three_a)
-
+    attn, two_a, flow_rows, projs, side = join(attn, two_a, flow_rows, projs, side)
     parts = [attn[0]] + [col_swap(attn[k], k) for k in range(1, cols)]
-    flow_rows[2] = row_shift(flow_rows[0], 2)
-    two_b = col_swap(near_own[1:2], 2)
+    two_b = col_swap(after(near_own[pair:], parts[1], parts[2], parts[3]), 2)
     if groups == 2:
         far_two_a = across_groups(two_a)
+        far_two_b = across_groups(two_b)
     else:
-        far_two_a = col_swap(own[half : half + 1], 2)
-    parts, flow_rows, two_b, far_two_a = join(parts, flow_rows, two_b, far_two_a)
-
+        far_two_a = col_swap(own[half : half + pair], 2)
+        far_two_b = col_swap(after(own[half + pair :], two_b), 2)
     mid, in_rows, stats = middle(place, toks, parts, projs, prev_logits.T, routes_t)
     x_rows = row_gather(in_rows)
-    two_c = col_swap(near_own[2:], 2)
-    three_b = col_swap(two_b, 1)
-    three_c = col_swap(two_c, 1)
-    if groups == 2:
-        far_two_b = across_groups(two_b)
-    else:
-        far_two_b = col_swap(own[half + 1 : half + 2], 2)
-    far_three_a = col_swap(far_two_a, 1)
+    three_a = col_swap(after(two_a, parts[1], parts[2], parts[3]), 1)
+    three_b = col_swap(after(two_b, mid), 1)
+    far_three_a = col_swap(after(far_two_a, mid), 1)
     far_three_b = col_swap(far_two_b, 1)
-    x_rows, two_c, three_b, three_c, far_two_b, far_three_a, far_three_b = join(
-        x_rows, two_c, three_b, three_c, far_two_b, far_three_a, far_three_b
-    )
-    flow_rows = [flow_rows[s] for s in range(rows)]
-
-    if groups == 2:
-        far_two_c = across_groups(two_c)
-    else:
-        far_two_c = col_swap(own[half + 2 :], 2)
-    far_three_c = col_swap(far_two_c, 1)
+    x_rows, far_two_a, far_three_a = join(x_rows, far_two_a, far_three_a)
+
     near_out = run_experts(
         order_near, x_rows, flow_rows, ranks, share, own, side,
-        [two_a, two_b, two_c], [three_a, three_b, three_c], None,
-    )
-    near_out, far_two_c, far_three_c = join(near_out, far_two_c, far_three_c)
-    *carried, near0, near1, near2, near3 = near_out
-
-    near1 = col_swap(near1, 1)
-    near3 = col_swap(near3, 1)
-    far_out = run_experts(
+        [two_a, two_b], [three_a, three_b], None,
+    )
+    *carried, near_mine, near_next = near_out
+    near_next = col_swap(near_next, 1)
+    y, dx, far_mine, far_next = run_experts(
         order_far, x_rows, flow_rows, ranks, share, own, side,
-        [far_two_a, far_two_b, far_two_c], [far_three_a, far_three_b, far_three_c], carried,
-    )
-    far_out, near1, near3 = join(far_out, near1, near3)
-    y, dx, far0, far1, far2, far3 = far_out
+        [far_two_a, far_two_b], [far_three_a, far_three_b], carried,
+    )
 
     def low_sum(left, right):
         return (left.astype(F32) + right.astype(F32)).astype(BF16)
@@ -960,39 +955,36 @@
     def row_scatter(value):
         return [value[0]] + [row_shift(value[s], -s) for s in range(1, rows)]
 
-    quarter = half // 2
+    def across_sums(sums):
+        return [across_groups(s) for s in sums] if groups == 2 else sums
+
+    near_next, dx, far_mine, far_next = join(near_next, dx, far_mine, far_next)
     dx = row_scatter(dx)
-    near_sent = [low_sum(near2[:quarter], near3[:quarter]), low_sum(near2[quarter:], near3[quarter:])]
-    near_kept = low_sum(near0, near1)
-    near_got = [col_swap(near_sent[0], 2)]
-    far1 = col_swap(far1, 1)
-    far3 = col_swap(far3, 1)
-    dx, near_got, near_sent, near_kept, far1, far3 = join(
-        dx, near_got, near_sent, near_kept, far1, far3
-    )
-
+    near_kept, near_sent = low_sum(near_mine[0], near_next[0]), low_sum(near_mine[1], near_next[1])
+    near_got = [col_swap(near_sent[:pair], 2), col_swap(after(near_sent[pair:], dx[1]), 2)]
+    far_next = col_swap(far_next, 1)
     low, grad_mid, grad_logits, small = middle_back(
         place, toks, mid, flow_quarter, stats, routes_t, dx, kinds
     )
+    near_sum = [low_sum(near_kept[:pair], near_got[0]), low_sum(near_kept[pair:], near_got[1])]
+    near_other = across_sums(near_sum)
     lows = col_gather(low)
-    near_sum = [low_sum(near_kept[:quarter], near_got[0])]
-    lows, near_sum = join(lows, near_sum)
-
-    y = row_scatter(y)
-    near_got.append(col_swap(near_sent[1], 2))
-    if groups == 2:
-        near_other = [across_groups(near_sum[0])]
-    far_sent = [low_sum(far2[:quarter], far3[:quarter]), low_sum(far2[quarter:], far3[quarter:])]
-    far_kept = low_sum(far0, far1)
+    lows, near_sum, near_other[0], far_next = join(lows, near_sum, near_other[0], far_next)
+
+    y = row_scatter(after(y, dx[1], dx[2], dx[3]))
+    far_kept, far_sent = low_sum(far_mine[0], far_next[0]), low_sum(far_mine[1], far_next[1])
+    far_got = [col_swap(far_sent[:pair], 2), col_swap(far_sent[pair:], 2)]
+    far_sum = [low_sum(far_kept[:pair], far_got[0]), low_sum(far_kept[pair:], far_got[1])]
+    far_other = across_sums(far_sum)
     tokens_parts, weight_parts, small = attend_back(
         place, toks, weight, cosine, sine,
         query, keys, values, attn, logsum, lows, grad_mid, small,
     )
-    y, near_got, far_sent, far_kept, tokens_parts, weight_parts, small = join(
-        y, near_got, far_sent, far_kept, tokens_parts, weight_parts, small
-    )
-    if groups == 2:
-        near_other, near_got = join(near_other, near_got)
+    tokens_parts, weight_parts, small, y, near_other, far_got[0] = join(
+        tokens_parts, weight_parts, small, y, near_other, far_got[0]
+    )
+    out = result(place, toks, mid, stats, routes_t, grad_logits, y)
+    tokens_parts, far_got[1] = join(tokens_parts, far_got[1])
 
     def col_scatter(value):
         total = value[0].astype(F32)
@@ -1000,30 +992,18 @@
             total = total + col_swap(value[k], k).astype(F32)
         return total
 
-    grad_tokens = col_scatter(tokens_parts)
+    small = row_total(col_scatter(small))
     total = collect(weight_parts[0], 0).astype(F32)
     for m in range(1, rows):
         total = total + collect(weight_parts[m], m).astype(F32)
-    small = col_scatter(small)
-    near_sum.append(low_sum(near_kept[quarter:], near_got[1]))
-    if groups == 2:
-        near_other.append(across_groups(near_sum[1]))
-    far_got = [col_swap(far_sent[0], 2)]
-    out = result(place, toks, mid, stats, routes_t, grad_logits, y)
-    grad_tokens, total, small, far_got, out = join(grad_tokens, total, small, far_got, out)
-
-    far_sum = [low_sum(far_kept[:quarter], far_got[0])]
-    far_got.append(col_swap(far_sent[1], 2))
-    far_sum.append(low_sum(far_kept[quarter:], far_got[1]))
-    total = dp_total(total.astype(BF16))
+    small, total = dp_total(small), dp_total(total.astype(BF16))
+    grad_tokens = col_scatter(tokens_parts)
     qkv_sum = jnp.stack([total[:, j * size : (j + 1) * size] for j in range(3)])
     proj_sum = total[:, 3 * size :].T
-    small = dp_total(row_total(small))
     out = jnp.stack([out[0]] + [col_swap(out[k], k) for k in range(1, cols)])
     out = jnp.take(out, col ^ jnp.arange(cols), axis=0)
     out = jnp.concatenate([out[i] for i in range(cols)], axis=1)
     if groups == 2:
-        far_other = [across_groups(s) for s in far_sum]
         near_start = first_half * half
         far_start = half - near_start
         grads = []
@@ -1036,7 +1016,7 @@
                     (far_start, far_sum[i], near_other[i]),
                 ):
                     both = mine[:, :, wide].astype(F32) + other[:, :, wide].astype(F32)
-                    grad = lax.dynamic_update_slice_in_dim(grad, both, start + i * quarter, 0)
+                    grad = lax.dynamic_update_slice_in_dim(grad, both, start + i * pair, 0)
             grads.append(grad)
     else:
         both = lax.psum(jnp.concatenate(near_sum + far_sum).astype(F32), "dp")

time: 607 us -> 539 us (0.89)
  starting transfers between devices: 151 us -> 88.1 us
  waiting for transfers between devices: 223 us -> 244 us
  local copies, waits for them, and re-layouts: 54.9 us -> 43.8 us
  other arithmetic: 51.3 us -> 41.7 us
    ppermute x42 -> x37, waiting for transfers between devices: 65.3 us -> 108 us  [col_swap(): return lax.ppermute(value, 'col', [(i, i ^ bits) for i in range(count)])]
    ppermute x4, starting transfers between devices: 36.6 us -> 4.78 us  [collect(): return lax.ppermute(value, ('row', 'col'), pairs)]
    ppermute x2, waiting for transfers between devices: 51.7 us -> 29.9 us  [dp_total(): other = lax.ppermute(value, 'dp', [(0, 1), (1, 0)])]
    ppermute x4, waiting for transfers between devices: 13 us -> 31 us  [collect(): return lax.ppermute(value, ('row', 'col'), pairs)]
    ppermute x12, waiting for transfers between devices: 46.4 us -> 30.3 us  [row_shift(): lax.ppermute(value, 'row', [(i, (i + steps) % count) for i in range(count)])]
    ppermute x12, starting transfers between devices: 40.3 us -> 27.9 us  [row_shift(): lax.ppermute(value, 'row', [(i, (i + steps) % count) for i in range(count)])]
    ppermute x42 -> x37, starting transfers between devices: 40.9 us -> 34.2 us  [col_swap(): return lax.ppermute(value, 'col', [(i, i ^ bits) for i in range(count)])]
    ppermute x4, starting transfers between devices: 18.7 us -> 12.5 us  [spread(): return lax.ppermute(value, ('row', 'col'), pairs)]
  transfers between devices with their start and end apart: 73 -> 67, of which waited for: 24 -> 29; matrix products, arithmetic and copies ran while one was open for 15% -> 13% of each run, Pallas kernels for 20% -> 21%
where the time goes in v3:
time: 539 us; the launch traced here: 532 us
  waiting for transfers between devices  244 us (45%)
  Pallas kernels  113 us (21%)
  starting transfers between devices  88.1 us (16%)
  local copies, waits for them, and re-layouts  43.8 us (8%)
  other arithmetic  41.7 us (8%)
    ppermute x37, waiting for transfers between devices, col_swap(): return lax.ppermute(value, 'col', [(i, i ^ bits) for i in range(count)])  108 us
    pallas_call x2, Pallas kernels, run_experts(): pl.pallas_call(body, name='experts', cost_estimate=span_of(36), grid_spec...  59.3 us
    ppermute x37, starting transfers between devices, col_swap(): return lax.ppermute(value, 'col', [(i, i ^ bits) for i in range(count)])  34.2 us
    ppermute x6, waiting for transfers between devices, across_groups(): return lax.ppermute(value, 'dp', [(0, 1), (1, 0)])  33.6 us
    ppermute x4, waiting for transfers between devices, collect(): return lax.ppermute(value, ('row', 'col'), pairs)  31 us
    ppermute x12, waiting for transfers between devices, row_shift(): lax.ppermute(value, 'row', [(i, (i + steps) % count) for i in range(count)])  30.3 us
    ppermute x2, waiting for transfers between devices, dp_total(): other = lax.ppermute(value, 'dp', [(0, 1), (1, 0)])  29.9 us
    ppermute x12, starting transfers between devices, row_shift(): lax.ppermute(value, 'row', [(i, (i + steps) % count) for i in range(count)])  27.9 us
  transfers between devices with their start and end apart: 67, of which 29 were waited for; matrix products, arithmetic and copies ran while one was open for 13% of the time, Pallas kernels for 21%

profile of v3, /device:TPU:0, one launch (start us, length us, event | category | flops | bytes accessed | tf_op | source)
XLA Modules:
  0.0 532.2 jit_solution(9755720197642118221)
XLA Ops:
  2.8 7.0 %collective-permute-start.6 = (bf16[192,768]{1,0:T(8,128)(2,1)S(1)}, bf16[192,768]{1,0:T(8,128)(2,1)S(1)}, u32[]{:S(2)}, u32[]{:S(2)}) collective-permute-start(bf16[192,768]{1,0:T(8,128)(2,1)S(1)} %pad_maximum_fusion.6), channel_id=1, source_target_pairs={{3,0},{6,1},{9,2},{12,3},{2,4},{7,5},{8,6},{13,7},{1,8},{4,9},{11,... | collective-permute-start | bytes 884744 | tf_op jit(solution)/shard_map/ppermute | solution.py:872
  9.8 2.3 collective-permute-start.5
  12.1 2.5 collective-permute-start.4
  15.3 4.0 pad_maximum_fusion.refs_11_
  19.3 4.2 collective-permute-done.5
  23.5 4.8 collective-permute-done.4
  28.5 1.5 collective-permute-start.17
  32.5 13.5 %collective-permute-start.1 = (bf16[192,1152]{1,0:T(8,128)(2,1)S(1)}, bf16[192,1152]{1,0:T(8,128)(2,1)}, u32[]{:S(2)}, u32[]{:S(2)}) collective-permute-start(bf16[192,1152]{1,0:T(8,128)(2,1)S(1)} %concatenate.21.t0.p0), channel_id=1, source_target_pairs={{0,2},{1,3},{2,0},{3,1},{4,6},{5,7},{6,4},{7,5},{8,10},{9,11},{10,... | collective-permute-start | bytes 1327112 | tf_op jit(solution)/shard_map/ppermute | solution.py:77
  47.3 2.3 reduce-window.6
  50.8 5.6 %collective-permute-done.1.t2.p2 = bf16[192,1152]{1,0:T(8,128)(2,1)} collective-permute-done((bf16[192,1152]{1,0:T(8,128)(2,1)S(1)}, bf16[192,1152]{1,0:T(8,128)(2,1)}, u32[]{:S(2)}, u32[]{:S(2)}) %collective-permute-start.1) | collective-permute-done | bytes 442400 | tf_op jit(solution)/shard_map/ppermute | solution.py:77
  62.9 2.0 collective-permute-done.8
  65.7 1.5 collective-permute-start.11
  70.2 1.8 constant_dynamic-slice_fusion.6
  72.0 1.7 collective-permute-start.12
  73.7 7.5 %collective-permute-done.15.o2 = bf16[4,192,192]{2,1,0:T(8,128)(2,1)} collective-permute-done((bf16[4,192,192]{2,1,0:T(8,128)(2,1)S(1)}, bf16[4,192,192]{2,1,0:T(8,128)(2,1)}, u32[]{:S(2)}, u32[]{:S(2)}) %collective-permute-start.15) | collective-permute-done | bytes 294944 | tf_op jit(solution)/shard_map/ppermute | solution.py:77
  81.2 2.4 collective-permute-start.13
  84.9 13.7 %attend.1 = (bf16[4,192,256]{2,1,0:T(8,128)(2,1)}, bf16[192,1024]{1,0:T(8,128)(2,1)}, bf16[192,1024]{1,0:T(8,128)(2,1)}, bf16[4,192,256]{2,1,0:T(8,128)(2,1)}, f32[8,1024]{1,0:T(8,128)}) custom-call(s32[4]{0:T(128)} %pad_add_fusion.place, bf16[192,1152]{1,0:T(8,128)(2,1)} %copy-done.11, bf16[192,1152]{1,0:T(8,128)(2,1)} %copy-done.33, ...), custom_call_target="tpu_custom_call" | custom-call | flops 15399999488 | bytes 50400000 | tf_op jit(solution)/shard_map/attend/pallas_call | solution.py:196
  98.6 1.5 collective-permute-done.13
  100.1 10.7 %collective-permute-done.10.refs_13_ = bf16[2,192,1536]{2,1,0:T(8,128)(2,1)} collective-permute-done((bf16[2,192,1536]{2,1,0:T(8,128)(2,1)S(1)}, bf16[2,192,1536]{2,1,0:T(8,128)(2,1)}, u32[]{:S(2)}, u32[]{:S(2)}) %collective-permute-start.10) | collective-permute-done | bytes 1179680 | tf_op jit(solution)/shard_map/ppermute | solution.py:77
  110.9 1.7 slice_bitcast_fusion.35
  114.5 1.6 collective-permute-start.24
  116.1 2.1 collective-permute-done.19.a2
  120.8 5.4 %middle.1 = (f32[768,256]{1,0:T(8,128)}, bf16[272,768]{1,0:T(8,128)(2,1)}, f32[8,256]{1,0:T(8,128)}) custom-call(s32[4]{0:T(128)} %pad_add_fusion.place, bf16[192,1152]{1,0:T(8,128)(2,1)} %copy-done.11, bf16[192,1152]{1,0:T(8,128)(2,1)} %copy-done.33, bf16[192,1152]{1,0:T(8,128)(2,1)} %collective-permute-done.1.t2.p2, bf16[192,1152]{1,0:T(8,128)(2,1)} %copy-done.34, ...), custom_call_target="tpu_custom_call" | custom-call | flops 6600000000 | bytes 21600000 | tf_op jit(solution)/shard_map/middle/pallas_call | solution.py:447
  126.7 16.4 %collective-permute-done.24.refs_13_ = bf16[2,192,1536]{2,1,0:T(8,128)(2,1)} collective-permute-done((bf16[2,192,1536]{2,1,0:T(8,128)(2,1)}, bf16[2,192,1536]{2,1,0:T(8,128)(2,1)}, u32[]{:S(2)}, u32[]{:S(2)}) %collective-permute-start.24) | collective-permute-done | bytes 1179680 | tf_op jit(solution)/shard_map/ppermute | solution.py:879
  143.1 5.0 collective-permute-done.26.refs_14_
  148.1 1.5 collective-permute-start.30
  151.2 19.5 %collective-permute-done.22.refs_3_ = bf16[272,768]{1,0:T(8,128)(2,1)S(1)} collective-permute-done((bf16[272,768]{1,0:T(8,128)(2,1)}, bf16[272,768]{1,0:T(8,128)(2,1)S(1)}, u32[]{:S(2)}, u32[]{:S(2)}) %collective-permute-start.22) | collective-permute-done | bytes 417824 | tf_op jit(solution)/shard_map/ppermute | solution.py:87
  177.0 5.6 %collective-permute-done.23.refs_4_ = bf16[272,768]{1,0:T(8,128)(2,1)S(1)} collective-permute-done((bf16[272,768]{1,0:T(8,128)(2,1)}, bf16[272,768]{1,0:T(8,128)(2,1)S(1)}, u32[]{:S(2)}, u32[]{:S(2)}) %collective-permute-start.23) | collective-permute-done | bytes 417824 | tf_op jit(solution)/shard_map/ppermute | solution.py:87
  183.3 31.5 %experts.2 = (f32[1024,768]{1,0:T(8,128)}, f32[1024,768]{1,0:T(8,128)}, f32[8,1024]{1,0:T(8,128)}, bf16[2,4,192,1536]{3,2,1,0:T(8,128)(2,1)}, bf16[2,4,192,1536]{3,2,1,0:T(8,128)(2,1)}) custom-call(s32[8]{0:T(128)} %pad_add_fusion.1.refs_0_, bf16[272,768]{1,0:T(8,128)(2,1)} %get-tuple-element.101.refs_1_, bf16[272,768]{1,0:T(8,128)(2,1)} %copy-done.35, ...), custom_call_target="tpu_custom_call" | custom-call | flops 39600001024 | bytes 129600000 | tf_op jit(solution)/shard_map/experts/pallas_call | solution.py:813
  217.0 27.8 %experts.3 = (bf16[4,256,768]{2,1,0:T(8,128)(2,1)}, bf16[4,272,768]{2,1,0:T(8,128)(2,1)}, bf16[2,4,192,1536]{3,2,1,0:T(8,128)(2,1)}, bf16[2,4,192,1536]{3,2,1,0:T(8,128)(2,1)}) custom-call(s32[8]{0:T(128)} %pad_add_fusion.2.refs_0_, bf16[272,768]{1,0:T(8,128)(2,1)} %get-tuple-element.101.refs_1_, bf16[272,768]{1,0:T(8,128)(2,1)} %copy-done.35, ...), custom_call_target="tpu_custom_call" | custom-call | flops 39600001024 | bytes 129600000 | tf_op jit(solution)/shard_map/experts/pallas_call | solution.py:813
  244.8 2.2 slice_bitcast_fusion.9
  247.1 14.2 %collective-permute-start.32 = (bf16[272,768]{1,0:T(8,128)(2,1)S(1)}, bf16[272,768]{1,0:T(8,128)(2,1)S(1)}, u32[]{:S(2)}, u32[]{:S(2)}) collective-permute-start(bf16[272,768]{1,0:T(8,128)(2,1)S(1)} %get-tuple-element.223), channel_id=1, source_target_pairs={{0,12},{4,0},{8,4},{12,8},{1,13},{5,1},{9,5},{13,9},{2,14},{6,2},{... | collective-permute-start | bytes 1253384 | tf_op jit(solution)/shard_map/ppermute | solution.py:87
  261.3 4.4 add_convert_fusion.3
  266.8 3.7 collective-permute-done.32.x1
  272.6 3.5 collective-permute-start.34
  276.1 18.6 %collective-permute-done.38 = bf16[2,192,1536]{2,1,0:T(8,128)(2,1)S(1)} collective-permute-done((bf16[2,192,1536]{2,1,0:T(8,128)(2,1)S(1)}, bf16[2,192,1536]{2,1,0:T(8,128)(2,1)S(1)}, u32[]{:S(2)}, u32[]{:S(2)}) %collective-permute-start.38) | collective-permute-done | bytes 1179680 | tf_op jit(solution)/shard_map/ppermute | solution.py:77
  294.7 24.8 %collective-permute-done.39 = bf16[2,192,1536]{2,1,0:T(8,128)(2,1)S(1)} collective-permute-done((bf16[2,192,1536]{2,1,0:T(8,128)(2,1)S(1)}, bf16[2,192,1536]{2,1,0:T(8,128)(2,1)S(1)}, u32[]{:S(2)}, u32[]{:S(2)}) %collective-permute-start.39) | collective-permute-done | bytes 1179680 | tf_op jit(solution)/shard_map/ppermute | solution.py:77
  322.5 6.6 %middle_back.1 = (bf16[768,256]{1,0:T(8,128)(2,1)}, f32[768,256]{1,0:T(8,128)}, f32[12,256]{1,0:T(8,128)}, f32[4,24,192]{2,1,0:T(8,128)}) custom-call(s32[4]{0:T(128)} %pad_add_fusion.place, bf16[192,1152]{1,0:T(8,128)(2,1)} %copy-done.11, bf16[192,1152]{1,0:T(8,128)(2,1)} %copy-done.33, bf16[192,1152]{1,0:T(8,128)(2,1)} %collective-permute-done.1.t2.p2, ...), custom_call_target="tpu_custom_call" | custom-call | flops 7699999744 | bytes 25200000 | tf_op jit(solution)/shard_map/middle_back/pallas_call | solution.py:568
  330.3 9.6 %collective-permute-done.36.d2 = bf16[768,256]{1,0:T(8,128)(2,1)} collective-permute-done((bf16[768,256]{1,0:T(8,128)(2,1)}, bf16[768,256]{1,0:T(8,128)(2,1)}, u32[]{:S(2)}, u32[]{:S(2)}) %collective-permute-start.36) | collective-permute-done | bytes 393248 | tf_op jit(solution)/shard_map/ppermute | solution.py:77
  339.9 2.4 slice_bitcast_fusion.16
  344.3 3.4 collective-permute-done.40
  348.8 4.4 add_convert_fusion
  353.2 1.6 slice_bitcast_fusion.2
  357.5 23.3 %attend_back.1 = (bf16[4,192,1024]{2,1,0:T(8,128)(2,1)}, bf16[4,192,768]{2,1,0:T(8,128)(2,1)}, f32[4,24,192]{2,1,0:T(8,128)}) custom-call(s32[4]{0:T(128)} %pad_add_fusion.place, bf16[192,1152]{1,0:T(8,128)(2,1)} %copy-done.11, bf16[192,1152]{1,0:T(8,128)(2,1)} %copy-done.33, bf16[192,1152]{1,0:T(8,128)(2,1)} %collective-permute-done.1.t2.p2, ...), custom_call_target="tpu_custom_call" | custom-call | flops 26400000000 | bytes 86400000 | tf_op jit(solution)/shard_map/attend_back/pallas_call | solution.py:345
  380.8 3.0 collective-permute-done.46
  386.5 4.4 result.1
  390.9 1.4 fusion.32
  392.9 16.2 %collective-permute-done.50 = bf16[2,192,1536]{2,1,0:T(8,128)(2,1)} collective-permute-done((bf16[2,192,1536]{2,1,0:T(8,128)(2,1)}, bf16[2,192,1536]{2,1,0:T(8,128)(2,1)}, u32[]{:S(2)}, u32[]{:S(2)}) %collective-permute-start.50) | collective-permute-done | bytes 1179680 | tf_op jit(solution)/shard_map/ppermute | solution.py:77
  413.1 1.6 collective-permute-done.57
  414.7 3.7 fusion
  421.3 1.9 collective-permute-done.59
  426.7 2.1 collective-permute-start.61
  428.8 1.6 collective-permute-start.60
  431.5 3.8 collective-permute-done.63
  435.3 2.6 collective-permute-start.52
  437.9 27.2 %collective-permute-done.62 = bf16[192,768]{1,0:T(8,128)(2,1)} collective-permute-done((bf16[192,768]{1,0:T(8,128)(2,1)}, bf16[192,768]{1,0:T(8,128)(2,1)}, u32[]{:S(2)}, u32[]{:S(2)}) %collective-permute-start.62) | collective-permute-done | bytes 294944 | tf_op jit(solution)/shard_map/ppermute | solution.py:876
  471.2 2.2 fusion.6
  473.4 28.0 %collective-permute-done.64 = bf16[192,768]{1,0:T(8,128)(2,1)S(1)} collective-permute-done((bf16[192,768]{1,0:T(8,128)(2,1)S(1)}, bf16[192,768]{1,0:T(8,128)(2,1)S(1)}, u32[]{:S(2)}, u32[]{:S(2)}) %collective-permute-start.64) | collective-permute-done | bytes 294944 | tf_op jit(solution)/shard_map/ppermute | solution.py:108
  502.4 1.7 copy.99
  504.1 2.1 pad_maximum_fusion.4
  510.8 1.7 add_dynamic-update-slice_fusion.2
  512.5 13.7 %collective-permute-done.66 = bf16[2,192,1536]{2,1,0:T(8,128)(2,1)S(1)} collective-permute-done((bf16[2,192,1536]{2,1,0:T(8,128)(2,1)S(1)}, bf16[2,192,1536]{2,1,0:T(8,128)(2,1)S(1)}, u32[]{:S(2)}, u32[]{:S(2)}) %collective-permute-start.66) | collective-permute-done | bytes 1179680 | tf_op jit(solution)/shard_map/ppermute | solution.py:879
  526.6 1.6 add_dynamic-update-slice_fusion
  528.3 1.6 copy-done.3
  (289 shorter events, 76.8 us)
Async XLA Ops:
  2.8 16.5 %collective-permute-start.6 = (bf16[192,768]{1,0:T(8,128)(2,1)S(1)}, bf16[192,768]{1,0:T(8,128)(2,1)S(1)}, u32[]{:S(2)}, u32[]{:S(2)}) collective-permute-start(bf16[192,768]{1,0:T(8,128)(2,1)S(1)} %pad_maximum_fusion.6), channel_id=1, source_target_pairs={{3,0},{6,1},{9,2},{12,3},{2,4},{7,5},{8,6},{13,7},{1,8},{4,9},{11,... | collective-permute-start | bytes 884744 | tf_op jit(solution)/shard_map/ppermute | solution.py:872
  9.8 13.7 %collective-permute-start.5 = (bf16[192,768]{1,0:T(8,128)(2,1)S(1)}, bf16[192,768]{1,0:T(8,128)(2,1)S(1)}, u32[]{:S(2)}, u32[]{:S(2)}) collective-permute-start(bf16[192,768]{1,0:T(8,128)(2,1)S(1)} %pad_maximum_fusion.6), channel_id=1, source_target_pairs={{2,0},{7,1},{8,2},{13,3},{3,4},{6,5},{9,6},{12,7},{0,8},{5,9},{10,... | collective-permute-start | bytes 884744 | tf_op jit(solution)/shard_map/ppermute | solution.py:872
  12.1 16.2 %collective-permute-start.4 = (bf16[192,768]{1,0:T(8,128)(2,1)S(1)}, bf16[192,768]{1,0:T(8,128)(2,1)S(1)}, u32[]{:S(2)}, u32[]{:S(2)}) collective-permute-start(bf16[192,768]{1,0:T(8,128)(2,1)S(1)} %pad_maximum_fusion.6), channel_id=1, source_target_pairs={{1,0},{4,1},{11,2},{14,3},{0,4},{5,5},{10,6},{15,7},{3,8},{6,9},{9... | collective-permute-start | bytes 884744 | tf_op jit(solution)/shard_map/ppermute | solution.py:872
  14.6 13.7 %collective-permute-start.3 = (bf16[192,768]{1,0:T(8,128)(2,1)S(1)}, bf16[192,768]{1,0:T(8,128)(2,1)S(1)}, u32[]{:S(2)}, u32[]{:S(2)}) collective-permute-start(bf16[192,768]{1,0:T(8,128)(2,1)S(1)} %pad_maximum_fusion.6), channel_id=1, source_target_pairs={{0,0},{5,1},{10,2},{15,3},{1,4},{4,5},{11,6},{14,7},{2,8},{7,9},{8... | collective-permute-start | bytes 884744 | tf_op jit(solution)/shard_map/ppermute | solution.py:872
  28.5 82.4 %collective-permute-start.17 = (bf16[8,192,1536]{2,1,0:T(8,128)(2,1)}, bf16[8,192,1536]{2,1,0:T(8,128)(2,1)}, u32[]{:S(2)}, u32[]{:S(2)}) collective-permute-start(bf16[8,192,1536]{2,1,0:T(8,128)(2,1)} %pad_maximum_fusion.refs_11_), channel_id=1, source_target_pairs={{0,1},{1,0},{2,3},{3,2},{4,5},{5,4},{6,7},{7,6},{8,9},{9,8},{10,11... | collective-permute-start | bytes 14155784 | tf_op jit(solution)/shard_map/ppermute | solution.py:77
  32.4 36.4 %collective-permute-start = (bf16[192,1152]{1,0:T(8,128)(2,1)S(1)}, bf16[192,1152]{1,0:T(8,128)(2,1)S(1)}, u32[]{:S(2)}, u32[]{:S(2)}) collective-permute-start(bf16[192,1152]{1,0:T(8,128)(2,1)S(1)} %concatenate.21.t0.p0), channel_id=1, source_target_pairs={{0,1},{1,0},{2,3},{3,2},{4,5},{5,4},{6,7},{7,6},{8,9},{9,8},{10,11... | collective-permute-start | bytes 1327112 | tf_op jit(solution)/shard_map/ppermute | solution.py:77
  32.5 24.0 %collective-permute-start.1 = (bf16[192,1152]{1,0:T(8,128)(2,1)S(1)}, bf16[192,1152]{1,0:T(8,128)(2,1)}, u32[]{:S(2)}, u32[]{:S(2)}) collective-permute-start(bf16[192,1152]{1,0:T(8,128)(2,1)S(1)} %concatenate.21.t0.p0), channel_id=1, source_target_pairs={{0,2},{1,3},{2,0},{3,1},{4,6},{5,7},{6,4},{7,5},{8,10},{9,11},{10,... | collective-permute-start | bytes 1327112 | tf_op jit(solution)/shard_map/ppermute | solution.py:77
  57.6 4.9 collective-permute-start.9
  58.2 6.6 %collective-permute-start.8 = (bf16[192,256]{1,0:T(8,128)(2,1)S(1)}, bf16[192,256]{1,0:T(8,128)(2,1)S(1)}, u32[]{:S(2)}, u32[]{:S(2)}) collective-permute-start(bf16[192,256]{1,0:T(8,128)(2,1)S(1)} %bitcast.201), channel_id=1, source_target_pairs={{0,2},{1,3},{2,0},{3,1},{4,6},{5,7},{6,4},{7,5},{8,10},{9,11},{10,... | collective-permute-start | bytes 294920 | tf_op jit(solution)/shard_map/ppermute | solution.py:77
  59.5 5.3 %collective-permute-start.7 = (bf16[192,256]{1,0:T(8,128)(2,1)S(1)}, bf16[192,256]{1,0:T(8,128)(2,1)S(1)}, u32[]{:S(2)}, u32[]{:S(2)}) collective-permute-start(bf16[192,256]{1,0:T(8,128)(2,1)S(1)} %bitcast.203), channel_id=1, source_target_pairs={{0,1},{1,0},{2,3},{3,2},{4,5},{5,4},{6,7},{7,6},{8,9},{9,8},{10,11... | collective-permute-start | bytes 294920 | tf_op jit(solution)/shard_map/ppermute | solution.py:77
  62.5 21.1 %collective-permute-start.2 = (bf16[192,1152]{1,0:T(8,128)(2,1)}, bf16[192,1152]{1,0:T(8,128)(2,1)S(1)}, u32[]{:S(2)}, u32[]{:S(2)}) collective-permute-start(bf16[192,1152]{1,0:T(8,128)(2,1)} %collective-permute-done.1.t2.p2), channel_id=1, source_target_pairs={{0,1},{1,0},{2,3},{3,2},{4,5},{5,4},{6,7},{7,6},{8,9},{9,8},{10,11... | collective-permute-start | bytes 1327112 | tf_op jit(solution)/shard_map/ppermute | solution.py:77
  65.7 18.4 %collective-permute-start.11 = (bf16[256,768]{0,1:T(8,128)(2,1)S(1)}, bf16[256,768]{0,1:T(8,128)(2,1)S(1)}, u32[]{:S(2)}, u32[]{:S(2)}) collective-permute-start(bf16[256,768]{0,1:T(8,128)(2,1)S(1)} %get-tuple-element.105), channel_id=1, source_target_pairs={{0,4},{4,8},{8,12},{12,0},{1,5},{5,9},{9,13},{13,1},{2,6},{6,10},{... | collective-permute-start | bytes 1179656 | tf_op jit(solution)/shard_map/ppermute | solution.py:87
  69.6 11.6 %collective-permute-start.15 = (bf16[4,192,192]{2,1,0:T(8,128)(2,1)S(1)}, bf16[4,192,192]{2,1,0:T(8,128)(2,1)}, u32[]{:S(2)}, u32[]{:S(2)}) collective-permute-start(bf16[4,192,192]{2,1,0:T(8,128)(2,1)S(1)} %slice.428.o0), channel_id=1, source_target_pairs={{0,2},{1,3},{2,0},{3,1},{4,6},{5,7},{6,4},{7,5},{8,10},{9,11},{10,... | collective-permute-start | bytes 884744 | tf_op jit(solution)/shard_map/ppermute | solution.py:77
  72.0 26.6 %collective-permute-start.12 = (bf16[256,768]{0,1:T(8,128)(2,1)S(1)}, bf16[256,768]{0,1:T(8,128)(2,1)S(1)}, u32[]{:S(2)}, u32[]{:S(2)}) collective-permute-start(bf16[256,768]{0,1:T(8,128)(2,1)S(1)} %get-tuple-element.105), channel_id=1, source_target_pairs={{0,8},{4,12},{8,0},{12,4},{1,9},{5,13},{9,1},{13,5},{2,10},{6,14},... | collective-permute-start | bytes 1179656 | tf_op jit(solution)/shard_map/ppermute | solution.py:87
  81.2 19.0 %collective-permute-start.13 = (bf16[256,768]{0,1:T(8,128)(2,1)S(1)}, bf16[256,768]{0,1:T(8,128)(2,1)S(1)}, u32[]{:S(2)}, u32[]{:S(2)}) collective-permute-start(bf16[256,768]{0,1:T(8,128)(2,1)S(1)} %get-tuple-element.105), channel_id=1, source_target_pairs={{0,12},{4,0},{8,4},{12,8},{1,13},{5,1},{9,5},{13,9},{2,14},{6,2},{... | collective-permute-start | bytes 1179656 | tf_op jit(solution)/shard_map/ppermute | solution.py:87
  83.6 27.3 %collective-permute-start.10 = (bf16[2,192,1536]{2,1,0:T(8,128)(2,1)S(1)}, bf16[2,192,1536]{2,1,0:T(8,128)(2,1)}, u32[]{:S(2)}, u32[]{:S(2)}) collective-permute-start(bf16[2,192,1536]{2,1,0:T(8,128)(2,1)S(1)} %get-tuple-element.88), channel_id=1, source_target_pairs={{0,2},{1,3},{2,0},{3,1},{4,6},{5,7},{6,4},{7,5},{8,10},{9,11},{10,... | collective-permute-start | bytes 3538952 | tf_op jit(solution)/shard_map/ppermute | solution.py:77
  84.8 15.3 %collective-permute-start.16 = (bf16[4,192,192]{2,1,0:T(8,128)(2,1)}, bf16[4,192,192]{2,1,0:T(8,128)(2,1)}, u32[]{:S(2)}, u32[]{:S(2)}) collective-permute-start(bf16[4,192,192]{2,1,0:T(8,128)(2,1)} %collective-permute-done.15.o2), channel_id=1, source_target_pairs={{0,1},{1,0},{2,3},{3,2},{4,5},{5,4},{6,7},{7,6},{8,9},{9,8},{10,11... | collective-permute-start | bytes 884744 | tf_op jit(solution)/shard_map/ppermute | solution.py:77
  112.6 5.7 %collective-permute-start.19 = (bf16[192,256]{1,0:T(8,128)(2,1)S(1)}, bf16[192,256]{1,0:T(8,128)(2,1)S(1)}, u32[]{:S(2)}, u32[]{:S(2)}) collective-permute-start(bf16[192,256]{1,0:T(8,128)(2,1)S(1)} %get-tuple-element.249), channel_id=1, source_target_pairs={{0,2},{1,3},{2,0},{3,1},{4,6},{5,7},{6,4},{7,5},{8,10},{9,11},{10,... | collective-permute-start | bytes 294920 | tf_op jit(solution)/shard_map/ppermute | solution.py:77
  113.0 6.4 %collective-permute-start.20 = (bf16[192,256]{1,0:T(8,128)(2,1)S(1)}, bf16[192,256]{1,0:T(8,128)(2,1)S(1)}, u32[]{:S(2)}, u32[]{:S(2)}) collective-permute-start(bf16[192,256]{1,0:T(8,128)(2,1)S(1)} %get-tuple-element.248), channel_id=1, source_target_pairs={{0,3},{1,2},{2,1},{3,0},{4,7},{5,6},{6,5},{7,4},{8,11},{9,10},{10,... | collective-permute-start | bytes 294920 | tf_op jit(solution)/shard_map/ppermute | solution.py:77
  114.5 28.5 %collective-permute-start.24 = (bf16[2,192,1536]{2,1,0:T(8,128)(2,1)}, bf16[2,192,1536]{2,1,0:T(8,128)(2,1)}, u32[]{:S(2)}, u32[]{:S(2)}) collective-permute-start(bf16[2,192,1536]{2,1,0:T(8,128)(2,1)} %collective-permute-done.10.refs_13_), channel_id=1, source_target_pairs={{0,16},{16,0},{1,17},{17,1},{2,18},{18,2},{3,19},{19,3},{4,20},{20... | collective-permute-start | bytes 3538952 | tf_op jit(solution)/shard_map/ppermute | solution.py:879
  119.4 28.7 %collective-permute-start.26 = (bf16[2,192,1536]{2,1,0:T(8,128)(2,1)S(1)}, bf16[2,192,1536]{2,1,0:T(8,128)(2,1)}, u32[]{:S(2)}, u32[]{:S(2)}) collective-permute-start(bf16[2,192,1536]{2,1,0:T(8,128)(2,1)S(1)} %get-tuple-element.110), channel_id=1, source_target_pairs={{0,2},{1,3},{2,0},{3,1},{4,6},{5,7},{6,4},{7,5},{8,10},{9,11},{10,... | collective-permute-start | bytes 3538952 | tf_op jit(solution)/shard_map/ppermute | solution.py:77
  126.2 23.6 %collective-permute-start.21 = (bf16[272,768]{1,0:T(8,128)(2,1)}, bf16[272,768]{1,0:T(8,128)(2,1)S(1)}, u32[]{:S(2)}, u32[]{:S(2)}) collective-permute-start(bf16[272,768]{1,0:T(8,128)(2,1)} %get-tuple-element.101.refs_1_), channel_id=1, source_target_pairs={{0,4},{4,8},{8,12},{12,0},{1,5},{5,9},{9,13},{13,1},{2,6},{6,10},{... | collective-permute-start | bytes 1253384 | tf_op jit(solution)/shard_map/ppermute | solution.py:87
  126.2 57.1 %collective-permute-start.27 = (bf16[2,192,1536]{2,1,0:T(8,128)(2,1)}, bf16[2,192,1536]{2,1,0:T(8,128)(2,1)}, u32[]{:S(2)}, u32[]{:S(2)}) collective-permute-start(bf16[2,192,1536]{2,1,0:T(8,128)(2,1)} %collective-permute-done.10.refs_13_), channel_id=1, source_target_pairs={{0,1},{1,0},{2,3},{3,2},{4,5},{5,4},{6,7},{7,6},{8,9},{9,8},{10,11... | collective-permute-start | bytes 3538952 | tf_op jit(solution)/shard_map/ppermute | solution.py:77
  143.1 39.5 %collective-permute-start.25 = (bf16[2,192,1536]{2,1,0:T(8,128)(2,1)}, bf16[2,192,1536]{2,1,0:T(8,128)(2,1)}, u32[]{:S(2)}, u32[]{:S(2)}) collective-permute-start(bf16[2,192,1536]{2,1,0:T(8,128)(2,1)} %collective-permute-done.24.refs_13_), channel_id=1, source_target_pairs={{0,1},{1,0},{2,3},{3,2},{4,5},{5,4},{6,7},{7,6},{8,9},{9,8},{10,11... | collective-permute-start | bytes 3538952 | tf_op jit(solution)/shard_map/ppermute | solution.py:77
  148.1 35.2 %collective-permute-start.28 = (bf16[2,192,1536]{2,1,0:T(8,128)(2,1)}, bf16[2,192,1536]{2,1,0:T(8,128)(2,1)}, u32[]{:S(2)}, u32[]{:S(2)}) collective-permute-start(bf16[2,192,1536]{2,1,0:T(8,128)(2,1)} %collective-permute-done.26.refs_14_), channel_id=1, source_target_pairs={{0,1},{1,0},{2,3},{3,2},{4,5},{5,4},{6,7},{7,6},{8,9},{9,8},{10,11... | collective-permute-start | bytes 3538952 | tf_op jit(solution)/shard_map/ppermute | solution.py:77
  148.1 35.2 %collective-permute-start.30 = (bf16[2,192,1536]{2,1,0:T(8,128)(2,1)}, bf16[2,192,1536]{2,1,0:T(8,128)(2,1)S(1)}, u32[]{:S(2)}, u32[]{:S(2)}) collective-permute-start(bf16[2,192,1536]{2,1,0:T(8,128)(2,1)} %collective-permute-done.26.refs_14_), channel_id=1, source_target_pairs={{0,16},{16,0},{1,17},{17,1},{2,18},{18,2},{3,19},{19,3},{4,20},{20... | collective-permute-start | bytes 3538952 | tf_op jit(solution)/shard_map/ppermute | solution.py:879
  149.8 20.9 %collective-permute-start.22 = (bf16[272,768]{1,0:T(8,128)(2,1)}, bf16[272,768]{1,0:T(8,128)(2,1)S(1)}, u32[]{:S(2)}, u32[]{:S(2)}) collective-permute-start(bf16[272,768]{1,0:T(8,128)(2,1)} %get-tuple-element.101.refs_1_), channel_id=1, source_target_pairs={{0,8},{4,12},{8,0},{12,4},{1,9},{5,13},{9,1},{13,5},{2,10},{6,14},... | collective-permute-start | bytes 1253384 | tf_op jit(solution)/shard_map/ppermute | solution.py:87
  170.7 11.8 %collective-permute-start.23 = (bf16[272,768]{1,0:T(8,128)(2,1)}, bf16[272,768]{1,0:T(8,128)(2,1)S(1)}, u32[]{:S(2)}, u32[]{:S(2)}) collective-permute-start(bf16[272,768]{1,0:T(8,128)(2,1)} %get-tuple-element.101.refs_1_), channel_id=1, source_target_pairs={{0,12},{4,0},{8,4},{12,8},{1,13},{5,1},{9,5},{13,9},{2,14},{6,2},{... | collective-permute-start | bytes 1253384 | tf_op jit(solution)/shard_map/ppermute | solution.py:87
  183.3 32.7 %collective-permute-start.31 = (bf16[2,192,1536]{2,1,0:T(8,128)(2,1)S(1)}, bf16[2,192,1536]{2,1,0:T(8,128)(2,1)S(1)}, u32[]{:S(2)}, u32[]{:S(2)}) collective-permute-start(bf16[2,192,1536]{2,1,0:T(8,128)(2,1)S(1)} %collective-permute-done.30.refs_14_), channel_id=1, source_target_pairs={{0,1},{1,0},{2,3},{3,2},{4,5},{5,4},{6,7},{7,6},{8,9},{9,8},{10,11... | collective-permute-start | bytes 3538952 | tf_op jit(solution)/shard_map/ppermute | solution.py:77
  214.9 30.0 %collective-permute-start.29 = (bf16[2,4,192,1536]{3,2,1,0:T(8,128)(2,1)}, bf16[2,4,192,1536]{3,2,1,0:T(8,128)(2,1)}, u32[]{:S(2)}, u32[]{:S(2)}) collective-permute-start(bf16[2,4,192,1536]{3,2,1,0:T(8,128)(2,1)} %get-tuple-element.113), channel_id=1, source_target_pairs={{0,1},{1,0},{2,3},{3,2},{4,5},{5,4},{6,7},{7,6},{8,9},{9,8},{10,11... | collective-permute-start | bytes 14155784 | tf_op jit(solution)/shard_map/ppermute | solution.py:77
  247.1 23.4 %collective-permute-start.32 = (bf16[272,768]{1,0:T(8,128)(2,1)S(1)}, bf16[272,768]{1,0:T(8,128)(2,1)S(1)}, u32[]{:S(2)}, u32[]{:S(2)}) collective-permute-start(bf16[272,768]{1,0:T(8,128)(2,1)S(1)} %get-tuple-element.223), channel_id=1, source_target_pairs={{0,12},{4,0},{8,4},{12,8},{1,13},{5,1},{9,5},{13,9},{2,14},{6,2},{... | collective-permute-start | bytes 1253384 | tf_op jit(solution)/shard_map/ppermute | solution.py:87
  261.3 87.5 %collective-permute-start.41 = (bf16[2,4,192,1536]{3,2,1,0:T(8,128)(2,1)}, bf16[2,4,192,1536]{3,2,1,0:T(8,128)(2,1)}, u32[]{:S(2)}, u32[]{:S(2)}) collective-permute-start(bf16[2,4,192,1536]{3,2,1,0:T(8,128)(2,1)} %get-tuple-element.132), channel_id=1, source_target_pairs={{0,1},{1,0},{2,3},{3,2},{4,5},{5,4},{6,7},{7,6},{8,9},{9,8},{10,11... | collective-permute-start | bytes 14155784 | tf_op jit(solution)/shard_map/ppermute | solution.py:77
  265.8 28.9 %collective-permute-start.38 = (bf16[2,192,1536]{2,1,0:T(8,128)(2,1)S(1)}, bf16[2,192,1536]{2,1,0:T(8,128)(2,1)S(1)}, u32[]{:S(2)}, u32[]{:S(2)}) collective-permute-start(bf16[2,192,1536]{2,1,0:T(8,128)(2,1)S(1)} %get-tuple-element.220), channel_id=1, source_target_pairs={{0,2},{1,3},{2,0},{3,1},{4,6},{5,7},{6,4},{7,5},{8,10},{9,11},{10,... | collective-permute-start | bytes 3538952 | tf_op jit(solution)/shard_map/ppermute | solution.py:77
  270.5 49.1 %collective-permute-start.39 = (bf16[2,192,1536]{2,1,0:T(8,128)(2,1)S(1)}, bf16[2,192,1536]{2,1,0:T(8,128)(2,1)S(1)}, u32[]{:S(2)}, u32[]{:S(2)}) collective-permute-start(bf16[2,192,1536]{2,1,0:T(8,128)(2,1)S(1)} %get-tuple-element.131), channel_id=1, source_target_pairs={{0,2},{1,3},{2,0},{3,1},{4,6},{5,7},{6,4},{7,5},{8,10},{9,11},{10,... | collective-permute-start | bytes 3538952 | tf_op jit(solution)/shard_map/ppermute | solution.py:77
  271.3 49.7 %collective-permute-start.33 = (bf16[272,768]{1,0:T(8,128)(2,1)S(1)}, bf16[272,768]{1,0:T(8,128)(2,1)S(1)}, u32[]{:S(2)}, u32[]{:S(2)}) collective-permute-start(bf16[272,768]{1,0:T(8,128)(2,1)S(1)} %get-tuple-element.222), channel_id=1, source_target_pairs={{0,8},{4,12},{8,0},{12,4},{1,9},{5,13},{9,1},{13,5},{2,10},{6,14},... | collective-permute-start | bytes 1253384 | tf_op jit(solution)/shard_map/ppermute | solution.py:87
  272.6 48.4 %collective-permute-start.34 = (bf16[272,768]{1,0:T(8,128)(2,1)S(1)}, bf16[272,768]{1,0:T(8,128)(2,1)S(1)}, u32[]{:S(2)}, u32[]{:S(2)}) collective-permute-start(bf16[272,768]{1,0:T(8,128)(2,1)S(1)} %get-tuple-element.221), channel_id=1, source_target_pairs={{0,4},{4,8},{8,12},{12,0},{1,5},{5,9},{9,13},{13,1},{2,6},{6,10},{... | collective-permute-start | bytes 1253384 | tf_op jit(solution)/shard_map/ppermute | solution.py:87
  320.2 27.6 %collective-permute-start.40 = (bf16[2,192,1536]{2,1,0:T(8,128)(2,1)S(1)}, bf16[2,192,1536]{2,1,0:T(8,128)(2,1)S(1)}, u32[]{:S(2)}, u32[]{:S(2)}) collective-permute-start(bf16[2,192,1536]{2,1,0:T(8,128)(2,1)S(1)} %get-tuple-element.155), channel_id=1, source_target_pairs={{0,16},{16,0},{1,17},{17,1},{2,18},{18,2},{3,19},{19,3},{4,20},{20... | collective-permute-start | bytes 3538952 | tf_op jit(solution)/shard_map/ppermute | solution.py:879
  329.1 10.8 %collective-permute-start.36 = (bf16[768,256]{1,0:T(8,128)(2,1)}, bf16[768,256]{1,0:T(8,128)(2,1)}, u32[]{:S(2)}, u32[]{:S(2)}) collective-permute-start(bf16[768,256]{1,0:T(8,128)(2,1)} %get-tuple-element.133.d0), channel_id=1, source_target_pairs={{0,2},{1,3},{2,0},{3,1},{4,6},{5,7},{6,4},{7,5},{8,10},{9,11},{10,... | collective-permute-start | bytes 1179656 | tf_op jit(solution)/shard_map/ppermute | solution.py:77
  330.3 12.0 %collective-permute-start.35 = (bf16[768,256]{1,0:T(8,128)(2,1)}, bf16[768,256]{1,0:T(8,128)(2,1)}, u32[]{:S(2)}, u32[]{:S(2)}) collective-permute-start(bf16[768,256]{1,0:T(8,128)(2,1)} %get-tuple-element.133.d0), channel_id=1, source_target_pairs={{0,1},{1,0},{2,3},{3,2},{4,5},{5,4},{6,7},{7,6},{8,9},{9,8},{10,11... | collective-permute-start | bytes 1179656 | tf_op jit(solution)/shard_map/ppermute | solution.py:77
  342.2 13.3 %collective-permute-start.42 = (bf16[256,768]{1,0:T(8,128)(2,1)S(1)}, bf16[256,768]{1,0:T(8,128)(2,1)S(1)}, u32[]{:S(2)}, u32[]{:S(2)}) collective-permute-start(bf16[256,768]{1,0:T(8,128)(2,1)S(1)} %get-tuple-element.230), channel_id=1, source_target_pairs={{0,12},{4,0},{8,4},{12,8},{1,13},{5,1},{9,5},{13,9},{2,14},{6,2},{... | collective-permute-start | bytes 1179656 | tf_op jit(solution)/shard_map/ppermute | solution.py:87
  342.3 38.5 %collective-permute-start.43 = (bf16[256,768]{1,0:T(8,128)(2,1)}, bf16[256,768]{1,0:T(8,128)(2,1)}, u32[]{:S(2)}, u32[]{:S(2)}) collective-permute-start(bf16[256,768]{1,0:T(8,128)(2,1)} %get-tuple-element.229), channel_id=1, source_target_pairs={{0,8},{4,12},{8,0},{12,4},{1,9},{5,13},{9,1},{13,5},{2,10},{6,14},... | collective-permute-start | bytes 1179656 | tf_op jit(solution)/shard_map/ppermute | solution.py:87
  343.2 37.6 %collective-permute-start.44 = (bf16[256,768]{1,0:T(8,128)(2,1)S(1)}, bf16[256,768]{1,0:T(8,128)(2,1)}, u32[]{:S(2)}, u32[]{:S(2)}) collective-permute-start(bf16[256,768]{1,0:T(8,128)(2,1)S(1)} %get-tuple-element.228), channel_id=1, source_target_pairs={{0,4},{4,8},{8,12},{12,0},{1,5},{5,9},{9,13},{13,1},{2,6},{6,10},{... | collective-permute-start | bytes 1179656 | tf_op jit(solution)/shard_map/ppermute | solution.py:87
  347.8 33.1 %collective-permute-start.45 = (bf16[2,192,1536]{2,1,0:T(8,128)(2,1)S(1)}, bf16[2,192,1536]{2,1,0:T(8,128)(2,1)}, u32[]{:S(2)}, u32[]{:S(2)}) collective-permute-start(bf16[2,192,1536]{2,1,0:T(8,128)(2,1)S(1)} %get-tuple-element.157), channel_id=1, source_target_pairs={{0,16},{16,0},{1,17},{17,1},{2,18},{18,2},{3,19},{19,3},{4,20},{20... | collective-permute-start | bytes 3538952 | tf_op jit(solution)/shard_map/ppermute | solution.py:879
  354.7 29.2 %collective-permute-start.46 = (bf16[2,192,1536]{2,1,0:T(8,128)(2,1)}, bf16[2,192,1536]{2,1,0:T(8,128)(2,1)}, u32[]{:S(2)}, u32[]{:S(2)}) collective-permute-start(bf16[2,192,1536]{2,1,0:T(8,128)(2,1)} %get-tuple-element.216), channel_id=1, source_target_pairs={{0,2},{1,3},{2,0},{3,1},{4,6},{5,7},{6,4},{7,5},{8,10},{9,11},{10,... | collective-permute-start | bytes 3538952 | tf_op jit(solution)/shard_map/ppermute | solution.py:77
  356.3 52.8 %collective-permute-start.50 = (bf16[2,192,1536]{2,1,0:T(8,128)(2,1)}, bf16[2,192,1536]{2,1,0:T(8,128)(2,1)}, u32[]{:S(2)}, u32[]{:S(2)}) collective-permute-start(bf16[2,192,1536]{2,1,0:T(8,128)(2,1)} %get-tuple-element.215), channel_id=1, source_target_pairs={{0,2},{1,3},{2,0},{3,1},{4,6},{5,7},{6,4},{7,5},{8,10},{9,11},{10,... | collective-permute-start | bytes 3538952 | tf_op jit(solution)/shard_map/ppermute | solution.py:77
  384.6 25.4 %collective-permute-start.56 = (f32[24,192]{1,0:T(8,128)S(1)}, f32[24,192]{1,0:T(8,128)S(1)}, u32[]{:S(2)}, u32[]{:S(2)}) collective-permute-start(f32[24,192]{1,0:T(8,128)S(1)} %get-tuple-element.266), channel_id=1, source_target_pairs={{0,3},{1,2},{2,1},{3,0},{4,7},{5,6},{6,5},{7,4},{8,11},{9,10},{10,... | collective-permute-start | bytes 55304 | tf_op jit(solution)/shard_map/ppermute | solution.py:77
  384.6 25.4 %collective-permute-start.55 = (f32[24,192]{1,0:T(8,128)S(1)}, f32[24,192]{1,0:T(8,128)S(1)}, u32[]{:S(2)}, u32[]{:S(2)}) collective-permute-start(f32[24,192]{1,0:T(8,128)S(1)} %get-tuple-element.267), channel_id=1, source_target_pairs={{0,2},{1,3},{2,0},{3,1},{4,6},{5,7},{6,4},{7,5},{8,10},{9,11},{10,... | collective-permute-start | bytes 55304 | tf_op jit(solution)/shard_map/ppermute | solution.py:77
  385.6 24.5 %collective-permute-start.54 = (f32[24,192]{1,0:T(8,128)S(1)}, f32[24,192]{1,0:T(8,128)S(1)}, u32[]{:S(2)}, u32[]{:S(2)}) collective-permute-start(f32[24,192]{1,0:T(8,128)S(1)} %get-tuple-element.265), channel_id=1, source_target_pairs={{0,1},{1,0},{2,3},{3,2},{4,5},{5,4},{6,7},{7,6},{8,9},{9,8},{10,11... | collective-permute-start | bytes 55304 | tf_op jit(solution)/shard_map/ppermute | solution.py:77
  392.4 33.2 %collective-permute-start.49 = (f32[208,256]{1,0:T(8,128)S(1)}, f32[208,256]{1,0:T(8,128)S(1)}, u32[]{:S(2)}, u32[]{:S(2)}) collective-permute-start(f32[208,256]{1,0:T(8,128)S(1)} %get-tuple-element.241), channel_id=1, source_target_pairs={{0,3},{1,2},{2,1},{3,0},{4,7},{5,6},{6,5},{7,4},{8,11},{9,10},{10,... | collective-permute-start | bytes 638984 | tf_op jit(solution)/shard_map/ppermute | solution.py:77
  409.1 17.6 %collective-permute-start.48 = (f32[208,256]{1,0:T(8,128)S(1)}, f32[208,256]{1,0:T(8,128)S(1)}, u32[]{:S(2)}, u32[]{:S(2)}) collective-permute-start(f32[208,256]{1,0:T(8,128)S(1)} %get-tuple-element.242), channel_id=1, source_target_pairs={{0,2},{1,3},{2,0},{3,1},{4,6},{5,7},{6,4},{7,5},{8,10},{9,11},{10,... | collective-permute-start | bytes 638984 | tf_op jit(solution)/shard_map/ppermute | solution.py:77
  410.0 18.8 %collective-permute-start.47 = (f32[208,256]{1,0:T(8,128)S(1)}, f32[208,256]{1,0:T(8,128)S(1)}, u32[]{:S(2)}, u32[]{:S(2)}) collective-permute-start(f32[208,256]{1,0:T(8,128)S(1)} %get-tuple-element.243), channel_id=1, source_target_pairs={{0,1},{1,0},{2,3},{3,2},{4,5},{5,4},{6,7},{7,6},{8,9},{9,8},{10,11... | collective-permute-start | bytes 638984 | tf_op jit(solution)/shard_map/ppermute | solution.py:77
  410.8 3.8 collective-permute-start.57
  411.9 58.2 %collective-permute-start.53 = (bf16[192,1024]{1,0:T(8,128)(2,1)}, bf16[192,1024]{1,0:T(8,128)(2,1)}, u32[]{:S(2)}, u32[]{:S(2)}) collective-permute-start(bf16[192,1024]{1,0:T(8,128)(2,1)} %get-tuple-element.226), channel_id=1, source_target_pairs={{0,3},{1,2},{2,1},{3,0},{4,7},{5,6},{6,5},{7,4},{8,11},{9,10},{10,... | collective-permute-start | bytes 1179656 | tf_op jit(solution)/shard_map/ppermute | solution.py:77
  414.7 4.7 collective-permute-start.58
  419.4 3.8 collective-permute-start.59
  423.2 12.1 %collective-permute-start.63 = (bf16[192,768]{1,0:T(8,128)(2,1)}, bf16[192,768]{1,0:T(8,128)(2,1)}, u32[]{:S(2)}, u32[]{:S(2)}) collective-permute-start(bf16[192,768]{1,0:T(8,128)(2,1)} %get-tuple-element.233), channel_id=1, source_target_pairs={{0,3},{1,7},{2,11},{3,15},{4,2},{5,6},{6,10},{7,14},{8,1},{9,5},{1... | collective-permute-start | bytes 884744 | tf_op jit(solution)/shard_map/ppermute | solution.py:876
  425.6 39.5 %collective-permute-start.62 = (bf16[192,768]{1,0:T(8,128)(2,1)}, bf16[192,768]{1,0:T(8,128)(2,1)}, u32[]{:S(2)}, u32[]{:S(2)}) collective-permute-start(bf16[192,768]{1,0:T(8,128)(2,1)} %get-tuple-element.234), channel_id=1, source_target_pairs={{0,2},{1,6},{2,10},{3,14},{4,3},{5,7},{6,11},{7,15},{8,0},{9,4},{1... | collective-permute-start | bytes 884744 | tf_op jit(solution)/shard_map/ppermute | solution.py:876
  426.7 39.3 %collective-permute-start.61 = (bf16[192,768]{1,0:T(8,128)(2,1)S(1)}, bf16[192,768]{1,0:T(8,128)(2,1)}, u32[]{:S(2)}, u32[]{:S(2)}) collective-permute-start(bf16[192,768]{1,0:T(8,128)(2,1)S(1)} %get-tuple-element.235), channel_id=1, source_target_pairs={{0,1},{1,5},{2,9},{3,13},{4,0},{5,4},{6,8},{7,12},{8,3},{9,7},{10,... | collective-permute-start | bytes 884744 | tf_op jit(solution)/shard_map/ppermute | solution.py:876
  428.8 38.2 %collective-permute-start.60 = (bf16[192,768]{1,0:T(8,128)(2,1)S(1)}, bf16[192,768]{1,0:T(8,128)(2,1)}, u32[]{:S(2)}, u32[]{:S(2)}) collective-permute-start(bf16[192,768]{1,0:T(8,128)(2,1)S(1)} %get-tuple-element.232), channel_id=1, source_target_pairs={{0,0},{1,4},{2,8},{3,12},{4,1},{5,5},{6,9},{7,13},{8,2},{9,6},{10,... | collective-permute-start | bytes 884744 | tf_op jit(solution)/shard_map/ppermute | solution.py:876
  435.3 35.9 %collective-permute-start.52 = (bf16[192,1024]{1,0:T(8,128)(2,1)S(1)}, bf16[192,1024]{1,0:T(8,128)(2,1)S(1)}, u32[]{:S(2)}, u32[]{:S(2)}) collective-permute-start(bf16[192,1024]{1,0:T(8,128)(2,1)S(1)} %copy-done.13), channel_id=1, source_target_pairs={{0,2},{1,3},{2,0},{3,1},{4,6},{5,7},{6,4},{7,5},{8,10},{9,11},{10,... | collective-permute-start | bytes 1179656 | tf_op jit(solution)/shard_map/ppermute | solution.py:77
  465.1 6.1 %collective-permute-start.51 = (bf16[192,1024]{1,0:T(8,128)(2,1)S(1)}, bf16[192,1024]{1,0:T(8,128)(2,1)S(1)}, u32[]{:S(2)}, u32[]{:S(2)}) collective-permute-start(bf16[192,1024]{1,0:T(8,128)(2,1)S(1)} %copy-done.12), channel_id=1, source_target_pairs={{0,1},{1,0},{2,3},{3,2},{4,5},{5,4},{6,7},{7,6},{8,9},{9,8},{10,11... | collective-permute-start | bytes 1179656 | tf_op jit(solution)/shard_map/ppermute | solution.py:77
  466.0 40.2 %collective-permute-start.65 = (bf16[2,192,1536]{2,1,0:T(8,128)(2,1)}, bf16[2,192,1536]{2,1,0:T(8,128)(2,1)}, u32[]{:S(2)}, u32[]{:S(2)}) collective-permute-start(bf16[2,192,1536]{2,1,0:T(8,128)(2,1)} %get-tuple-element.214), channel_id=1, source_target_pairs={{0,16},{16,0},{1,17},{17,1},{2,18},{18,2},{3,19},{19,3},{4,20},{20... | collective-permute-start | bytes 3538952 | tf_op jit(solution)/shard_map/ppermute | solution.py:879
  468.4 32.9 %collective-permute-start.64 = (bf16[192,768]{1,0:T(8,128)(2,1)S(1)}, bf16[192,768]{1,0:T(8,128)(2,1)S(1)}, u32[]{:S(2)}, u32[]{:S(2)}) collective-permute-start(bf16[192,768]{1,0:T(8,128)(2,1)S(1)} %add_convert_fusion.4), channel_id=1, source_target_pairs={{0,16},{16,0},{1,17},{17,1},{2,18},{18,2},{3,19},{19,3},{4,20},{20... | collective-permute-start | bytes 884744 | tf_op jit(solution)/shard_map/ppermute | solution.py:108
  470.1 56.1 %collective-permute-start.66 = (bf16[2,192,1536]{2,1,0:T(8,128)(2,1)S(1)}, bf16[2,192,1536]{2,1,0:T(8,128)(2,1)S(1)}, u32[]{:S(2)}, u32[]{:S(2)}) collective-permute-start(bf16[2,192,1536]{2,1,0:T(8,128)(2,1)S(1)} %copy-done), channel_id=1, source_target_pairs={{0,16},{16,0},{1,17},{17,1},{2,18},{18,2},{3,19},{19,3},{4,20},{20... | collective-permute-start | bytes 3538952 | tf_op jit(solution)/shard_map/ppermute | solution.py:879
  (50 other events, 651.6 us)

commit v4 on v3

--- a/solution.py
+++ b/solution.py
@@ -18,6 +18,7 @@
 GAIN1, GAIN2, VALUE0, VALUE1 = 16, 19, 22, 25
 SUM_GAIN2, SUM_VALUE0, SUM_VALUE1, SUM_GAIN1 = 16, 17, 18, 19
 EXTRA = 16
+SMALL = 24
 
 
 def mm(left, right, over_left, over_right, precision=None):
@@ -51,6 +52,13 @@
     packed = jnp.concatenate(out, axis=0)
     rest = jnp.zeros((EXTRA, width - packed.shape[1]), F32)
     return jnp.concatenate([packed, rest], axis=1).astype(BF16)
+
+
+def parts_in_rows(value, height):
+    high = value.astype(BF16).astype(F32)
+    middle = (value - high).astype(BF16).astype(F32)
+    rest = jnp.zeros((height - 3 * value.shape[0], value.shape[1]), F32)
+    return jnp.concatenate([high, middle, value - high - middle, rest], axis=0)
 
 
 def unpack_row(ref, base, span, k):
@@ -227,7 +235,7 @@
 def attend_back_kernel(
     place, t0, t1, t2, t3, weight, cosine, sine,
     query, keys, values, attn, logsum, d0, d1, d2, d3, grad_mid, small,
-    tokens_out, weight_out, small_out,
+    tokens_out, weight_out,
     dmid, proj_all, proj_acc, key_acc, value_acc, grad_all,
 ):
     block = pl.program_id(0)
@@ -304,7 +312,7 @@
             hidden = refs[k][:, :length].astype(F32)
             act = (hidden * inverse * gains[k]).astype(BF16)
             weight_out[row ^ col ^ k, :, : 3 * width] = mm(act, grad_all[...], 1, 1).astype(BF16)
-            weight_out[row ^ col ^ k, :, 3 * width :] = proj_acc[
+            weight_out[row ^ col ^ k, :, 3 * width : 4 * width] = proj_acc[
                 k * size : (k + 1) * size
             ].astype(BF16)
             back = mm(weight[row ^ k, :, : 3 * width], grad_all[...], 1, 0)
@@ -312,7 +320,8 @@
             summed = jnp.sum(hidden * inverse * back, axis=1, keepdims=True)
             turned = jnp.transpose(jnp.broadcast_to(summed, (size, 128)))[: small.shape[1]]
             places = lax.broadcasted_iota(jnp.int32, turned.shape, 0)
-            small_out[k] = jnp.where(places == SUM_GAIN1, turned, small[k])
+            rows = parts_in_rows(jnp.where(places == SUM_GAIN1, turned, small[k]), PARAMS)
+            weight_out[row ^ col ^ k, :, 4 * width :] = jnp.transpose(rows).astype(BF16)
             backs.append(back)
         inner = inner * (inverse * inverse * inverse) / (size * count)
         for k in range(count):
@@ -352,8 +361,7 @@
             in_specs=specs,
             out_specs=[
                 pl.BlockSpec((count, size, length), lambda q, s: (0, 0, 0)),
-                pl.BlockSpec((count, size, 4 * width), lambda q, s: (0, 0, 0)),
-                pl.BlockSpec(small.shape, lambda q, s: (0, 0, 0)),
+                pl.BlockSpec((count, size, 4 * width + PARAMS), lambda q, s: (0, 0, 0)),
             ],
             scratch_shapes=[
                 pltpu.VMEM((size * count, span), BF16),
@@ -366,8 +374,7 @@
         ),
         out_shape=[
             jax.ShapeDtypeStruct((count, size, length), BF16),
-            jax.ShapeDtypeStruct((count, size, 4 * width), BF16),
-            jax.ShapeDtypeStruct(small.shape, F32),
+            jax.ShapeDtypeStruct((count, size, 4 * width + PARAMS), BF16),
         ],
         compiler_params=pltpu.CompilerParams(vmem_limit_bytes=VMEM_LIMIT),
     )(place, *args)
@@ -540,7 +547,7 @@
         for lane, terms in columns:
             total = jnp.sum(terms, axis=1, keepdims=True)
             small = jnp.where(lanes == lane, total, small)
-        small_out[j] = jnp.transpose(small)[:24]
+        small_out[j] = jnp.transpose(small)[:SMALL]
         gain = column(params[j], GAIN2)
         inner = inner + jnp.sum(mid[here] * gain * back, axis=0, keepdims=True)
         backs.append(back)
@@ -577,14 +584,14 @@
                 pl.BlockSpec((full, span), lambda i, s: (0, 0)),
                 pl.BlockSpec((full, span), lambda i, s: (0, 0)),
                 pl.BlockSpec((kinds, span), lambda i, s: (0, 0)),
-                pl.BlockSpec((count, 24, size), lambda i, s: (0, 0, 0)),
+                pl.BlockSpec((count, SMALL, size), lambda i, s: (0, 0, 0)),
             ],
         ),
         out_shape=[
             jax.ShapeDtypeStruct((full, span), BF16),
             jax.ShapeDtypeStruct((full, span), F32),
             jax.ShapeDtypeStruct((kinds, span), F32),
-            jax.ShapeDtypeStruct((count, 24, size), F32),
+            jax.ShapeDtypeStruct((count, SMALL, size), F32),
         ],
         compiler_params=pltpu.CompilerParams(vmem_limit_bytes=VMEM_LIMIT),
     )(place, *args)
@@ -904,7 +911,6 @@
     near_own = lax.dynamic_slice_in_dim(own, first_half * half, half, 0)
     pair = half // 2
     two_a = col_swap(after(near_own[:pair], flow_quarter), 2)
-    side = col_swap(after(own, weight), 1)
     projs = col_gather(after(weight[:, :, 3 * size :], toks[2]))
 
     routes_t = routes.T
@@ -921,29 +927,34 @@
     order_far = jnp.concatenate([order[half:], tiles[half:]]).astype(jnp.int32)
 
     query, keys, values, attn, logsum = attend(place, toks, weight, cosine, sine)
-    attn, two_a, flow_rows, projs, side = join(attn, two_a, flow_rows, projs, side)
+    attn, two_a, flow_rows, projs = join(attn, two_a, flow_rows, projs)
     parts = [attn[0]] + [col_swap(attn[k], k) for k in range(1, cols)]
     two_b = col_swap(after(near_own[pair:], parts[1], parts[2], parts[3]), 2)
     if groups == 2:
         far_two_a = across_groups(two_a)
-        far_two_b = across_groups(two_b)
     else:
         far_two_a = col_swap(own[half : half + pair], 2)
-        far_two_b = col_swap(after(own[half + pair :], two_b), 2)
+    side = col_swap(after(own, attn), 1)
     mid, in_rows, stats = middle(place, toks, parts, projs, prev_logits.T, routes_t)
     x_rows = row_gather(in_rows)
     three_a = col_swap(after(two_a, parts[1], parts[2], parts[3]), 1)
-    three_b = col_swap(after(two_b, mid), 1)
-    far_three_a = col_swap(after(far_two_a, mid), 1)
-    far_three_b = col_swap(far_two_b, 1)
-    x_rows, far_two_a, far_three_a = join(x_rows, far_two_a, far_three_a)
+    two_b, far_two_a = join(after(two_b, *x_rows[1:]), after(far_two_a, *x_rows[1:]))
+    if groups == 2:
+        far_two_b = across_groups(two_b)
+    else:
+        far_two_b = col_swap(own[half + pair :], 2)
+    three_b = col_swap(two_b, 1)
+    far_three_a = col_swap(far_two_a, 1)
+    x_rows, far_three_a = join(x_rows, far_three_a)
 
     near_out = run_experts(
         order_near, x_rows, flow_rows, ranks, share, own, side,
         [two_a, two_b], [three_a, three_b], None,
     )
+    near_out, far_two_b = join(near_out, far_two_b)
     *carried, near_mine, near_next = near_out
-    near_next = col_swap(near_next, 1)
+    far_three_b = col_swap(far_two_b, 1)
+    near_next = col_swap(after(near_next, far_three_b), 1)
     y, dx, far_mine, far_next = run_experts(
         order_far, x_rows, flow_rows, ranks, share, own, side,
         [far_two_a, far_two_b], [far_three_a, far_three_b], carried,
@@ -956,35 +967,48 @@
         return [value[0]] + [row_shift(value[s], -s) for s in range(1, rows)]
 
     def across_sums(sums):
-        return [across_groups(s) for s in sums] if groups == 2 else sums
-
-    near_next, dx, far_mine, far_next = join(near_next, dx, far_mine, far_next)
-    dx = row_scatter(dx)
+        return [across_groups(s) for s in sums] if groups == 2 else list(sums)
+
     near_kept, near_sent = low_sum(near_mine[0], near_next[0]), low_sum(near_mine[1], near_next[1])
-    near_got = [col_swap(near_sent[:pair], 2), col_swap(after(near_sent[pair:], dx[1]), 2)]
+    dx_first = row_shift(dx[1], -1)
+    dx, dx_first, near_sent, near_kept, far_next = join(
+        dx, dx_first, near_sent, near_kept, far_next
+    )
+    near_got = [col_swap(near_sent[:pair], 2), col_swap(near_sent[pair:], 2)]
+    dx = [dx[0], dx_first] + [row_shift(dx[s], -s) for s in range(2, rows)]
     far_next = col_swap(far_next, 1)
+    dx, near_got[0] = join(dx, near_got[0])
+    near_sum = [low_sum(near_kept[:pair], near_got[0])]
+    near_other = across_sums(near_sum)
     low, grad_mid, grad_logits, small = middle_back(
         place, toks, mid, flow_quarter, stats, routes_t, dx, kinds
     )
-    near_sum = [low_sum(near_kept[:pair], near_got[0]), low_sum(near_kept[pair:], near_got[1])]
-    near_other = across_sums(near_sum)
     lows = col_gather(low)
-    lows, near_sum, near_other[0], far_next = join(lows, near_sum, near_other[0], far_next)
+    near_sum.append(low_sum(after(near_kept, low)[pair:], near_got[1]))
+    lows, near_sum, near_other, far_mine, far_next = join(
+        lows, near_sum, near_other, far_mine, far_next
+    )
+    near_other += across_sums(near_sum[1:])
 
     y = row_scatter(after(y, dx[1], dx[2], dx[3]))
     far_kept, far_sent = low_sum(far_mine[0], far_next[0]), low_sum(far_mine[1], far_next[1])
-    far_got = [col_swap(far_sent[:pair], 2), col_swap(far_sent[pair:], 2)]
-    far_sum = [low_sum(far_kept[:pair], far_got[0]), low_sum(far_kept[pair:], far_got[1])]
-    far_other = across_sums(far_sum)
-    tokens_parts, weight_parts, small = attend_back(
+    far_got = [col_swap(far_sent[:pair], 2)]
+    tokens_parts, weight_parts = attend_back(
         place, toks, weight, cosine, sine,
         query, keys, values, attn, logsum, lows, grad_mid, small,
     )
-    tokens_parts, weight_parts, small, y, near_other, far_got[0] = join(
-        tokens_parts, weight_parts, small, y, near_other, far_got[0]
-    )
+    tokens_parts, weight_parts, y, near_other, far_got[0], far_sent = join(
+        tokens_parts, weight_parts, y, near_other, far_got[0], far_sent
+    )
+    far_got.append(col_swap(far_sent[pair:], 2))
+    far_sum = [low_sum(far_kept[:pair], far_got[0])]
+    far_other = across_sums(far_sum)
     out = result(place, toks, mid, stats, routes_t, grad_logits, y)
-    tokens_parts, far_got[1] = join(tokens_parts, far_got[1])
+    tokens_parts, weight_parts, out, far_got[1], far_other[0] = join(
+        tokens_parts, weight_parts, out, far_got[1], far_other[0]
+    )
+    far_sum.append(low_sum(far_kept[pair:], far_got[1]))
+    far_other += across_sums(far_sum[1:])
 
     def col_scatter(value):
         total = value[0].astype(F32)
@@ -992,11 +1016,14 @@
             total = total + col_swap(value[k], k).astype(F32)
         return total
 
-    small = row_total(col_scatter(small))
     total = collect(weight_parts[0], 0).astype(F32)
     for m in range(1, rows):
         total = total + collect(weight_parts[m], m).astype(F32)
-    small, total = dp_total(small), dp_total(total.astype(BF16))
+    packed = total[:, 4 * size : 4 * size + 3 * SMALL]
+    small = packed[:, :SMALL] + packed[:, SMALL : 2 * SMALL] + packed[:, 2 * SMALL :]
+    small = dp_total(row_total(small.T))
+    total, far_other = join(total, far_other)
+    total = dp_total(total[:, : 4 * size].astype(BF16))
     grad_tokens = col_scatter(tokens_parts)
     qkv_sum = jnp.stack([total[:, j * size : (j + 1) * size] for j in range(3)])
     proj_sum = total[:, 3 * size :].T

time: 539 us -> 508 us (0.942)
  waiting for transfers between devices: 244 us -> 168 us
  starting transfers between devices: 88.1 us -> 108 us
  other arithmetic: 41.7 us -> 61.4 us
    ppermute x37 -> x34, waiting for transfers between devices: 108 us -> 57.6 us  [col_swap(): return lax.ppermute(value, 'col', [(i, i ^ bits) for i in range(count)])]
    ppermute x12, waiting for transfers between devices: 30.3 us -> 64.1 us  [row_shift(): lax.ppermute(value, 'row', [(i, (i + steps) % count) for i in range(count)])]
    ppermute x2, waiting for transfers between devices: 29.9 us -> 2.67 us  [dp_total(): other = lax.ppermute(value, 'dp', [(0, 1), (1, 0)])]
    ppermute x4, waiting for transfers between devices: 31 us -> 13.2 us  [collect(): return lax.ppermute(value, ('row', 'col'), pairs)]
    convert_element_type x4 -> x6, other arithmetic: 13.1 us -> 28.5 us  [low_sum(): return (left.astype(F32) + right.astype(F32)).astype(BF16)]
    ppermute x6, waiting for transfers between devices: 33.6 us -> 21.4 us  [across_groups(): return lax.ppermute(value, 'dp', [(0, 1), (1, 0)])]
    ppermute x6, starting transfers between devices: 6.68 us -> 15.8 us  [across_groups(): return lax.ppermute(value, 'dp', [(0, 1), (1, 0)])]
    ppermute x4, waiting for transfers between devices: 8.98 us -> 0.01 us  [spread(): return lax.ppermute(value, ('row', 'col'), pairs)]
  transfers between devices with their start and end apart: 67 -> 64, of which waited for: 29 -> 24; matrix products, arithmetic and copies ran while one was open for 13% -> 18% of each run, Pallas kernels for 21% -> 23%
where the time goes in v4:
time: 508 us; the launch traced here: 500 us
  waiting for transfers between devices  168 us (33%)
  Pallas kernels  113 us (22%)
  starting transfers between devices  108 us (21%)
  other arithmetic  61.4 us (12%)
  local copies, waits for them, and re-layouts  47.7 us (9%)
    ppermute x12, waiting for transfers between devices, row_shift(): lax.ppermute(value, 'row', [(i, (i + steps) % count) for i in range(count)])  64.1 us
    pallas_call x2, Pallas kernels, run_experts(): pl.pallas_call(body, name='experts', cost_estimate=span_of(36), grid_spec...  59.3 us
    ppermute x34, waiting for transfers between devices, col_swap(): return lax.ppermute(value, 'col', [(i, i ^ bits) for i in range(count)])  57.6 us
    ppermute x34, starting transfers between devices, col_swap(): return lax.ppermute(value, 'col', [(i, i ^ bits) for i in range(count)])  30.2 us
    convert_element_type x6, other arithmetic, low_sum(): return (left.astype(F32) + right.astype(F32)).astype(BF16)  28.5 us
    ppermute x12, starting transfers between devices, row_shift(): lax.ppermute(value, 'row', [(i, (i + steps) % count) for i in range(count)])  25.4 us
    pallas_call x1, Pallas kernels, attend_back(): pl.pallas_call(attend_back_kernel, name='attend_back', cost_estimate=span...  23.5 us
    ppermute x6, waiting for transfers between devices, across_groups(): return lax.ppermute(value, 'dp', [(0, 1), (1, 0)])  21.4 us
  transfers between devices with their start and end apart: 64, of which 24 were waited for; matrix products, arithmetic and copies ran while one was open for 18% of the time, Pallas kernels for 23%

profile of v4, /device:TPU:0, one launch (start us, length us, event | category | flops | bytes accessed | tf_op | source)
XLA Modules:
  0.0 500.2 jit_solution(15885094128870898233)
XLA Ops:
  3.7 5.0 collective-permute-start.4
  8.6 5.4 %collective-permute-start.5 = (bf16[192,768]{1,0:T(8,128)(2,1)}, bf16[192,768]{1,0:T(8,128)(2,1)}, u32[]{:S(2)}, u32[]{:S(2)}) collective-permute-start(bf16[192,768]{1,0:T(8,128)(2,1)} %pad_maximum_fusion.6), channel_id=1, source_target_pairs={{2,0},{7,1},{8,2},{13,3},{3,4},{6,5},{9,6},{12,7},{0,8},{5,9},{10,... | collective-permute-start | bytes 884744 | tf_op jit(solution)/shard_map/ppermute | solution.py:879
  14.1 3.4 collective-permute-start.6
  17.5 3.8 collective-permute-start.3
  33.3 2.1 concatenate.21.t0.p0
  36.0 3.5 pad_maximum_fusion.refs_11_
  39.6 2.9 constant_dynamic-slice_fusion.6
  42.5 4.5 collective-permute-done.1.t2.p2
  51.3 1.6 collective-permute-start.15
  55.5 9.2 %collective-permute-done.8 = bf16[192,256]{1,0:T(8,128)(2,1)S(1)} collective-permute-done((bf16[192,256]{1,0:T(8,128)(2,1)S(1)}, bf16[192,256]{1,0:T(8,128)(2,1)S(1)}, u32[]{:S(2)}, u32[]{:S(2)}) %collective-permute-start.8) | collective-permute-done | bytes 98336 | tf_op jit(solution)/shard_map/ppermute | solution.py:85
  66.3 3.3 collective-permute-done.9
  70.4 2.7 collective-permute-start.11
  73.1 2.4 collective-permute-start.13
  76.9 13.6 %attend.1 = (bf16[4,192,256]{2,1,0:T(8,128)(2,1)}, bf16[192,1024]{1,0:T(8,128)(2,1)}, bf16[192,1024]{1,0:T(8,128)(2,1)}, bf16[4,192,256]{2,1,0:T(8,128)(2,1)}, f32[8,1024]{1,0:T(8,128)}) custom-call(s32[4]{0:T(128)} %pad_add_fusion.place, bf16[192,1152]{1,0:T(8,128)(2,1)} %concatenate.21.t0.p0, bf16[192,1152]{1,0:T(8,128)(2,1)} %collective-permute-done.t1.p1, ...), custom_call_target="tpu_custom_call" | custom-call | flops 15399999488 | bytes 50400000 | tf_op jit(solution)/shard_map/attend/pallas_call | solution.py:204
  90.5 9.8 %collective-permute-done.12 = bf16[256,768]{0,1:T(8,128)(2,1)S(1)} collective-permute-done((bf16[256,768]{0,1:T(8,128)(2,1)S(1)}, bf16[256,768]{0,1:T(8,128)(2,1)S(1)}, u32[]{:S(2)}, u32[]{:S(2)}) %collective-permute-start.12) | collective-permute-done | bytes 393248 | tf_op jit(solution)/shard_map/ppermute | solution.py:95
  100.3 2.9 collective-permute-done.10.refs_13_
  105.3 2.3 reduce-window.6
  107.5 1.7 slice_bitcast_fusion.32
  111.5 1.5 collective-permute-start.24
  113.1 2.3 collective-permute-done.18.a2
  116.9 5.4 %middle.1 = (f32[768,256]{1,0:T(8,128)}, bf16[272,768]{1,0:T(8,128)(2,1)}, f32[8,256]{1,0:T(8,128)}) custom-call(s32[4]{0:T(128)} %pad_add_fusion.place, bf16[192,1152]{1,0:T(8,128)(2,1)} %concatenate.21.t0.p0, bf16[192,1152]{1,0:T(8,128)(2,1)} %collective-permute-done.t1.p1, bf16[192,1152]{1,0:T(8,128)(2,1)} %collective-permute-done.1.t2.p2, ...), custom_call_target="tpu_custom_call" | custom-call | flops 6600000000 | bytes 21600000 | tf_op jit(solution)/shard_map/middle/pallas_call | solution.py:454
  122.3 6.1 %collective-permute-start.20 = (bf16[272,768]{1,0:T(8,128)(2,1)}, bf16[272,768]{1,0:T(8,128)(2,1)S(1)}, u32[]{:S(2)}, u32[]{:S(2)}) collective-permute-start(bf16[272,768]{1,0:T(8,128)(2,1)} %get-tuple-element.128.refs_1_), channel_id=1, source_target_pairs={{0,4},{4,8},{8,12},{12,0},{1,5},{5,9},{9,13},{13,1},{2,6},{6,10},{... | collective-permute-start | bytes 1253384 | tf_op jit(solution)/shard_map/ppermute | solution.py:95
  128.8 1.5 collective-permute-start.21
  130.3 9.8 %collective-permute-done.20.refs_2_ = bf16[272,768]{1,0:T(8,128)(2,1)S(1)} collective-permute-done((bf16[272,768]{1,0:T(8,128)(2,1)}, bf16[272,768]{1,0:T(8,128)(2,1)S(1)}, u32[]{:S(2)}, u32[]{:S(2)}) %collective-permute-start.20) | collective-permute-done | bytes 417824 | tf_op jit(solution)/shard_map/ppermute | solution.py:95
  140.1 2.5 collective-permute-start.22
  143.3 14.7 %collective-permute-done.21.refs_3_ = bf16[272,768]{1,0:T(8,128)(2,1)} collective-permute-done((bf16[272,768]{1,0:T(8,128)(2,1)}, bf16[272,768]{1,0:T(8,128)(2,1)}, u32[]{:S(2)}, u32[]{:S(2)}) %collective-permute-start.21) | collective-permute-done | bytes 417824 | tf_op jit(solution)/shard_map/ppermute | solution.py:95
  158.0 2.6 collective-permute-done.22.refs_4_
  166.7 1.5 collective-permute-start.29
  168.3 31.5 %experts.2 = (f32[1024,768]{1,0:T(8,128)}, f32[1024,768]{1,0:T(8,128)}, f32[8,1024]{1,0:T(8,128)}, bf16[2,4,192,1536]{3,2,1,0:T(8,128)(2,1)}, bf16[2,4,192,1536]{3,2,1,0:T(8,128)(2,1)}) custom-call(s32[8]{0:T(128)} %pad_add_fusion.2.refs_0_, bf16[272,768]{1,0:T(8,128)(2,1)} %get-tuple-element.128.refs_1_, bf16[272,768]{1,0:T(8,128)(2,1)} %copy-done.23, ...), custom_call_target="tpu_custom_call" | custom-call | flops 39600001024 | bytes 129600000 | tf_op jit(solution)/shard_map/experts/pallas_call | solution.py:820
  200.0 3.0 collective-permute-done.30.refs_16_
  204.1 27.8 %experts.3 = (bf16[4,256,768]{2,1,0:T(8,128)(2,1)}, bf16[4,272,768]{2,1,0:T(8,128)(2,1)}, bf16[2,4,192,1536]{3,2,1,0:T(8,128)(2,1)}, bf16[2,4,192,1536]{3,2,1,0:T(8,128)(2,1)}) custom-call(s32[8]{0:T(128)} %pad_add_fusion.1.refs_0_, bf16[272,768]{1,0:T(8,128)(2,1)} %get-tuple-element.128.refs_1_, bf16[272,768]{1,0:T(8,128)(2,1)} %copy-done.23, ...), custom_call_target="tpu_custom_call" | custom-call | flops 39600001024 | bytes 129600000 | tf_op jit(solution)/shard_map/experts/pallas_call | solution.py:820
  232.9 7.9 %collective-permute-start.31 = (bf16[272,768]{1,0:T(8,128)(2,1)S(1)}, bf16[272,768]{1,0:T(8,128)(2,1)S(1)}, u32[]{:S(2)}, u32[]{:S(2)}) collective-permute-start(bf16[272,768]{1,0:T(8,128)(2,1)S(1)} %slice_bitcast_fusion.7), channel_id=1, source_target_pairs={{0,12},{4,0},{8,4},{12,8},{1,13},{5,1},{9,5},{13,9},{2,14},{6,2},{... | collective-permute-start | bytes 1253384 | tf_op jit(solution)/shard_map/ppermute | solution.py:95
  240.8 16.0 %fusion.1 = (bf16[4,192,1536]{2,1,0:T(8,128)(2,1)S(1)}, bf16[4,192,1536]{2,1,0:T(8,128)(2,1)S(1)}) fusion(bf16[2,4,192,1536]{3,2,1,0:T(8,128)(2,1)} %collective-permute-done.32, bf16[2,4,192,1536]{3,2,1,0:T(8,128)(2,1)} %get-tuple-element.150), kind=kLoop, calls=%fused_computation.9 | loop fusion | flops 9437184 | bytes 14155776 | tf_op jit(solution)/shard_map/convert_element_type | solution.py:964
  262.0 27.2 %collective-permute-done.33.x2 = bf16[272,768]{1,0:T(8,128)(2,1)S(1)} collective-permute-done((bf16[272,768]{1,0:T(8,128)(2,1)S(1)}, bf16[272,768]{1,0:T(8,128)(2,1)S(1)}, u32[]{:S(2)}, u32[]{:S(2)}) %collective-permute-start.33) | collective-permute-done | bytes 417824 | tf_op jit(solution)/shard_map/ppermute | solution.py:95
  290.6 5.3 %collective-permute-start.40 = (bf16[2,192,1536]{2,1,0:T(8,128)(2,1)}, bf16[2,192,1536]{2,1,0:T(8,128)(2,1)}, u32[]{:S(2)}, u32[]{:S(2)}) collective-permute-start(bf16[2,192,1536]{2,1,0:T(8,128)(2,1)} %add_convert_fusion.5), channel_id=1, source_target_pairs={{0,16},{16,0},{1,17},{17,1},{2,18},{18,2},{3,19},{19,3},{4,20},{20... | collective-permute-start | bytes 3538952 | tf_op jit(solution)/shard_map/ppermute | solution.py:886
  295.9 6.8 %middle_back.1 = (bf16[768,256]{1,0:T(8,128)(2,1)}, f32[768,256]{1,0:T(8,128)}, f32[12,256]{1,0:T(8,128)}, f32[4,24,192]{2,1,0:T(8,128)}) custom-call(s32[4]{0:T(128)} %pad_add_fusion.place, bf16[192,1152]{1,0:T(8,128)(2,1)} %concatenate.21.t0.p0, bf16[192,1152]{1,0:T(8,128)(2,1)} %collective-permute-done.t1.p1, ...), custom_call_target="tpu_custom_call" | custom-call | flops 7699999744 | bytes 25200000 | tf_op jit(solution)/shard_map/middle_back/pallas_call | solution.py:575
  305.0 7.4 %collective-permute-done.39 = bf16[2,192,1536]{2,1,0:T(8,128)(2,1)} collective-permute-done((bf16[2,192,1536]{2,1,0:T(8,128)(2,1)}, bf16[2,192,1536]{2,1,0:T(8,128)(2,1)}, u32[]{:S(2)}, u32[]{:S(2)}) %collective-permute-start.39) | collective-permute-done | bytes 1179680 | tf_op jit(solution)/shard_map/ppermute | solution.py:85
  312.8 7.4 %collective-permute-done.37.d2 = bf16[768,256]{1,0:T(8,128)(2,1)S(1)} collective-permute-done((bf16[768,256]{1,0:T(8,128)(2,1)}, bf16[768,256]{1,0:T(8,128)(2,1)S(1)}, u32[]{:S(2)}, u32[]{:S(2)}) %collective-permute-start.37) | collective-permute-done | bytes 393248 | tf_op jit(solution)/shard_map/ppermute | solution.py:85
  320.3 1.7 add_convert_fusion.4
  323.3 4.4 add_convert_fusion
  331.1 5.3 %collective-permute-start.45 = (bf16[2,192,1536]{2,1,0:T(8,128)(2,1)S(1)}, bf16[2,192,1536]{2,1,0:T(8,128)(2,1)}, u32[]{:S(2)}, u32[]{:S(2)}) collective-permute-start(bf16[2,192,1536]{2,1,0:T(8,128)(2,1)S(1)} %add_convert_fusion.4), channel_id=1, source_target_pairs={{0,16},{16,0},{1,17},{17,1},{2,18},{18,2},{3,19},{19,3},{4,20},{20... | collective-permute-start | bytes 3538952 | tf_op jit(solution)/shard_map/ppermute | solution.py:886
  336.4 23.5 %attend_back.1 = (bf16[4,192,1024]{2,1,0:T(8,128)(2,1)}, bf16[4,192,896]{2,1,0:T(8,128)(2,1)}) custom-call(s32[4]{0:T(128)} %pad_add_fusion.place, bf16[192,1152]{1,0:T(8,128)(2,1)} %concatenate.21.t0.p0, bf16[192,1152]{1,0:T(8,128)(2,1)} %collective-permute-done.t1.p1, bf16[192,1152]{1,0:T(8,128)(2,1)} %collective-permute-done.1.t2.p2, ...), custom_call_target="tpu_custom_call" | custom-call | flops 26400000000 | bytes 86400000 | tf_op jit(solution)/shard_map/attend_back/pallas_call | solution.py:354
  360.0 2.5 collective-permute-done.45
  362.5 2.6 fusion.3
  365.1 1.7 collective-permute-start.48
  369.2 4.4 result.1
  373.6 18.9 %collective-permute-done.48 = bf16[2,192,1536]{2,1,0:T(8,128)(2,1)} collective-permute-done((bf16[2,192,1536]{2,1,0:T(8,128)(2,1)}, bf16[2,192,1536]{2,1,0:T(8,128)(2,1)}, u32[]{:S(2)}, u32[]{:S(2)}) %collective-permute-start.48) | collective-permute-done | bytes 1179680 | tf_op jit(solution)/shard_map/ppermute | solution.py:886
  392.5 2.4 collective-permute-done.47
  395.0 2.6 fusion.2
  399.0 4.3 collective-permute-start.55
  403.5 1.8 collective-permute-start.50
  406.7 8.0 %collective-permute-done.50 = f32[208,256]{1,0:T(8,128)S(1)} collective-permute-done((f32[208,256]{1,0:T(8,128)S(1)}, f32[208,256]{1,0:T(8,128)S(1)}, u32[]{:S(2)}, u32[]{:S(2)}) %collective-permute-start.50) | collective-permute-done | bytes 213024 | tf_op jit(solution)/shard_map/ppermute | solution.py:85
  414.7 3.0 collective-permute-start.57
  417.7 6.8 %collective-permute-done.51 = f32[208,256]{1,0:T(8,128)S(1)} collective-permute-done((f32[208,256]{1,0:T(8,128)S(1)}, f32[208,256]{1,0:T(8,128)S(1)}, u32[]{:S(2)}, u32[]{:S(2)}) %collective-permute-start.51) | collective-permute-done | bytes 213024 | tf_op jit(solution)/shard_map/ppermute | solution.py:85
  424.5 2.6 collective-permute-start.58
  429.0 13.8 %collective-permute-start.53 = (bf16[192,1024]{1,0:T(8,128)(2,1)S(1)}, bf16[192,1024]{1,0:T(8,128)(2,1)S(1)}, u32[]{:S(2)}, u32[]{:S(2)}) collective-permute-start(bf16[192,1024]{1,0:T(8,128)(2,1)S(1)} %copy-done.14), channel_id=1, source_target_pairs={{0,2},{1,3},{2,0},{3,1},{4,6},{5,7},{6,4},{7,5},{8,10},{9,11},{10,... | collective-permute-start | bytes 1179656 | tf_op jit(solution)/shard_map/ppermute | solution.py:85
  442.7 13.2 %collective-permute-done.57 = bf16[192,896]{1,0:T(8,128)(2,1)} collective-permute-done((bf16[192,896]{1,0:T(8,128)(2,1)}, bf16[192,896]{1,0:T(8,128)(2,1)}, u32[]{:S(2)}, u32[]{:S(2)}) %collective-permute-start.57) | collective-permute-done | bytes 344096 | tf_op jit(solution)/shard_map/ppermute | solution.py:883
  459.0 4.2 collective-permute-done.59
  463.3 6.1 %collective-permute-start.60 = (f32[24,192]{0,1:T(8,128)S(1)}, f32[24,192]{0,1:T(8,128)S(1)}, u32[]{:S(2)}, u32[]{:S(2)}) collective-permute-start(f32[24,192]{0,1:T(8,128)S(1)} %fusion.36), channel_id=1, source_target_pairs={{0,8},{4,12},{8,0},{12,4},{1,9},{5,13},{9,1},{13,5},{2,10},{6,14},... | collective-permute-start | bytes 55304 | tf_op jit(solution)/shard_map/ppermute | solution.py:90
  470.0 4.7 collective-permute-done.60
  476.1 2.1 fusion.6
  489.0 2.0 add_dynamic-update-slice_fusion.2
  491.0 1.6 add_dynamic-update-slice_fusion.1
  492.6 2.0 add_dynamic-update-slice_fusion
  (266 shorter events, 83.7 us)
Async XLA Ops:
  3.7 44.5 %collective-permute-start.4 = (bf16[192,768]{1,0:T(8,128)(2,1)}, bf16[192,768]{1,0:T(8,128)(2,1)}, u32[]{:S(2)}, u32[]{:S(2)}) collective-permute-start(bf16[192,768]{1,0:T(8,128)(2,1)} %pad_maximum_fusion.6), channel_id=1, source_target_pairs={{1,0},{4,1},{11,2},{14,3},{0,4},{5,5},{10,6},{15,7},{3,8},{6,9},{9... | collective-permute-start | bytes 884744 | tf_op jit(solution)/shard_map/ppermute | solution.py:879
  8.6 40.2 %collective-permute-start.5 = (bf16[192,768]{1,0:T(8,128)(2,1)}, bf16[192,768]{1,0:T(8,128)(2,1)}, u32[]{:S(2)}, u32[]{:S(2)}) collective-permute-start(bf16[192,768]{1,0:T(8,128)(2,1)} %pad_maximum_fusion.6), channel_id=1, source_target_pairs={{2,0},{7,1},{8,2},{13,3},{3,4},{6,5},{9,6},{12,7},{0,8},{5,9},{10,... | collective-permute-start | bytes 884744 | tf_op jit(solution)/shard_map/ppermute | solution.py:879
  14.1 34.7 %collective-permute-start.6 = (bf16[192,768]{1,0:T(8,128)(2,1)}, bf16[192,768]{1,0:T(8,128)(2,1)}, u32[]{:S(2)}, u32[]{:S(2)}) collective-permute-start(bf16[192,768]{1,0:T(8,128)(2,1)} %pad_maximum_fusion.6), channel_id=1, source_target_pairs={{3,0},{6,1},{9,2},{12,3},{2,4},{7,5},{8,6},{13,7},{1,8},{4,9},{11,... | collective-permute-start | bytes 884744 | tf_op jit(solution)/shard_map/ppermute | solution.py:879
  17.5 31.3 %collective-permute-start.3 = (bf16[192,768]{1,0:T(8,128)(2,1)}, bf16[192,768]{1,0:T(8,128)(2,1)}, u32[]{:S(2)}, u32[]{:S(2)}) collective-permute-start(bf16[192,768]{1,0:T(8,128)(2,1)} %pad_maximum_fusion.6), channel_id=1, source_target_pairs={{0,0},{5,1},{10,2},{15,3},{1,4},{4,5},{11,6},{14,7},{2,8},{7,9},{8... | collective-permute-start | bytes 884744 | tf_op jit(solution)/shard_map/ppermute | solution.py:879
  35.5 11.6 %collective-permute-start.1 = (bf16[192,1152]{1,0:T(8,128)(2,1)}, bf16[192,1152]{1,0:T(8,128)(2,1)}, u32[]{:S(2)}, u32[]{:S(2)}) collective-permute-start(bf16[192,1152]{1,0:T(8,128)(2,1)} %concatenate.21.t0.p0), channel_id=1, source_target_pairs={{0,2},{1,3},{2,0},{3,1},{4,6},{5,7},{6,4},{7,5},{8,10},{9,11},{10,... | collective-permute-start | bytes 1327112 | tf_op jit(solution)/shard_map/ppermute | solution.py:85
  47.1 26.0 %collective-permute-start = (bf16[192,1152]{1,0:T(8,128)(2,1)S(1)}, bf16[192,1152]{1,0:T(8,128)(2,1)}, u32[]{:S(2)}, u32[]{:S(2)}) collective-permute-start(bf16[192,1152]{1,0:T(8,128)(2,1)S(1)} %copy-done.13), channel_id=1, source_target_pairs={{0,1},{1,0},{2,3},{3,2},{4,5},{5,4},{6,7},{7,6},{8,9},{9,8},{10,11... | collective-permute-start | bytes 1327112 | tf_op jit(solution)/shard_map/ppermute | solution.py:85
  48.2 5.2 %collective-permute-start.7 = (bf16[192,256]{1,0:T(8,128)(2,1)S(1)}, bf16[192,256]{1,0:T(8,128)(2,1)S(1)}, u32[]{:S(2)}, u32[]{:S(2)}) collective-permute-start(bf16[192,256]{1,0:T(8,128)(2,1)S(1)} %bitcast.177), channel_id=1, source_target_pairs={{0,1},{1,0},{2,3},{3,2},{4,5},{5,4},{6,7},{7,6},{8,9},{9,8},{10,11... | collective-permute-start | bytes 294920 | tf_op jit(solution)/shard_map/ppermute | solution.py:85
  51.3 21.8 %collective-permute-start.15 = (bf16[4,192,192]{2,1,0:T(8,128)(2,1)}, bf16[4,192,192]{2,1,0:T(8,128)(2,1)}, u32[]{:S(2)}, u32[]{:S(2)}) collective-permute-start(bf16[4,192,192]{2,1,0:T(8,128)(2,1)} %slice.419.o0), channel_id=1, source_target_pairs={{0,2},{1,3},{2,0},{3,1},{4,6},{5,7},{6,4},{7,5},{8,10},{9,11},{10,... | collective-permute-start | bytes 884744 | tf_op jit(solution)/shard_map/ppermute | solution.py:85
  52.9 22.5 %collective-permute-start.14 = (bf16[4,192,192]{2,1,0:T(8,128)(2,1)}, bf16[4,192,192]{2,1,0:T(8,128)(2,1)}, u32[]{:S(2)}, u32[]{:S(2)}) collective-permute-start(bf16[4,192,192]{2,1,0:T(8,128)(2,1)} %slice.419.o0), channel_id=1, source_target_pairs={{0,1},{1,0},{2,3},{3,2},{4,5},{5,4},{6,7},{7,6},{8,9},{9,8},{10,11... | collective-permute-start | bytes 884744 | tf_op jit(solution)/shard_map/ppermute | solution.py:85
  53.0 11.7 %collective-permute-start.8 = (bf16[192,256]{1,0:T(8,128)(2,1)S(1)}, bf16[192,256]{1,0:T(8,128)(2,1)S(1)}, u32[]{:S(2)}, u32[]{:S(2)}) collective-permute-start(bf16[192,256]{1,0:T(8,128)(2,1)S(1)} %bitcast.178), channel_id=1, source_target_pairs={{0,2},{1,3},{2,0},{3,1},{4,6},{5,7},{6,4},{7,5},{8,10},{9,11},{10,... | collective-permute-start | bytes 294920 | tf_op jit(solution)/shard_map/ppermute | solution.py:85
  53.4 23.4 %collective-permute-start.2 = (bf16[192,1152]{1,0:T(8,128)(2,1)}, bf16[192,1152]{1,0:T(8,128)(2,1)}, u32[]{:S(2)}, u32[]{:S(2)}) collective-permute-start(bf16[192,1152]{1,0:T(8,128)(2,1)} %collective-permute-done.1.t2.p2), channel_id=1, source_target_pairs={{0,1},{1,0},{2,3},{3,2},{4,5},{5,4},{6,7},{7,6},{8,9},{9,8},{10,11... | collective-permute-start | bytes 1327112 | tf_op jit(solution)/shard_map/ppermute | solution.py:85
  64.7 4.9 collective-permute-start.9
  70.4 20.1 %collective-permute-start.11 = (bf16[256,768]{0,1:T(8,128)(2,1)S(1)}, bf16[256,768]{0,1:T(8,128)(2,1)S(1)}, u32[]{:S(2)}, u32[]{:S(2)}) collective-permute-start(bf16[256,768]{0,1:T(8,128)(2,1)S(1)} %get-tuple-element.132), channel_id=1, source_target_pairs={{0,4},{4,8},{8,12},{12,0},{1,5},{5,9},{9,13},{13,1},{2,6},{6,10},{... | collective-permute-start | bytes 1179656 | tf_op jit(solution)/shard_map/ppermute | solution.py:95
  73.1 27.2 %collective-permute-start.12 = (bf16[256,768]{0,1:T(8,128)(2,1)S(1)}, bf16[256,768]{0,1:T(8,128)(2,1)S(1)}, u32[]{:S(2)}, u32[]{:S(2)}) collective-permute-start(bf16[256,768]{0,1:T(8,128)(2,1)S(1)} %get-tuple-element.132), channel_id=1, source_target_pairs={{0,8},{4,12},{8,0},{12,4},{1,9},{5,13},{9,1},{13,5},{2,10},{6,14},... | collective-permute-start | bytes 1179656 | tf_op jit(solution)/shard_map/ppermute | solution.py:95
  73.1 27.2 %collective-permute-start.13 = (bf16[256,768]{0,1:T(8,128)(2,1)S(1)}, bf16[256,768]{0,1:T(8,128)(2,1)S(1)}, u32[]{:S(2)}, u32[]{:S(2)}) collective-permute-start(bf16[256,768]{0,1:T(8,128)(2,1)S(1)} %get-tuple-element.132), channel_id=1, source_target_pairs={{0,12},{4,0},{8,4},{12,8},{1,13},{5,1},{9,5},{13,9},{2,14},{6,2},{... | collective-permute-start | bytes 1179656 | tf_op jit(solution)/shard_map/ppermute | solution.py:95
  75.5 27.7 %collective-permute-start.10 = (bf16[2,192,1536]{2,1,0:T(8,128)(2,1)}, bf16[2,192,1536]{2,1,0:T(8,128)(2,1)}, u32[]{:S(2)}, u32[]{:S(2)}) collective-permute-start(bf16[2,192,1536]{2,1,0:T(8,128)(2,1)} %get-tuple-element.112), channel_id=1, source_target_pairs={{0,2},{1,3},{2,0},{3,1},{4,6},{5,7},{6,4},{7,5},{8,10},{9,11},{10,... | collective-permute-start | bytes 3538952 | tf_op jit(solution)/shard_map/ppermute | solution.py:85
  76.9 23.5 %collective-permute-start.16 = (bf16[4,192,192]{2,1,0:T(8,128)(2,1)}, bf16[4,192,192]{2,1,0:T(8,128)(2,1)}, u32[]{:S(2)}, u32[]{:S(2)}) collective-permute-start(bf16[4,192,192]{2,1,0:T(8,128)(2,1)} %collective-permute-done.15.o2), channel_id=1, source_target_pairs={{0,1},{1,0},{2,3},{3,2},{4,5},{5,4},{6,7},{7,6},{8,9},{9,8},{10,11... | collective-permute-start | bytes 884744 | tf_op jit(solution)/shard_map/ppermute | solution.py:85
  103.2 65.1 %collective-permute-start.26 = (bf16[8,192,1536]{2,1,0:T(8,128)(2,1)}, bf16[8,192,1536]{2,1,0:T(8,128)(2,1)}, u32[]{:S(2)}, u32[]{:S(2)}) collective-permute-start(bf16[8,192,1536]{2,1,0:T(8,128)(2,1)} %pad_maximum_fusion.refs_11_), channel_id=1, source_target_pairs={{0,1},{1,0},{2,3},{3,2},{4,5},{5,4},{6,7},{7,6},{8,9},{9,8},{10,11... | collective-permute-start | bytes 14155784 | tf_op jit(solution)/shard_map/ppermute | solution.py:85
  109.2 3.8 collective-permute-start.17
  109.8 5.7 %collective-permute-start.18 = (bf16[192,256]{1,0:T(8,128)(2,1)S(1)}, bf16[192,256]{1,0:T(8,128)(2,1)S(1)}, u32[]{:S(2)}, u32[]{:S(2)}) collective-permute-start(bf16[192,256]{1,0:T(8,128)(2,1)S(1)} %get-tuple-element.286), channel_id=1, source_target_pairs={{0,2},{1,3},{2,0},{3,1},{4,6},{5,7},{6,4},{7,5},{8,10},{9,11},{10,... | collective-permute-start | bytes 294920 | tf_op jit(solution)/shard_map/ppermute | solution.py:85
  110.5 5.1 %collective-permute-start.19 = (bf16[192,256]{1,0:T(8,128)(2,1)S(1)}, bf16[192,256]{1,0:T(8,128)(2,1)S(1)}, u32[]{:S(2)}, u32[]{:S(2)}) collective-permute-start(bf16[192,256]{1,0:T(8,128)(2,1)S(1)} %get-tuple-element.285), channel_id=1, source_target_pairs={{0,3},{1,2},{2,1},{3,0},{4,7},{5,6},{6,5},{7,4},{8,11},{9,10},{10,... | collective-permute-start | bytes 294920 | tf_op jit(solution)/shard_map/ppermute | solution.py:85
  111.5 49.0 %collective-permute-start.24 = (bf16[2,192,1536]{2,1,0:T(8,128)(2,1)}, bf16[2,192,1536]{2,1,0:T(8,128)(2,1)}, u32[]{:S(2)}, u32[]{:S(2)}) collective-permute-start(bf16[2,192,1536]{2,1,0:T(8,128)(2,1)} %collective-permute-done.10.refs_13_), channel_id=1, source_target_pairs={{0,16},{16,0},{1,17},{17,1},{2,18},{18,2},{3,19},{19,3},{4,20},{20... | collective-permute-start | bytes 3538952 | tf_op jit(solution)/shard_map/ppermute | solution.py:886
  115.6 45.0 %collective-permute-start.23 = (bf16[2,192,1536]{2,1,0:T(8,128)(2,1)S(1)}, bf16[2,192,1536]{2,1,0:T(8,128)(2,1)}, u32[]{:S(2)}, u32[]{:S(2)}) collective-permute-start(bf16[2,192,1536]{2,1,0:T(8,128)(2,1)S(1)} %get-tuple-element.123), channel_id=1, source_target_pairs={{0,2},{1,3},{2,0},{3,1},{4,6},{5,7},{6,4},{7,5},{8,10},{9,11},{10,... | collective-permute-start | bytes 3538952 | tf_op jit(solution)/shard_map/ppermute | solution.py:85
  122.3 17.8 %collective-permute-start.20 = (bf16[272,768]{1,0:T(8,128)(2,1)}, bf16[272,768]{1,0:T(8,128)(2,1)S(1)}, u32[]{:S(2)}, u32[]{:S(2)}) collective-permute-start(bf16[272,768]{1,0:T(8,128)(2,1)} %get-tuple-element.128.refs_1_), channel_id=1, source_target_pairs={{0,4},{4,8},{8,12},{12,0},{1,5},{5,9},{9,13},{13,1},{2,6},{6,10},{... | collective-permute-start | bytes 1253384 | tf_op jit(solution)/shard_map/ppermute | solution.py:95
  128.8 29.2 %collective-permute-start.21 = (bf16[272,768]{1,0:T(8,128)(2,1)}, bf16[272,768]{1,0:T(8,128)(2,1)}, u32[]{:S(2)}, u32[]{:S(2)}) collective-permute-start(bf16[272,768]{1,0:T(8,128)(2,1)} %get-tuple-element.128.refs_1_), channel_id=1, source_target_pairs={{0,8},{4,12},{8,0},{12,4},{1,9},{5,13},{9,1},{13,5},{2,10},{6,14},... | collective-permute-start | bytes 1253384 | tf_op jit(solution)/shard_map/ppermute | solution.py:95
  140.1 20.5 %collective-permute-start.22 = (bf16[272,768]{1,0:T(8,128)(2,1)}, bf16[272,768]{1,0:T(8,128)(2,1)}, u32[]{:S(2)}, u32[]{:S(2)}) collective-permute-start(bf16[272,768]{1,0:T(8,128)(2,1)} %get-tuple-element.128.refs_1_), channel_id=1, source_target_pairs={{0,12},{4,0},{8,4},{12,8},{1,13},{5,1},{9,5},{13,9},{2,14},{6,2},{... | collective-permute-start | bytes 1253384 | tf_op jit(solution)/shard_map/ppermute | solution.py:95
  158.0 10.3 %collective-permute-start.27 = (bf16[2,192,1536]{2,1,0:T(8,128)(2,1)}, bf16[2,192,1536]{2,1,0:T(8,128)(2,1)}, u32[]{:S(2)}, u32[]{:S(2)}) collective-permute-start(bf16[2,192,1536]{2,1,0:T(8,128)(2,1)} %collective-permute-done.10.refs_13_), channel_id=1, source_target_pairs={{0,1},{1,0},{2,3},{3,2},{4,5},{5,4},{6,7},{7,6},{8,9},{9,8},{10,11... | collective-permute-start | bytes 3538952 | tf_op jit(solution)/shard_map/ppermute | solution.py:85
  160.6 7.7 %collective-permute-start.25 = (bf16[2,192,1536]{2,1,0:T(8,128)(2,1)}, bf16[2,192,1536]{2,1,0:T(8,128)(2,1)S(1)}, u32[]{:S(2)}, u32[]{:S(2)}) collective-permute-start(bf16[2,192,1536]{2,1,0:T(8,128)(2,1)} %collective-permute-done.24.refs_13_), channel_id=1, source_target_pairs={{0,1},{1,0},{2,3},{3,2},{4,5},{5,4},{6,7},{7,6},{8,9},{9,8},{10,11... | collective-permute-start | bytes 3538952 | tf_op jit(solution)/shard_map/ppermute | solution.py:85
  160.6 7.7 %collective-permute-start.28 = (bf16[2,192,1536]{2,1,0:T(8,128)(2,1)}, bf16[2,192,1536]{2,1,0:T(8,128)(2,1)}, u32[]{:S(2)}, u32[]{:S(2)}) collective-permute-start(bf16[2,192,1536]{2,1,0:T(8,128)(2,1)} %collective-permute-done.23.refs_14_), channel_id=1, source_target_pairs={{0,1},{1,0},{2,3},{3,2},{4,5},{5,4},{6,7},{7,6},{8,9},{9,8},{10,11... | collective-permute-start | bytes 3538952 | tf_op jit(solution)/shard_map/ppermute | solution.py:85
  166.7 33.1 %collective-permute-start.29 = (bf16[2,192,1536]{2,1,0:T(8,128)(2,1)}, bf16[2,192,1536]{2,1,0:T(8,128)(2,1)}, u32[]{:S(2)}, u32[]{:S(2)}) collective-permute-start(bf16[2,192,1536]{2,1,0:T(8,128)(2,1)} %collective-permute-done.23.refs_14_), channel_id=1, source_target_pairs={{0,16},{16,0},{1,17},{17,1},{2,18},{18,2},{3,19},{19,3},{4,20},{20... | collective-permute-start | bytes 3538952 | tf_op jit(solution)/shard_map/ppermute | solution.py:886
  199.9 3.1 collective-permute-start.30
  203.0 37.8 %collective-permute-start.32 = (bf16[2,4,192,1536]{3,2,1,0:T(8,128)(2,1)}, bf16[2,4,192,1536]{3,2,1,0:T(8,128)(2,1)}, u32[]{:S(2)}, u32[]{:S(2)}) collective-permute-start(bf16[2,4,192,1536]{3,2,1,0:T(8,128)(2,1)} %get-tuple-element.152), channel_id=1, source_target_pairs={{0,1},{1,0},{2,3},{3,2},{4,5},{5,4},{6,7},{7,6},{8,9},{9,8},{10,11... | collective-permute-start | bytes 14155784 | tf_op jit(solution)/shard_map/ppermute | solution.py:85
  232.9 23.9 %collective-permute-start.31 = (bf16[272,768]{1,0:T(8,128)(2,1)S(1)}, bf16[272,768]{1,0:T(8,128)(2,1)S(1)}, u32[]{:S(2)}, u32[]{:S(2)}) collective-permute-start(bf16[272,768]{1,0:T(8,128)(2,1)S(1)} %slice_bitcast_fusion.7), channel_id=1, source_target_pairs={{0,12},{4,0},{8,4},{12,8},{1,13},{5,1},{9,5},{13,9},{2,14},{6,2},{... | collective-permute-start | bytes 1253384 | tf_op jit(solution)/shard_map/ppermute | solution.py:95
  256.9 66.0 %collective-permute-start.41 = (bf16[2,4,192,1536]{3,2,1,0:T(8,128)(2,1)}, bf16[2,4,192,1536]{3,2,1,0:T(8,128)(2,1)}, u32[]{:S(2)}, u32[]{:S(2)}) collective-permute-start(bf16[2,4,192,1536]{3,2,1,0:T(8,128)(2,1)} %get-tuple-element.166), channel_id=1, source_target_pairs={{0,1},{1,0},{2,3},{3,2},{4,5},{5,4},{6,7},{7,6},{8,9},{9,8},{10,11... | collective-permute-start | bytes 14155784 | tf_op jit(solution)/shard_map/ppermute | solution.py:85
  258.2 31.1 %collective-permute-start.35 = (bf16[2,192,1536]{2,1,0:T(8,128)(2,1)S(1)}, bf16[2,192,1536]{2,1,0:T(8,128)(2,1)S(1)}, u32[]{:S(2)}, u32[]{:S(2)}) collective-permute-start(bf16[2,192,1536]{2,1,0:T(8,128)(2,1)S(1)} %get-tuple-element.258), channel_id=1, source_target_pairs={{0,2},{1,3},{2,0},{3,1},{4,6},{5,7},{6,4},{7,5},{8,10},{9,11},{10,... | collective-permute-start | bytes 3538952 | tf_op jit(solution)/shard_map/ppermute | solution.py:85
  259.8 29.4 %collective-permute-start.33 = (bf16[272,768]{1,0:T(8,128)(2,1)S(1)}, bf16[272,768]{1,0:T(8,128)(2,1)S(1)}, u32[]{:S(2)}, u32[]{:S(2)}) collective-permute-start(bf16[272,768]{1,0:T(8,128)(2,1)S(1)} %get-tuple-element.260), channel_id=1, source_target_pairs={{0,8},{4,12},{8,0},{12,4},{1,9},{5,13},{9,1},{13,5},{2,10},{6,14},... | collective-permute-start | bytes 1253384 | tf_op jit(solution)/shard_map/ppermute | solution.py:95
  260.4 28.8 %collective-permute-start.34 = (bf16[272,768]{1,0:T(8,128)(2,1)S(1)}, bf16[272,768]{1,0:T(8,128)(2,1)S(1)}, u32[]{:S(2)}, u32[]{:S(2)}) collective-permute-start(bf16[272,768]{1,0:T(8,128)(2,1)S(1)} %get-tuple-element.259), channel_id=1, source_target_pairs={{0,4},{4,8},{8,12},{12,0},{1,5},{5,9},{9,13},{13,1},{2,6},{6,10},{... | collective-permute-start | bytes 1253384 | tf_op jit(solution)/shard_map/ppermute | solution.py:95
  260.8 51.6 %collective-permute-start.39 = (bf16[2,192,1536]{2,1,0:T(8,128)(2,1)}, bf16[2,192,1536]{2,1,0:T(8,128)(2,1)}, u32[]{:S(2)}, u32[]{:S(2)}) collective-permute-start(bf16[2,192,1536]{2,1,0:T(8,128)(2,1)} %get-tuple-element.257), channel_id=1, source_target_pairs={{0,2},{1,3},{2,0},{3,1},{4,6},{5,7},{6,4},{7,5},{8,10},{9,11},{10,... | collective-permute-start | bytes 3538952 | tf_op jit(solution)/shard_map/ppermute | solution.py:85
  290.6 32.3 %collective-permute-start.40 = (bf16[2,192,1536]{2,1,0:T(8,128)(2,1)}, bf16[2,192,1536]{2,1,0:T(8,128)(2,1)}, u32[]{:S(2)}, u32[]{:S(2)}) collective-permute-start(bf16[2,192,1536]{2,1,0:T(8,128)(2,1)} %add_convert_fusion.5), channel_id=1, source_target_pairs={{0,16},{16,0},{1,17},{17,1},{2,18},{18,2},{3,19},{19,3},{4,20},{20... | collective-permute-start | bytes 3538952 | tf_op jit(solution)/shard_map/ppermute | solution.py:886
  302.7 17.6 %collective-permute-start.37 = (bf16[768,256]{1,0:T(8,128)(2,1)}, bf16[768,256]{1,0:T(8,128)(2,1)S(1)}, u32[]{:S(2)}, u32[]{:S(2)}) collective-permute-start(bf16[768,256]{1,0:T(8,128)(2,1)} %get-tuple-element.167.d0), channel_id=1, source_target_pairs={{0,2},{1,3},{2,0},{3,1},{4,6},{5,7},{6,4},{7,5},{8,10},{9,11},{10,... | collective-permute-start | bytes 1179656 | tf_op jit(solution)/shard_map/ppermute | solution.py:85
  303.8 18.2 %collective-permute-start.36 = (bf16[768,256]{1,0:T(8,128)(2,1)}, bf16[768,256]{1,0:T(8,128)(2,1)S(1)}, u32[]{:S(2)}, u32[]{:S(2)}) collective-permute-start(bf16[768,256]{1,0:T(8,128)(2,1)} %get-tuple-element.167.d0), channel_id=1, source_target_pairs={{0,1},{1,0},{2,3},{3,2},{4,5},{5,4},{6,7},{7,6},{8,9},{9,8},{10,11... | collective-permute-start | bytes 1179656 | tf_op jit(solution)/shard_map/ppermute | solution.py:85
  312.4 47.6 %collective-permute-start.42 = (bf16[256,768]{1,0:T(8,128)(2,1)}, bf16[256,768]{1,0:T(8,128)(2,1)S(1)}, u32[]{:S(2)}, u32[]{:S(2)}) collective-permute-start(bf16[256,768]{1,0:T(8,128)(2,1)} %get-tuple-element.267), channel_id=1, source_target_pairs={{0,12},{4,0},{8,4},{12,8},{1,13},{5,1},{9,5},{13,9},{2,14},{6,2},{... | collective-permute-start | bytes 1179656 | tf_op jit(solution)/shard_map/ppermute | solution.py:95
  320.3 2.3 collective-permute-start.38
  322.0 38.0 %collective-permute-start.43 = (bf16[256,768]{1,0:T(8,128)(2,1)}, bf16[256,768]{1,0:T(8,128)(2,1)}, u32[]{:S(2)}, u32[]{:S(2)}) collective-permute-start(bf16[256,768]{1,0:T(8,128)(2,1)} %get-tuple-element.266), channel_id=1, source_target_pairs={{0,8},{4,12},{8,0},{12,4},{1,9},{5,13},{9,1},{13,5},{2,10},{6,14},... | collective-permute-start | bytes 1179656 | tf_op jit(solution)/shard_map/ppermute | solution.py:95
  322.5 37.5 %collective-permute-start.44 = (bf16[256,768]{1,0:T(8,128)(2,1)}, bf16[256,768]{1,0:T(8,128)(2,1)}, u32[]{:S(2)}, u32[]{:S(2)}) collective-permute-start(bf16[256,768]{1,0:T(8,128)(2,1)} %get-tuple-element.265), channel_id=1, source_target_pairs={{0,4},{4,8},{8,12},{12,0},{1,5},{5,9},{9,13},{13,1},{2,6},{6,10},{... | collective-permute-start | bytes 1179656 | tf_op jit(solution)/shard_map/ppermute | solution.py:95
  330.2 29.8 %collective-permute-start.46 = (bf16[2,192,1536]{2,1,0:T(8,128)(2,1)}, bf16[2,192,1536]{2,1,0:T(8,128)(2,1)}, u32[]{:S(2)}, u32[]{:S(2)}) collective-permute-start(bf16[2,192,1536]{2,1,0:T(8,128)(2,1)} %slice_bitcast_fusion.2), channel_id=1, source_target_pairs={{0,2},{1,3},{2,0},{3,1},{4,6},{5,7},{6,4},{7,5},{8,10},{9,11},{10,... | collective-permute-start | bytes 3538952 | tf_op jit(solution)/shard_map/ppermute | solution.py:85
  331.1 31.4 %collective-permute-start.45 = (bf16[2,192,1536]{2,1,0:T(8,128)(2,1)S(1)}, bf16[2,192,1536]{2,1,0:T(8,128)(2,1)}, u32[]{:S(2)}, u32[]{:S(2)}) collective-permute-start(bf16[2,192,1536]{2,1,0:T(8,128)(2,1)S(1)} %add_convert_fusion.4), channel_id=1, source_target_pairs={{0,16},{16,0},{1,17},{17,1},{2,18},{18,2},{3,19},{19,3},{4,20},{20... | collective-permute-start | bytes 3538952 | tf_op jit(solution)/shard_map/ppermute | solution.py:886
  365.1 27.4 %collective-permute-start.48 = (bf16[2,192,1536]{2,1,0:T(8,128)(2,1)}, bf16[2,192,1536]{2,1,0:T(8,128)(2,1)}, u32[]{:S(2)}, u32[]{:S(2)}) collective-permute-start(bf16[2,192,1536]{2,1,0:T(8,128)(2,1)} %fusion.3), channel_id=1, source_target_pairs={{0,16},{16,0},{1,17},{17,1},{2,18},{18,2},{3,19},{19,3},{4,20},{20... | collective-permute-start | bytes 3538952 | tf_op jit(solution)/shard_map/ppermute | solution.py:886
  367.9 27.1 %collective-permute-start.47 = (bf16[2,192,1536]{2,1,0:T(8,128)(2,1)}, bf16[2,192,1536]{2,1,0:T(8,128)(2,1)}, u32[]{:S(2)}, u32[]{:S(2)}) collective-permute-start(bf16[2,192,1536]{2,1,0:T(8,128)(2,1)} %slice.353), channel_id=1, source_target_pairs={{0,2},{1,3},{2,0},{3,1},{4,6},{5,7},{6,4},{7,5},{8,10},{9,11},{10,... | collective-permute-start | bytes 3538952 | tf_op jit(solution)/shard_map/ppermute | solution.py:85
  397.5 85.1 %collective-permute-start.62 = (bf16[2,192,1536]{2,1,0:T(8,128)(2,1)}, bf16[2,192,1536]{2,1,0:T(8,128)(2,1)}, u32[]{:S(2)}, u32[]{:S(2)}) collective-permute-start(bf16[2,192,1536]{2,1,0:T(8,128)(2,1)} %fusion.2), channel_id=1, source_target_pairs={{0,16},{16,0},{1,17},{17,1},{2,18},{18,2},{3,19},{19,3},{4,20},{20... | collective-permute-start | bytes 3538952 | tf_op jit(solution)/shard_map/ppermute | solution.py:886
  399.0 29.1 %collective-permute-start.55 = (bf16[192,896]{1,0:T(8,128)(2,1)}, bf16[192,896]{1,0:T(8,128)(2,1)}, u32[]{:S(2)}, u32[]{:S(2)}) collective-permute-start(bf16[192,896]{1,0:T(8,128)(2,1)} %get-tuple-element.269), channel_id=1, source_target_pairs={{0,0},{1,4},{2,8},{3,12},{4,1},{5,5},{6,9},{7,13},{8,2},{9,6},{10,... | collective-permute-start | bytes 1032200 | tf_op jit(solution)/shard_map/ppermute | solution.py:883
  403.4 2.9 collective-permute-start.49
  403.5 11.2 %collective-permute-start.50 = (f32[208,256]{1,0:T(8,128)S(1)}, f32[208,256]{1,0:T(8,128)S(1)}, u32[]{:S(2)}, u32[]{:S(2)}) collective-permute-start(f32[208,256]{1,0:T(8,128)S(1)} %get-tuple-element.279), channel_id=1, source_target_pairs={{0,2},{1,3},{2,0},{3,1},{4,6},{5,7},{6,4},{7,5},{8,10},{9,11},{10,... | collective-permute-start | bytes 638984 | tf_op jit(solution)/shard_map/ppermute | solution.py:85
  405.3 19.2 %collective-permute-start.51 = (f32[208,256]{1,0:T(8,128)S(1)}, f32[208,256]{1,0:T(8,128)S(1)}, u32[]{:S(2)}, u32[]{:S(2)}) collective-permute-start(f32[208,256]{1,0:T(8,128)S(1)} %get-tuple-element.278), channel_id=1, source_target_pairs={{0,3},{1,2},{2,1},{3,0},{4,7},{5,6},{6,5},{7,4},{8,11},{9,10},{10,... | collective-permute-start | bytes 638984 | tf_op jit(solution)/shard_map/ppermute | solution.py:85
  406.4 22.5 %collective-permute-start.56 = (bf16[192,896]{1,0:T(8,128)(2,1)}, bf16[192,896]{1,0:T(8,128)(2,1)}, u32[]{:S(2)}, u32[]{:S(2)}) collective-permute-start(bf16[192,896]{1,0:T(8,128)(2,1)} %get-tuple-element.272), channel_id=1, source_target_pairs={{0,1},{1,5},{2,9},{3,13},{4,0},{5,4},{6,8},{7,12},{8,3},{9,7},{10,... | collective-permute-start | bytes 1032200 | tf_op jit(solution)/shard_map/ppermute | solution.py:883
  414.7 41.2 %collective-permute-start.57 = (bf16[192,896]{1,0:T(8,128)(2,1)}, bf16[192,896]{1,0:T(8,128)(2,1)}, u32[]{:S(2)}, u32[]{:S(2)}) collective-permute-start(bf16[192,896]{1,0:T(8,128)(2,1)} %get-tuple-element.271), channel_id=1, source_target_pairs={{0,2},{1,6},{2,10},{3,14},{4,3},{5,7},{6,11},{7,15},{8,0},{9,4},{1... | collective-permute-start | bytes 1032200 | tf_op jit(solution)/shard_map/ppermute | solution.py:883
  424.5 31.4 %collective-permute-start.58 = (bf16[192,896]{1,0:T(8,128)(2,1)}, bf16[192,896]{1,0:T(8,128)(2,1)}, u32[]{:S(2)}, u32[]{:S(2)}) collective-permute-start(bf16[192,896]{1,0:T(8,128)(2,1)} %get-tuple-element.270), channel_id=1, source_target_pairs={{0,3},{1,7},{2,11},{3,15},{4,2},{5,6},{6,10},{7,14},{8,1},{9,5},{1... | collective-permute-start | bytes 1032200 | tf_op jit(solution)/shard_map/ppermute | solution.py:883
  428.8 47.2 %collective-permute-start.52 = (bf16[192,1024]{1,0:T(8,128)(2,1)S(1)}, bf16[192,1024]{1,0:T(8,128)(2,1)S(1)}, u32[]{:S(2)}, u32[]{:S(2)}) collective-permute-start(bf16[192,1024]{1,0:T(8,128)(2,1)S(1)} %copy-done.15), channel_id=1, source_target_pairs={{0,1},{1,0},{2,3},{3,2},{4,5},{5,4},{6,7},{7,6},{8,9},{9,8},{10,11... | collective-permute-start | bytes 1179656 | tf_op jit(solution)/shard_map/ppermute | solution.py:85
  429.0 47.1 %collective-permute-start.53 = (bf16[192,1024]{1,0:T(8,128)(2,1)S(1)}, bf16[192,1024]{1,0:T(8,128)(2,1)S(1)}, u32[]{:S(2)}, u32[]{:S(2)}) collective-permute-start(bf16[192,1024]{1,0:T(8,128)(2,1)S(1)} %copy-done.14), channel_id=1, source_target_pairs={{0,2},{1,3},{2,0},{3,1},{4,6},{5,7},{6,4},{7,5},{8,10},{9,11},{10,... | collective-permute-start | bytes 1179656 | tf_op jit(solution)/shard_map/ppermute | solution.py:85
  455.9 20.2 %collective-permute-start.54 = (bf16[192,1024]{1,0:T(8,128)(2,1)S(1)}, bf16[192,1024]{1,0:T(8,128)(2,1)S(1)}, u32[]{:S(2)}, u32[]{:S(2)}) collective-permute-start(bf16[192,1024]{1,0:T(8,128)(2,1)S(1)} %get-tuple-element.263), channel_id=1, source_target_pairs={{0,3},{1,2},{2,1},{3,0},{4,7},{5,6},{6,5},{7,4},{8,11},{9,10},{10,... | collective-permute-start | bytes 1179656 | tf_op jit(solution)/shard_map/ppermute | solution.py:85
  457.5 5.7 %collective-permute-start.59 = (f32[24,192]{0,1:T(8,128)S(1)}, f32[24,192]{0,1:T(8,128)S(1)}, u32[]{:S(2)}, u32[]{:S(2)}) collective-permute-start(f32[24,192]{0,1:T(8,128)S(1)} %fusion.11), channel_id=1, source_target_pairs={{0,4},{4,0},{8,12},{12,8},{1,5},{5,1},{9,13},{13,9},{2,6},{6,2},{1... | collective-permute-start | bytes 55304 | tf_op jit(solution)/shard_map/ppermute | solution.py:90
  463.3 11.4 %collective-permute-start.60 = (f32[24,192]{0,1:T(8,128)S(1)}, f32[24,192]{0,1:T(8,128)S(1)}, u32[]{:S(2)}, u32[]{:S(2)}) collective-permute-start(f32[24,192]{0,1:T(8,128)S(1)} %fusion.36), channel_id=1, source_target_pairs={{0,8},{4,12},{8,0},{12,4},{1,9},{5,13},{9,1},{13,5},{2,10},{6,14},... | collective-permute-start | bytes 55304 | tf_op jit(solution)/shard_map/ppermute | solution.py:90
  474.8 4.9 collective-permute-start.61
  487.7 8.2 %collective-permute-start.63 = (bf16[192,768]{1,0:T(8,128)(2,1)S(1)}, bf16[192,768]{1,0:T(8,128)(2,1)S(1)}, u32[]{:S(2)}, u32[]{:S(2)}) collective-permute-start(bf16[192,768]{1,0:T(8,128)(2,1)S(1)} %slice.555), channel_id=1, source_target_pairs={{0,16},{16,0},{1,17},{17,1},{2,18},{18,2},{3,19},{19,3},{4,20},{20... | collective-permute-start | bytes 884744 | tf_op jit(solution)/shard_map/ppermute | solution.py:116
  (35 other events, 414.6 us)

commit v5 on v4

--- a/solution.py
+++ b/solution.py
@@ -935,6 +935,7 @@
     else:
         far_two_a = col_swap(own[half : half + pair], 2)
     side = col_swap(after(own, attn), 1)
+    parts[1], side = join(parts[1], side)
     mid, in_rows, stats = middle(place, toks, parts, projs, prev_logits.T, routes_t)
     x_rows = row_gather(in_rows)
     three_a = col_swap(after(two_a, parts[1], parts[2], parts[3]), 1)
@@ -969,13 +970,11 @@
     def across_sums(sums):
         return [across_groups(s) for s in sums] if groups == 2 else list(sums)
 
+    dx = row_scatter(dx)
+    near_mine = after(near_mine, dx[1])
     near_kept, near_sent = low_sum(near_mine[0], near_next[0]), low_sum(near_mine[1], near_next[1])
-    dx_first = row_shift(dx[1], -1)
-    dx, dx_first, near_sent, near_kept, far_next = join(
-        dx, dx_first, near_sent, near_kept, far_next
-    )
+    near_sent, near_kept, far_next = join(near_sent, near_kept, far_next)
     near_got = [col_swap(near_sent[:pair], 2), col_swap(near_sent[pair:], 2)]
-    dx = [dx[0], dx_first] + [row_shift(dx[s], -s) for s in range(2, rows)]
     far_next = col_swap(far_next, 1)
     dx, near_got[0] = join(dx, near_got[0])
     near_sum = [low_sum(near_kept[:pair], near_got[0])]
@@ -1004,30 +1003,25 @@
     far_sum = [low_sum(far_kept[:pair], far_got[0])]
     far_other = across_sums(far_sum)
     out = result(place, toks, mid, stats, routes_t, grad_logits, y)
-    tokens_parts, weight_parts, out, far_got[1], far_other[0] = join(
-        tokens_parts, weight_parts, out, far_got[1], far_other[0]
-    )
+    weight_parts, out, far_kept = join(weight_parts, out, far_kept)
+    totals = [collect(weight_parts[m], m) for m in range(rows)]
     far_sum.append(low_sum(far_kept[pair:], far_got[1]))
     far_other += across_sums(far_sum[1:])
-
-    def col_scatter(value):
-        total = value[0].astype(F32)
-        for k in range(1, cols):
-            total = total + col_swap(value[k], k).astype(F32)
-        return total
-
-    total = collect(weight_parts[0], 0).astype(F32)
-    for m in range(1, rows):
-        total = total + collect(weight_parts[m], m).astype(F32)
+    totals[-1] = after(totals[-1], *far_other)
+    out = after(out, far_got[1])
+
+    total = sum(part.astype(F32) for part in totals)
     packed = total[:, 4 * size : 4 * size + 3 * SMALL]
     small = packed[:, :SMALL] + packed[:, SMALL : 2 * SMALL] + packed[:, 2 * SMALL :]
     small = dp_total(row_total(small.T))
-    total, far_other = join(total, far_other)
+    tokens_got = [tokens_parts[0]] + [col_swap(tokens_parts[k], k) for k in range(1, cols)]
+    out = [out[0]] + [col_swap(out[k], k) for k in range(1, cols)]
+    total, tokens_got = join(total, tokens_got)
     total = dp_total(total[:, : 4 * size].astype(BF16))
-    grad_tokens = col_scatter(tokens_parts)
+    grad_tokens = sum(part.astype(F32) for part in tokens_got)
     qkv_sum = jnp.stack([total[:, j * size : (j + 1) * size] for j in range(3)])
     proj_sum = total[:, 3 * size :].T
-    out = jnp.stack([out[0]] + [col_swap(out[k], k) for k in range(1, cols)])
+    out = jnp.stack(out)
     out = jnp.take(out, col ^ jnp.arange(cols), axis=0)
     out = jnp.concatenate([out[i] for i in range(cols)], axis=1)
     if groups == 2:

time: 508 us -> 493 us (0.970)
  other arithmetic: 61.4 us -> 50.4 us
  starting transfers between devices: 108 us -> 97 us
  Pallas kernels: 113 us -> 122 us
    ppermute x34, waiting for transfers between devices: 57.6 us -> 85.3 us  [col_swap(): return lax.ppermute(value, 'col', [(i, i ^ bits) for i in range(count)])]
    convert_element_type x6, other arithmetic: 28.5 us -> 16.1 us  [low_sum(): return (left.astype(F32) + right.astype(F32)).astype(BF16)]
    ppermute x12, starting transfers between devices: 25.4 us -> 37.3 us  [row_shift(): lax.ppermute(value, 'row', [(i, (i + steps) % count) for i in range(count)])]
    ppermute x6, waiting for transfers between devices: 21.4 us -> 9.65 us  [across_groups(): return lax.ppermute(value, 'dp', [(0, 1), (1, 0)])]
    ppermute x34, starting transfers between devices: 30.2 us -> 21 us  [col_swap(): return lax.ppermute(value, 'col', [(i, i ^ bits) for i in range(count)])]
    ppermute x6, starting transfers between devices: 15.8 us -> 6.96 us  [across_groups(): return lax.ppermute(value, 'dp', [(0, 1), (1, 0)])]
    pallas_call x2, Pallas kernels: 59.3 us -> 68.1 us  [run_experts(): pl.pallas_call(body, name='experts', cost_estimate=span_of(36), grid_spec...]
    ppermute x2, waiting for transfers between devices: 8.91 us -> 1.49 us  [row_swap(): return lax.ppermute(value, 'row', [(i, i ^ bits) for i in range(count)])]
  transfers between devices with their start and end apart: 64 -> 64, of which waited for: 24 -> 20; matrix products, arithmetic and copies ran while one was open for 18% -> 17% of each run, Pallas kernels for 23% -> 25%
where the time goes in v5:
time: 493 us; the launch traced here: 487 us
  waiting for transfers between devices  168 us (34%)
  Pallas kernels  122 us (25%)
  starting transfers between devices  97 us (20%)
  other arithmetic  50.4 us (10%)
  local copies, waits for them, and re-layouts  48.2 us (10%)
    ppermute x34, waiting for transfers between devices, col_swap(): return lax.ppermute(value, 'col', [(i, i ^ bits) for i in range(count)])  85.3 us
    pallas_call x2, Pallas kernels, run_experts(): pl.pallas_call(body, name='experts', cost_estimate=span_of(36), grid_spec...  68.1 us
    ppermute x12, waiting for transfers between devices, row_shift(): lax.ppermute(value, 'row', [(i, (i + steps) % count) for i in range(count)])  57.8 us
    ppermute x12, starting transfers between devices, row_shift(): lax.ppermute(value, 'row', [(i, (i + steps) % count) for i in range(count)])  37.3 us
    pallas_call x1, Pallas kernels, attend_back(): pl.pallas_call(attend_back_kernel, name='attend_back', cost_estimate=span...  23.5 us
    ppermute x34, starting transfers between devices, col_swap(): return lax.ppermute(value, 'col', [(i, i ^ bits) for i in range(count)])  21 us
    convert_element_type x6, other arithmetic, low_sum(): return (left.astype(F32) + right.astype(F32)).astype(BF16)  16.1 us
    ppermute x4, starting transfers between devices, spread(): return lax.ppermute(value, ('row', 'col'), pairs)  15.5 us
  transfers between devices with their start and end apart: 64, of which 20 were waited for; matrix products, arithmetic and copies ran while one was open for 17% of the time, Pallas kernels for 25%

profile of v5, /device:TPU:0, one launch (start us, length us, event | category | flops | bytes accessed | tf_op | source)
XLA Modules:
  0.0 486.8 jit_solution(1662050960107843089)
XLA Ops:
  3.7 7.0 %collective-permute-start.6 = (bf16[192,768]{1,0:T(8,128)(2,1)}, bf16[192,768]{1,0:T(8,128)(2,1)}, u32[]{:S(2)}, u32[]{:S(2)}) collective-permute-start(bf16[192,768]{1,0:T(8,128)(2,1)} %pad_maximum_fusion.6), channel_id=1, source_target_pairs={{3,0},{6,1},{9,2},{12,3},{2,4},{7,5},{8,6},{13,7},{1,8},{4,9},{11,... | collective-permute-start | bytes 884744 | tf_op jit(solution)/shard_map/ppermute | solution.py:879
  10.7 2.3 collective-permute-start.5
  12.9 2.5 collective-permute-start.4
  15.5 3.8 collective-permute-start.3
  32.0 2.1 concatenate.21.t0.p0
  34.1 1.9 collective-permute-start.1
  36.0 3.5 pad_maximum_fusion.refs_11_
  39.5 2.9 constant_dynamic-slice_fusion.6
  42.5 3.8 collective-permute-done.1.t2.p2
  47.4 2.3 collective-permute-start.9
  52.7 1.7 collective-permute-start.8
  56.2 9.9 %collective-permute-done.8 = bf16[192,256]{1,0:T(8,128)(2,1)S(1)} collective-permute-done((bf16[192,256]{1,0:T(8,128)(2,1)S(1)}, bf16[192,256]{1,0:T(8,128)(2,1)S(1)}, u32[]{:S(2)}, u32[]{:S(2)}) %collective-permute-start.8) | collective-permute-done | bytes 98336 | tf_op jit(solution)/shard_map/ppermute | solution.py:85
  68.8 3.4 collective-permute-start.12
  73.8 1.7 collective-permute-start.10
  75.5 13.6 %attend.1 = (bf16[4,192,256]{2,1,0:T(8,128)(2,1)}, bf16[192,1024]{1,0:T(8,128)(2,1)}, bf16[192,1024]{1,0:T(8,128)(2,1)}, bf16[4,192,256]{2,1,0:T(8,128)(2,1)}, f32[8,1024]{1,0:T(8,128)}) custom-call(s32[4]{0:T(128)} %pad_add_fusion.place, bf16[192,1152]{1,0:T(8,128)(2,1)} %concatenate.21.t0.p0, bf16[192,1152]{1,0:T(8,128)(2,1)} %collective-permute-done.t1.p1, ...), custom_call_target="tpu_custom_call" | custom-call | flops 15399999488 | bytes 50400000 | tf_op jit(solution)/shard_map/attend/pallas_call | solution.py:204
  89.2 9.3 %collective-permute-done.12 = bf16[256,768]{0,1:T(8,128)(2,1)S(1)} collective-permute-done((bf16[256,768]{0,1:T(8,128)(2,1)S(1)}, bf16[256,768]{0,1:T(8,128)(2,1)S(1)}, u32[]{:S(2)}, u32[]{:S(2)}) %collective-permute-start.12) | collective-permute-done | bytes 393248 | tf_op jit(solution)/shard_map/ppermute | solution.py:95
  98.4 3.2 collective-permute-done.10.refs_13_
  103.7 2.3 reduce-window.6
  106.6 1.7 slice_bitcast_fusion.32
  108.8 1.7 collective-permute-start.19
  110.7 1.9 collective-permute-start.25
  113.7 1.9 collective-permute-done.20.a3
  116.4 5.4 %middle.1 = (f32[768,256]{1,0:T(8,128)}, bf16[272,768]{1,0:T(8,128)(2,1)}, f32[8,256]{1,0:T(8,128)}) custom-call(s32[4]{0:T(128)} %pad_add_fusion.place, bf16[192,1152]{1,0:T(8,128)(2,1)} %concatenate.21.t0.p0, bf16[192,1152]{1,0:T(8,128)(2,1)} %collective-permute-done.t1.p1, bf16[192,1152]{1,0:T(8,128)(2,1)} %collective-permute-done.1.t2.p2, ...), custom_call_target="tpu_custom_call" | custom-call | flops 6600000000 | bytes 21600000 | tf_op jit(solution)/shard_map/middle/pallas_call | solution.py:454
  121.8 5.8 %collective-permute-start.21 = (bf16[272,768]{1,0:T(8,128)(2,1)}, bf16[272,768]{1,0:T(8,128)(2,1)S(1)}, u32[]{:S(2)}, u32[]{:S(2)}) collective-permute-start(bf16[272,768]{1,0:T(8,128)(2,1)} %get-tuple-element.133.refs_1_), channel_id=1, source_target_pairs={{0,4},{4,8},{8,12},{12,0},{1,5},{5,9},{9,13},{13,1},{2,6},{6,10},{... | collective-permute-start | bytes 1253384 | tf_op jit(solution)/shard_map/ppermute | solution.py:95
  127.7 1.8 collective-permute-start.22
  130.8 13.0 %collective-permute-done.24.refs_14_ = bf16[2,192,1536]{2,1,0:T(8,128)(2,1)} collective-permute-done((bf16[2,192,1536]{2,1,0:T(8,128)(2,1)S(1)}, bf16[2,192,1536]{2,1,0:T(8,128)(2,1)}, u32[]{:S(2)}, u32[]{:S(2)}) %collective-permute-start.24) | collective-permute-done | bytes 1179680 | tf_op jit(solution)/shard_map/ppermute | solution.py:85
  143.8 13.9 %collective-permute-done.22.refs_3_ = bf16[272,768]{1,0:T(8,128)(2,1)} collective-permute-done((bf16[272,768]{1,0:T(8,128)(2,1)}, bf16[272,768]{1,0:T(8,128)(2,1)}, u32[]{:S(2)}, u32[]{:S(2)}) %collective-permute-start.22) | collective-permute-done | bytes 417824 | tf_op jit(solution)/shard_map/ppermute | solution.py:95
  163.8 1.8 collective-permute-start.29
  165.7 31.5 %experts.2 = (f32[1024,768]{1,0:T(8,128)}, f32[1024,768]{1,0:T(8,128)}, f32[8,1024]{1,0:T(8,128)}, bf16[2,4,192,1536]{3,2,1,0:T(8,128)(2,1)}, bf16[2,4,192,1536]{3,2,1,0:T(8,128)(2,1)}) custom-call(s32[8]{0:T(128)} %pad_add_fusion.2.refs_0_, bf16[272,768]{1,0:T(8,128)(2,1)} %get-tuple-element.133.refs_1_, bf16[272,768]{1,0:T(8,128)(2,1)} %copy-done.22, ...), custom_call_target="tpu_custom_call" | custom-call | flops 39600001024 | bytes 129600000 | tf_op jit(solution)/shard_map/experts/pallas_call | solution.py:820
  197.3 3.0 collective-permute-done.30.refs_16_
  201.4 36.6 %experts.3 = (bf16[4,256,768]{2,1,0:T(8,128)(2,1)}, bf16[4,272,768]{2,1,0:T(8,128)(2,1)}, bf16[2,4,192,1536]{3,2,1,0:T(8,128)(2,1)}, bf16[2,4,192,1536]{3,2,1,0:T(8,128)(2,1)}) custom-call(s32[8]{0:T(128)} %pad_add_fusion.1.refs_0_, bf16[272,768]{1,0:T(8,128)(2,1)} %get-tuple-element.133.refs_1_, bf16[272,768]{1,0:T(8,128)(2,1)} %copy-done.22, ...), custom_call_target="tpu_custom_call" | custom-call | flops 39600001024 | bytes 129600000 | tf_op jit(solution)/shard_map/experts/pallas_call | solution.py:820
  238.0 2.2 slice_bitcast_fusion.3
  240.2 10.3 %collective-permute-start.31 = (bf16[272,768]{1,0:T(8,128)(2,1)S(1)}, bf16[272,768]{1,0:T(8,128)(2,1)S(1)}, u32[]{:S(2)}, u32[]{:S(2)}) collective-permute-start(bf16[272,768]{1,0:T(8,128)(2,1)S(1)} %get-tuple-element.267), channel_id=1, source_target_pairs={{0,12},{4,0},{8,4},{12,8},{1,13},{5,1},{9,5},{13,9},{2,14},{6,2},{... | collective-permute-start | bytes 1253384 | tf_op jit(solution)/shard_map/ppermute | solution.py:95
  250.5 9.5 %collective-permute-done.31.x1 = bf16[272,768]{1,0:T(8,128)(2,1)S(1)} collective-permute-done((bf16[272,768]{1,0:T(8,128)(2,1)S(1)}, bf16[272,768]{1,0:T(8,128)(2,1)S(1)}, u32[]{:S(2)}, u32[]{:S(2)}) %collective-permute-start.31) | collective-permute-done | bytes 417824 | tf_op jit(solution)/shard_map/ppermute | solution.py:95
  260.1 4.5 fusion.1
  268.0 3.5 collective-permute-start.33
  272.4 25.1 %collective-permute-done.32.x2 = bf16[272,768]{1,0:T(8,128)(2,1)S(1)} collective-permute-done((bf16[272,768]{1,0:T(8,128)(2,1)S(1)}, bf16[272,768]{1,0:T(8,128)(2,1)S(1)}, u32[]{:S(2)}, u32[]{:S(2)}) %collective-permute-start.32) | collective-permute-done | bytes 417824 | tf_op jit(solution)/shard_map/ppermute | solution.py:95
  298.8 6.7 %middle_back.1 = (bf16[768,256]{1,0:T(8,128)(2,1)}, f32[768,256]{1,0:T(8,128)}, f32[12,256]{1,0:T(8,128)}, f32[4,24,192]{2,1,0:T(8,128)}) custom-call(s32[4]{0:T(128)} %pad_add_fusion.place, bf16[192,1152]{1,0:T(8,128)(2,1)} %concatenate.21.t0.p0, bf16[192,1152]{1,0:T(8,128)(2,1)} %collective-permute-done.t1.p1, ...), custom_call_target="tpu_custom_call" | custom-call | flops 7699999744 | bytes 25200000 | tf_op jit(solution)/shard_map/middle_back/pallas_call | solution.py:575
  306.6 2.5 slice_bitcast_fusion.11
  309.1 10.9 %collective-permute-done.39 = bf16[2,192,1536]{2,1,0:T(8,128)(2,1)S(1)} collective-permute-done((bf16[2,192,1536]{2,1,0:T(8,128)(2,1)}, bf16[2,192,1536]{2,1,0:T(8,128)(2,1)S(1)}, u32[]{:S(2)}, u32[]{:S(2)}) %collective-permute-start.39) | collective-permute-done | bytes 1179680 | tf_op jit(solution)/shard_map/ppermute | solution.py:85
  320.0 3.9 collective-permute-start.42
  324.0 4.1 collective-permute-done.37.d2
  330.7 3.7 collective-permute-start.44
  334.5 4.4 add_convert_fusion
  342.5 23.5 %attend_back.1 = (bf16[4,192,1024]{2,1,0:T(8,128)(2,1)}, bf16[4,192,896]{2,1,0:T(8,128)(2,1)}) custom-call(s32[4]{0:T(128)} %pad_add_fusion.place, bf16[192,1152]{1,0:T(8,128)(2,1)} %concatenate.21.t0.p0, bf16[192,1152]{1,0:T(8,128)(2,1)} %collective-permute-done.t1.p1, bf16[192,1152]{1,0:T(8,128)(2,1)} %collective-permute-done.1.t2.p2, ...), custom_call_target="tpu_custom_call" | custom-call | flops 26400000000 | bytes 86400000 | tf_op jit(solution)/shard_map/attend_back/pallas_call | solution.py:354
  366.0 3.5 collective-permute-done.46
  369.5 2.4 slice.354
  373.0 4.4 result.1
  377.4 1.7 fusion.2
  379.1 1.8 collective-permute-start.55
  383.4 18.1 %collective-permute-done.47 = bf16[2,192,1536]{2,1,0:T(8,128)(2,1)} collective-permute-done((bf16[2,192,1536]{2,1,0:T(8,128)(2,1)}, bf16[2,192,1536]{2,1,0:T(8,128)(2,1)}, u32[]{:S(2)}, u32[]{:S(2)}) %collective-permute-start.47) | collective-permute-done | bytes 1179680 | tf_op jit(solution)/shard_map/ppermute | solution.py:85
  401.9 2.2 collective-permute-start.49
  404.2 2.6 add_convert_fusion.4
  414.6 1.8 collective-permute-start.53
  416.4 2.5 collective-permute-start.52
  418.9 4.3 collective-permute-start.51
  425.9 9.6 %collective-permute-done.56 = bf16[2,192,1536]{2,1,0:T(8,128)(2,1)} collective-permute-done((bf16[2,192,1536]{2,1,0:T(8,128)(2,1)}, bf16[2,192,1536]{2,1,0:T(8,128)(2,1)}, u32[]{:S(2)}, u32[]{:S(2)}) %collective-permute-start.56) | collective-permute-done | bytes 1179680 | tf_op jit(solution)/shard_map/ppermute | solution.py:886
  436.8 11.3 %collective-permute-done.53 = bf16[192,896]{1,0:T(8,128)(2,1)} collective-permute-done((bf16[192,896]{1,0:T(8,128)(2,1)}, bf16[192,896]{1,0:T(8,128)(2,1)}, u32[]{:S(2)}, u32[]{:S(2)}) %collective-permute-start.53) | collective-permute-done | bytes 344096 | tf_op jit(solution)/shard_map/ppermute | solution.py:883
  449.8 12.6 %collective-permute-done.59 = bf16[192,1024]{1,0:T(8,128)(2,1)S(1)} collective-permute-done((bf16[192,1024]{1,0:T(8,128)(2,1)S(1)}, bf16[192,1024]{1,0:T(8,128)(2,1)S(1)}, u32[]{:S(2)}, u32[]{:S(2)}) %collective-permute-start.59) | collective-permute-done | bytes 393248 | tf_op jit(solution)/shard_map/ppermute | solution.py:85
  462.4 2.7 collective-permute-start.60
  466.1 2.7 add_dynamic-update-slice_fusion.1
  468.9 2.4 collective-permute-start.61
  471.3 3.2 add_dynamic-update-slice_fusion
  478.5 2.2 collective-permute-done.62
  (261 shorter events, 81.0 us)
Async XLA Ops:
  3.7 43.8 %collective-permute-start.6 = (bf16[192,768]{1,0:T(8,128)(2,1)}, bf16[192,768]{1,0:T(8,128)(2,1)}, u32[]{:S(2)}, u32[]{:S(2)}) collective-permute-start(bf16[192,768]{1,0:T(8,128)(2,1)} %pad_maximum_fusion.6), channel_id=1, source_target_pairs={{3,0},{6,1},{9,2},{12,3},{2,4},{7,5},{8,6},{13,7},{1,8},{4,9},{11,... | collective-permute-start | bytes 884744 | tf_op jit(solution)/shard_map/ppermute | solution.py:879
  10.7 39.1 %collective-permute-start.5 = (bf16[192,768]{1,0:T(8,128)(2,1)}, bf16[192,768]{1,0:T(8,128)(2,1)}, u32[]{:S(2)}, u32[]{:S(2)}) collective-permute-start(bf16[192,768]{1,0:T(8,128)(2,1)} %pad_maximum_fusion.6), channel_id=1, source_target_pairs={{2,0},{7,1},{8,2},{13,3},{3,4},{6,5},{9,6},{12,7},{0,8},{5,9},{10,... | collective-permute-start | bytes 884744 | tf_op jit(solution)/shard_map/ppermute | solution.py:879
  12.9 36.8 %collective-permute-start.4 = (bf16[192,768]{1,0:T(8,128)(2,1)}, bf16[192,768]{1,0:T(8,128)(2,1)}, u32[]{:S(2)}, u32[]{:S(2)}) collective-permute-start(bf16[192,768]{1,0:T(8,128)(2,1)} %pad_maximum_fusion.6), channel_id=1, source_target_pairs={{1,0},{4,1},{11,2},{14,3},{0,4},{5,5},{10,6},{15,7},{3,8},{6,9},{9... | collective-permute-start | bytes 884744 | tf_op jit(solution)/shard_map/ppermute | solution.py:879
  15.5 34.3 %collective-permute-start.3 = (bf16[192,768]{1,0:T(8,128)(2,1)}, bf16[192,768]{1,0:T(8,128)(2,1)}, u32[]{:S(2)}, u32[]{:S(2)}) collective-permute-start(bf16[192,768]{1,0:T(8,128)(2,1)} %pad_maximum_fusion.6), channel_id=1, source_target_pairs={{0,0},{5,1},{10,2},{15,3},{1,4},{4,5},{11,6},{14,7},{2,8},{7,9},{8... | collective-permute-start | bytes 884744 | tf_op jit(solution)/shard_map/ppermute | solution.py:879
  34.1 12.2 %collective-permute-start.1 = (bf16[192,1152]{1,0:T(8,128)(2,1)}, bf16[192,1152]{1,0:T(8,128)(2,1)}, u32[]{:S(2)}, u32[]{:S(2)}) collective-permute-start(bf16[192,1152]{1,0:T(8,128)(2,1)} %concatenate.21.t0.p0), channel_id=1, source_target_pairs={{0,2},{1,3},{2,0},{3,1},{4,6},{5,7},{6,4},{7,5},{8,10},{9,11},{10,... | collective-permute-start | bytes 1327112 | tf_op jit(solution)/shard_map/ppermute | solution.py:85
  46.3 22.5 %collective-permute-start = (bf16[192,1152]{1,0:T(8,128)(2,1)S(1)}, bf16[192,1152]{1,0:T(8,128)(2,1)}, u32[]{:S(2)}, u32[]{:S(2)}) collective-permute-start(bf16[192,1152]{1,0:T(8,128)(2,1)S(1)} %copy-done.12), channel_id=1, source_target_pairs={{0,1},{1,0},{2,3},{3,2},{4,5},{5,4},{6,7},{7,6},{8,9},{9,8},{10,11... | collective-permute-start | bytes 1327112 | tf_op jit(solution)/shard_map/ppermute | solution.py:85
  47.4 6.9 %collective-permute-start.9 = (bf16[192,256]{1,0:T(8,128)(2,1)S(1)}, bf16[192,256]{1,0:T(8,128)(2,1)S(1)}, u32[]{:S(2)}, u32[]{:S(2)}) collective-permute-start(bf16[192,256]{1,0:T(8,128)(2,1)S(1)} %bitcast.173), channel_id=1, source_target_pairs={{0,3},{1,2},{2,1},{3,0},{4,7},{5,6},{6,5},{7,4},{8,11},{9,10},{10,... | collective-permute-start | bytes 294920 | tf_op jit(solution)/shard_map/ppermute | solution.py:85
  52.2 19.9 %collective-permute-start.14 = (bf16[4,192,192]{2,1,0:T(8,128)(2,1)}, bf16[4,192,192]{2,1,0:T(8,128)(2,1)}, u32[]{:S(2)}, u32[]{:S(2)}) collective-permute-start(bf16[4,192,192]{2,1,0:T(8,128)(2,1)} %slice.418.o0), channel_id=1, source_target_pairs={{0,1},{1,0},{2,3},{3,2},{4,5},{5,4},{6,7},{7,6},{8,9},{9,8},{10,11... | collective-permute-start | bytes 884744 | tf_op jit(solution)/shard_map/ppermute | solution.py:85
  52.2 21.5 %collective-permute-start.15 = (bf16[4,192,192]{2,1,0:T(8,128)(2,1)}, bf16[4,192,192]{2,1,0:T(8,128)(2,1)}, u32[]{:S(2)}, u32[]{:S(2)}) collective-permute-start(bf16[4,192,192]{2,1,0:T(8,128)(2,1)} %slice.418.o0), channel_id=1, source_target_pairs={{0,2},{1,3},{2,0},{3,1},{4,6},{5,7},{6,4},{7,5},{8,10},{9,11},{10,... | collective-permute-start | bytes 884744 | tf_op jit(solution)/shard_map/ppermute | solution.py:85
  52.7 13.4 %collective-permute-start.8 = (bf16[192,256]{1,0:T(8,128)(2,1)S(1)}, bf16[192,256]{1,0:T(8,128)(2,1)S(1)}, u32[]{:S(2)}, u32[]{:S(2)}) collective-permute-start(bf16[192,256]{1,0:T(8,128)(2,1)S(1)} %bitcast.174), channel_id=1, source_target_pairs={{0,2},{1,3},{2,0},{3,1},{4,6},{5,7},{6,4},{7,5},{8,10},{9,11},{10,... | collective-permute-start | bytes 294920 | tf_op jit(solution)/shard_map/ppermute | solution.py:85
  54.3 21.2 %collective-permute-start.2 = (bf16[192,1152]{1,0:T(8,128)(2,1)}, bf16[192,1152]{1,0:T(8,128)(2,1)}, u32[]{:S(2)}, u32[]{:S(2)}) collective-permute-start(bf16[192,1152]{1,0:T(8,128)(2,1)} %collective-permute-done.1.t2.p2), channel_id=1, source_target_pairs={{0,1},{1,0},{2,3},{3,2},{4,5},{5,4},{6,7},{7,6},{8,9},{9,8},{10,11... | collective-permute-start | bytes 1327112 | tf_op jit(solution)/shard_map/ppermute | solution.py:85
  66.1 1.3 collective-permute-start.7
  68.2 21.0 %collective-permute-start.11 = (bf16[256,768]{0,1:T(8,128)(2,1)S(1)}, bf16[256,768]{0,1:T(8,128)(2,1)S(1)}, u32[]{:S(2)}, u32[]{:S(2)}) collective-permute-start(bf16[256,768]{0,1:T(8,128)(2,1)S(1)} %get-tuple-element.137), channel_id=1, source_target_pairs={{0,4},{4,8},{8,12},{12,0},{1,5},{5,9},{9,13},{13,1},{2,6},{6,10},{... | collective-permute-start | bytes 1179656 | tf_op jit(solution)/shard_map/ppermute | solution.py:95
  68.8 29.6 %collective-permute-start.12 = (bf16[256,768]{0,1:T(8,128)(2,1)S(1)}, bf16[256,768]{0,1:T(8,128)(2,1)S(1)}, u32[]{:S(2)}, u32[]{:S(2)}) collective-permute-start(bf16[256,768]{0,1:T(8,128)(2,1)S(1)} %get-tuple-element.137), channel_id=1, source_target_pairs={{0,8},{4,12},{8,0},{12,4},{1,9},{5,13},{9,1},{13,5},{2,10},{6,14},... | collective-permute-start | bytes 1179656 | tf_op jit(solution)/shard_map/ppermute | solution.py:95
  72.2 26.3 %collective-permute-start.13 = (bf16[256,768]{0,1:T(8,128)(2,1)S(1)}, bf16[256,768]{0,1:T(8,128)(2,1)S(1)}, u32[]{:S(2)}, u32[]{:S(2)}) collective-permute-start(bf16[256,768]{0,1:T(8,128)(2,1)S(1)} %get-tuple-element.137), channel_id=1, source_target_pairs={{0,12},{4,0},{8,4},{12,8},{1,13},{5,1},{9,5},{13,9},{2,14},{6,2},{... | collective-permute-start | bytes 1179656 | tf_op jit(solution)/shard_map/ppermute | solution.py:95
  73.8 27.8 %collective-permute-start.10 = (bf16[2,192,1536]{2,1,0:T(8,128)(2,1)}, bf16[2,192,1536]{2,1,0:T(8,128)(2,1)}, u32[]{:S(2)}, u32[]{:S(2)}) collective-permute-start(bf16[2,192,1536]{2,1,0:T(8,128)(2,1)} %get-tuple-element.115), channel_id=1, source_target_pairs={{0,2},{1,3},{2,0},{3,1},{4,6},{5,7},{6,4},{7,5},{8,10},{9,11},{10,... | collective-permute-start | bytes 3538952 | tf_op jit(solution)/shard_map/ppermute | solution.py:85
  75.5 22.9 %collective-permute-start.16 = (bf16[4,192,192]{2,1,0:T(8,128)(2,1)}, bf16[4,192,192]{2,1,0:T(8,128)(2,1)}, u32[]{:S(2)}, u32[]{:S(2)}) collective-permute-start(bf16[4,192,192]{2,1,0:T(8,128)(2,1)} %collective-permute-done.15.o2), channel_id=1, source_target_pairs={{0,1},{1,0},{2,3},{3,2},{4,5},{5,4},{6,7},{7,6},{8,9},{9,8},{10,11... | collective-permute-start | bytes 884744 | tf_op jit(solution)/shard_map/ppermute | solution.py:85
  101.6 14.8 %collective-permute-start.18 = (bf16[8,192,1536]{2,1,0:T(8,128)(2,1)}, bf16[8,192,1536]{2,1,0:T(8,128)(2,1)}, u32[]{:S(2)}, u32[]{:S(2)}) collective-permute-start(bf16[8,192,1536]{2,1,0:T(8,128)(2,1)} %pad_maximum_fusion.refs_11_), channel_id=1, source_target_pairs={{0,1},{1,0},{2,3},{3,2},{4,5},{5,4},{6,7},{7,6},{8,9},{9,8},{10,11... | collective-permute-start | bytes 14155784 | tf_op jit(solution)/shard_map/ppermute | solution.py:85
  108.3 4.3 collective-permute-start.17
  108.8 4.9 %collective-permute-start.19 = (bf16[192,256]{1,0:T(8,128)(2,1)S(1)}, bf16[192,256]{1,0:T(8,128)(2,1)S(1)}, u32[]{:S(2)}, u32[]{:S(2)}) collective-permute-start(bf16[192,256]{1,0:T(8,128)(2,1)S(1)} %get-tuple-element.294), channel_id=1, source_target_pairs={{0,2},{1,3},{2,0},{3,1},{4,6},{5,7},{6,4},{7,5},{8,10},{9,11},{10,... | collective-permute-start | bytes 294920 | tf_op jit(solution)/shard_map/ppermute | solution.py:85
  110.5 5.1 %collective-permute-start.20 = (bf16[192,256]{1,0:T(8,128)(2,1)S(1)}, bf16[192,256]{1,0:T(8,128)(2,1)S(1)}, u32[]{:S(2)}, u32[]{:S(2)}) collective-permute-start(bf16[192,256]{1,0:T(8,128)(2,1)S(1)} %get-tuple-element.293), channel_id=1, source_target_pairs={{0,3},{1,2},{2,1},{3,0},{4,7},{5,6},{6,5},{7,4},{8,11},{9,10},{10,... | collective-permute-start | bytes 294920 | tf_op jit(solution)/shard_map/ppermute | solution.py:85
  110.7 47.0 %collective-permute-start.25 = (bf16[2,192,1536]{2,1,0:T(8,128)(2,1)}, bf16[2,192,1536]{2,1,0:T(8,128)(2,1)}, u32[]{:S(2)}, u32[]{:S(2)}) collective-permute-start(bf16[2,192,1536]{2,1,0:T(8,128)(2,1)} %collective-permute-done.10.refs_13_), channel_id=1, source_target_pairs={{0,16},{16,0},{1,17},{17,1},{2,18},{18,2},{3,19},{19,3},{4,20},{20... | collective-permute-start | bytes 3538952 | tf_op jit(solution)/shard_map/ppermute | solution.py:886
  115.6 28.2 %collective-permute-start.24 = (bf16[2,192,1536]{2,1,0:T(8,128)(2,1)S(1)}, bf16[2,192,1536]{2,1,0:T(8,128)(2,1)}, u32[]{:S(2)}, u32[]{:S(2)}) collective-permute-start(bf16[2,192,1536]{2,1,0:T(8,128)(2,1)S(1)} %get-tuple-element.128), channel_id=1, source_target_pairs={{0,2},{1,3},{2,0},{3,1},{4,6},{5,7},{6,4},{7,5},{8,10},{9,11},{10,... | collective-permute-start | bytes 3538952 | tf_op jit(solution)/shard_map/ppermute | solution.py:85
  121.8 22.0 %collective-permute-start.21 = (bf16[272,768]{1,0:T(8,128)(2,1)}, bf16[272,768]{1,0:T(8,128)(2,1)S(1)}, u32[]{:S(2)}, u32[]{:S(2)}) collective-permute-start(bf16[272,768]{1,0:T(8,128)(2,1)} %get-tuple-element.133.refs_1_), channel_id=1, source_target_pairs={{0,4},{4,8},{8,12},{12,0},{1,5},{5,9},{9,13},{13,1},{2,6},{6,10},{... | collective-permute-start | bytes 1253384 | tf_op jit(solution)/shard_map/ppermute | solution.py:95
  127.7 30.0 %collective-permute-start.22 = (bf16[272,768]{1,0:T(8,128)(2,1)}, bf16[272,768]{1,0:T(8,128)(2,1)}, u32[]{:S(2)}, u32[]{:S(2)}) collective-permute-start(bf16[272,768]{1,0:T(8,128)(2,1)} %get-tuple-element.133.refs_1_), channel_id=1, source_target_pairs={{0,8},{4,12},{8,0},{12,4},{1,9},{5,13},{9,1},{13,5},{2,10},{6,14},... | collective-permute-start | bytes 1253384 | tf_op jit(solution)/shard_map/ppermute | solution.py:95
  129.4 28.2 %collective-permute-start.23 = (bf16[272,768]{1,0:T(8,128)(2,1)}, bf16[272,768]{1,0:T(8,128)(2,1)}, u32[]{:S(2)}, u32[]{:S(2)}) collective-permute-start(bf16[272,768]{1,0:T(8,128)(2,1)} %get-tuple-element.133.refs_1_), channel_id=1, source_target_pairs={{0,12},{4,0},{8,4},{12,8},{1,13},{5,1},{9,5},{13,9},{2,14},{6,2},{... | collective-permute-start | bytes 1253384 | tf_op jit(solution)/shard_map/ppermute | solution.py:95
  143.8 21.9 %collective-permute-start.27 = (bf16[2,192,1536]{2,1,0:T(8,128)(2,1)}, bf16[2,192,1536]{2,1,0:T(8,128)(2,1)}, u32[]{:S(2)}, u32[]{:S(2)}) collective-permute-start(bf16[2,192,1536]{2,1,0:T(8,128)(2,1)} %collective-permute-done.10.refs_13_), channel_id=1, source_target_pairs={{0,1},{1,0},{2,3},{3,2},{4,5},{5,4},{6,7},{7,6},{8,9},{9,8},{10,11... | collective-permute-start | bytes 3538952 | tf_op jit(solution)/shard_map/ppermute | solution.py:85
  157.7 8.0 %collective-permute-start.26 = (bf16[2,192,1536]{2,1,0:T(8,128)(2,1)}, bf16[2,192,1536]{2,1,0:T(8,128)(2,1)S(1)}, u32[]{:S(2)}, u32[]{:S(2)}) collective-permute-start(bf16[2,192,1536]{2,1,0:T(8,128)(2,1)} %collective-permute-done.25.refs_13_), channel_id=1, source_target_pairs={{0,1},{1,0},{2,3},{3,2},{4,5},{5,4},{6,7},{7,6},{8,9},{9,8},{10,11... | collective-permute-start | bytes 3538952 | tf_op jit(solution)/shard_map/ppermute | solution.py:85
  157.7 7.9 %collective-permute-start.28 = (bf16[2,192,1536]{2,1,0:T(8,128)(2,1)}, bf16[2,192,1536]{2,1,0:T(8,128)(2,1)}, u32[]{:S(2)}, u32[]{:S(2)}) collective-permute-start(bf16[2,192,1536]{2,1,0:T(8,128)(2,1)} %collective-permute-done.24.refs_14_), channel_id=1, source_target_pairs={{0,1},{1,0},{2,3},{3,2},{4,5},{5,4},{6,7},{7,6},{8,9},{9,8},{10,11... | collective-permute-start | bytes 3538952 | tf_op jit(solution)/shard_map/ppermute | solution.py:85
  163.8 33.4 %collective-permute-start.29 = (bf16[2,192,1536]{2,1,0:T(8,128)(2,1)}, bf16[2,192,1536]{2,1,0:T(8,128)(2,1)}, u32[]{:S(2)}, u32[]{:S(2)}) collective-permute-start(bf16[2,192,1536]{2,1,0:T(8,128)(2,1)} %collective-permute-done.24.refs_14_), channel_id=1, source_target_pairs={{0,16},{16,0},{1,17},{17,1},{2,18},{18,2},{3,19},{19,3},{4,20},{20... | collective-permute-start | bytes 3538952 | tf_op jit(solution)/shard_map/ppermute | solution.py:886
  197.2 3.1 collective-permute-start.30
  200.3 59.7 %collective-permute-start.34 = (bf16[2,4,192,1536]{3,2,1,0:T(8,128)(2,1)}, bf16[2,4,192,1536]{3,2,1,0:T(8,128)(2,1)}, u32[]{:S(2)}, u32[]{:S(2)}) collective-permute-start(bf16[2,4,192,1536]{3,2,1,0:T(8,128)(2,1)} %get-tuple-element.158), channel_id=1, source_target_pairs={{0,1},{1,0},{2,3},{3,2},{4,5},{5,4},{6,7},{7,6},{8,9},{9,8},{10,11... | collective-permute-start | bytes 14155784 | tf_op jit(solution)/shard_map/ppermute | solution.py:85
  240.2 19.8 %collective-permute-start.31 = (bf16[272,768]{1,0:T(8,128)(2,1)S(1)}, bf16[272,768]{1,0:T(8,128)(2,1)S(1)}, u32[]{:S(2)}, u32[]{:S(2)}) collective-permute-start(bf16[272,768]{1,0:T(8,128)(2,1)S(1)} %get-tuple-element.267), channel_id=1, source_target_pairs={{0,12},{4,0},{8,4},{12,8},{1,13},{5,1},{9,5},{13,9},{2,14},{6,2},{... | collective-permute-start | bytes 1253384 | tf_op jit(solution)/shard_map/ppermute | solution.py:95
  264.6 69.8 %collective-permute-start.41 = (bf16[2,4,192,1536]{3,2,1,0:T(8,128)(2,1)}, bf16[2,4,192,1536]{3,2,1,0:T(8,128)(2,1)}, u32[]{:S(2)}, u32[]{:S(2)}) collective-permute-start(bf16[2,4,192,1536]{3,2,1,0:T(8,128)(2,1)} %get-tuple-element.170), channel_id=1, source_target_pairs={{0,1},{1,0},{2,3},{3,2},{4,5},{5,4},{6,7},{7,6},{8,9},{9,8},{10,11... | collective-permute-start | bytes 14155784 | tf_op jit(solution)/shard_map/ppermute | solution.py:85
  265.9 31.6 %collective-permute-start.35 = (bf16[2,192,1536]{2,1,0:T(8,128)(2,1)S(1)}, bf16[2,192,1536]{2,1,0:T(8,128)(2,1)S(1)}, u32[]{:S(2)}, u32[]{:S(2)}) collective-permute-start(bf16[2,192,1536]{2,1,0:T(8,128)(2,1)S(1)} %get-tuple-element.264), channel_id=1, source_target_pairs={{0,2},{1,3},{2,0},{3,1},{4,6},{5,7},{6,4},{7,5},{8,10},{9,11},{10,... | collective-permute-start | bytes 3538952 | tf_op jit(solution)/shard_map/ppermute | solution.py:85
  266.9 30.6 %collective-permute-start.32 = (bf16[272,768]{1,0:T(8,128)(2,1)S(1)}, bf16[272,768]{1,0:T(8,128)(2,1)S(1)}, u32[]{:S(2)}, u32[]{:S(2)}) collective-permute-start(bf16[272,768]{1,0:T(8,128)(2,1)S(1)} %get-tuple-element.266), channel_id=1, source_target_pairs={{0,8},{4,12},{8,0},{12,4},{1,9},{5,13},{9,1},{13,5},{2,10},{6,14},... | collective-permute-start | bytes 1253384 | tf_op jit(solution)/shard_map/ppermute | solution.py:95
  268.0 29.5 %collective-permute-start.33 = (bf16[272,768]{1,0:T(8,128)(2,1)S(1)}, bf16[272,768]{1,0:T(8,128)(2,1)S(1)}, u32[]{:S(2)}, u32[]{:S(2)}) collective-permute-start(bf16[272,768]{1,0:T(8,128)(2,1)S(1)} %get-tuple-element.265), channel_id=1, source_target_pairs={{0,4},{4,8},{8,12},{12,0},{1,5},{5,9},{9,13},{13,1},{2,6},{6,10},{... | collective-permute-start | bytes 1253384 | tf_op jit(solution)/shard_map/ppermute | solution.py:95
  271.5 48.5 %collective-permute-start.39 = (bf16[2,192,1536]{2,1,0:T(8,128)(2,1)}, bf16[2,192,1536]{2,1,0:T(8,128)(2,1)S(1)}, u32[]{:S(2)}, u32[]{:S(2)}) collective-permute-start(bf16[2,192,1536]{2,1,0:T(8,128)(2,1)} %get-tuple-element.263), channel_id=1, source_target_pairs={{0,2},{1,3},{2,0},{3,1},{4,6},{5,7},{6,4},{7,5},{8,10},{9,11},{10,... | collective-permute-start | bytes 3538952 | tf_op jit(solution)/shard_map/ppermute | solution.py:85
  298.8 35.6 %collective-permute-start.40 = (bf16[2,192,1536]{2,1,0:T(8,128)(2,1)}, bf16[2,192,1536]{2,1,0:T(8,128)(2,1)}, u32[]{:S(2)}, u32[]{:S(2)}) collective-permute-start(bf16[2,192,1536]{2,1,0:T(8,128)(2,1)} %add_convert_fusion.6), channel_id=1, source_target_pairs={{0,16},{16,0},{1,17},{17,1},{2,18},{18,2},{3,19},{19,3},{4,20},{20... | collective-permute-start | bytes 3538952 | tf_op jit(solution)/shard_map/ppermute | solution.py:886
  305.5 22.6 %collective-permute-start.37 = (bf16[768,256]{1,0:T(8,128)(2,1)}, bf16[768,256]{1,0:T(8,128)(2,1)}, u32[]{:S(2)}, u32[]{:S(2)}) collective-permute-start(bf16[768,256]{1,0:T(8,128)(2,1)} %get-tuple-element.171.d0), channel_id=1, source_target_pairs={{0,2},{1,3},{2,0},{3,1},{4,6},{5,7},{6,4},{7,5},{8,10},{9,11},{10,... | collective-permute-start | bytes 1179656 | tf_op jit(solution)/shard_map/ppermute | solution.py:85
  306.5 23.1 %collective-permute-start.36 = (bf16[768,256]{1,0:T(8,128)(2,1)}, bf16[768,256]{1,0:T(8,128)(2,1)S(1)}, u32[]{:S(2)}, u32[]{:S(2)}) collective-permute-start(bf16[768,256]{1,0:T(8,128)(2,1)} %get-tuple-element.171.d0), channel_id=1, source_target_pairs={{0,1},{1,0},{2,3},{3,2},{4,5},{5,4},{6,7},{7,6},{8,9},{9,8},{10,11... | collective-permute-start | bytes 1179656 | tf_op jit(solution)/shard_map/ppermute | solution.py:85
  320.0 45.9 %collective-permute-start.42 = (bf16[256,768]{1,0:T(8,128)(2,1)}, bf16[256,768]{1,0:T(8,128)(2,1)}, u32[]{:S(2)}, u32[]{:S(2)}) collective-permute-start(bf16[256,768]{1,0:T(8,128)(2,1)} %get-tuple-element.275), channel_id=1, source_target_pairs={{0,12},{4,0},{8,4},{12,8},{1,13},{5,1},{9,5},{13,9},{2,14},{6,2},{... | collective-permute-start | bytes 1179656 | tf_op jit(solution)/shard_map/ppermute | solution.py:95
  328.1 2.6 collective-permute-start.38
  329.7 36.3 %collective-permute-start.43 = (bf16[256,768]{1,0:T(8,128)(2,1)}, bf16[256,768]{1,0:T(8,128)(2,1)S(1)}, u32[]{:S(2)}, u32[]{:S(2)}) collective-permute-start(bf16[256,768]{1,0:T(8,128)(2,1)} %get-tuple-element.274), channel_id=1, source_target_pairs={{0,8},{4,12},{8,0},{12,4},{1,9},{5,13},{9,1},{13,5},{2,10},{6,14},... | collective-permute-start | bytes 1179656 | tf_op jit(solution)/shard_map/ppermute | solution.py:95
  330.7 35.3 %collective-permute-start.44 = (bf16[256,768]{1,0:T(8,128)(2,1)}, bf16[256,768]{1,0:T(8,128)(2,1)}, u32[]{:S(2)}, u32[]{:S(2)}) collective-permute-start(bf16[256,768]{1,0:T(8,128)(2,1)} %get-tuple-element.273), channel_id=1, source_target_pairs={{0,4},{4,8},{8,12},{12,0},{1,5},{5,9},{9,13},{13,1},{2,6},{6,10},{... | collective-permute-start | bytes 1179656 | tf_op jit(solution)/shard_map/ppermute | solution.py:95
  334.4 31.6 %collective-permute-start.45 = (bf16[2,192,1536]{2,1,0:T(8,128)(2,1)S(1)}, bf16[2,192,1536]{2,1,0:T(8,128)(2,1)}, u32[]{:S(2)}, u32[]{:S(2)}) collective-permute-start(bf16[2,192,1536]{2,1,0:T(8,128)(2,1)S(1)} %add_convert_fusion.5), channel_id=1, source_target_pairs={{0,16},{16,0},{1,17},{17,1},{2,18},{18,2},{3,19},{19,3},{4,20},{20... | collective-permute-start | bytes 3538952 | tf_op jit(solution)/shard_map/ppermute | solution.py:886
  341.4 28.1 %collective-permute-start.46 = (bf16[2,192,1536]{2,1,0:T(8,128)(2,1)}, bf16[2,192,1536]{2,1,0:T(8,128)(2,1)}, u32[]{:S(2)}, u32[]{:S(2)}) collective-permute-start(bf16[2,192,1536]{2,1,0:T(8,128)(2,1)} %slice_bitcast_fusion.1), channel_id=1, source_target_pairs={{0,2},{1,3},{2,0},{3,1},{4,6},{5,7},{6,4},{7,5},{8,10},{9,11},{10,... | collective-permute-start | bytes 3538952 | tf_op jit(solution)/shard_map/ppermute | solution.py:85
  371.9 29.6 %collective-permute-start.47 = (bf16[2,192,1536]{2,1,0:T(8,128)(2,1)}, bf16[2,192,1536]{2,1,0:T(8,128)(2,1)}, u32[]{:S(2)}, u32[]{:S(2)}) collective-permute-start(bf16[2,192,1536]{2,1,0:T(8,128)(2,1)} %slice.354), channel_id=1, source_target_pairs={{0,2},{1,3},{2,0},{3,1},{4,6},{5,7},{6,4},{7,5},{8,10},{9,11},{10,... | collective-permute-start | bytes 3538952 | tf_op jit(solution)/shard_map/ppermute | solution.py:85
  379.1 27.7 %collective-permute-start.55 = (bf16[2,192,1536]{2,1,0:T(8,128)(2,1)S(1)}, bf16[2,192,1536]{2,1,0:T(8,128)(2,1)S(1)}, u32[]{:S(2)}, u32[]{:S(2)}) collective-permute-start(bf16[2,192,1536]{2,1,0:T(8,128)(2,1)S(1)} %fusion.2), channel_id=1, source_target_pairs={{0,16},{16,0},{1,17},{17,1},{2,18},{18,2},{3,19},{19,3},{4,20},{20... | collective-permute-start | bytes 3538952 | tf_op jit(solution)/shard_map/ppermute | solution.py:886
  382.0 43.9 %collective-permute-start.54 = (bf16[192,896]{1,0:T(8,128)(2,1)}, bf16[192,896]{1,0:T(8,128)(2,1)}, u32[]{:S(2)}, u32[]{:S(2)}) collective-permute-start(bf16[192,896]{1,0:T(8,128)(2,1)} %get-tuple-element.278), channel_id=1, source_target_pairs={{0,3},{1,7},{2,11},{3,15},{4,2},{5,6},{6,10},{7,14},{8,1},{9,5},{1... | collective-permute-start | bytes 1032200 | tf_op jit(solution)/shard_map/ppermute | solution.py:883
  401.6 13.0 %collective-permute-start.50 = (f32[208,256]{1,0:T(8,128)S(1)}, f32[208,256]{1,0:T(8,128)S(1)}, u32[]{:S(2)}, u32[]{:S(2)}) collective-permute-start(f32[208,256]{1,0:T(8,128)S(1)} %get-tuple-element.286), channel_id=1, source_target_pairs={{0,3},{1,2},{2,1},{3,0},{4,7},{5,6},{6,5},{7,4},{8,11},{9,10},{10,... | collective-permute-start | bytes 638984 | tf_op jit(solution)/shard_map/ppermute | solution.py:85
  401.9 14.4 %collective-permute-start.49 = (f32[208,256]{1,0:T(8,128)S(1)}, f32[208,256]{1,0:T(8,128)S(1)}, u32[]{:S(2)}, u32[]{:S(2)}) collective-permute-start(f32[208,256]{1,0:T(8,128)S(1)} %get-tuple-element.287), channel_id=1, source_target_pairs={{0,2},{1,3},{2,0},{3,1},{4,6},{5,7},{6,4},{7,5},{8,10},{9,11},{10,... | collective-permute-start | bytes 638984 | tf_op jit(solution)/shard_map/ppermute | solution.py:85
  404.2 14.7 %collective-permute-start.48 = (f32[208,256]{1,0:T(8,128)S(1)}, f32[208,256]{1,0:T(8,128)S(1)}, u32[]{:S(2)}, u32[]{:S(2)}) collective-permute-start(f32[208,256]{1,0:T(8,128)S(1)} %get-tuple-element.288), channel_id=1, source_target_pairs={{0,1},{1,0},{2,3},{3,2},{4,5},{5,4},{6,7},{7,6},{8,9},{9,8},{10,11... | collective-permute-start | bytes 638984 | tf_op jit(solution)/shard_map/ppermute | solution.py:85
  406.9 28.7 %collective-permute-start.56 = (bf16[2,192,1536]{2,1,0:T(8,128)(2,1)}, bf16[2,192,1536]{2,1,0:T(8,128)(2,1)}, u32[]{:S(2)}, u32[]{:S(2)}) collective-permute-start(bf16[2,192,1536]{2,1,0:T(8,128)(2,1)} %add_convert_fusion.4), channel_id=1, source_target_pairs={{0,16},{16,0},{1,17},{17,1},{2,18},{18,2},{3,19},{19,3},{4,20},{20... | collective-permute-start | bytes 3538952 | tf_op jit(solution)/shard_map/ppermute | solution.py:886
  414.6 33.5 %collective-permute-start.53 = (bf16[192,896]{1,0:T(8,128)(2,1)}, bf16[192,896]{1,0:T(8,128)(2,1)}, u32[]{:S(2)}, u32[]{:S(2)}) collective-permute-start(bf16[192,896]{1,0:T(8,128)(2,1)} %get-tuple-element.279), channel_id=1, source_target_pairs={{0,2},{1,6},{2,10},{3,14},{4,3},{5,7},{6,11},{7,15},{8,0},{9,4},{1... | collective-permute-start | bytes 1032200 | tf_op jit(solution)/shard_map/ppermute | solution.py:883
  416.4 31.8 %collective-permute-start.52 = (bf16[192,896]{1,0:T(8,128)(2,1)}, bf16[192,896]{1,0:T(8,128)(2,1)}, u32[]{:S(2)}, u32[]{:S(2)}) collective-permute-start(bf16[192,896]{1,0:T(8,128)(2,1)} %get-tuple-element.280), channel_id=1, source_target_pairs={{0,1},{1,5},{2,9},{3,13},{4,0},{5,4},{6,8},{7,12},{8,3},{9,7},{10,... | collective-permute-start | bytes 1032200 | tf_op jit(solution)/shard_map/ppermute | solution.py:883
  418.9 29.2 %collective-permute-start.51 = (bf16[192,896]{1,0:T(8,128)(2,1)}, bf16[192,896]{1,0:T(8,128)(2,1)}, u32[]{:S(2)}, u32[]{:S(2)}) collective-permute-start(bf16[192,896]{1,0:T(8,128)(2,1)} %get-tuple-element.277), channel_id=1, source_target_pairs={{0,0},{1,4},{2,8},{3,12},{4,1},{5,5},{6,9},{7,13},{8,2},{9,6},{10,... | collective-permute-start | bytes 1032200 | tf_op jit(solution)/shard_map/ppermute | solution.py:883
  425.9 23.9 %collective-permute-start.57 = (bf16[192,1024]{1,0:T(8,128)(2,1)S(1)}, bf16[192,1024]{1,0:T(8,128)(2,1)S(1)}, u32[]{:S(2)}, u32[]{:S(2)}) collective-permute-start(bf16[192,1024]{1,0:T(8,128)(2,1)S(1)} %copy-done.15), channel_id=1, source_target_pairs={{0,1},{1,0},{2,3},{3,2},{4,5},{5,4},{6,7},{7,6},{8,9},{9,8},{10,11... | collective-permute-start | bytes 1179656 | tf_op jit(solution)/shard_map/ppermute | solution.py:85
  435.5 14.2 %collective-permute-start.58 = (bf16[192,1024]{1,0:T(8,128)(2,1)S(1)}, bf16[192,1024]{1,0:T(8,128)(2,1)S(1)}, u32[]{:S(2)}, u32[]{:S(2)}) collective-permute-start(bf16[192,1024]{1,0:T(8,128)(2,1)S(1)} %copy-done.14), channel_id=1, source_target_pairs={{0,2},{1,3},{2,0},{3,1},{4,6},{5,7},{6,4},{7,5},{8,10},{9,11},{10,... | collective-permute-start | bytes 1179656 | tf_op jit(solution)/shard_map/ppermute | solution.py:85
  448.1 14.3 %collective-permute-start.59 = (bf16[192,1024]{1,0:T(8,128)(2,1)S(1)}, bf16[192,1024]{1,0:T(8,128)(2,1)S(1)}, u32[]{:S(2)}, u32[]{:S(2)}) collective-permute-start(bf16[192,1024]{1,0:T(8,128)(2,1)S(1)} %copy-done.13), channel_id=1, source_target_pairs={{0,3},{1,2},{2,1},{3,0},{4,7},{5,6},{6,5},{7,4},{8,11},{9,10},{10,... | collective-permute-start | bytes 1179656 | tf_op jit(solution)/shard_map/ppermute | solution.py:85
  462.4 6.4 %collective-permute-start.60 = (f32[24,192]{0,1:T(8,128)S(1)}, f32[24,192]{0,1:T(8,128)S(1)}, u32[]{:S(2)}, u32[]{:S(2)}) collective-permute-start(f32[24,192]{0,1:T(8,128)S(1)} %fusion.7), channel_id=1, source_target_pairs={{0,4},{4,0},{8,12},{12,8},{1,5},{5,1},{9,13},{13,9},{2,6},{6,2},{1... | collective-permute-start | bytes 55304 | tf_op jit(solution)/shard_map/ppermute | solution.py:90
  465.1 18.6 %collective-permute-start.63 = (bf16[192,768]{1,0:T(8,128)(2,1)S(1)}, bf16[192,768]{1,0:T(8,128)(2,1)}, u32[]{:S(2)}, u32[]{:S(2)}) collective-permute-start(bf16[192,768]{1,0:T(8,128)(2,1)S(1)} %slice.557), channel_id=1, source_target_pairs={{0,16},{16,0},{1,17},{17,1},{2,18},{18,2},{3,19},{19,3},{4,20},{20... | collective-permute-start | bytes 884744 | tf_op jit(solution)/shard_map/ppermute | solution.py:116
  468.9 7.0 %collective-permute-start.61 = (f32[24,192]{0,1:T(8,128)S(1)}, f32[24,192]{0,1:T(8,128)S(1)}, u32[]{:S(2)}, u32[]{:S(2)}) collective-permute-start(f32[24,192]{0,1:T(8,128)S(1)} %fusion.32), channel_id=1, source_target_pairs={{0,8},{4,12},{8,0},{12,4},{1,9},{5,13},{9,1},{13,5},{2,10},{6,14},... | collective-permute-start | bytes 55304 | tf_op jit(solution)/shard_map/ppermute | solution.py:90
  476.0 4.7 collective-permute-start.62
  (33 other events, 373.9 us)
